TPU v7x, 32 devices: a whole 2x2x4 slice. The times are simulated.
32 devices in a mesh: section: 2 (over core), dp: 16 (over z, y, x).
Axes of the slice: x: 2, y: 2, z: 4, core: 2. Of those that a mesh axis runs over, the one named last changes fastest.
Arguments:
- pixels: bfloat16 [32, 1024, 192], P('dp'), may hold values from -6 to 6
- visible: int32 [32, 256], P('dp'), may hold values from 0 to 1023, as said below
- masked: int32 [32, 768], P('dp'), may hold values from 0 to 1023
- loss_mask: int32 [32, 768], P('dp'), may hold values 0 or 1
- master: float32 [2, 7225344], P('section', 'dp')
- momentum: float32 [2, 7225344], P('section', 'dp'), may hold values from -5.9604645e-07 to 5.9604645e-07
- vectors: float32 [2, 11520], P('section')
- vec_moment: float32 [2, 11520], P('section'), may hold values from -1.9073486e-06 to 1.9073486e-06
- factors: float32 [2, 8, 7680], P('section'), may hold values from -6 to 6
- errors: bfloat16 [2, 16, 7225344], P('section', 'dp'), may hold values from -0.005859375 to 0.005859375
Outputs:
- new_master: float32 [2, 7225344], P('section', 'dp')
- new_low: bfloat16 [2, 7225344], P('section', 'dp')
- new_moment: float32 [2, 7225344], P('section', 'dp')
- new_vectors: float32 [2, 11520], P('section')
- new_vec_moment: float32 [2, 11520], P('section')
- new_factors: float32 [2, 8, 7680], P('section')
- new_errors: float32 [2, 16, 7225344], P('section', 'dp')
- loss: float32 [1], replicated
- grad_norm: float32 [1], replicated
Inputs may be any that keep to these rules, and one draw needn't show every extreme that they name: Per sample, visible and masked together hold each token index below 1024 exactly once.
All inputs are finite; a program needn't handle non-finite values. No bound on the sum of `loss_mask` on one device may be relied on, other than what follows from the above.
Results may differ from a plain program's by a relative error of at most 0.0083.
The roundings to bfloat16 on the way count: a program that leaves them out, or rounds other values in their place, can miss the bound.
Values may be sent and summed in bfloat16 or wider, within the bound.
A program may use at most 512 MiB of HBM per device.

v0:
```python
import math

import jax
import jax.numpy as jnp
from jax import lax
from jax.sharding import PartitionSpec as P

DE = 768
FFE = 3072
HEADS_ENC = 12
DD = 512
FFD = 2048
HEADS_DEC = 16
PATCH = 192
RANK = 8
SEQ = 1024
VIS = 256
MB = 2
SAMP_MB = 1
FLAT = 7225344
VLEN = 11520
LR = 5568


highest = lax.Precision.HIGHEST
clip_limit = 0.0001
moment_decay = 0.9
rate_base = 0.5
block_rows = 512


def from_behind(block, axis, distance):
    devices = range(lax.axis_size(axis))
    route = [(i - distance, i) for i in devices if i - distance in devices]
    return lax.ppermute(block, axis, route)


def matmul(left, right):
    return jnp.dot(left, right, preferred_element_type=jnp.float32)


def matmul_tn(left, right):
    return lax.dot_general(
        left, right, (((0,), (0,)), ((), ())), preferred_element_type=jnp.float32
    )


def matmul_nt(left, right):
    return lax.dot_general(
        left, right, (((1,), (1,)), ((), ())), preferred_element_type=jnp.float32
    )


def layer_norm(tokens, gain, shift):
    centred = tokens - jnp.mean(tokens, axis=-1, keepdims=True)
    spread = jnp.mean(centred * centred, axis=-1, keepdims=True)
    return centred * lax.rsqrt(spread + 1e-06) * gain + shift


def positions(width):
    places = jnp.arange(SEQ, dtype=jnp.float32)[:, None]
    column = jnp.arange(width)
    freqs = jnp.exp(-(column // 2 * 2).astype(jnp.float32) / width * math.log(10000.0))
    return jnp.sin(places * freqs + (column % 2).astype(jnp.float32) * (math.pi / 2))


def section_shapes(section):
    if section == 0:
        return [(DE, 3 * DE), (DE, DE), (DE, FFE), (FFE, DE), (PATCH, DE)]
    return [(DD, 3 * DD), (DD, DD), (DD, FFD), (FFD, DD), (PATCH, DD), (DE, DD)]


def unpack_mats(flat, shapes):
    pieces = []
    offset = 0
    for rows_n, cols_n in shapes:
        pieces.append(
            lax.slice_in_dim(flat, offset, offset + rows_n * cols_n, axis=0).reshape(rows_n, cols_n)
        )
        offset += rows_n * cols_n
    return pieces


def unpack_vecs(flat, width, hidden):
    return (
        flat[: 11 * width].reshape(11, width),
        flat[11 * width : 11 * width + hidden],
        flat[11 * width + hidden : 12 * width + hidden],
    )


def pack_flat(pieces, length):
    parts = [piece.reshape(-1) for piece in pieces]
    used = sum((part.shape[0] for part in parts))
    if used < length:
        parts.append(jnp.zeros((length - used,), parts[0].dtype))
    return jnp.concatenate(parts)


def learning_rate():
    return rate_base * math.sqrt(2.0 * (FLAT + VLEN) / DD) / clip_limit


def orthonormal(left):
    columns = []
    for column in range(RANK):
        vector_now = left[:, column]
        for basis in columns:
            vector_now = vector_now - jnp.sum(basis * vector_now) * basis
        columns.append(vector_now * lax.rsqrt(jnp.sum(vector_now * vector_now) + 1e-12))
    return jnp.stack(columns, axis=1)


def pick_rows(source, where_at):
    return jax.vmap(lambda rows_in, index_in: rows_in[index_in])(source, where_at)


def to_heads(flat_rows, samples_n, head_count):
    return flat_rows.reshape(samples_n, -1, head_count, flat_rows.shape[1] // head_count).transpose(
        0, 2, 1, 3
    )


def from_heads(heads_view):
    samples_n, head_count, seq_len, head_size = heads_view.shape
    return heads_view.transpose(0, 2, 1, 3).reshape(samples_n * seq_len, head_count * head_size)


def join_blocks(block_vals, samples_n):
    blocks_n = block_vals.shape[0] // samples_n
    shaped = block_vals.reshape((samples_n, blocks_n) + block_vals.shape[1:])
    shaped = jnp.swapaxes(shaped, 1, 2)
    return shaped.reshape(
        (samples_n, shaped.shape[1], blocks_n * shaped.shape[3]) + shaped.shape[4:]
    )


def attend(queries, keys_all, values_all, scale):
    samples_n, head_count, seq_len, head_size = queries.shape
    rows_blk = min(block_rows, seq_len)
    blocks_n = seq_len // rows_blk

    def one_block(block_id):
        sample_at = block_id // blocks_n
        start_at = block_id % blocks_n * rows_blk
        query_blk = lax.dynamic_slice_in_dim(queries[sample_at], start_at, rows_blk, 1)
        scores = (
            jnp.einsum(
                "hqd,hkd->hqk", query_blk, keys_all[sample_at], preferred_element_type=jnp.float32
            )
            * scale
        )
        row_peak = jnp.max(scores, axis=-1, keepdims=True)
        exponent = jnp.exp(scores - row_peak)
        row_total = jnp.sum(exponent, axis=-1, keepdims=True)
        probs = (exponent / row_total).astype(jnp.bfloat16)
        out_blk = jnp.einsum(
            "hqk,hkd->hqd", probs, values_all[sample_at], preferred_element_type=jnp.float32
        )
        return (out_blk, (row_peak + jnp.log(row_total))[..., 0])

    block_outs, block_lse = lax.map(one_block, jnp.arange(samples_n * blocks_n, dtype=jnp.int32))
    return (join_blocks(block_outs, samples_n), join_blocks(block_lse, samples_n))


def attend_back(queries, keys_all, values_all, lse, grad_out, scale):
    seq_len = queries.shape[2]
    rows_blk = min(block_rows, seq_len)
    blocks_n = seq_len // rows_blk

    def one_sample(inputs):
        query_one, keys_one, values_one, lse_one, grad_one = inputs
        grad_keys = jnp.zeros(keys_one.shape, jnp.float32)
        grad_values = jnp.zeros(values_one.shape, jnp.float32)
        grad_parts = []
        for block_id in range(blocks_n):
            start_at = block_id * rows_blk
            query_blk = query_one[:, start_at : start_at + rows_blk]
            grad_blk = grad_one[:, start_at : start_at + rows_blk]
            lse_blk = lse_one[:, start_at : start_at + rows_blk]
            scores = (
                jnp.einsum("hqd,hkd->hqk", query_blk, keys_one, preferred_element_type=jnp.float32)
                * scale
            )
            probs_full = jnp.exp(scores - lse_blk[..., None])
            probs = probs_full.astype(jnp.bfloat16)
            grad_probs = jnp.einsum(
                "hqd,hkd->hqk", grad_blk, values_one, preferred_element_type=jnp.float32
            )
            row_delta = jnp.sum(probs_full * grad_probs, axis=-1, keepdims=True)
            grad_scores = (probs_full * (grad_probs - row_delta)).astype(jnp.bfloat16)
            grad_parts.append(
                jnp.einsum(
                    "hqk,hkd->hqd", grad_scores, keys_one, preferred_element_type=jnp.float32
                )
                * scale
            )
            grad_keys = (
                grad_keys
                + jnp.einsum(
                    "hqk,hqd->hkd", grad_scores, query_blk, preferred_element_type=jnp.float32
                )
                * scale
            )
            grad_values = grad_values + jnp.einsum(
                "hqk,hqd->hkd", probs, grad_blk, preferred_element_type=jnp.float32
            )
        return (jnp.concatenate(grad_parts, axis=1), grad_keys, grad_values)

    return lax.map(one_sample, (queries, keys_all, values_all, lse, grad_out))


def block_forward(tokens, mats, rows, bias_up, head_count, samples_n):
    width = tokens.shape[1]
    scale = (width // head_count) ** (-0.5)
    normed = layer_norm(tokens, rows[0], rows[1]).astype(jnp.bfloat16)
    qkv_bias = jnp.concatenate([rows[6], jnp.zeros_like(rows[6]), rows[7]])
    joined = (matmul(normed, mats[0]) + qkv_bias).astype(jnp.bfloat16)
    queries = to_heads(joined[:, :width], samples_n, head_count)
    keys_all = to_heads(joined[:, width : 2 * width], samples_n, head_count)
    values_all = to_heads(joined[:, 2 * width :], samples_n, head_count)
    attended_heads, lse = attend(queries, keys_all, values_all, scale)
    attended = from_heads(attended_heads).astype(jnp.bfloat16)
    middle = tokens + matmul(attended, mats[1]) + rows[8]
    second = layer_norm(middle, rows[2], rows[3]).astype(jnp.bfloat16)
    hidden = matmul(second, mats[2]) + bias_up
    active = jax.nn.gelu(hidden, approximate=False).astype(jnp.bfloat16)
    result = middle + matmul(active, mats[3]) + rows[9]
    kept = (
        tokens,
        normed,
        queries,
        keys_all,
        values_all,
        lse,
        attended,
        middle,
        second,
        hidden,
        active,
    )
    return (result, kept)


def block_backward(kept, grad_result, mats, rows, head_count):
    tokens, normed, queries, keys_all, values_all, lse, attended, middle, second, hidden, active = (
        kept
    )
    samples_n = queries.shape[0]
    width = tokens.shape[1]
    scale = (width // head_count) ** (-0.5)
    grad_branch = grad_result.astype(jnp.bfloat16)
    grad_down_bias = jnp.sum(grad_branch.astype(jnp.float32), axis=0)
    grad_down = matmul_tn(active, grad_branch)
    grad_active = matmul_nt(grad_branch, mats[3])
    unused, gelu_pull = jax.vjp(lambda values_in: jax.nn.gelu(values_in, approximate=False), hidden)
    grad_hidden = gelu_pull(grad_active)[0].astype(jnp.bfloat16)
    grad_up_bias = jnp.sum(grad_hidden.astype(jnp.float32), axis=0)
    grad_up = matmul_tn(second, grad_hidden)
    grad_second = matmul_nt(grad_hidden, mats[2])
    unused, norm_pull = jax.vjp(layer_norm, middle, rows[2], rows[3])
    grad_mid_norm, grad_gain_two, grad_shift_two = norm_pull(grad_second)
    grad_middle = grad_result + grad_mid_norm
    grad_branch = grad_middle.astype(jnp.bfloat16)
    grad_proj_bias = jnp.sum(grad_branch.astype(jnp.float32), axis=0)
    grad_proj = matmul_tn(attended, grad_branch)
    grad_attended = matmul_nt(grad_branch, mats[1]).astype(jnp.bfloat16)
    grad_query, grad_keys, grad_values = attend_back(
        queries, keys_all, values_all, lse, to_heads(grad_attended, samples_n, head_count), scale
    )
    grad_joined = jnp.concatenate(
        [from_heads(grad_query), from_heads(grad_keys), from_heads(grad_values)], axis=1
    )
    grad_joined = grad_joined.astype(jnp.bfloat16)
    joined_sums = jnp.sum(grad_joined.astype(jnp.float32), axis=0)
    grad_qkv = matmul_tn(normed, grad_joined)
    grad_normed = matmul_nt(grad_joined, mats[0])
    unused, norm_pull = jax.vjp(layer_norm, tokens, rows[0], rows[1])
    grad_tok_norm, grad_gain_one, grad_shift_one = norm_pull(grad_normed)
    grad_tokens = grad_middle + grad_tok_norm
    empty_row = jnp.zeros((width,), jnp.float32)
    grad_rows = jnp.stack(
        [
            grad_gain_one,
            grad_shift_one,
            grad_gain_two,
            grad_shift_two,
            empty_row,
            empty_row,
            joined_sums[:width],
            joined_sums[2 * width :],
            grad_proj_bias,
            grad_down_bias,
            empty_row,
        ]
    )
    return (grad_tokens, [grad_qkv, grad_proj, grad_up, grad_down], grad_rows, grad_up_bias)


def encode_rows(pixels_mb, visible_mb, mats, rows, bias_up, table):
    pix_vis = pick_rows(pixels_mb, visible_mb).reshape(-1, PATCH)
    embedded = matmul(pix_vis, mats[4]) + rows[10] + table[visible_mb.reshape(-1)]
    result, kept = block_forward(embedded, mats, rows, bias_up, HEADS_ENC, pixels_mb.shape[0])
    return (pix_vis, result, kept)


def encoder_back(pixels_mb, visible_mb, grad_sent, mats, rows, bias_up, table, flat_len, vec_len):
    pix_vis, result, kept = encode_rows(pixels_mb, visible_mb, mats, rows, bias_up, table)
    unused, norm_pull = jax.vjp(layer_norm, result, rows[4], rows[5])
    grad_result, grad_gain, grad_shift = norm_pull(grad_sent.astype(jnp.float32))
    grad_start, grad_mats, grad_rows, grad_bias = block_backward(
        kept, grad_result, mats, rows, HEADS_ENC
    )
    grad_start_low = grad_start.astype(jnp.bfloat16)
    grad_embed = matmul_tn(pix_vis, grad_start_low)
    grad_rows = grad_rows.at[4].set(grad_gain).at[5].set(grad_shift)
    grad_rows = grad_rows.at[10].set(jnp.sum(grad_start_low.astype(jnp.float32), axis=0))
    return (
        pack_flat(grad_mats + [grad_embed], flat_len),
        pack_flat([grad_rows, grad_bias], vec_len),
    )


def decode_step(
    received,
    pixels_mb,
    visible_mb,
    masked_mb,
    mask_mb,
    mats,
    rows,
    bias_up,
    extra,
    table,
    count,
    flat_len,
    vec_len,
):
    samples_n = pixels_mb.shape[0]
    projected = matmul(received, mats[5]) + extra

    def fill_one(got, vis_at, mask_at):
        canvas = jnp.zeros((SEQ, DD), jnp.float32).at[vis_at].set(got)
        return canvas.at[mask_at].set(jnp.broadcast_to(rows[10], (mask_at.shape[0], DD)))

    filled = jax.vmap(fill_one)(projected.reshape(samples_n, VIS, DD), visible_mb, masked_mb)
    filled = (filled + table).reshape(-1, DD)
    result, kept = block_forward(filled, mats, rows, bias_up, HEADS_DEC, samples_n)
    picked = pick_rows(result.reshape(samples_n, SEQ, DD), masked_mb).reshape(-1, DD)
    final_norm, norm_pull = jax.vjp(layer_norm, picked, rows[4], rows[5])
    final_low = final_norm.astype(jnp.bfloat16)
    predicted = matmul_nt(final_low, mats[4])
    target = pick_rows(pixels_mb, masked_mb).reshape(-1, PATCH).astype(jnp.float32)
    residual_px = predicted - target
    weights_row = mask_mb.reshape(-1).astype(jnp.float32)
    loss_part = jnp.sum(weights_row * jnp.mean(residual_px * residual_px, axis=1)) / count
    grad_pred = (weights_row[:, None] * (2.0 * residual_px / PATCH) / count).astype(jnp.bfloat16)
    grad_head = matmul_tn(grad_pred, final_low)
    grad_final = matmul(grad_pred, mats[4])
    grad_picked, grad_gain, grad_shift = norm_pull(grad_final)
    grad_result = jax.vmap(
        lambda got, mask_at: jnp.zeros((SEQ, DD), jnp.float32).at[mask_at].set(got)
    )(grad_picked.reshape(samples_n, -1, DD), masked_mb).reshape(-1, DD)
    grad_filled, grad_mats, grad_rows, grad_bias = block_backward(
        kept, grad_result, mats, rows, HEADS_DEC
    )
    grad_filled = grad_filled.reshape(samples_n, SEQ, DD)
    grad_projected = pick_rows(grad_filled, visible_mb).reshape(-1, DD).astype(jnp.bfloat16)
    grad_extra = jnp.sum(grad_projected.astype(jnp.float32), axis=0)
    grad_embed_dec = matmul_tn(received, grad_projected)
    grad_sent = matmul_nt(grad_projected, mats[5]).astype(jnp.bfloat16)
    grad_token = jnp.sum(pick_rows(grad_filled, masked_mb), axis=(0, 1))
    grad_rows = grad_rows.at[4].set(grad_gain).at[5].set(grad_shift).at[10].set(grad_token)
    flat_grads = pack_flat(grad_mats + [grad_head, grad_embed_dec], flat_len)
    return (
        flat_grads,
        pack_flat([grad_rows, grad_bias, grad_extra], vec_len),
        grad_sent,
        loss_part,
    )


def local(
    pixels, visible, masked, loss_mask, master, momentum, vectors, vec_moment, factors, errors
):
    section_id = lax.axis_index("section")
    replicas = lax.axis_size("dp")
    replica_id = lax.axis_index("dp")
    low_flat = lax.all_gather(master[0].astype(jnp.bfloat16), "dp", axis=0, tiled=True)
    flat_len = low_flat.shape[0]
    vec_flat = vectors[0]
    vec_len = vec_flat.shape[0]
    count = lax.psum(jnp.sum(loss_mask).astype(jnp.float32), "dp")
    zero_sent = jnp.zeros((SAMP_MB * VIS, DE), jnp.bfloat16)

    def batch(source, micro_idx):
        return source[micro_idx * SAMP_MB : (micro_idx + 1) * SAMP_MB]

    def enc_parts():
        rows, bias_up, unused = unpack_vecs(vec_flat, DE, FFE)
        return (unpack_mats(low_flat, section_shapes(0)), rows, bias_up, positions(DE))

    grad_flat = jnp.zeros((flat_len,), jnp.float32)
    grad_vec = jnp.zeros((vec_len,), jnp.float32)
    loss_sum = jnp.zeros((), jnp.float32)
    for micro_idx in range(MB):

        def run_encoder():
            mats, rows, bias_up, table = enc_parts()
            pix_vis, result, kept = encode_rows(
                batch(pixels, micro_idx), batch(visible, micro_idx), mats, rows, bias_up, table
            )
            return layer_norm(result, rows[4], rows[5]).astype(jnp.bfloat16)

        outgoing = lax.cond(section_id == 0, run_encoder, lambda: zero_sent)
        incoming = from_behind(outgoing, "section", 1)

        def run_decoder(state):
            rows, bias_up, extra = unpack_vecs(vec_flat, DD, FFD)
            mats = unpack_mats(low_flat, section_shapes(1))
            dec_flat, dec_vec, grad_out, part = decode_step(
                incoming,
                batch(pixels, micro_idx),
                batch(visible, micro_idx),
                batch(masked, micro_idx),
                batch(loss_mask, micro_idx),
                mats,
                rows,
                bias_up,
                extra,
                positions(DD),
                count,
                flat_len,
                vec_len,
            )
            return (state[0] + dec_flat, state[1] + dec_vec, grad_out, part)

        def skip_decoder(state):
            return (state[0], state[1], zero_sent, jnp.zeros((), jnp.float32))

        grad_flat, grad_vec, grad_sent, loss_part = lax.cond(
            section_id == 1, run_decoder, skip_decoder, (grad_flat, grad_vec)
        )
        grad_in = from_behind(grad_sent, "section", -1)

        def run_back(state):
            mats, rows, bias_up, table = enc_parts()
            enc_flat, enc_vec = encoder_back(
                batch(pixels, micro_idx),
                batch(visible, micro_idx),
                grad_in,
                mats,
                rows,
                bias_up,
                table,
                flat_len,
                vec_len,
            )
            return (state[0] + enc_flat, state[1] + enc_vec)

        grad_flat, grad_vec = lax.cond(
            section_id == 0, run_back, lambda state: state, (grad_flat, grad_vec)
        )
        loss_sum = loss_sum + loss_part
    merged = replicas * grad_flat + errors[0, 0].astype(jnp.float32)
    factor_now = factors[0]
    rows_total = LR
    cols_total = factor_now.shape[1]

    def lefts_for(section):

        def lefts_run():
            shapes = section_shapes(section)
            pieces = []
            col_at = 0
            for matrix, (rows_n, cols_n) in zip(unpack_mats(merged, shapes), shapes):
                part = factor_now[:, col_at : col_at + cols_n]
                col_at += cols_n
                pieces.append(
                    lax.dot_general(matrix, part, (((1,), (1,)), ((), ())), precision=highest)
                )
            joined = jnp.concatenate(pieces, axis=0)
            return jnp.pad(joined, ((0, rows_total - joined.shape[0]), (0, 0)))

        return lefts_run

    left_pad = lax.cond(section_id == 0, lefts_for(0), lefts_for(1))
    left_sum, row_total, loss_total = lax.psum((left_pad, grad_vec, loss_sum), "dp")

    def rights_for(section):

        def rights_run():
            shapes = section_shapes(section)
            orthos = []
            rights = []
            row_at = 0
            for matrix, (rows_n, cols_n) in zip(unpack_mats(merged, shapes), shapes):
                ortho = orthonormal(left_sum[row_at : row_at + rows_n] / replicas)
                row_at += rows_n
                orthos.append(ortho)
                rights.append(
                    lax.dot_general(ortho, matrix, (((0,), (0,)), ((), ())), precision=highest)
                )
            ortho_all = jnp.concatenate(orthos, axis=0)
            right_all = jnp.concatenate(rights, axis=1)
            return (
                jnp.pad(ortho_all, ((0, rows_total - ortho_all.shape[0]), (0, 0))),
                jnp.pad(right_all, ((0, 0), (0, cols_total - right_all.shape[1]))),
            )

        return rights_run

    ortho_pad, right_pad = lax.cond(section_id == 0, rights_for(0), rights_for(1))
    right_sum = lax.psum(right_pad, "dp")
    new_factors = right_sum / replicas

    def approx_for(section):

        def approx_run():
            pieces = []
            square_sum = jnp.zeros((), jnp.float32)
            row_at = 0
            col_at = 0
            for rows_n, cols_n in section_shapes(section):
                piece = jnp.dot(
                    ortho_pad[row_at : row_at + rows_n],
                    new_factors[:, col_at : col_at + cols_n],
                    precision=highest,
                )
                square_sum = square_sum + jnp.sum(piece * piece)
                pieces.append(piece)
                row_at += rows_n
                col_at += cols_n
            return (pack_flat(pieces, flat_len), square_sum)

        return approx_run

    flat_approx, square_mats = lax.cond(section_id == 0, approx_for(0), approx_for(1))
    square_part = square_mats + jnp.sum(row_total * row_total)
    square_all, loss_all = lax.psum((square_part, loss_total), "section")
    norm = jnp.sqrt(square_all)
    scale = jnp.minimum(1.0, clip_limit / (norm + 1e-06))
    shard_len = master.shape[1]
    own_part = lax.dynamic_slice_in_dim(flat_approx, replica_id * shard_len, shard_len)
    rate = learning_rate()
    new_moment = moment_decay * momentum[0] + scale * own_part
    new_master = master[0] - rate * new_moment
    new_vm = moment_decay * vec_moment[0] + scale * row_total
    new_vectors = vectors[0] - rate * new_vm
    new_errors = merged - flat_approx
    return (
        new_master[None],
        new_master.astype(jnp.bfloat16)[None],
        new_moment[None],
        new_vectors[None],
        new_vm[None],
        new_factors[None],
        new_errors[None, None],
        loss_all.reshape(1),
        norm.reshape(1),
    )


def solution(mesh):
    return jax.shard_map(
        local,
        mesh=mesh,
        in_specs=(
            P("dp", None, None),
            P("dp", None),
            P("dp", None),
            P("dp", None),
            P("section", "dp"),
            P("section", "dp"),
            P("section", None),
            P("section", None),
            P("section", None, None),
            P("section", "dp", None),
        ),
        out_specs=(
            P("section", "dp"),
            P("section", "dp"),
            P("section", "dp"),
            P("section", None),
            P("section", None),
            P("section", None, None),
            P("section", "dp", None),
            P(),
            P(),
        ),
        check_vma=False,
    )
```

profile of v0, /device:TPU:1, one launch (start us, length us, event | category | flops | bytes accessed | tf_op | source)
XLA Modules:
  0.0 2592.0 jit_solution(5419660278353522845)
XLA Ops:
  10.6 171.1 %all-gather.2.cloned.1.call-done = bf16[7225344]{0:T(1024)(128)(2,1)} async-done(((bf16[451584]{0:T(1024)(128)(2,1)}), bf16[7225344]{0:T(1024)(128)(2,1)}) %all-gather.2.cloned.1.call-update) | async-done | bytes 14450704 | tf_op jit(solution)/shard_map/all_gather | solution.py:389
  191.9 32.9 %psum.49 = f32[]{:T(128)} all-reduce(f32[]{:T(128)S(6)} %convert_element_type.534), channel_id=1, replica_groups=mesh['section'=2,'dp'=16] {'dp'}, use_global_device_ids=true, to_apply=%region_11.12 | all-reduce | flops 1 | bytes 8 | tf_op jit(solution)/shard_map/psum | solution.py:393
  224.8 43.9 %collective-permute-done = bf16[256,768]{1,0:T(8,128)(2,1)S(1)} collective-permute-done((bf16[256,768]{1,0:T(8,128)(2,1)}, bf16[256,768]{1,0:T(8,128)(2,1)S(1)}, u32[]{:S(2)}, u32[]{:S(2)}) %collective-permute-start) | collective-permute-done | bytes 393248 | tf_op jit(solution)/shard_map/ppermute | solution.py:35
  268.7 567.0 %conditional.10 = (f32[7225344]{0:T(1024)}, f32[11520]{0:T(1024)}, bf16[256,768]{1,0:T(8,128)(2,1)}, f32[]{:T(128)}) conditional(s32[]{:T(128)} %convert_element_type.532, () %tuple.159, (s32[2,256]{1,0:T(2,128)S(1)}, bf16[7225344]{0:T(1024)(128)(2,1)}, bf16[256,768]{1,0:T(8,128)(2,1)S(1)}, f32[11520]{0:T(1024)}, s32[2,768]{1,0:T(2,128)}, ...), branch_computations={%region_12.13_spmd, %region_13.49_spmd} | conditional | flops 27384887296 | bytes 1296709760 | solution.py:441
  323.2 92.0 %while.54 = (s32[]{:T(128)}, bf16[2,16,512,32]{2,3,1,0:T(8,128)(2,1)}, f32[2,16,512]{2,1,0:T(8,128)}, s32[2]{0:T(128)S(1)}, bf16[1,16,1024,32]{2,3,1,0:T(8,128)(...) while((s32[]{:T(128)}, ...), condition=%wide.region_21.21_spmd, body=%wide.region_18.20_spmd.sunk | while | flops 1149231104 | bytes 104596768 | solution.py:162
  326.1 14.3 multiply_reduce_fusion.466
  340.4 14.2 fusion.786
  355.2 14.1 fusion.787
  372.0 14.3 multiply_reduce_fusion.466
  386.3 14.2 fusion.786
  401.2 14.1 fusion.787
  442.4 24.6 multiply_convert_fusion.6
  517.1 10.5 convert_reduce_fusion.12
  546.5 14.2 fusion.394
  560.7 23.5 multiply_reduce_fusion.435
  584.2 28.2 %multiply_convert_fusion.4 = bf16[16,512,1024]{2,1,0:T(8,128)(2,1)} fusion(f32[16,512,1024]{2,1,0:T(8,128)} %get-tuple-element.1854, f32[16,512,1024]{2,1,0:T(8,128)} %fusion.394, f32[16,512]{1,0:T(8,128)S(1)} %get-tuple-element.1853, f32[16,512]{1,0:T(8,128)S(1)} %get-tuple-element.1826), kind=kLoop, calls=%fused_computation.1504 | loop fusion | flops 41943040 | bytes 83951616 | tf_op jit(solution)/shard_map/cond/branch_1_fun/while/body/eval_jaxpr/convert_element_type | solution.py:191
  621.0 14.2 fusion.401
  635.2 23.5 multiply_reduce_fusion.436
  658.7 27.8 %multiply_convert_fusion.5 = bf16[16,512,1024]{2,1,0:T(8,128)(2,1)} fusion(f32[16,512,1024]{2,1,0:T(8,128)} %get-tuple-element.1852, f32[16,512,1024]{2,1,0:T(8,128)} %fusion.401, f32[16,512]{1,0:T(8,128)S(1)} %get-tuple-element.1851, f32[16,512]{1,0:T(8,128)S(1)} %get-tuple-element.1825), kind=kLoop, calls=%fused_computation.1507 | loop fusion | flops 41943040 | bytes 83951616 | tf_op jit(solution)/shard_map/cond/branch_1_fun/while/body/eval_jaxpr/convert_element_type | solution.py:191
  709.1 12.4 fusion.366
  721.5 12.8 add_convert_fusion.32
  760.6 10.4 add_bitcast_fusion
  791.9 10.6 fusion.432
  837.8 12.7 conditional.12
  851.8 16.4 conditional.11
  868.2 599.1 %conditional.13 = (f32[7225344]{0:T(1024)}, f32[11520]{0:T(1024)}, bf16[256,768]{1,0:T(8,128)(2,1)}, f32[]{:T(128)}) conditional(s32[]{:T(128)} %convert_element_type.532, (f32[7225344]{0:T(1024)}, f32[11520]{0:T(1024)}) %get-tuple-element.2107, (s32[2,256]{1,0:T(2,128)}, bf16[7225344]{0:T(1024)(128)(2,1)}, bf16[256,768]{1,0:T(8,128)(2,1)}, ...), branch_computations={%region_87.88_spmd, %region_88.124_spmd} | conditional | flops 27392122880 | bytes 1381862528 | solution.py:441
  911.5 10.1 add_convert_fusion.41
  925.0 92.3 %while.55 = (s32[]{:T(128)}, bf16[2,16,512,32]{2,3,1,0:T(8,128)(2,1)}, f32[2,16,512]{2,1,0:T(8,128)}, s32[2]{0:T(128)S(1)}, bf16[1,16,1024,32]{2,3,1,0:T(8,128)(...) while((s32[]{:T(128)}, ...), condition=%wide.region_96.96_spmd, body=%wide.region_93.95_spmd.sunk | while | flops 1149231104 | bytes 104596768 | solution.py:162
  928.1 14.3 multiply_reduce_fusion.465
  942.4 14.2 fusion.783
  957.2 14.1 fusion.784
  974.0 14.3 multiply_reduce_fusion.465
  988.3 14.2 fusion.783
  1003.2 14.1 fusion.784
  1043.8 24.4 multiply_convert_fusion.10
  1118.6 10.5 convert_reduce_fusion.18
  1148.0 14.2 fusion.465
  1162.2 23.5 multiply_reduce_fusion.448
  1185.7 28.0 %multiply_convert_fusion.8 = bf16[16,512,1024]{2,1,0:T(8,128)(2,1)} fusion(f32[16,512,1024]{2,1,0:T(8,128)} %get-tuple-element.1897, f32[16,512,1024]{2,1,0:T(8,128)} %fusion.465, f32[16,512]{1,0:T(8,128)S(1)} %get-tuple-element.1896, f32[16,512]{1,0:T(8,128)S(1)} %get-tuple-element.1869), kind=kLoop, calls=%fused_computation.1669 | loop fusion | flops 41943040 | bytes 83951616 | tf_op jit(solution)/shard_map/cond/branch_1_fun/while/body/eval_jaxpr/convert_element_type | solution.py:191
  1222.3 14.2 fusion.472
  1236.5 23.5 multiply_reduce_fusion.449
  1260.0 27.8 %multiply_convert_fusion.9 = bf16[16,512,1024]{2,1,0:T(8,128)(2,1)} fusion(f32[16,512,1024]{2,1,0:T(8,128)} %get-tuple-element.1895, f32[16,512,1024]{2,1,0:T(8,128)} %fusion.472, f32[16,512]{1,0:T(8,128)S(1)} %get-tuple-element.1894, f32[16,512]{1,0:T(8,128)S(1)} %get-tuple-element.1868), kind=kLoop, calls=%fused_computation.1672 | loop fusion | flops 41943040 | bytes 83951616 | tf_op jit(solution)/shard_map/cond/branch_1_fun/while/body/eval_jaxpr/convert_element_type | solution.py:191
  1310.6 12.4 fusion.437
  1323.0 12.8 add_convert_fusion.42
  1361.9 10.4 add_bitcast_fusion.2
  1394.0 10.6 fusion.503
  1435.7 29.0 %add.1241 = f32[7225344]{0:T(1024)} add(f32[7225344]{0:T(1024)} %get-tuple-element.648, f32[7225344]{0:T(1024)} %broadcast_dynamic-update-slice_fusion.2) | non-fusion elementwise | flops 7225344 | bytes 86704128 | tf_op jit(solution)/shard_map/cond/branch_1_fun/add | solution.py:436
  1468.8 32.9 %convert_element_type.540 = f32[1,1,7225344]{2,1,0:T(1,128)} convert(bf16[1,1,7225344]{2,1,0:T(2,128)(2,1)} %param.65) | non-fusion elementwise | flops 7225344 | bytes 43352064 | tf_op jit(solution)/shard_map/convert_element_type | solution.py:465
  1510.9 29.1 %multiply_add_fusion.12 = f32[7225344]{0:T(1024)} fusion(f32[7225344]{0:T(1024)} %bitcast.776, f32[7225344]{0:T(1024)} %get-tuple-element.712), kind=kLoop, calls=%fused_computation.1834 | loop fusion | flops 14450688 | bytes 86704128 | tf_op jit(solution)/shard_map/add | solution.py:465
  1540.0 53.7 %conditional.15 = (f32[5568,8]{0,1:T(8,128)}) conditional(s32[]{:T(128)} %convert_element_type.531, (f32[7225344]{0:T(1024)}, f32[8,7680]{1,0:T(8,128)S(1)}) %tuple.1000, (f32[7225344]{0:T(1024)}, f32[8,7680]{1,0:T(8,128)S(1)}) %tuple.1001), branch_computations={%region_152.153_spmd, %region_153.154_spmd} | conditional | flops 693633024 | bytes 144932864 | solution.py:487
  1598.3 318.5 %all-reduce.8.cloned.1.call-done = f32[5568,8]{0,1:T(8,128)} async-done(((f32[5568,8]{0,1:T(8,128)}), f32[5568,8]{0,1:T(8,128)}) %all-reduce.8.cloned.1.call-update) | async-done | bytes 178192 | tf_op jit(solution)/shard_map/psum | solution.py:488
  1916.7 419.7 %conditional.16 = (f32[5568,8]{0,1:T(8,128)}, f32[8,7680]{1,0:T(8,128)}) conditional(s32[]{:T(128)} %convert_element_type.531, (f32[5568,8]{0,1:T(8,128)}, f32[7225344]{0:T(1024)}) %tuple.170, (f32[5568,8]{0,1:T(8,128)}, f32[7225344]{0:T(1024)}) %tuple.170), branch_computations={%region_155.372_spmd, %region_372.553_spmd} | conditional | flops 695027776 | bytes 149158816 | solution.py:513
  1961.0 17.6 subtract_multiply_fusion.28
  2030.2 17.6 subtract_multiply_fusion.21
  2092.8 17.6 subtract_multiply_fusion.14
  2169.8 17.7 subtract_multiply_fusion
  2239.8 17.5 subtract_multiply_fusion.35
  2302.1 17.6 subtract_multiply_fusion.7
  2337.4 61.7 %all-reduce.3 = (f32[11520]{0:T(1024)S(1)}, f32[]{:T(128)}) all-reduce(f32[11520]{0:T(1024)} %get-tuple-element.716, f32[]{:T(128)S(6)} %add.1389), channel_id=1, replica_groups=mesh['section'=2,'dp'=16] {'dp'}, use_global_device_ids=true, to_apply=%region_567.568 | all-reduce | flops 11521 | bytes 92168 | tf_op jit(solution)/shard_map/psum | solution.py:488
  2399.7 41.3 %all-reduce.10.cloned.1.call-done = f32[8,7680]{1,0:T(8,128)} async-done(((f32[8,7680]{1,0:T(8,128)}), f32[8,7680]{1,0:T(8,128)}) %all-reduce.10.cloned.1.call-update) | async-done | bytes 245776 | tf_op jit(solution)/shard_map/psum | solution.py:514
  2442.7 60.3 %conditional.17 = (f32[7225344]{0:T(1024)}, f32[]{:T(128)}) conditional(s32[]{:T(128)} %convert_element_type.531, (f32[5568,8]{0,1:T(8,128)}, f32[8,7680]{1,0:T(8,128)S(1)}) %tuple.171, (f32[5568,8]{0,1:T(8,128)}, f32[8,7680]{1,0:T(8,128)S(1)}) %tuple.171), branch_computations={%region_554.561_spmd, %region_561.567_spmd} | conditional | flops 708083712 | bytes 144932960 | solution.py:538
  2503.0 29.2 %sub.2916 = f32[7225344]{0:T(1024)} subtract(f32[7225344]{0:T(1024)} %multiply_add_fusion.12, f32[7225344]{0:T(1024)} %get-tuple-element.717) | non-fusion elementwise | flops 7225344 | bytes 86704128 | tf_op jit(solution)/shard_map/sub | solution.py:550
  2532.8 33.2 %all-reduce.4 = (f32[]{:T(128)}, f32[1]{0:T(128)}) all-reduce(f32[]{:T(128)S(6)} %add.1384, f32[1]{0:T(128)} %bitcast.296), channel_id=1, replica_groups=mesh['section'=2,'dp'=16] {'section'}, use_global_device_ids=true, to_apply=%region_569.570 | all-reduce | flops 2 | bytes 16 | tf_op jit(solution)/shard_map/psum | solution.py:540
  2573.1 11.0 broadcast_in_dim.379
  (848 shorter events, 918.9 us)
Async XLA Ops:
  7.2 174.6 %copy-start.16 = (bf16[2,1024,192]{1,2,0:T(8,128)(2,1)S(1)}, bf16[2,1024,192]{1,2,0:T(8,128)(2,1)}, u32[]{:S(2)}) copy-start(bf16[2,1024,192]{1,2,0:T(8,128)(2,1)} %param.56) | copy-start | bytes 2359300
  7.2 174.5 %copy-start.169 = (s32[2,256]{1,0:T(2,128)S(1)}, s32[2,256]{1,0:T(2,128)}, u32[]{:S(2)}) copy-start(s32[2,256]{1,0:T(2,128)} %param.57) | copy-start | bytes 6148
  7.2 174.5 %all-gather.2.cloned.1.call-start = ((), (), s32[]{:S(2)}) async-start(), calls=%async_computation | async-start | bytes 15353856 | tf_op jit(solution)/shard_map/all_gather | solution.py:389
  9.8 1906.9 %all-reduce.8.cloned.1.call-start = ((), (), s32[]{:S(2)}) async-start(), calls=%async_computation.1 | async-start | bytes 360448 | tf_op jit(solution)/shard_map/psum | solution.py:488
  181.7 8.8 copy-start.218
  189.3 79.4 %collective-permute-start = (bf16[256,768]{1,0:T(8,128)(2,1)}, bf16[256,768]{1,0:T(8,128)(2,1)S(1)}, u32[]{:S(2)}, u32[]{:S(2)}) collective-permute-start(bf16[256,768]{1,0:T(8,128)(2,1)} %get-tuple-element.2106), channel_id=1, source_target_pairs={{0,16},{1,17},{2,18},{3,19},{4,20},{5,21},{6,22},{7,23},{8,24},{9,... | collective-permute-start | bytes 1179656 | tf_op jit(solution)/shard_map/ppermute | solution.py:35
  268.7 569.1 %copy-start.170 = (s32[2,256]{1,0:T(2,128)S(1)}, s32[2,256]{1,0:T(2,128)}, u32[]{:S(2)}) copy-start(s32[2,256]{1,0:T(2,128)} %param.57) | copy-start | bytes 6148
  270.1 39.5 %copy-start.208 = (f32[512]{0:T(512)}, f32[512]{0:T(512)S(1)}, u32[]{:S(2)}) copy-start(f32[512]{0:T(512)S(1)} %get-tuple-element.1835) | copy-start | bytes 6148 | tf_op jit(solution)/shard_map/cond
  270.1 39.6 %copy-start.292 = (f32[512]{0:T(512)}, f32[512]{0:T(512)S(1)}, u32[]{:S(2)}) copy-start(f32[512]{0:T(512)S(1)} %get-tuple-element.1834) | copy-start | bytes 6148 | tf_op jit(solution)/shard_map/cond
  276.3 10.3 copy-start.270
  286.5 23.1 copy-start.8
  286.6 23.1 copy-start.159
  286.6 23.1 copy-start.162
  294.4 15.3 copy-start.151
  430.7 107.3 %copy-start.167 = (f32[1024]{0:T(1024)}, f32[1024]{0:T(1024)S(1)}, u32[]{:S(2)}) copy-start(f32[1024]{0:T(1024)S(1)} %broadcast_multiply_fusion.48) | copy-start | bytes 12292 | tf_op jit(solution)/shard_map/cond
  432.3 10.1 copy-start.203
  442.4 24.6 copy-start.258
  506.2 10.8 copy-start.259
  517.1 10.5 copy-start.43
  517.1 10.5 copy-start.107
  686.6 18.4 slice-start
  686.6 18.4 slice-start.1
  686.6 18.4 slice-start.2
  695.6 39.3 %copy-start.77 = (bf16[16,1024,32]{1,2,0:T(8,128)(2,1)}, bf16[16,1024,32]{1,2,0:T(8,128)(2,1)S(1)}, u32[]{:S(2)}) copy-start(bf16[16,1024,32]{1,2,0:T(8,128)(2,1)S(1)} %pad_maximum_fusion.11) | copy-start | bytes 3145732 | tf_op jit(solution)/shard_map/cond
  695.6 9.4 slice-start.3
  742.3 9.2 copy-start.187
  742.4 9.2 copy-start.14
  742.4 9.2 copy-start.179
  751.6 8.7 copy-start.250
  751.6 8.7 copy-start.252
  751.6 8.7 copy-start.284
  751.6 8.8 copy-start.300
  751.6 8.9 copy-start.298
  751.6 9.0 copy-start.181
  835.7 16.1 collective-permute-start.1
  850.5 17.7 collective-permute-start.2
  869.6 41.8 %copy-start.206 = (f32[512]{0:T(512)}, f32[512]{0:T(512)S(1)}, u32[]{:S(2)}) copy-start(f32[512]{0:T(512)S(1)} %get-tuple-element.1878) | copy-start | bytes 6148 | tf_op jit(solution)/shard_map/cond
  869.6 41.8 %copy-start.290 = (f32[512]{0:T(512)}, f32[512]{0:T(512)S(1)}, u32[]{:S(2)}) copy-start(f32[512]{0:T(512)S(1)} %get-tuple-element.1877) | copy-start | bytes 6148 | tf_op jit(solution)/shard_map/cond
  888.0 23.5 copy-start.4
  888.0 23.5 copy-start.153
  888.0 23.5 copy-start.156
  895.8 15.7 copy-start.149
  1032.6 106.8 %copy-start.165 = (f32[1024]{0:T(1024)}, f32[1024]{0:T(1024)S(1)}, u32[]{:S(2)}) copy-start(f32[1024]{0:T(1024)S(1)} %broadcast_multiply_fusion.52) | copy-start | bytes 12292 | tf_op jit(solution)/shard_map/cond
  1034.3 9.6 copy-start.200
  1043.8 24.5 copy-start.260
  1107.7 10.8 copy-start.261
  1118.6 10.5 copy-start.40
  1118.6 10.5 copy-start.108
  1287.8 18.6 slice-start.4
  1287.9 18.6 slice-start.5
  1287.9 18.6 slice-start.6
  1297.1 39.3 %copy-start.75 = (bf16[16,1024,32]{1,2,0:T(8,128)(2,1)}, bf16[16,1024,32]{1,2,0:T(8,128)(2,1)S(1)}, u32[]{:S(2)}) copy-start(bf16[16,1024,32]{1,2,0:T(8,128)(2,1)S(1)} %pad_maximum_fusion.17) | copy-start | bytes 3145732 | tf_op jit(solution)/shard_map/cond
  1297.1 9.4 slice-start.7
  1343.9 9.2 copy-start.189
  1343.9 9.2 copy-start.15
  1343.9 9.2 copy-start.177
  1435.7 29.0 %copy-start.68 = (bf16[768,512]{1,0:T(8,128)(2,1)S(1)}, bf16[768,512]{1,0:T(8,128)(2,1)}, u32[]{:S(2)}) copy-start(bf16[768,512]{1,0:T(8,128)(2,1)} %copy-done.67) | copy-start | bytes 2359300 | tf_op jit(solution)/shard_map/cond
  1467.3 34.4 %copy-start.17 = (bf16[2,1024,192]{1,2,0:T(8,128)(2,1)S(1)}, bf16[2,1024,192]{1,2,0:T(8,128)(2,1)}, u32[]{:S(2)}) copy-start(bf16[2,1024,192]{1,2,0:T(8,128)(2,1)} %param.56) | copy-start | bytes 2359300
  1467.4 34.4 %copy-start.171 = (s32[2,256]{1,0:T(2,128)S(1)}, s32[2,256]{1,0:T(2,128)}, u32[]{:S(2)}) copy-start(s32[2,256]{1,0:T(2,128)} %param.57) | copy-start | bytes 6148
  1467.4 34.3 %collective-permute-start.3 = (bf16[256,768]{1,0:T(8,128)(2,1)}, bf16[256,768]{1,0:T(8,128)(2,1)S(1)}, u32[]{:S(2)}, u32[]{:S(2)}) collective-permute-start(bf16[256,768]{1,0:T(8,128)(2,1)} %get-tuple-element.711), channel_id=1, source_target_pairs={{16,0},{17,1},{18,2},{19,3},{20,4},{21,5},{22,6},{23,7},{24,8},{25... | collective-permute-start | bytes 1179656 | tf_op jit(solution)/shard_map/ppermute | solution.py:35
  1510.9 29.1 %copy-start.134 = (f32[1,8,7680]{2,1,0:T(8,128)S(1)}, f32[1,8,7680]{2,1,0:T(8,128)}, u32[]{:S(2)}) copy-start(f32[1,8,7680]{2,1,0:T(8,128)} %param.64) | copy-start | bytes 737284
  1593.7 847.3 %all-reduce.10.cloned.1.call-start = ((), (), s32[]{:S(2)}) async-start(), calls=%async_computation.2 | async-start | bytes 491520 | tf_op jit(solution)/shard_map/psum | solution.py:514
  2126.9 60.7 %copy-start.143 = (f32[8,5632]{1,0:T(8,128)}, f32[8,5632]{1,0:T(8,128)S(1)}, u32[]{:S(2)}) copy-start(f32[8,5632]{1,0:T(8,128)S(1)} %convolution_dynamic-update-slice_fusion.5) | copy-start | bytes 540676 | tf_op jit(solution)/shard_map/cond
  2503.0 65.9 %copy-start.62 = (f32[1,451584]{1,0:T(1,128)S(1)}, f32[1,451584]{1,0:T(1,128)}, u32[]{:S(2)}) copy-start(f32[1,451584]{1,0:T(1,128)} %param.60) | copy-start | bytes 5419012
  (145 other events, 583.8 us)
Sparse Core Ops, SparseCore 0:
  11.3 170.4 all-gather.1
  1593.8 322.8 all-reduce.7
  2336.6 104.3 all-reduce.9
where the time goes:
time: 2620 us; the launch traced here: 2590 us
  other arithmetic  784 us (30%)
  matrix products  620 us (24%)
  waiting for transfers between devices  575 us (22%)
  local copies, waits for them, and re-layouts  335 us (13%)
  blocking collectives  128 us (5%)
  loops' own time  127 us (5%)
    psum x1, waiting for transfers between devices, local(): lax.psum((left_pad, grad_vec, loss_sum), 'dp')  318 us
    reduce_sum x58, other arithmetic, orthonormal(): vector_now = vector_now - jnp.sum(basis * vector_now) * basis  175 us
    all_gather x1, waiting for transfers between devices, local(): lax.all_gather(master[0].astype(jnp.bfloat16), 'dp', axis=0, tiled=True)  171 us
    slice x44, local copies, waits for them, and re-layouts, unpack_mats(): lax.slice_in_dim(flat, offset, offset + rows_n * cols_n, axis=0)  115 us
    convert_element_type x4, other arithmetic, one_sample(): grad_scores = (probs_full * (grad_probs - row_delta)).astype(jnp.bfloat16)  112 us
    dot_general x12, matrix products, matmul(): return jnp.dot(left, right, preferred_element_type=jnp.float32)  108 us
    mul x7, other arithmetic, orthonormal(): vector_now * lax.rsqrt(jnp.sum(vector_now * vector_now) + 1e-12)  106 us
    dot_general x4, matrix products, one_sample(): jnp.einsum('hqd,hkd->hqk', grad_blk, values_one, preferred_element_type=j...  94 us
  transfers between devices with their start and end apart: 7, of which 4 were waited for; matrix products, arithmetic and copies ran while one was open for 2% of the time, Pallas kernels for 0%

commit v1 on v0

v1 whole, which is shorter than its diff:
```python
import functools
import math

import jax
import jax.numpy as jnp
from jax import lax
from jax.experimental import pallas as pl
from jax.experimental.pallas import tpu as pltpu
from jax.sharding import PartitionSpec as P

DE = 768
FFE = 3072
HEADS_ENC = 12
DD = 512
FFD = 2048
HEADS_DEC = 16
PATCH = 192
RANK = 8
SEQ = 1024
VIS = 256
FLAT = 7225344
VLEN = 11520

f32 = jnp.float32
bf16 = jnp.bfloat16
clip_limit = 0.0001
moment_decay = 0.9
rate_base = 0.5
LANES = 128
BIG = 66000000


def nn(left, right):
    return lax.dot_general(left, right, (((1,), (0,)), ((), ())), preferred_element_type=f32)


def nt(left, right):
    return lax.dot_general(left, right, (((1,), (1,)), ((), ())), preferred_element_type=f32)


def tn(left, right):
    return lax.dot_general(left, right, (((0,), (0,)), ((), ())), preferred_element_type=f32)


def split3(value):
    high = value.astype(bf16)
    rest = value - high.astype(f32)
    middle = rest.astype(bf16)
    return jnp.concatenate([high, middle, (rest - middle.astype(f32)).astype(bf16)], axis=0)


def join3(value):
    return value[:RANK] + value[RANK : 2 * RANK] + value[2 * RANK :]


def layer_norm(tokens, gain, shift):
    centred = tokens - jnp.mean(tokens, axis=-1, keepdims=True)
    spread = jnp.mean(centred * centred, axis=-1, keepdims=True)
    return centred * lax.rsqrt(spread + 1e-06) * gain + shift


def positions_at(places, width):
    column = jnp.arange(width)
    freqs = jnp.exp(-(column // 2 * 2).astype(f32) / width * math.log(10000.0))
    return jnp.sin(places.astype(f32)[:, None] * freqs + (column % 2).astype(f32) * (math.pi / 2))


def section_shapes(section):
    if section == 0:
        return [(DE, 3 * DE), (DE, DE), (DE, FFE), (FFE, DE), (PATCH, DE)]
    return [(DD, 3 * DD), (DD, DD), (DD, FFD), (FFD, DD), (PATCH, DD), (DE, DD)]


ROWS_L = [sum(rows for rows, cols in section_shapes(s)) for s in range(2)]
COLS_R = [sum(cols for rows, cols in section_shapes(s)) for s in range(2)]


def unpack_vecs(flat, width, hidden):
    return (
        flat[: 11 * width].reshape(11, width),
        flat[11 * width : 11 * width + hidden],
        flat[11 * width + hidden : 12 * width + hidden],
    )


def learning_rate():
    return rate_base * math.sqrt(2.0 * (FLAT + VLEN) / DD) / clip_limit


def unflat_body(src_ref, out_ref, wide_ref, *, blocks, rows, stacked):
    wide_ref[...] = src_ref[...].astype(f32)
    for block in range(blocks):
        part = wide_ref[pl.ds(block, rows, stride=blocks), :].astype(bf16)
        if stacked:
            out_ref[block] = part
        else:
            out_ref[:, block * LANES : (block + 1) * LANES] = part


def unflat(flat, start, rows_n, cols_n, stacked=False):
    blocks = cols_n // LANES
    rows = 192 if rows_n == PATCH else 128 if blocks > 8 else 256
    if stacked:
        out_shape = jax.ShapeDtypeStruct((blocks, rows_n, LANES), bf16)
        out_spec = pl.BlockSpec((blocks, rows, LANES), lambda i: (0, i, 0))
    else:
        out_shape = jax.ShapeDtypeStruct((rows_n, cols_n), bf16)
        out_spec = pl.BlockSpec((rows, cols_n), lambda i: (i, 0))
    step = rows * blocks
    return pl.pallas_call(
        functools.partial(unflat_body, blocks=blocks, rows=rows, stacked=stacked),
        grid=(rows_n // rows,),
        in_specs=[pl.BlockSpec((pl.Element(step), pl.Element(LANES)), lambda i: (pl.multiple_of(start // LANES + i * step, 16), 0))],
        out_specs=out_spec,
        out_shape=out_shape,
        scratch_shapes=[pltpu.VMEM((step, LANES), f32)],
        name="unflat",
    )(flat)


def unflat_all(flat, start, section, stacked=False):
    mats = []
    for rows_n, cols_n in section_shapes(section):
        mats.append(unflat(flat, start, rows_n, cols_n, stacked))
        start += rows_n * cols_n
    return mats


def head_mask(head, size):
    lane = lax.broadcasted_iota(jnp.int32, (1, LANES), 1)
    return (lane // size == head).astype(bf16)


def attend_body(q_ref, k_ref, v_ref, o_ref, lse_ref, *, size, rows_q):
    seq = k_ref.shape[0]
    scale = size ** (-0.5)
    fold = scale * math.log2(math.e)

    def one(step, carry):
        at = pl.ds(pl.multiple_of(step * rows_q, rows_q), rows_q)
        queries = q_ref[at, :]
        total = jnp.zeros((rows_q, LANES), f32)
        for head in range(LANES // size):
            mask = head_mask(head, size)
            scores = nt(k_ref[...], queries * mask)
            peak = jnp.max(scores, axis=0, keepdims=True) * fold
            power = jnp.exp2(scores * fold - peak)
            mass = jnp.sum(power, axis=0, keepdims=True)
            probs = (power * (1.0 / mass)).astype(bf16)
            total = total + tn(probs, v_ref[...] * mask)
            lse_ref[0, head : head + 1, at] = peak + jnp.log2(mass)
        o_ref[at, :] = total
        return carry

    lax.fori_loop(0, seq // rows_q, one, 0)


def attend(joined, heads):
    seq, width = joined.shape[0], joined.shape[1] // 3
    size = width // heads
    groups = width // LANES
    per = LANES // size
    rows_q = min(512, seq)
    return pl.pallas_call(
        functools.partial(attend_body, size=size, rows_q=rows_q),
        grid=(groups,),
        in_specs=[
            pl.BlockSpec((seq, LANES), lambda g: (0, g)),
            pl.BlockSpec((seq, LANES), lambda g: (0, groups + g)),
            pl.BlockSpec((seq, LANES), lambda g: (0, 2 * groups + g)),
        ],
        out_specs=[
            pl.BlockSpec((seq, LANES), lambda g: (0, g)),
            pl.BlockSpec((1, per, seq), lambda g: (g, 0, 0)),
        ],
        out_shape=[
            jax.ShapeDtypeStruct((seq, width), f32),
            jax.ShapeDtypeStruct((groups, per, seq), f32),
        ],
        name="attend",
    )(joined, joined, joined)


def attend_back_body(q_ref, k_ref, v_ref, do_ref, o_ref, lse_ref, dq_ref, dk_ref, dv_ref, dk_sum, dv_sum, *, size, rows_q):
    seq = k_ref.shape[0]
    scale = size ** (-0.5)
    fold = scale * math.log2(math.e)
    dk_sum[...] = jnp.zeros_like(dk_sum)
    dv_sum[...] = jnp.zeros_like(dv_sum)

    def one(step, carry):
        at = pl.ds(pl.multiple_of(step * rows_q, rows_q), rows_q)
        queries = q_ref[at, :]
        grads = do_ref[at, :]
        prod = grads.astype(f32) * o_ref[at, :]
        total = jnp.zeros((rows_q, LANES), f32)
        high = prod.astype(bf16)
        rest = prod - high.astype(f32)
        middle = rest.astype(bf16)
        for head in range(LANES // size):
            mask = head_mask(head, size)
            wide = jnp.broadcast_to(mask, (16, LANES))
            delta = (nt(wide, high) + nt(wide, middle))[0:1]
            q_one = queries * mask
            g_one = grads * mask
            scores = nt(k_ref[...], q_one)
            probs = jnp.exp2(scores * fold - lse_ref[0, head : head + 1, at])
            slope = nt(v_ref[...], g_one)
            grad_s = (probs * (slope - delta)).astype(bf16)
            dv_sum[...] += nn(probs.astype(bf16), g_one)
            dk_sum[...] += nn(grad_s, q_one)
            total = total + tn(grad_s, k_ref[...] * mask)
        dq_ref[at, :] = (total * scale).astype(bf16)
        return carry

    lax.fori_loop(0, seq // rows_q, one, 0)
    dk_ref[...] = (dk_sum[...] * scale).astype(bf16)
    dv_ref[...] = dv_sum[...].astype(bf16)


def attend_back(joined, grad_out, out, lse, heads):
    seq, width = joined.shape[0], joined.shape[1] // 3
    size = width // heads
    groups = width // LANES
    per = LANES // size
    rows_q = min(512, seq)
    col = pl.BlockSpec((seq, LANES), lambda g: (0, g))
    return pl.pallas_call(
        functools.partial(attend_back_body, size=size, rows_q=rows_q),
        grid=(groups,),
        in_specs=[
            col,
            pl.BlockSpec((seq, LANES), lambda g: (0, groups + g)),
            pl.BlockSpec((seq, LANES), lambda g: (0, 2 * groups + g)),
            col,
            col,
            pl.BlockSpec((1, per, seq), lambda g: (g, 0, 0)),
        ],
        out_specs=[col, col, col],
        out_shape=[jax.ShapeDtypeStruct((seq, width), bf16)] * 3,
        scratch_shapes=[pltpu.VMEM((seq, LANES), f32)] * 2,
        name="attend_back",
    )(joined, joined, joined, grad_out, out, lse)


def block_forward(tokens, mats, rows, bias_up, heads):
    normed = layer_norm(tokens, rows[0], rows[1]).astype(bf16)
    qkv_bias = jnp.concatenate([rows[6], jnp.zeros_like(rows[6]), rows[7]])
    joined = (nn(normed, mats[0]) + qkv_bias).astype(bf16)
    out, lse = attend(joined, heads)
    attended = out.astype(bf16)
    middle = tokens + nn(attended, mats[1]) + rows[8]
    second = layer_norm(middle, rows[2], rows[3]).astype(bf16)
    hidden = nn(second, mats[2]) + bias_up
    active = jax.nn.gelu(hidden, approximate=False).astype(bf16)
    result = middle + nn(active, mats[3]) + rows[9]
    return result, (tokens, normed, joined, out, lse, attended, middle, second, hidden, active)


def block_backward(kept, grad_result, mats, rows, heads):
    tokens, normed, joined, out, lse, attended, middle, second, hidden, active = kept
    width = tokens.shape[1]
    b_down = grad_result.astype(bf16)
    v_down = jnp.sum(b_down.astype(f32), axis=0)
    grad_active = nt(b_down, mats[3])
    unused, pull = jax.vjp(lambda v: jax.nn.gelu(v, approximate=False), hidden)
    b_up = pull(grad_active)[0].astype(bf16)
    v_up = jnp.sum(b_up.astype(f32), axis=0)
    grad_second = nt(b_up, mats[2])
    unused, pull = jax.vjp(layer_norm, middle, rows[2], rows[3])
    grad_norm, v_gain2, v_shift2 = pull(grad_second)
    grad_middle = grad_result + grad_norm
    b_proj = grad_middle.astype(bf16)
    v_proj = jnp.sum(b_proj.astype(f32), axis=0)
    grad_att = nt(b_proj, mats[1]).astype(bf16)
    dq, dk, dv = attend_back(joined, grad_att, out, lse, heads)
    b_qkv = jnp.concatenate([dq, dk, dv], axis=1)
    v_q = jnp.sum(dq.astype(f32), axis=0)
    v_v = jnp.sum(dv.astype(f32), axis=0)
    grad_normed = nt(b_qkv, mats[0])
    unused, pull = jax.vjp(layer_norm, tokens, rows[0], rows[1])
    grad_norm, v_gain1, v_shift1 = pull(grad_normed)
    grad_tokens = grad_middle + grad_norm
    pairs = [(normed, b_qkv), (attended, b_proj), (second, b_up), (active, b_down)]
    return grad_tokens, pairs, [v_gain1, v_shift1, v_gain2, v_shift2, None, None, v_q, v_v, v_proj, v_down, None], v_up


def skinny_body(*refs, counts):
    n = counts
    x_refs, u_refs, v_refs, outs = refs[:n], refs[n : 2 * n], refs[2 * n : 3 * n], refs[3 * n :]
    for x_ref, u_ref, v_ref, o_ref in zip(x_refs, u_refs, v_refs, outs):
        part = join3(nt(split3(x_ref[...]), u_ref[...]))
        o_ref[...] = join3(nn(split3(part), v_ref[...]))


def skinny(xs, us, vs):
    n = len(xs)
    full = pl.BlockSpec(memory_space=pltpu.VMEM)
    return pl.pallas_call(
        functools.partial(skinny_body, counts=n),
        in_specs=[full] * (3 * n),
        out_specs=[full] * n,
        out_shape=[jax.ShapeDtypeStruct((RANK, v.shape[1]), f32) for v in vs],
        compiler_params=pltpu.CompilerParams(vmem_limit_bytes=BIG),
        name="skinny",
    )(*xs, *us, *vs)


def ortho_body(left_ref, out_ref, *, widths, scale):
    at = 0
    rank_id = lax.broadcasted_iota(jnp.int32, (RANK, 1), 0)
    for width in widths:
        basis = left_ref[:, at : at + width] * scale
        for column in range(RANK):
            current = basis[column : column + 1]
            current = current * lax.rsqrt(jnp.sum(current * current, axis=1, keepdims=True) + 1e-12)
            dots = jnp.sum(basis * current, axis=1, keepdims=True)
            basis = jnp.where(
                rank_id > column, basis - dots * current, jnp.where(rank_id == column, current, basis)
            )
        out_ref[:, at : at + width] = basis
        at += width


def orthonormal(left, widths, scale):
    full = pl.BlockSpec(memory_space=pltpu.VMEM)
    return pl.pallas_call(
        functools.partial(ortho_body, widths=widths, scale=scale),
        in_specs=[full],
        out_specs=full,
        out_shape=jax.ShapeDtypeStruct(left.shape, f32),
        name="orthonormal",
    )(left)


def err_left_body(x_ref, e_ref, o_ref):
    total = jnp.zeros((e_ref.shape[1], 3 * RANK), f32)
    pieces = split3(x_ref[...])
    for block in range(e_ref.shape[0]):
        total = total + nt(e_ref[block], pieces[:, block * LANES : (block + 1) * LANES])
    o_ref[...] = join3(total.T)


def err_left(factor, err):
    full = pl.BlockSpec(memory_space=pltpu.VMEM)
    return pl.pallas_call(
        err_left_body,
        in_specs=[full] * 2,
        out_specs=full,
        out_shape=jax.ShapeDtypeStruct((RANK, err.shape[1]), f32),
        compiler_params=pltpu.CompilerParams(vmem_limit_bytes=BIG),
        name="err_left",
    )(factor, err)


def err_right_body(x_ref, e_ref, o_ref, *, offset):
    pieces = split3(x_ref[...])
    rows = pieces.shape[1]
    blocks = o_ref.shape[1] // LANES

    for block in range(blocks):
        o_ref[:, block * LANES : (block + 1) * LANES] = join3(nn(pieces, e_ref[block * rows : (block + 1) * rows]))


def err_right(ortho, err, start, cols_n):
    rows = ortho.shape[1]
    full = pl.BlockSpec(memory_space=pltpu.VMEM)
    step = rows * cols_n // LANES
    return pl.pallas_call(
        functools.partial(err_right_body, offset=0),
        grid=(1,),
        in_specs=[
            pl.BlockSpec((RANK, rows), lambda i: (0, 0)),
            pl.BlockSpec((pl.Element(step), pl.Element(LANES)), lambda i: (start // LANES, 0)),
        ],
        out_specs=pl.BlockSpec((RANK, cols_n), lambda i: (0, 0)),
        out_shape=jax.ShapeDtypeStruct((RANK, cols_n), f32),
        compiler_params=pltpu.CompilerParams(vmem_limit_bytes=BIG),
        name="err_right",
    )(ortho, err)


def finish_body(a0, a1, b0, b1, e_ref, o_ref, r_ref, *rest, rows, blocks, gain):
    err_out, app_out = rest[-2:]
    o_high = o_ref[...].astype(bf16)
    o_low = (o_ref[...] - o_high.astype(f32)).astype(bf16)
    left = jnp.concatenate([o_high, o_low, o_high], axis=0)
    lhs0 = a0[...].T
    lhs1 = a1[...].T
    left_t = left.T
    for block in range(blocks):
        cols = slice(block * LANES, (block + 1) * LANES)
        r_part = r_ref[:, cols]
        r_high = r_part.astype(bf16)
        r_low = (r_part - r_high.astype(f32)).astype(bf16)
        approx = nn(left_t, jnp.concatenate([r_high, r_high, r_low], axis=0))
        grad = nn(lhs0, b0[:, cols]) + nn(lhs1, b1[:, cols])
        at = pl.ds(block, rows, stride=blocks)
        app_out[at, :] = approx
        err_out[at, :] = (gain * grad + e_ref[block].astype(f32)) - approx


def finish(pair0, pair1, err3, ortho, right, start, gain, bufs):
    a0, b0 = pair0
    a1, b1 = pair1
    rows_n, cols_n = a0.shape[1], b0.shape[1]
    seq = a0.shape[0]
    blocks = cols_n // LANES
    rows = 128 if rows_n % 128 == 0 else rows_n
    step = rows * blocks
    flat_rows = FLAT // LANES
    whole = lambda i: (0, 0)
    flat_spec = pl.BlockSpec((pl.Element(step), pl.Element(LANES)), lambda i: (pl.multiple_of(start // LANES + i * step, 16), 0))
    in_specs = [
        pl.BlockSpec((seq, rows), lambda i: (0, i)),
        pl.BlockSpec((seq, rows), lambda i: (0, i)),
        pl.BlockSpec((seq, cols_n), whole, pipeline_mode=pl.Buffered(1)),
        pl.BlockSpec((seq, cols_n), whole, pipeline_mode=pl.Buffered(1)),
        pl.BlockSpec((blocks, rows, LANES), lambda i: (0, i, 0)),
        pl.BlockSpec((RANK, rows), lambda i: (0, i)),
        pl.BlockSpec((RANK, cols_n), whole, pipeline_mode=pl.Buffered(1)),
    ]
    args = [a0, a1, b0, b1, err3, ortho, right]
    aliases = {}
    if bufs is not None:
        in_specs += [pl.BlockSpec(memory_space=pl.ANY)] * 2
        args += list(bufs)
        aliases = {7: 0, 8: 1}
    return pl.pallas_call(
        functools.partial(finish_body, rows=rows, blocks=blocks, gain=gain),
        grid=(rows_n // rows,),
        in_specs=in_specs,
        out_specs=[flat_spec, flat_spec],
        out_shape=[jax.ShapeDtypeStruct((flat_rows, LANES), f32)] * 2,
        input_output_aliases=aliases,
        compiler_params=pltpu.CompilerParams(vmem_limit_bytes=BIG),
        name="finish",
    )(*args)


def tail_body(e_ref, buf0, buf1, err_out, app_out):
    err_out[...] = e_ref[...].astype(f32)
    app_out[...] = jnp.zeros_like(app_out)


def finish_tail(err_flat, start, bufs):
    flat_rows = FLAT // LANES
    count = flat_rows - start // LANES
    steps = 12
    step = count // steps
    assert step * steps == count and step % 16 == 0
    spec = pl.BlockSpec((pl.Element(step), pl.Element(LANES)), lambda i: (pl.multiple_of(start // LANES + i * step, 16), 0))
    return pl.pallas_call(
        tail_body,
        grid=(steps,),
        in_specs=[spec] + [pl.BlockSpec(memory_space=pl.ANY)] * 2,
        out_specs=[spec, spec],
        out_shape=[jax.ShapeDtypeStruct((flat_rows, LANES), f32)] * 2,
        input_output_aliases={1: 0, 2: 1},
        compiler_params=pltpu.CompilerParams(vmem_limit_bytes=BIG),
        name="finish_tail",
    )(err_flat, *bufs)


def swap_body(*refs, n_enc, n_dec):
    n = n_enc + n_dec
    src, dst = refs[:n], refs[n : 2 * n]
    send, recv = refs[2 * n :]
    me = lax.axis_index("section")
    other = 1 - me
    barrier = pltpu.get_barrier_semaphore()
    pl.semaphore_signal(barrier, inc=1, device_id={"section": other}, device_id_type=pl.DeviceIdType.MESH)
    pl.semaphore_wait(barrier, 1)

    def copy(i):
        return pltpu.make_async_remote_copy(
            src_ref=src[i],
            dst_ref=dst[i],
            send_sem=send.at[i],
            recv_sem=recv.at[i],
            device_id={"section": other},
            device_id_type=pl.DeviceIdType.MESH,
        )

    enc, dec = range(n_enc), range(n_enc, n)

    @pl.when(me == 0)
    def _():
        for i in dec:
            copy(i).start()
        for i in dec:
            copy(i).wait_send()
        for i in enc:
            copy(i).wait_recv()

    @pl.when(me == 1)
    def _():
        for i in enc:
            copy(i).start()
        for i in enc:
            copy(i).wait_send()
        for i in dec:
            copy(i).wait_recv()


def swap(enc, dec):
    arrays = list(enc) + list(dec)
    n = len(arrays)
    outs = pl.pallas_call(
        functools.partial(swap_body, n_enc=len(enc), n_dec=len(dec)),
        in_specs=[pl.BlockSpec(memory_space=pl.ANY)] * n,
        out_specs=[pl.BlockSpec(memory_space=pl.ANY)] * n,
        out_shape=[jax.ShapeDtypeStruct(a.shape, a.dtype) for a in arrays],
        scratch_shapes=[pltpu.SemaphoreType.DMA((n,)), pltpu.SemaphoreType.DMA((n,))],
        compiler_params=pltpu.CompilerParams(collective_id=1, has_side_effects=True),
        name="swap",
    )(*arrays)
    return outs[: len(enc)], outs[len(enc) :]


def pack_rows(rows, pieces, width, length):
    empty = jnp.zeros((width,), f32)
    parts = [empty if row is None else row for row in rows] + pieces
    used = sum(part.shape[0] for part in parts)
    return jnp.concatenate(parts + [jnp.zeros((length - used,), f32)])


def local(pixels, visible, masked, loss_mask, master, momentum, vectors, vec_moment, factors, errors):
    sec = lax.axis_index("section")
    replicas = lax.axis_size("dp")
    replica_id = lax.axis_index("dp")

    low_own = lax.all_gather(master[0].astype(bf16), "dp", axis=0, tiled=True)
    low_both = lax.all_gather(low_own, "section", axis=0, tiled=True).reshape(-1, LANES)
    vec_both = lax.all_gather(vectors[0], "section", axis=0)
    fac_both = lax.all_gather(factors[0], "section", axis=0)
    count = lax.psum(jnp.sum(loss_mask).astype(f32), "dp")

    vis = lax.dynamic_index_in_dim(visible, sec, 0, keepdims=False)
    mas = lax.dynamic_index_in_dim(masked, sec, 0, keepdims=False)
    mask_row = lax.dynamic_index_in_dim(loss_mask, sec, 0, keepdims=False).astype(f32)
    order = jnp.concatenate([vis, mas])
    pix = lax.dynamic_index_in_dim(pixels, sec, 0, keepdims=False)
    pick = (order[:, None] == jnp.arange(SEQ, dtype=jnp.int32)[None, :]).astype(bf16)
    pix_order = nn(pick, pix).astype(bf16)
    pix_vis = pix_order[:VIS]
    target = pix_order[VIS:].astype(f32)
    table_dec = positions_at(order, DD)
    table_enc = positions_at(vis, DE)
    err_flat = errors.reshape(FLAT // LANES, LANES)

    def errs_for(section):
        def run():
            stacks = unflat_all(err_flat, 0, section, stacked=True)
            lefts = []
            col_at = 0
            for stack, (rows_n, cols_n) in zip(stacks, section_shapes(section)):
                lefts.append(err_left(factors[0][:, col_at : col_at + cols_n], stack))
                col_at += cols_n
            flat = jnp.concatenate([stack.reshape(-1, LANES) for stack in stacks])
            pad = FLAT // LANES - flat.shape[0]
            flat = jnp.concatenate([flat, jnp.zeros((pad, LANES), bf16)]) if pad else flat
            zero = [jnp.zeros((RANK, n), f32) for n in ROWS_L]
            zero[section] = jnp.concatenate(lefts, axis=1)
            return flat, jnp.concatenate(zero, axis=1)

        return run

    err_stack, err_lefts = lax.cond(sec == 0, errs_for(0), errs_for(1))

    enc = unflat_all(low_both, 0, 0)
    dec = unflat_all(low_both, FLAT, 1)
    rows_e, bias_e, unused = unpack_vecs(vec_both[0], DE, FFE)
    rows_d, bias_d, extra_d = unpack_vecs(vec_both[1], DD, FFD)

    embedded = nn(pix_vis, enc[4]) + rows_e[10] + table_enc
    coded, kept_e = block_forward(embedded, enc, rows_e, bias_e, HEADS_ENC)
    sent_full, sent_pull = jax.vjp(layer_norm, coded, rows_e[4], rows_e[5])
    sent = sent_full.astype(bf16)
    projected = nn(sent, dec[5]) + extra_d
    filled = jnp.concatenate([projected, jnp.broadcast_to(rows_d[10], (SEQ - VIS, DD))]) + table_dec
    result, kept_d = block_forward(filled, dec, rows_d, bias_d, HEADS_DEC)
    final_full, final_pull = jax.vjp(layer_norm, result[VIS:], rows_d[4], rows_d[5])
    final = final_full.astype(bf16)
    residual = nt(final, dec[4]) - target
    loss_part = jnp.sum(mask_row * jnp.mean(residual * residual, axis=1)) / count
    grad_pred = (mask_row[:, None] * (2.0 * residual / PATCH) / count).astype(bf16)
    grad_picked, v_gain3, v_shift3 = final_pull(nn(grad_pred, dec[4]))
    grad_result = jnp.concatenate([jnp.zeros((VIS, DD), f32), grad_picked])
    grad_filled, pairs_d, vrows_d, v_up_d = block_backward(kept_d, grad_result, dec, rows_d, HEADS_DEC)
    b_proj = grad_filled[:VIS].astype(bf16)
    pairs_d = pairs_d + [(grad_pred, final), (sent, b_proj)]
    vrows_d[4], vrows_d[5], vrows_d[10] = v_gain3, v_shift3, jnp.sum(grad_filled[VIS:], axis=0)
    vec_d = pack_rows(vrows_d, [v_up_d, jnp.sum(b_proj.astype(f32), axis=0)], DD, VLEN)
    grad_sent = nt(b_proj, dec[5]).astype(bf16)
    grad_coded, v_gain3, v_shift3 = sent_pull(grad_sent.astype(f32))
    grad_start, pairs_e, vrows_e, v_up_e = block_backward(kept_e, grad_coded, enc, rows_e, HEADS_ENC)
    b_start = grad_start.astype(bf16)
    pairs_e = pairs_e + [(pix_vis, b_start)]
    vrows_e[4], vrows_e[5], vrows_e[10] = v_gain3, v_shift3, jnp.sum(b_start.astype(f32), axis=0)
    vec_e = pack_rows(vrows_e, [v_up_e], DE, VLEN)

    pairs = pairs_e + pairs_d
    gain = float(replicas)
    xs = []
    for section in range(2):
        col_at = 0
        for rows_n, cols_n in section_shapes(section):
            xs.append(fac_both[section][:, col_at : col_at + cols_n])
            col_at += cols_n
    lefts = skinny(xs, [b for a, b in pairs], [a for a, b in pairs])
    left_part = gain * jnp.concatenate(lefts, axis=1) + err_lefts
    left_sum, vec_sum, loss_sum = lax.psum((left_part, jnp.stack([vec_e, vec_d]), loss_part), ("section", "dp"))

    n_enc = len(pairs_e)
    flat_e = [x for pair in pairs_e for x in pair]
    flat_d = [x for pair in pairs_d for x in pair]
    other_e, other_d = swap(flat_e, flat_d)

    widths = [rows_n for s in range(2) for rows_n, cols_n in section_shapes(s)]
    ortho = orthonormal(left_sum, widths, 1.0 / replicas)
    orthos = []
    at = 0
    for width in widths:
        orthos.append(ortho[:, at : at + width])
        at += width
    rights = skinny(orthos, [a for a, b in pairs], [b for a, b in pairs])

    def err_rights_for(section):
        def run():
            start = 0
            outs = []
            base = 0 if section == 0 else n_enc
            for i, (rows_n, cols_n) in enumerate(section_shapes(section)):
                outs.append(err_right(orthos[base + i], err_stack, start, cols_n))
                start += rows_n * cols_n
            zero = [jnp.zeros((RANK, n), f32) for n in COLS_R]
            zero[section] = jnp.concatenate(outs, axis=1)
            return jnp.concatenate(zero, axis=1)

        return run

    right_part = gain * jnp.concatenate(rights, axis=1) + lax.cond(sec == 0, err_rights_for(0), err_rights_for(1))
    right_sum = lax.psum(right_part, ("section", "dp")) / replicas

    squares = jnp.sum(vec_sum * vec_sum)
    row_at = col_at = 0
    for section in range(2):
        for rows_n, cols_n in section_shapes(section):
            o_part = ortho[:, row_at : row_at + rows_n]
            r_part = right_sum[:, col_at : col_at + cols_n]
            gram_o = jnp.sum(o_part[:, None, :] * o_part[None, :, :], axis=-1)
            gram_r = jnp.sum(r_part[:, None, :] * r_part[None, :, :], axis=-1)
            squares = squares + jnp.sum(gram_o * gram_r)
            row_at += rows_n
            col_at += cols_n
    norm = jnp.sqrt(squares)
    scale = jnp.minimum(1.0, clip_limit / (norm + 1e-06))

    def finish_for(section):
        def run():
            mine = pairs_e if section == 0 else pairs_d
            flat = other_e if section == 0 else other_d
            theirs = [(flat[2 * i], flat[2 * i + 1]) for i in range(len(mine))]
            bufs = None
            start = 0
            base = 0 if section == 0 else n_enc
            col_at = 0 if section == 0 else COLS_R[0]
            for i, (rows_n, cols_n) in enumerate(section_shapes(section)):
                blocks = cols_n // LANES
                stack = lax.slice_in_dim(err_stack, start // LANES, (start + rows_n * cols_n) // LANES, axis=0)
                stack = stack.reshape(blocks, rows_n, LANES)
                bufs = finish(
                    mine[i], theirs[i], stack, orthos[base + i],
                    right_sum[:, col_at : col_at + cols_n], start, gain, bufs,
                )
                start += rows_n * cols_n
                col_at += cols_n
            if start < FLAT:
                bufs = finish_tail(err_flat, start, bufs)
            return bufs

        return run

    new_errors, approx = lax.cond(sec == 0, finish_for(0), finish_for(1))
    shard_len = master.shape[1]
    own_part = lax.dynamic_slice_in_dim(approx.reshape(-1), replica_id * shard_len, shard_len)
    rate = learning_rate()
    new_moment = moment_decay * momentum[0] + scale * own_part
    new_master = master[0] - rate * new_moment
    vec_own = lax.dynamic_index_in_dim(vec_sum, sec, 0, keepdims=False)
    new_vm = moment_decay * vec_moment[0] + scale * vec_own
    new_vectors = vectors[0] - rate * new_vm
    right_e, right_d = right_sum[:, : COLS_R[0]], right_sum[:, COLS_R[0] :]
    cols_total = factors.shape[2]
    right_d = jnp.pad(right_d, ((0, 0), (0, cols_total - COLS_R[1])))
    right_e = jnp.pad(right_e, ((0, 0), (0, cols_total - COLS_R[0])))
    new_factors = jnp.where(sec == 0, right_e, right_d)
    return (
        new_master[None],
        new_master.astype(bf16)[None],
        new_moment[None],
        new_vectors[None],
        new_vm[None],
        new_factors[None],
        new_errors.reshape(1, 1, -1),
        loss_sum.reshape(1),
        norm.reshape(1),
    )


def solution(mesh):
    return jax.shard_map(
        local,
        mesh=mesh,
        in_specs=(
            P("dp", None, None),
            P("dp", None),
            P("dp", None),
            P("dp", None),
            P("section", "dp"),
            P("section", "dp"),
            P("section", None),
            P("section", None),
            P("section", None, None),
            P("section", "dp", None),
        ),
        out_specs=(
            P("section", "dp"),
            P("section", "dp"),
            P("section", "dp"),
            P("section", None),
            P("section", None),
            P("section", None, None),
            P("section", "dp", None),
            P(),
            P(),
        ),
        check_vma=False,
    )
```

time: 2620 us -> 1430 us (0.55)
  matrix products: 620 us -> 99 us
  other arithmetic: 784 us -> 402 us
  Pallas kernels: 0 us -> 345 us
  local copies, waits for them, and re-layouts: 335 us -> 96.7 us
  waiting for transfers between devices: 575 us -> 353 us
  loops' own time: 127 us -> 0.72 us
  blocking collectives: 128 us -> 90.3 us
    dot_general x82 -> x22, matrix products: 620 us -> 99 us  [the longest x12 65.3 us: nn(): lax.dot_general(left, right, (((1,), (0,)), ((), ())), preferred_element_...]
    pallas_call x0 -> x44, Pallas kernels: none -> 345 us  [the longest x17 68.6 us: unflat(): pl.pallas_call(functools.partial(unflat_body, blocks=blocks, rows=rows, s...]
    unnamed x1 -> x6, other arithmetic: 0.73 us -> 306 us
    reduce_sum x106 -> x47, other arithmetic: 294 us -> 30.2 us  [the longest x11 13.1 us: local(): gram_o = jnp.sum(o_part[:, None, :] * o_part[None, :, :], axis=-1)]
    psum x2, waiting for transfers between devices: 360 us -> 182 us  [the longest x1 127 us: local(): right_sum = lax.psum(right_part, ('section', 'dp')) / replicas]
    convert_element_type x11 -> x13, other arithmetic: 156 us -> 23.5 us  [the longest x2 10.2 us: block_forward(): normed = layer_norm(tokens, rows[0], rows[1]).astype(bf16)]
    another operation x11 -> x3, loops' own time: 127 us -> 0.72 us  [the longest x1 0.47 us: local(): new_errors, approx = lax.cond(sec == 0, finish_for(0), finish_for(1))]
    mul x8 -> x1, other arithmetic: 107 us -> 0.59 us  [local(): mask_row[:, None] * (2.0 * residual / PATCH) / count]
  transfers between devices with their start and end apart: 7 -> 4, of which waited for: 4 -> 3; matrix products, arithmetic and copies ran while one was open for 2% -> 24% of each run, Pallas kernels for 0% -> 5%
where the time goes in v1:
time: 1430 us; the launch traced here: 1410 us
  other arithmetic  402 us (28%)
  waiting for transfers between devices  353 us (25%)
  Pallas kernels  345 us (24%)
  matrix products  99 us (7%)
  local copies, waits for them, and re-layouts  96.7 us (7%)
  blocking collectives  90.3 us (6%)
  between operations  27 us (2%)
    unnamed x6, other arithmetic  306 us
    all_gather x1, waiting for transfers between devices, local(): low_own = lax.all_gather(master[0].astype(bf16), 'dp', axis=0, tiled=True)  171 us
    psum x1, waiting for transfers between devices, local(): right_sum = lax.psum(right_part, ('section', 'dp')) / replicas  127 us
    pallas_call x17, Pallas kernels, unflat(): pl.pallas_call(functools.partial(unflat_body, blocks=blocks, rows=rows, s...  68.6 us
    dot_general x12, matrix products, nn(): lax.dot_general(left, right, (((1,), (0,)), ((), ())), preferred_element_...  65.3 us
    pallas_call x6, Pallas kernels, finish(): pl.pallas_call(functools.partial(finish_body, rows=rows, blocks=blocks, g...  65.2 us
    pallas_call x2, Pallas kernels, attend_back(): pl.pallas_call(functools.partial(attend_back_body, size=size, rows_q=rows...  60.5 us
    psum x1, waiting for transfers between devices, local(): lax.psum((left_part, jnp.stack([vec_e, vec_d]), loss_part), ('section', '...  54.5 us
  transfers between devices with their start and end apart: 4, of which 3 were waited for; matrix products, arithmetic and copies ran while one was open for 24% of the time, Pallas kernels for 5%

profile of v1, /device:TPU:1, one launch (start us, length us, event | category | flops | bytes accessed | tf_op | source)
XLA Modules:
  0.0 1413.4 jit_solution(9834034449229139147)
XLA Ops:
  7.3 2.6 convert_element_type.185
  11.2 170.5 %all-gather.4.cloned.1.call-done = bf16[7225344]{0:T(1024)(128)(2,1)} async-done(((bf16[451584]{0:T(1024)(128)(2,1)}), bf16[7225344]{0:T(1024)(128)(2,1)}) %all-gather.4.cloned.1.call-update) | async-done | bytes 14450704 | tf_op jit(solution)/shard_map/all_gather | solution.py:533
  183.2 2.9 broadcast_multiply_fusion
  186.2 33.0 %psum.35 = f32[]{:T(128)} all-reduce(f32[]{:T(128)S(6)} %convert_element_type.207), channel_id=1, replica_groups=mesh['section'=2,'dp'=16] {'dp'}, use_global_device_ids=true, to_apply=%region_13.14 | all-reduce | flops 1 | bytes 8 | tf_op jit(solution)/shard_map/psum | solution.py:537
  219.2 9.3 all-gather
  238.1 306.0 %reduce.13 = bf16[7225344]{0:T(1024)(128)(2,1)} reduce(bf16[1,1,7225344]{2,1,0:T(2,128)(2,1)} %param.25, bf16[]{:T(256)} %constant.292), dimensions={0,1}, to_apply=%param.25.reduce_sub_computation | reduce | bytes 28901378 | tf_op args[9]
  544.1 49.6 %conditional.3 = (bf16[56448,128]{1,0:T(8,128)(2,1)}, f32[8,10112]{1,0:T(8,128)S(1)}) conditional(s32[]{:T(128)} %convert_element_type.232, (bf16[56448,128]{1,0:T(8,128)(2,1)}, f32[1,8,7680]{2,1,0:T(8,128)S(1)}) %tuple.175, (bf16[56448,128]{1,0:T(8,128)(2,1)}, f32[1,8,7680]{2,1,0:T(8,128)S(1)}) %tuple.176), branch_computations={%region_53.54_spmd, %region_54.55_spmd} | conditional | bytes 65009948 | solution.py:569
  544.3 5.8 unflat.25.e_ref
  550.8 3.0 err_left.14
  553.7 2.9 unflat.27.e_ref
  566.1 4.5 unflat.24.e_ref
  571.2 3.0 err_left.13
  574.2 3.8 unflat.22.e_ref
  578.5 2.7 err_left.11
  582.3 2.7 constant_dynamic-update-slice_fusion.5
  590.4 3.3 broadcast_dynamic-update-slice_fusion
  602.0 6.3 unflat.34
  608.2 3.3 unflat.35
  611.5 7.0 unflat.36
  618.5 9.1 unflat.37
  627.6 3.0 unflat.38
  630.5 3.7 unflat.39
  636.1 4.5 unflat.41
  640.7 5.9 unflat.42
  648.3 4.0 fusion.93
  655.0 6.1 attend.2
  663.9 11.4 multiply_convert_fusion.1
  678.0 8.6 fusion.16
  686.6 8.7 multiply_reduce_fusion.5
  695.3 11.8 add_convert_fusion.1.q_ref.k_ref.v_ref
  707.1 36.8 %attend.3 = (f32[1024,512]{1,0:T(8,128)}, f32[4,4,1024]{2,1,0:T(4,128)}) custom-call(bf16[1024,1536]{1,0:T(8,128)(2,1)} %add_convert_fusion.1.q_ref.k_ref.v_ref, bf16[1024,1536]{1,0:T(8,128)(2,1)} %add_convert_fusion.1.q_ref.k_ref.v_ref, bf16[1024,1536]{1,0:T(8,128)(2,1)} %add_convert_fusion.1.q_ref.k_ref.v_ref), custom_call_target="tpu_custom_call" | custom-call | tf_op jit(solution)/shard_map/attend/pallas_call | solution.py:164
  745.7 7.6 fusion.96
  754.9 21.5 %multiply_convert_fusion = (bf16[1024,2048]{1,0:T(8,128)(2,1)S(1)}, f32[1024,2048]{1,0:T(8,128)}, f32[1024,2048]{1,0:T(8,128)}) fusion(f32[2048]{0:T(1024)S(1)} %bitcast.190, bf16[1024,512]{1,0:T(8,128)(2,1)S(1)} %add_convert_fusion.3.refs_29_.refs_18_.refs_14_, bf16[512,2048]{1,0:T(8,128)(2,1)S(1)} %copy-done.56), kind=kOutput, calls=%fused_computation.29 | convolution fusion | flops 2285895680 | bytes 24125440 | tf_op jit(solution)/shard_map/dot_general | solution.py:34
  776.5 2.3 fusion.97
  785.0 9.6 convert_reduce_fusion
  794.6 3.3 multiply_reduce_fusion
  802.7 53.0 %attend_back.2 = (bf16[1024,512]{1,0:T(8,128)(2,1)}, bf16[1024,512]{1,0:T(8,128)(2,1)}, bf16[1024,512]{1,0:T(8,128)(2,1)}) custom-call(bf16[1024,1536]{1,0:T(8,128)(2,1)} %add_convert_fusion.1.q_ref.k_ref.v_ref, bf16[1024,1536]{1,0:T(8,128)(2,1)} %add_convert_fusion.1.q_ref.k_ref.v_ref, bf16[1024,1536]{1,0:T(8,128)(2,1)} %add_convert_fusion.1.q_ref.k_ref.v_ref, ...), custom_call_target="tpu_custom_call" | custom-call | tf_op jit(solution)/shard_map/attend_back/pallas_call | solution.py:228
  858.5 9.3 fusion.65
  867.9 10.3 multiply_reduce_fusion.1
  878.2 10.0 add_convert_fusion.4
  899.3 7.5 attend_back.3
  915.8 16.4 %skinny.2 = (f32[8,768]{1,0:T(8,128)}, f32[8,768]{1,0:T(8,128)}, f32[8,768]{1,0:T(8,128)}, f32[8,3072]{1,0:T(8,128)}, f32[8,192]{1,0:T(8,128)}, /*index=5*/f32[8...) custom-call(f32[8,2304]{1,0:T(8,128)} %slice.493.refs_0_, ...), custom_call_target="tpu_custom_call" | custom-call | tf_op jit(solution)/shard_map/skinny/pallas_call | solution.py:299
  937.9 45.9 %psum.39 = f32[1]{0:T(128)} all-reduce(f32[1]{0:T(128)} %bitcast.53), channel_id=1, replica_groups=mesh['section'=2,'dp'=16] {'section','dp'}, use_global_device_ids=true, to_apply=%region_96.97 | all-reduce | flops 1 | bytes 8 | tf_op jit(solution)/shard_map/psum | solution.py:613
  983.8 28.7 %swap.1 = (bf16[256,768]{1,0:T(8,128)(2,1)}, bf16[256,2304]{1,0:T(8,128)(2,1)}, bf16[256,768]{1,0:T(8,128)(2,1)}, bf16[256,768]{1,0:T(8,128)(2,1)}, bf16[256,768...) custom-call(bf16[256,768]{1,0:T(8,128)(2,1)} %copy-done.36, ...), custom_call_target="tpu_custom_call" | custom-call | tf_op jit(solution)/shard_map/swap/pallas_call | solution.py:509
  1012.5 54.5 %all-reduce.6.cloned.1.call-done.left_ref = f32[8,10112]{1,0:T(8,128)} async-done(((f32[8,10112]{1,0:T(8,128)}), f32[8,10112]{1,0:T(8,128)}) %all-reduce.6.cloned.1.call-update) | async-done | bytes 323600 | tf_op jit(solution)/shard_map/psum | solution.py:613
  1067.0 5.1 orthonormal.1
  1079.0 16.1 %skinny.3 = (f32[8,2304]{1,0:T(8,128)}, f32[8,768]{1,0:T(8,128)}, f32[8,3072]{1,0:T(8,128)}, f32[8,768]{1,0:T(8,128)}, f32[8,768]{1,0:T(8,128)}, /*index=5*/f32[...) custom-call(f32[8,768]{1,0:T(8,128)} %get-tuple-element.494.refs_0_,, ...), custom_call_target="tpu_custom_call" | custom-call | tf_op jit(solution)/shard_map/skinny/pallas_call | solution.py:299
  1121.4 22.2 %conditional.4 = (f32[8,13312]{1,0:T(8,128)}) conditional(s32[]{:T(128)} %convert_element_type.232, (f32[8,512]{1,0:T(8,128)}, bf16[56448,128]{1,0:T(8,128)(2,1)}, f32[8,512]{1,0:T(8,128)}, f32[8,512]{1,0:T(8,128)}, f32[8,2048]{1,0:T(8,128)}, /*index=5*/f32[8,192]{1,0:T(8,128)}, f32[8,768]{1,0:T(8,128)S(1)}) %tuple.35, (f32[8,768]{1,0:T(8,128)}, ...), branch_computations={%region_57.58_spmd, %region_58.59_spmd} | conditional | bytes 671752 | solution.py:643
  1121.4 2.4 err_right.11
  1129.1 2.6 err_right.13
  1133.2 2.6 err_right.14
  1147.6 127.5 %all-reduce.8.cloned.1.call-done = (f32[8,13312]{1,0:T(8,128)}, f32[2,11520]{1,0:T(2,128)}) async-done(((f32[8,13312]{1,0:T(8,128)}, f32[2,11520]{1,0:T(2,128)}), (f32[8,13312]{1,0:T(8,128)}, f32[2,11520]{1,0:T(2,128)})) %all-reduce.8.cloned.1.call-update) | async-done | bytes 518160 | tf_op jit(solution)/shard_map/psum | solution.py:644
  1294.0 95.5 %conditional.5 = (f32[1,1,7225344]{2,1,0:T(1,128)}, f32[7225344]{0:T(1024)}) conditional(s32[]{:T(128)} %convert_element_type.232, (bf16[56448,128]{1,0:T(8,128)(2,1)}, f32[8,13312]{1,0:T(8,128)S(1)}, bf16[1024,512]{1,0:T(8,128)(2,1)}, bf16[1024,512]{1,0:T(8,128)(2,1)}, bf16[1024,1536]{1,0:T(8,128)(2,1)}, /*index=5*/bf16[1024,1536]{1,0:T(8,128)(2,1)}, ...), branch_computations={%region_92.93_spmd, %region_93.94_spmd} | conditional | bytes 39182604 | solution.py:685
  1294.2 2.8 slice.304
  1297.6 12.3 finish.11
  1313.1 6.2 finish.12
  1319.4 4.5 fusion.79
  1325.3 19.1 %finish.13 = (f32[56448,128]{1,0:T(8,128)}, f32[56448,128]{1,0:T(8,128)}) custom-call(bf16[1024,512]{1,0:T(8,128)(2,1)} %get-tuple-element.198.a0, bf16[1024,512]{1,0:T(8,128)(2,1)} %get-tuple-element.199.a1, bf16[1024,2048]{1,0:T(8,128)(2,1)} %get-tuple-element.200.b0, ...), custom_call_target="tpu_custom_call", output_to_operand_aliasing={{0}: (7, {}), {1}: (8, {})} | custom-call | tf_op jit(solution)/shard_map/cond/branch_0_fun/finish/pallas_call | solution.py:429
  1344.4 18.5 %finish.14 = (f32[56448,128]{1,0:T(8,128)}, f32[56448,128]{1,0:T(8,128)}) custom-call(bf16[1024,2048]{1,0:T(8,128)(2,1)} %get-tuple-element.193.a0, bf16[1024,2048]{1,0:T(8,128)(2,1)} %get-tuple-element.194.a1, bf16[1024,512]{1,0:T(8,128)(2,1)} %get-tuple-element.195.b0, ...), custom_call_target="tpu_custom_call", output_to_operand_aliasing={{0}: (7, {}), {1}: (8, {})} | custom-call | tf_op jit(solution)/shard_map/cond/branch_0_fun/finish/pallas_call | solution.py:429
  1364.6 3.1 finish.15
  1369.8 6.0 finish.16
  1375.8 13.5 finish_tail.1
  1389.5 4.8 fusion.66
  1394.3 11.0 broadcast_in_dim.57
  (522 shorter events, 161.6 us)
Async XLA Ops:
  7.2 228.6 %copy-start = (bf16[2,1024,192]{1,2,0:T(8,128)(2,1)S(1)}, bf16[2,1024,192]{1,2,0:T(8,128)(2,1)}, u32[]{:S(2)}) copy-start(bf16[2,1024,192]{1,2,0:T(8,128)(2,1)} %param.16) | copy-start | bytes 2359300
  7.2 174.5 %all-gather.4.cloned.1.call-start = ((), (), s32[]{:S(2)}) async-start(), calls=%async_computation | async-start | bytes 15353856 | tf_op jit(solution)/shard_map/all_gather | solution.py:533
  9.8 590.3 %all-gather.6.cloned.1.call-start = ((), (), s32[]{:S(2)}) async-start(), calls=%async_computation.1 | async-start | bytes 43352064 | tf_op jit(solution)/shard_map/all_gather | solution.py:534
  181.8 37.4 %copy-start.81 = (f32[1,11520]{1,0:T(1,128)S(1)}, f32[1,11520]{1,0:T(1,128)}, u32[]{:S(2)}) copy-start(f32[1,11520]{1,0:T(1,128)} %param.22) | copy-start | bytes 138244
  181.8 48.0 %copy-start.58 = (f32[1,8,7680]{2,1,0:T(8,128)S(1)}, f32[1,8,7680]{2,1,0:T(8,128)}, u32[]{:S(2)}) copy-start(f32[1,8,7680]{2,1,0:T(8,128)} %param.24) | copy-start | bytes 737284
  181.8 52.8 %copy-start.146 = (s32[2,256]{1,0:T(2,128)S(1)}, s32[2,256]{1,0:T(2,128)}, u32[]{:S(2)}) copy-start(s32[2,256]{1,0:T(2,128)} %param.17) | copy-start | bytes 6148
  181.8 53.4 %copy-start.144 = (s32[2,768]{1,0:T(2,128)S(1)}, s32[2,768]{1,0:T(2,128)}, u32[]{:S(2)}) copy-start(s32[2,768]{1,0:T(2,128)} %param.18) | copy-start | bytes 18436
  181.8 885.2 %all-reduce.6.cloned.1.call-start = ((), (), s32[]{:S(2)}) async-start(), calls=%async_computation.2 | async-start | bytes 647168 | tf_op jit(solution)/shard_map/psum | solution.py:613
  574.2 7.0 copy-start.78
  574.2 7.1 copy-start.86
  574.2 7.1 copy-start.96
  577.9 7.0 copy-start.46
  581.2 4.6 copy-start.18
  593.7 8.3 copy-start.64
  594.4 7.6 copy-start.94
  596.7 55.9 %copy-start.90 = (f32[768]{0:T(1024)}, f32[768]{0:T(1024)S(1)}, u32[]{:S(2)}) copy-start(f32[768]{0:T(1024)S(1)} %get-tuple-element.417) | copy-start | bytes 9220
  596.7 67.0 %copy-start.92 = (f32[768]{0:T(1024)}, f32[768]{0:T(1024)S(1)}, u32[]{:S(2)}) copy-start(f32[768]{0:T(1024)S(1)} %get-tuple-element.412) | copy-start | bytes 9220
  648.3 4.5 copy-start.49
  652.3 10.0 copy-start.24
  655.0 7.4 copy-start.28
  662.3 13.0 copy-start.19
  662.3 13.0 slice-start.6
  662.9 12.4 copy-start.26
  662.9 12.4 copy-start.103
  663.2 12.1 copy-start.117
  663.9 11.4 copy-start.31
  663.9 11.4 slice-start.7
  676.9 9.7 copy-start.39
  677.4 17.9 %copy-start.21 = (bf16[256,768]{1,0:T(8,128)(2,1)}, bf16[256,768]{1,0:T(8,128)(2,1)S(1)}, u32[]{:S(2)}) copy-start(bf16[256,768]{1,0:T(8,128)(2,1)S(1)} %add_convert_fusion.7.refs_32_.refs_21_.refs_20_) | copy-start | bytes 1179652
  677.8 17.6 %copy-start.62 = (bf16[512,1536]{1,0:T(8,128)(2,1)S(1)}, bf16[512,1536]{1,0:T(8,128)(2,1)}, u32[]{:S(2)}) copy-start(bf16[512,1536]{1,0:T(8,128)(2,1)} %unflat.39) | copy-start | bytes 4718596
  745.7 7.6 copy-start.5
  754.2 22.3 %copy-start.6 = (bf16[1024,512]{1,0:T(8,128)(2,1)}, bf16[1024,512]{1,0:T(8,128)(2,1)S(1)}, u32[]{:S(2)}) copy-start(bf16[1024,512]{1,0:T(8,128)(2,1)S(1)} %add_convert_fusion.3.refs_29_.refs_18_.refs_14_) | copy-start | bytes 3145732
  754.9 21.6 %copy-start.57 = (bf16[2048,512]{1,0:T(8,128)(2,1)S(1)}, bf16[2048,512]{1,0:T(8,128)(2,1)}, u32[]{:S(2)}) copy-start(bf16[2048,512]{1,0:T(8,128)(2,1)} %unflat.42) | copy-start | bytes 6291460
  784.0 14.8 %copy-start.9 = (f32[768,512]{1,0:T(8,128)}, f32[768,512]{1,0:T(8,128)S(1)}, u32[]{:S(2)}) copy-start(f32[768,512]{1,0:T(8,128)S(1)} %broadcast_add_fusion) | copy-start | bytes 4718596
  785.0 9.6 copy-start.7
  858.5 9.4 copy-start.4
  867.9 10.3 copy-start.10
  867.9 10.3 copy-start.16
  878.2 12.4 slice-start.8
  878.2 10.7 copy-start.40
  878.2 10.7 copy-start.53
  878.2 12.3 slice-start.9
  888.9 5.5 slice-start.4
  899.3 11.5 copy-start.48
  906.8 4.4 copy-start.61
  915.8 20.2 %copy-start.95 = (f32[768]{0:T(1024)S(1)}, f32[768]{0:T(1024)}, u32[]{:S(2)}) copy-start(f32[768]{0:T(1024)} %copy-done.94) | copy-start | bytes 9220
  915.8 20.2 %copy-start.133 = (f32[768]{0:T(1024)S(1)}, f32[768]{0:T(1024)}, u32[]{:S(2)}) copy-start(f32[768]{0:T(1024)} %get-tuple-element.478) | copy-start | bytes 9220
  932.2 51.6 %copy-start.12 = (bf16[256,3072]{1,0:T(8,128)(2,1)S(1)}, bf16[256,3072]{1,0:T(8,128)(2,1)}, u32[]{:S(2)}) copy-start(bf16[256,3072]{1,0:T(8,128)(2,1)} %copy-done.11) | copy-start | bytes 4718596
  935.2 339.9 %all-reduce.8.cloned.1.call-start = ((), (), s32[]{:S(2)}) async-start(), calls=%async_computation.3 | async-start | bytes 1036288 | tf_op jit(solution)/shard_map/psum | solution.py:644
  1143.5 135.3 %copy-start.112 = (f32[8,8]{1,0:T(8,128)S(1)}, f32[8,8]{1,0:T(8,128)}, u32[]{:S(2)}) copy-start(f32[8,8]{1,0:T(8,128)} %multiply_reduce_fusion.25) | copy-start | bytes 772
  1143.5 136.0 %copy-start.108 = (f32[8,8]{1,0:T(8,128)S(1)}, f32[8,8]{1,0:T(8,128)}, u32[]{:S(2)}) copy-start(f32[8,8]{1,0:T(8,128)} %multiply_reduce_fusion.40) | copy-start | bytes 772
  1143.5 137.2 %copy-start.107 = (f32[8,8]{1,0:T(8,128)S(1)}, f32[8,8]{1,0:T(8,128)}, u32[]{:S(2)}) copy-start(f32[8,8]{1,0:T(8,128)} %multiply_reduce_fusion.35) | copy-start | bytes 772
  1143.6 137.8 %copy-start.106 = (f32[8,8]{1,0:T(8,128)S(1)}, f32[8,8]{1,0:T(8,128)}, u32[]{:S(2)}) copy-start(f32[8,8]{1,0:T(8,128)} %multiply_reduce_fusion.37) | copy-start | bytes 772
  1143.6 138.5 %copy-start.105 = (f32[8,8]{1,0:T(8,128)S(1)}, f32[8,8]{1,0:T(8,128)}, u32[]{:S(2)}) copy-start(f32[8,8]{1,0:T(8,128)} %multiply_reduce_fusion.38) | copy-start | bytes 772
  1143.6 140.3 %copy-start.111 = (f32[8,8]{1,0:T(8,128)S(1)}, f32[8,8]{1,0:T(8,128)}, u32[]{:S(2)}) copy-start(f32[8,8]{1,0:T(8,128)} %multiply_reduce_fusion.28) | copy-start | bytes 772
  1143.6 140.8 %copy-start.110 = (f32[8,8]{1,0:T(8,128)S(1)}, f32[8,8]{1,0:T(8,128)}, u32[]{:S(2)}) copy-start(f32[8,8]{1,0:T(8,128)} %multiply_reduce_fusion.30) | copy-start | bytes 772
  1143.6 141.4 %copy-start.109 = (f32[8,8]{1,0:T(8,128)S(1)}, f32[8,8]{1,0:T(8,128)}, u32[]{:S(2)}) copy-start(f32[8,8]{1,0:T(8,128)} %multiply_reduce_fusion.31) | copy-start | bytes 772
  1143.6 149.6 %copy-start.82 = (f32[1,11520]{1,0:T(1,128)S(1)}, f32[1,11520]{1,0:T(1,128)}, u32[]{:S(2)}) copy-start(f32[1,11520]{1,0:T(1,128)} %param.22) | copy-start | bytes 138244
  1143.6 149.6 %copy-start.89 = (f32[1,11520]{1,0:T(1,128)S(1)}, f32[1,11520]{1,0:T(1,128)}, u32[]{:S(2)}) copy-start(f32[1,11520]{1,0:T(1,128)} %param.23) | copy-start | bytes 138244
  1297.6 15.5 %copy-start.69 = (f32[8,512]{1,0:T(8,128)S(1)}, f32[8,512]{1,0:T(8,128)}, u32[]{:S(2)}) copy-start(f32[8,512]{1,0:T(8,128)} %get-tuple-element.207.o_ref) | copy-start | bytes 49156 | tf_op jit(solution)/shard_map/cond
  1319.4 6.0 copy-start.71
  1325.3 19.1 %copy-start.55 = (f32[8,2048]{1,0:T(8,128)S(1)}, f32[8,2048]{1,0:T(8,128)}, u32[]{:S(2)}) copy-start(f32[8,2048]{1,0:T(8,128)} %get-tuple-element.197.o_ref) | copy-start | bytes 196612 | tf_op jit(solution)/shard_map/cond
  1344.4 20.2 %copy-start.77 = (f32[8,192]{1,0:T(8,128)S(1)}, f32[8,192]{1,0:T(8,128)}, u32[]{:S(2)}) copy-start(f32[8,192]{1,0:T(8,128)} %get-tuple-element.192.o_ref) | copy-start | bytes 18436 | tf_op jit(solution)/shard_map/cond
  1389.5 15.8 %copy-start.1 = (bf16[2,1024,192]{1,2,0:T(8,128)(2,1)S(1)}, bf16[2,1024,192]{1,2,0:T(8,128)(2,1)}, u32[]{:S(2)}) copy-start(bf16[2,1024,192]{1,2,0:T(8,128)(2,1)} %param.16) | copy-start | bytes 2359300
  (80 other events, 170.3 us)
Sparse Core Ops, SparseCore 0:
  11.3 170.4 all-gather.3
  183.3 45.5 all-gather.5
  935.3 131.6 all-reduce.5
  1145.7 129.3 all-reduce.7

commit v2 on v1

--- a/solution.py
+++ b/solution.py
@@ -69,10 +69,6 @@
     if section == 0:
         return [(DE, 3 * DE), (DE, DE), (DE, FFE), (FFE, DE), (PATCH, DE)]
     return [(DD, 3 * DD), (DD, DD), (DD, FFD), (FFD, DD), (PATCH, DD), (DE, DD)]
-
-
-ROWS_L = [sum(rows for rows, cols in section_shapes(s)) for s in range(2)]
-COLS_R = [sum(cols for rows, cols in section_shapes(s)) for s in range(2)]
 
 
 def unpack_vecs(flat, width, hidden):
@@ -285,32 +281,71 @@
     return grad_tokens, pairs, [v_gain1, v_shift1, v_gain2, v_shift2, None, None, v_q, v_v, v_proj, v_down, None], v_up
 
 
-def skinny_body(*refs, counts):
-    n = counts
-    x_refs, u_refs, v_refs, outs = refs[:n], refs[n : 2 * n], refs[2 * n : 3 * n], refs[3 * n :]
-    for x_ref, u_ref, v_ref, o_ref in zip(x_refs, u_refs, v_refs, outs):
-        part = join3(nt(split3(x_ref[...]), u_ref[...]))
-        o_ref[...] = join3(nn(split3(part), v_ref[...]))
-
-
-def skinny(xs, us, vs):
-    n = len(xs)
+def tiles_of(width):
+    return -(-width // LANES)
+
+
+def spans(which):
+    at, found = [], []
+    for section in range(2):
+        start = 0
+        for shape in section_shapes(section):
+            found.append((section, start, shape[which]))
+            start += tiles_of(shape[which]) * LANES
+        at.append(start)
+    return found, at
+
+
+ROW_SPANS, ROW_WIDTHS = spans(0)
+COL_SPANS, COL_WIDTHS = spans(1)
+ROW_PAD = max(ROW_WIDTHS)
+VEC_TILES = -(-VLEN // (RANK * LANES))
+
+
+def sum_rows(replicas, tiles):
+    return -(-tiles // replicas) * replicas * RANK
+
+
+def put_tiles(out_ref, section, start, value):
+    width = value.shape[1]
+    for tile in range(tiles_of(width)):
+        here = min(LANES, width - tile * LANES)
+        row = (start // LANES + tile) * RANK
+        out_ref[section, row : row + RANK, :here] = value[:, tile * LANES : tile * LANES + here]
+
+
+def skinny_body(*refs, n, x_spans, y_spans, extra_row):
+    x_ref, u_refs, v_refs, tail_ref, out_ref = refs[0], refs[1 : 1 + n], refs[1 + n : 1 + 2 * n], refs[-2], refs[-1]
+    out_ref[...] = jnp.zeros_like(out_ref)
+    gain_ref = None
+    for u_ref, v_ref, (section, start, width), (out_section, out_start, unused) in zip(u_refs, v_refs, x_spans, y_spans):
+        part = join3(nt(split3(x_ref[section, :, start : start + width]), u_ref[...]))
+        put_tiles(out_ref, out_section, out_start, extra_row[1] * join3(nn(split3(part), v_ref[...])))
+    if extra_row[0]:
+        out_ref[:, extra_row[0] : extra_row[0] + tail_ref.shape[1]] = tail_ref[...]
+
+
+def skinny(x, us, vs, x_spans, y_spans, tail, tail_row, gain, rows):
+    n = len(us)
     full = pl.BlockSpec(memory_space=pltpu.VMEM)
     return pl.pallas_call(
-        functools.partial(skinny_body, counts=n),
-        in_specs=[full] * (3 * n),
-        out_specs=[full] * n,
-        out_shape=[jax.ShapeDtypeStruct((RANK, v.shape[1]), f32) for v in vs],
+        functools.partial(skinny_body, n=n, x_spans=x_spans, y_spans=y_spans, extra_row=(tail_row, gain)),
+        in_specs=[full] * (2 * n + 2),
+        out_specs=full,
+        out_shape=jax.ShapeDtypeStruct((2, rows, LANES), f32),
         compiler_params=pltpu.CompilerParams(vmem_limit_bytes=BIG),
         name="skinny",
-    )(*xs, *us, *vs)
-
-
-def ortho_body(left_ref, out_ref, *, widths, scale):
-    at = 0
+    )(x, *us, *vs, tail)
+
+
+def ortho_body(sum_ref, out_ref, wide, *, scale):
     rank_id = lax.broadcasted_iota(jnp.int32, (RANK, 1), 0)
-    for width in widths:
-        basis = left_ref[:, at : at + width] * scale
+    for section, start, width in ROW_SPANS:
+        padded = tiles_of(width) * LANES
+        for tile in range(padded // LANES):
+            row = (start // LANES + tile) * RANK
+            wide[:, tile * LANES : (tile + 1) * LANES] = sum_ref[section, row : row + RANK] * scale
+        basis = wide[:, :padded]
         for column in range(RANK):
             current = basis[column : column + 1]
             current = current * lax.rsqrt(jnp.sum(current * current, axis=1, keepdims=True) + 1e-12)
@@ -318,109 +353,203 @@
             basis = jnp.where(
                 rank_id > column, basis - dots * current, jnp.where(rank_id == column, current, basis)
             )
-        out_ref[:, at : at + width] = basis
-        at += width
-
-
-def orthonormal(left, widths, scale):
+        out_ref[section, :, start : start + padded] = basis
+
+
+def orthonormal(sums, scale):
     full = pl.BlockSpec(memory_space=pltpu.VMEM)
     return pl.pallas_call(
-        functools.partial(ortho_body, widths=widths, scale=scale),
+        functools.partial(ortho_body, scale=scale),
         in_specs=[full],
         out_specs=full,
-        out_shape=jax.ShapeDtypeStruct(left.shape, f32),
+        out_shape=jax.ShapeDtypeStruct((2, RANK, ROW_PAD), f32),
+        scratch_shapes=[pltpu.VMEM((RANK, FFE), f32)],
         name="orthonormal",
-    )(left)
-
-
-def err_left_body(x_ref, e_ref, o_ref):
-    total = jnp.zeros((e_ref.shape[1], 3 * RANK), f32)
+    )(sums)
+
+
+def chunk_rows(rows_n, cols_n):
+    if rows_n == PATCH:
+        return PATCH
+    return 128 if cols_n > 8 * LANES else 256
+
+
+def err_prep_body(e_ref, x_ref, *rest, blocks, rows):
+    out_ref, left_ref, wide = rest[-3:]
+    wide[...] = e_ref[0].reshape(rows * blocks, LANES).astype(f32)
     pieces = split3(x_ref[...])
-    for block in range(e_ref.shape[0]):
-        total = total + nt(e_ref[block], pieces[:, block * LANES : (block + 1) * LANES])
-    o_ref[...] = join3(total.T)
-
-
-def err_left(factor, err):
+    total = jnp.zeros((rows, 3 * RANK), f32)
+    for block in range(blocks):
+        part = wide[pl.ds(block, rows, stride=blocks), :].astype(bf16)
+        out_ref[block * rows : (block + 1) * rows, :] = part
+        total = total + nt(part, pieces[:, block * LANES : (block + 1) * LANES])
+    value = join3(total.T)
+    left_ref[...] = jnp.zeros_like(left_ref)
+    for tile in range(tiles_of(rows)):
+        here = min(LANES, rows - tile * LANES)
+        left_ref[tile * RANK : (tile + 1) * RANK, :here] = value[:, tile * LANES : tile * LANES + here]
+
+
+def err_prep(errors, factor, start, rows_n, cols_n, buf):
+    blocks = cols_n // LANES
+    rows = chunk_rows(rows_n, cols_n)
+    step = rows * blocks
+    steps = rows_n // rows
+    tiles = tiles_of(rows)
+    in_specs = [
+        pl.BlockSpec((pl.Element(1), pl.Element(1), pl.Element(step * LANES)), lambda i: (0, 0, pl.multiple_of(start + i * step * LANES, 1024))),
+        pl.BlockSpec((RANK, cols_n), lambda i: (0, 0)),
+    ]
+    args = [errors, factor]
+    aliases = {}
+    if buf is not None:
+        in_specs.append(pl.BlockSpec(memory_space=pl.ANY))
+        args.append(buf)
+        aliases = {2: 0}
+    return pl.pallas_call(
+        functools.partial(err_prep_body, blocks=blocks, rows=rows),
+        grid=(steps,),
+        in_specs=in_specs,
+        out_specs=[
+            pl.BlockSpec((pl.Element(step), pl.Element(LANES)), lambda i: (pl.multiple_of(start // LANES + i * step, 16), 0)),
+            pl.BlockSpec((tiles * RANK, LANES), lambda i: (i, 0)),
+        ],
+        out_shape=[
+            jax.ShapeDtypeStruct((FLAT // LANES, LANES), bf16),
+            jax.ShapeDtypeStruct((steps * tiles * RANK, LANES), f32),
+        ],
+        input_output_aliases=aliases,
+        scratch_shapes=[pltpu.VMEM((step, LANES), f32)],
+        name="err_prep",
+    )(*args)
+
+
+def err_right_body(x_ref, e_ref, o_ref, bufs, sems, *, section, scale):
+    plan = []
+    start = 0
+    for (rows_n, cols_n), row_span, col_span in zip(
+        section_shapes(section),
+        [span for span in ROW_SPANS if span[0] == section],
+        [span for span in COL_SPANS if span[0] == section],
+    ):
+        rows = chunk_rows(rows_n, cols_n)
+        blocks = cols_n // LANES
+        for chunk in range(rows_n // rows):
+            plan.append((start // LANES + chunk * rows * blocks, rows, blocks, row_span[1] + chunk * rows, col_span[1], chunk))
+        start += rows_n * cols_n
+    depth = bufs.shape[0]
+
+    def fetch(index):
+        at, rows, blocks = plan[index][:3]
+        slot = index % depth
+        return pltpu.make_async_copy(
+            e_ref.at[pl.ds(at, rows * blocks)], bufs.at[slot, pl.ds(0, rows * blocks)], sems.at[slot]
+        )
+
+    o_ref[...] = jnp.zeros_like(o_ref)
+    for index in range(min(depth - 1, len(plan))):
+        fetch(index).start()
+    for index, (at, rows, blocks, row_at, col_at, chunk) in enumerate(plan):
+        if index + depth - 1 < len(plan):
+            fetch(index + depth - 1).start()
+        fetch(index).wait()
+        pieces = split3(x_ref[section, :, row_at : row_at + rows])
+        for block in range(blocks):
+            part = join3(nn(pieces, bufs[index % depth, block * rows : (block + 1) * rows]))
+            row = (col_at // LANES + block) * RANK
+            if chunk == 0:
+                o_ref[row : row + RANK] = part
+            else:
+                o_ref[row : row + RANK] += part
+
+
+def err_right(ortho, err, section, rows):
     full = pl.BlockSpec(memory_space=pltpu.VMEM)
+    most = max(chunk_rows(*shape) * shape[1] // LANES for shape in section_shapes(section))
     return pl.pallas_call(
-        err_left_body,
-        in_specs=[full] * 2,
+        functools.partial(err_right_body, section=section, scale=1.0),
+        in_specs=[full, pl.BlockSpec(memory_space=pl.ANY)],
         out_specs=full,
-        out_shape=jax.ShapeDtypeStruct((RANK, err.shape[1]), f32),
-        compiler_params=pltpu.CompilerParams(vmem_limit_bytes=BIG),
-        name="err_left",
-    )(factor, err)
-
-
-def err_right_body(x_ref, e_ref, o_ref, *, offset):
-    pieces = split3(x_ref[...])
-    rows = pieces.shape[1]
-    blocks = o_ref.shape[1] // LANES
-
-    for block in range(blocks):
-        o_ref[:, block * LANES : (block + 1) * LANES] = join3(nn(pieces, e_ref[block * rows : (block + 1) * rows]))
-
-
-def err_right(ortho, err, start, cols_n):
-    rows = ortho.shape[1]
-    full = pl.BlockSpec(memory_space=pltpu.VMEM)
-    step = rows * cols_n // LANES
-    return pl.pallas_call(
-        functools.partial(err_right_body, offset=0),
-        grid=(1,),
-        in_specs=[
-            pl.BlockSpec((RANK, rows), lambda i: (0, 0)),
-            pl.BlockSpec((pl.Element(step), pl.Element(LANES)), lambda i: (start // LANES, 0)),
-        ],
-        out_specs=pl.BlockSpec((RANK, cols_n), lambda i: (0, 0)),
-        out_shape=jax.ShapeDtypeStruct((RANK, cols_n), f32),
+        out_shape=jax.ShapeDtypeStruct((rows, LANES), f32),
+        scratch_shapes=[pltpu.VMEM((4, most, LANES), bf16), pltpu.SemaphoreType.DMA((4,))],
         compiler_params=pltpu.CompilerParams(vmem_limit_bytes=BIG),
         name="err_right",
     )(ortho, err)
 
 
+def final_right_body(sum_ref, ortho_ref, vec_ref, right_ref, norm_ref, *, scale):
+    squares = jnp.sum(vec_ref[...] * vec_ref[...], keepdims=True)[0]
+    for (section, start, width), (unused, row_at, row_width) in zip(COL_SPANS, ROW_SPANS):
+        for tile in range(width // LANES):
+            row = (start // LANES + tile) * RANK
+            right_ref[section, :, start + tile * LANES : start + (tile + 1) * LANES] = sum_ref[section, row : row + RANK] * scale
+        o_part = ortho_ref[section, :, row_at : row_at + tiles_of(row_width) * LANES]
+        r_part = right_ref[section, :, start : start + width]
+        for line in range(RANK):
+            gram_o = jnp.sum(o_part * o_part[line : line + 1], axis=1, keepdims=True)
+            gram_r = jnp.sum(r_part * r_part[line : line + 1], axis=1, keepdims=True)
+            squares = squares + jnp.sum(gram_o * gram_r, keepdims=True)
+    for section in range(2):
+        used = COL_WIDTHS[section]
+        if used < right_ref.shape[2]:
+            right_ref[section, :, used:] = jnp.zeros((RANK, right_ref.shape[2] - used), f32)
+    norm_ref[...] = jnp.broadcast_to(jnp.sqrt(squares), norm_ref.shape)
+
+
+def final_right(sums, ortho, vecs, cols, scale):
+    full = pl.BlockSpec(memory_space=pltpu.VMEM)
+    return pl.pallas_call(
+        functools.partial(final_right_body, scale=scale),
+        in_specs=[full] * 3,
+        out_specs=[full] * 2,
+        out_shape=[jax.ShapeDtypeStruct((2, RANK, cols), f32), jax.ShapeDtypeStruct((1, LANES), f32)],
+        name="final_right",
+    )(sums, ortho, vecs)
+
+
 def finish_body(a0, a1, b0, b1, e_ref, o_ref, r_ref, *rest, rows, blocks, gain):
     err_out, app_out = rest[-2:]
-    o_high = o_ref[...].astype(bf16)
-    o_low = (o_ref[...] - o_high.astype(f32)).astype(bf16)
-    left = jnp.concatenate([o_high, o_low, o_high], axis=0)
+    o_part = o_ref[0]
+    o_high = o_part.astype(bf16)
+    o_low = (o_part - o_high.astype(f32)).astype(bf16)
+    left_t = jnp.concatenate([o_high, o_low, o_high], axis=0).T[:rows]
     lhs0 = a0[...].T
     lhs1 = a1[...].T
-    left_t = left.T
     for block in range(blocks):
         cols = slice(block * LANES, (block + 1) * LANES)
-        r_part = r_ref[:, cols]
+        r_part = r_ref[0, :, cols]
         r_high = r_part.astype(bf16)
         r_low = (r_part - r_high.astype(f32)).astype(bf16)
         approx = nn(left_t, jnp.concatenate([r_high, r_high, r_low], axis=0))
         grad = nn(lhs0, b0[:, cols]) + nn(lhs1, b1[:, cols])
         at = pl.ds(block, rows, stride=blocks)
         app_out[at, :] = approx
-        err_out[at, :] = (gain * grad + e_ref[block].astype(f32)) - approx
-
-
-def finish(pair0, pair1, err3, ortho, right, start, gain, bufs):
+        err_out[at, :] = (gain * grad + e_ref[block * rows : (block + 1) * rows].astype(f32)) - approx
+
+
+def finish(pair0, pair1, err, ortho, right, section, row_at, col_at, start, gain, bufs):
     a0, b0 = pair0
     a1, b1 = pair1
     rows_n, cols_n = a0.shape[1], b0.shape[1]
     seq = a0.shape[0]
     blocks = cols_n // LANES
-    rows = 128 if rows_n % 128 == 0 else rows_n
+    rows = chunk_rows(rows_n, cols_n)
     step = rows * blocks
     flat_rows = FLAT // LANES
     whole = lambda i: (0, 0)
     flat_spec = pl.BlockSpec((pl.Element(step), pl.Element(LANES)), lambda i: (pl.multiple_of(start // LANES + i * step, 16), 0))
+    wide_rows = tiles_of(rows) * LANES
     in_specs = [
         pl.BlockSpec((seq, rows), lambda i: (0, i)),
         pl.BlockSpec((seq, rows), lambda i: (0, i)),
         pl.BlockSpec((seq, cols_n), whole, pipeline_mode=pl.Buffered(1)),
         pl.BlockSpec((seq, cols_n), whole, pipeline_mode=pl.Buffered(1)),
-        pl.BlockSpec((blocks, rows, LANES), lambda i: (0, i, 0)),
-        pl.BlockSpec((RANK, rows), lambda i: (0, i)),
-        pl.BlockSpec((RANK, cols_n), whole, pipeline_mode=pl.Buffered(1)),
+        flat_spec,
+        pl.BlockSpec((1, RANK, wide_rows), lambda i: (section, 0, row_at // wide_rows + i)),
+        pl.BlockSpec((pl.Element(1), pl.Element(RANK), pl.Element(cols_n)), lambda i: (section, 0, col_at), pipeline_mode=pl.Buffered(1)),
     ]
-    args = [a0, a1, b0, b1, err3, ortho, right]
+    assert row_at % wide_rows == 0
+    args = [a0, a1, b0, b1, err, ortho, right]
     aliases = {}
     if bufs is not None:
         in_specs += [pl.BlockSpec(memory_space=pl.ANY)] * 2
@@ -439,11 +568,11 @@
 
 
 def tail_body(e_ref, buf0, buf1, err_out, app_out):
-    err_out[...] = e_ref[...].astype(f32)
+    err_out[...] = e_ref[0].reshape(err_out.shape).astype(f32)
     app_out[...] = jnp.zeros_like(app_out)
 
 
-def finish_tail(err_flat, start, bufs):
+def finish_tail(errors, start, bufs):
     flat_rows = FLAT // LANES
     count = flat_rows - start // LANES
     steps = 12
@@ -453,13 +582,330 @@
     return pl.pallas_call(
         tail_body,
         grid=(steps,),
-        in_specs=[spec] + [pl.BlockSpec(memory_space=pl.ANY)] * 2,
+        in_specs=[pl.BlockSpec((pl.Element(1), pl.Element(1), pl.Element(step * LANES)), lambda i: (0, 0, pl.multiple_of(start + i * step * LANES, 1024)))]
+        + [pl.BlockSpec(memory_space=pl.ANY)] * 2,
         out_specs=[spec, spec],
         out_shape=[jax.ShapeDtypeStruct((flat_rows, LANES), f32)] * 2,
         input_output_aliases={1: 0, 2: 1},
         compiler_params=pltpu.CompilerParams(vmem_limit_bytes=BIG),
         name="finish_tail",
-    )(err_flat, *bufs)
+    )(errors, *bufs)
+
+
+MESH = pl.DeviceIdType.MESH
+
+
+def grid_of(replicas):
+    side = 2 if replicas < 64 else 4
+    return replicas // (side * side), side, side
+
+
+def used_rows(section):
+    counts = [sum(rows * cols for rows, cols in section_shapes(s)) // LANES for s in range(2)]
+    return jnp.where(section == 0, counts[0], counts[1])
+
+
+def meet(replicas):
+    section, me = lax.axis_index("section"), lax.axis_index("dp")
+    barrier = pltpu.get_barrier_semaphore()
+    pl.semaphore_signal(barrier, inc=1, device_id={"section": 1 - section}, device_id_type=MESH)
+    for step in range(1, replicas):
+        pl.semaphore_signal(
+            barrier, inc=1, device_id={"dp": lax.rem(me + step, replicas)}, device_id_type=MESH
+        )
+    pl.semaphore_wait(barrier, replicas)
+
+
+def gather_body(
+    low_ref, cnt_ref, vec_ref, fac_ref, flat_ref, cnts_ref, vec2_ref, fac2_ref,
+    send_sem, recv_sem, swap_sem, cnt_send, cnt_recv, side_send, side_recv, own_sem, *, replicas, size,
+):
+    section, me = lax.axis_index("section"), lax.axis_index("dp")
+    other = 1 - section
+    nz, ny, nx = grid_of(replicas)
+    x, y, z = lax.rem(me, nx), lax.rem(me // nx, ny), me // (nx * ny)
+    cut = size // 2 // 8 * 8 if size % 8 == 0 else size
+    halves = [(0, cut), (cut, size - cut)] if cut < size else [(0, cut)]
+    used = used_rows(section)
+    used_other = used_rows(other)
+
+    def block_id(at_z, at_y, at_x):
+        return (at_z * ny + at_y) * nx + at_x
+
+    meet(replicas)
+
+    def side(src, dst, slot):
+        return pltpu.make_async_remote_copy(
+            src_ref=src, dst_ref=dst.at[section], send_sem=side_send.at[slot], recv_sem=side_recv.at[slot],
+            device_id={"section": other}, device_id_type=MESH,
+        )
+
+    def count_copy(step):
+        return pltpu.make_async_remote_copy(
+            src_ref=cnt_ref, dst_ref=cnts_ref.at[me], send_sem=cnt_send.at[step],
+            recv_sem=cnt_recv.at[step], device_id={"dp": lax.rem(me + step, replicas)}, device_id_type=MESH,
+        )
+
+    for step in range(1, replicas):
+        count_copy(step).start()
+    side(vec_ref, vec2_ref, 0).start()
+    side(fac_ref, fac2_ref, 1).start()
+    own = pltpu.make_async_copy(low_ref, flat_ref.at[section * replicas + me], own_sem)
+    own.start()
+
+    def copy(block, half, target, way, mine=False, swap=False):
+        start, rows = halves[half]
+        at = flat_ref.at[section * replicas + block, pl.ds(start, rows)]
+        src = low_ref.at[pl.ds(start, rows)] if mine else at
+        return pltpu.make_async_remote_copy(
+            src_ref=src, dst_ref=at, send_sem=send_sem.at[block, half, way],
+            recv_sem=(swap_sem if swap else recv_sem).at[block, half], device_id=target, device_id_type=MESH,
+        )
+
+    def needed(block, half, limit):
+        return block * size + halves[half][0] < limit
+
+    def at_z(value):
+        return {"dp": block_id(value, y, x)}
+
+    def along_x(block, half, mine=False):
+        for step in range(1, nx):
+            copy(block, half, {"dp": block_id(z, y, lax.rem(x + step, nx))}, 1 + step, mine).start()
+
+    def along_y(block, half, mine=False):
+        for step in range(1, ny):
+            copy(block, half, {"dp": block_id(z, lax.rem(y + step, ny), x)}, nx + step, mine).start()
+
+    def across(block, half, mine=False):
+        copy(block, half, {"section": other}, nx + ny, mine, True).start()
+
+    def arrived(block, half):
+        copy(block, half, {"section": other}, 0).wait_recv()
+
+    def layers(k):
+        return [z] if k == 0 else [z - k, z + k]
+
+    def valid(at):
+        return (at >= 0) & (at < nz)
+
+    def first(k):
+        for which, layer in enumerate(layers(k)):
+            block = block_id(layer, y, x)
+            for half in range(len(halves)):
+
+                @pl.when(valid(layer) & needed(block, half, used))
+                def _():
+                    if k > 0:
+                        arrived(block, half)
+                    mine = k == 0
+                    if k == 0 or which == 0:
+
+                        @pl.when(z + 1 < nz)
+                        def _():
+                            copy(block, half, at_z(z + 1), 0, mine).start()
+
+                    if k == 0 or which == 1:
+
+                        @pl.when(z > 0)
+                        def _():
+                            copy(block, half, at_z(z - 1), 1, mine).start()
+
+                    if half == 0:
+                        along_x(block, half, mine)
+                        along_y(block, half, mine)
+                    else:
+                        along_y(block, half, mine)
+                        along_x(block, half, mine)
+                    across(block, half, mine)
+
+    def second(k):
+        for layer in layers(k):
+            for half in range(len(halves)):
+                for step in range(1, nx if half == 0 else ny):
+                    if half == 0:
+                        block = block_id(layer, y, lax.rem(x + step, nx))
+                    else:
+                        block = block_id(layer, lax.rem(y + step, ny), x)
+
+                    @pl.when(valid(layer) & needed(block, half, used))
+                    def _():
+                        arrived(block, half)
+                        if half == 0:
+                            along_y(block, half)
+                        else:
+                            along_x(block, half)
+                        across(block, half)
+
+    def third(k):
+        for layer in layers(k):
+            for half in range(len(halves)):
+                for far in range(1, ny if half == 0 else nx):
+                    for near in range(nx if half == 0 else ny):
+                        if half == 0:
+                            block = block_id(layer, lax.rem(y + far, ny), lax.rem(x + near, nx))
+                        else:
+                            block = block_id(layer, lax.rem(y + near, ny), lax.rem(x + far, nx))
+
+                        @pl.when(valid(layer) & needed(block, half, used))
+                        def _():
+                            arrived(block, half)
+                            across(block, half)
+
+    for k in range(nz + 2):
+        if k < nz:
+            first(k)
+        if 0 <= k - 1 < nz:
+            second(k - 1)
+        if 0 <= k - 2 < nz:
+            third(k - 2)
+
+    def drain(block, carry):
+        at_x_, at_y_, at_z_ = lax.rem(block, nx), lax.rem(block // nx, ny), block // (nx * ny)
+        for half in range(len(halves)):
+            column = (at_x_ == x) & (at_y_ == y)
+
+            @pl.when(needed(block, half, used))
+            def _():
+                @pl.when(column & (at_z_ <= z) & (z + 1 < nz))
+                def _():
+                    copy(block, half, {"section": other}, 0).wait_send()
+
+                @pl.when(column & (at_z_ >= z) & (z > 0))
+                def _():
+                    copy(block, half, {"section": other}, 1).wait_send()
+
+                single = len(halves) == 1
+                sent_x = (column if half == 0 else at_x_ == x)
+                sent_y = (at_y_ == y) if half == 0 else column
+
+                @pl.when(sent_x)
+                def _():
+                    for step in range(1, nx):
+                        copy(block, half, {"section": other}, 1 + step).wait_send()
+
+                @pl.when(sent_y)
+                def _():
+                    for step in range(1, ny):
+                        copy(block, half, {"section": other}, nx + step).wait_send()
+
+                copy(block, half, {"section": other}, nx + ny).wait_send()
+
+            @pl.when(needed(block, half, used_other))
+            def _():
+                copy(block, half, {"section": other}, 0, False, True).wait_recv()
+
+        return carry
+
+    lax.fori_loop(0, replicas, drain, 0)
+    own.wait()
+    for step in range(1, replicas):
+        count_copy(step).wait()
+    cnts_ref[me] = cnt_ref[...]
+    vec2_ref[section] = vec_ref[...]
+    fac2_ref[section] = fac_ref[...]
+    side(vec_ref, vec2_ref, 0).wait()
+    side(fac_ref, fac2_ref, 1).wait()
+
+
+def gather(low, cnt, vec, fac, replicas):
+    size = low.shape[0]
+    vmem = pl.BlockSpec(memory_space=pltpu.VMEM)
+    nz, ny, nx = grid_of(replicas)
+    dma = pltpu.SemaphoreType.DMA
+    return pl.pallas_call(
+        functools.partial(gather_body, replicas=replicas, size=size),
+        in_specs=[vmem] * 4,
+        out_specs=[pl.BlockSpec(memory_space=pl.ANY), vmem, vmem, vmem],
+        out_shape=[
+            jax.ShapeDtypeStruct((2 * replicas, size, LANES), bf16),
+            jax.ShapeDtypeStruct((replicas,) + cnt.shape, f32),
+            jax.ShapeDtypeStruct((2,) + vec.shape, f32),
+            jax.ShapeDtypeStruct((2,) + fac.shape, f32),
+        ],
+        scratch_shapes=[
+            dma((replicas, 2, nx + ny + 1)), dma((replicas, 2)), dma((replicas, 2)),
+            dma((replicas,)), dma((replicas,)), dma((2,)), dma((2,)), dma(()),
+        ],
+        compiler_params=pltpu.CompilerParams(collective_id=2, has_side_effects=True),
+        name="gather",
+    )(low, cnt, vec, fac)
+
+
+def sum_body(
+    part_ref, extra_ref, total_ref, mine, came, slots, seg, swap_send, swap_recv, send_a, recv_a, send_b, recv_b,
+    *, replicas,
+):
+    section, me = lax.axis_index("section"), lax.axis_index("dp")
+    other = 1 - section
+    rows = part_ref.shape[1]
+    size = rows // replicas
+    meet(replicas)
+
+    def rows_of(index):
+        return pl.ds(pl.multiple_of(index * size, 8), size)
+
+    swap = pltpu.make_async_remote_copy(
+        src_ref=part_ref.at[other], dst_ref=came, send_sem=swap_send.at[0], recv_sem=swap_recv.at[0],
+        device_id={"section": other}, device_id_type=MESH,
+    )
+    swap.start()
+    mine[...] = part_ref[section] + extra_ref[...]
+    swap.wait()
+    mine[...] = mine[...] + came[...]
+
+    def scatter(step):
+        peer = lax.rem(me + step, replicas)
+        return pltpu.make_async_remote_copy(
+            src_ref=mine.at[rows_of(peer)], dst_ref=slots.at[step], send_sem=send_a.at[step],
+            recv_sem=recv_a.at[step], device_id={"dp": peer}, device_id_type=MESH,
+        )
+
+    def spread(step):
+        peer = lax.rem(me + step, replicas)
+        return pltpu.make_async_remote_copy(
+            src_ref=seg, dst_ref=total_ref.at[section, rows_of(me)], send_sem=send_b.at[step],
+            recv_sem=recv_b.at[step], device_id={"dp": peer}, device_id_type=MESH,
+        )
+
+    for step in range(1, replicas):
+        scatter(step).start()
+    total = mine[rows_of(me), :]
+    for step in range(1, replicas):
+        scatter(step).wait_recv()
+        total = total + slots[step]
+    seg[...] = total
+    for step in range(1, replicas):
+        spread(step).start()
+    total_ref[section, rows_of(me)] = total
+    for step in range(1, replicas):
+        scatter(step).wait_send()
+        spread(step).wait()
+    back = pltpu.make_async_remote_copy(
+        src_ref=total_ref.at[section], dst_ref=total_ref.at[section], send_sem=swap_send.at[1],
+        recv_sem=swap_recv.at[1], device_id={"section": other}, device_id_type=MESH,
+    )
+    back.start()
+    back.wait()
+
+
+def all_sum(part, extra, replicas, collective_id):
+    rows = part.shape[1]
+    vmem = pl.BlockSpec(memory_space=pltpu.VMEM)
+    dma = pltpu.SemaphoreType.DMA
+    size = rows // replicas
+    return pl.pallas_call(
+        functools.partial(sum_body, replicas=replicas),
+        in_specs=[vmem, vmem],
+        out_specs=vmem,
+        out_shape=jax.ShapeDtypeStruct(part.shape, f32),
+        scratch_shapes=[
+            pltpu.VMEM((rows, LANES), f32), pltpu.VMEM((rows, LANES), f32),
+            pltpu.VMEM((replicas, size, LANES), f32), pltpu.VMEM((size, LANES), f32),
+            dma((2,)), dma((2,)), dma((replicas,)), dma((replicas,)), dma((replicas,)), dma((replicas,)),
+        ],
+        compiler_params=pltpu.CompilerParams(collective_id=collective_id, has_side_effects=True),
+        name="all_sum",
+    )(part, extra)
 
 
 def swap_body(*refs, n_enc, n_dec):
@@ -530,11 +976,19 @@
     replicas = lax.axis_size("dp")
     replica_id = lax.axis_index("dp")
 
-    low_own = lax.all_gather(master[0].astype(bf16), "dp", axis=0, tiled=True)
-    low_both = lax.all_gather(low_own, "section", axis=0, tiled=True).reshape(-1, LANES)
-    vec_both = lax.all_gather(vectors[0], "section", axis=0)
-    fac_both = lax.all_gather(factors[0], "section", axis=0)
-    count = lax.psum(jnp.sum(loss_mask).astype(f32), "dp")
+    replicas_n = replicas
+    shard_len = master.shape[1]
+    size = shard_len // LANES
+    gain = float(replicas)
+
+    count_tile = jnp.full((RANK, LANES), jnp.sum(loss_mask).astype(f32))
+    vec_tile = jnp.pad(vectors[0], (0, VEC_TILES * RANK * LANES - VLEN)).reshape(-1, LANES)
+    flat_both, counts, vec_both, fac_both = gather(
+        master[0].astype(bf16).reshape(size, LANES), count_tile, vec_tile, factors[0], replicas
+    )
+    low_both = flat_both.reshape(-1, LANES)
+    vec_both = vec_both.reshape(2, -1)
+    count = jnp.sum(counts[:, 0, 0])
 
     vis = lax.dynamic_index_in_dim(visible, sec, 0, keepdims=False)
     mas = lax.dynamic_index_in_dim(masked, sec, 0, keepdims=False)
@@ -547,22 +1001,25 @@
     target = pix_order[VIS:].astype(f32)
     table_dec = positions_at(order, DD)
     table_enc = positions_at(vis, DE)
-    err_flat = errors.reshape(FLAT // LANES, LANES)
+    tail_row = ROW_PAD // LANES * RANK
+    tail_rows = (VEC_TILES + 1) * RANK
+    left_rows = sum_rows(replicas, ROW_PAD // LANES + VEC_TILES + 1)
+    right_rows = sum_rows(replicas, max(COL_WIDTHS) // LANES)
 
     def errs_for(section):
         def run():
-            stacks = unflat_all(err_flat, 0, section, stacked=True)
+            buf = None
             lefts = []
+            start = 0
             col_at = 0
-            for stack, (rows_n, cols_n) in zip(stacks, section_shapes(section)):
-                lefts.append(err_left(factors[0][:, col_at : col_at + cols_n], stack))
+            for rows_n, cols_n in section_shapes(section):
+                buf, left = err_prep(errors, factors[0][:, col_at : col_at + cols_n], start, rows_n, cols_n, buf)
+                lefts.append(left)
+                start += rows_n * cols_n
                 col_at += cols_n
-            flat = jnp.concatenate([stack.reshape(-1, LANES) for stack in stacks])
-            pad = FLAT // LANES - flat.shape[0]
-            flat = jnp.concatenate([flat, jnp.zeros((pad, LANES), bf16)]) if pad else flat
-            zero = [jnp.zeros((RANK, n), f32) for n in ROWS_L]
-            zero[section] = jnp.concatenate(lefts, axis=1)
-            return flat, jnp.concatenate(zero, axis=1)
+            done = sum(left.shape[0] for left in lefts)
+            lefts.append(jnp.zeros((left_rows - done, LANES), f32))
+            return buf, jnp.concatenate(lefts)
 
         return run
 
@@ -601,60 +1058,32 @@
     vec_e = pack_rows(vrows_e, [v_up_e], DE, VLEN)
 
     pairs = pairs_e + pairs_d
-    gain = float(replicas)
-    xs = []
-    for section in range(2):
-        col_at = 0
-        for rows_n, cols_n in section_shapes(section):
-            xs.append(fac_both[section][:, col_at : col_at + cols_n])
-            col_at += cols_n
-    lefts = skinny(xs, [b for a, b in pairs], [a for a, b in pairs])
-    left_part = gain * jnp.concatenate(lefts, axis=1) + err_lefts
-    left_sum, vec_sum, loss_sum = lax.psum((left_part, jnp.stack([vec_e, vec_d]), loss_part), ("section", "dp"))
-
     n_enc = len(pairs_e)
     flat_e = [x for pair in pairs_e for x in pair]
     flat_d = [x for pair in pairs_d for x in pair]
+    vec_tiles = jnp.pad(jnp.stack([vec_e, vec_d]), ((0, 0), (0, VEC_TILES * RANK * LANES - VLEN))).reshape(2, -1, LANES)
+    loss_tile = jnp.stack([jnp.full((RANK, LANES), loss_part), jnp.zeros((RANK, LANES), f32)])
+    tail = jnp.concatenate([vec_tiles, loss_tile], axis=1)
+    left_part = skinny(
+        fac_both, [b for a, b in pairs], [a for a, b in pairs], COL_SPANS, ROW_SPANS, tail, tail_row, gain, left_rows
+    )
     other_e, other_d = swap(flat_e, flat_d)
-
-    widths = [rows_n for s in range(2) for rows_n, cols_n in section_shapes(s)]
-    ortho = orthonormal(left_sum, widths, 1.0 / replicas)
-    orthos = []
-    at = 0
-    for width in widths:
-        orthos.append(ortho[:, at : at + width])
-        at += width
-    rights = skinny(orthos, [a for a, b in pairs], [b for a, b in pairs])
-
-    def err_rights_for(section):
-        def run():
-            start = 0
-            outs = []
-            base = 0 if section == 0 else n_enc
-            for i, (rows_n, cols_n) in enumerate(section_shapes(section)):
-                outs.append(err_right(orthos[base + i], err_stack, start, cols_n))
-                start += rows_n * cols_n
-            zero = [jnp.zeros((RANK, n), f32) for n in COLS_R]
-            zero[section] = jnp.concatenate(outs, axis=1)
-            return jnp.concatenate(zero, axis=1)
-
-        return run
-
-    right_part = gain * jnp.concatenate(rights, axis=1) + lax.cond(sec == 0, err_rights_for(0), err_rights_for(1))
-    right_sum = lax.psum(right_part, ("section", "dp")) / replicas
-
-    squares = jnp.sum(vec_sum * vec_sum)
-    row_at = col_at = 0
-    for section in range(2):
-        for rows_n, cols_n in section_shapes(section):
-            o_part = ortho[:, row_at : row_at + rows_n]
-            r_part = right_sum[:, col_at : col_at + cols_n]
-            gram_o = jnp.sum(o_part[:, None, :] * o_part[None, :, :], axis=-1)
-            gram_r = jnp.sum(r_part[:, None, :] * r_part[None, :, :], axis=-1)
-            squares = squares + jnp.sum(gram_o * gram_r)
-            row_at += rows_n
-            col_at += cols_n
-    norm = jnp.sqrt(squares)
+    left_sum = all_sum(left_part, err_lefts, replicas, 3)
+    vec_sum = left_sum[:, tail_row : tail_row + VEC_TILES * RANK]
+    loss_sum = left_sum[0, tail_row + VEC_TILES * RANK, 0]
+
+    ortho = orthonormal(left_sum, 1.0 / replicas)
+    right_part = skinny(
+        ortho, [a for a, b in pairs], [b for a, b in pairs], ROW_SPANS, COL_SPANS, tail, 0, gain, right_rows
+    )
+    err_rights = lax.cond(
+        sec == 0,
+        lambda: err_right(ortho, err_stack, 0, right_rows),
+        lambda: err_right(ortho, err_stack, 1, right_rows),
+    )
+    sums = all_sum(right_part, err_rights, replicas, 4)
+    right_both, norm_row = final_right(sums, ortho, vec_sum, factors.shape[2], 1.0 / replicas)
+    norm = norm_row[0, 0]
     scale = jnp.minimum(1.0, clip_limit / (norm + 1e-06))
 
     def finish_for(section):
@@ -665,37 +1094,27 @@
             bufs = None
             start = 0
             base = 0 if section == 0 else n_enc
-            col_at = 0 if section == 0 else COLS_R[0]
             for i, (rows_n, cols_n) in enumerate(section_shapes(section)):
-                blocks = cols_n // LANES
-                stack = lax.slice_in_dim(err_stack, start // LANES, (start + rows_n * cols_n) // LANES, axis=0)
-                stack = stack.reshape(blocks, rows_n, LANES)
                 bufs = finish(
-                    mine[i], theirs[i], stack, orthos[base + i],
-                    right_sum[:, col_at : col_at + cols_n], start, gain, bufs,
+                    mine[i], theirs[i], err_stack, ortho, right_both, section,
+                    ROW_SPANS[base + i][1], COL_SPANS[base + i][1], start, gain, bufs,
                 )
                 start += rows_n * cols_n
-                col_at += cols_n
             if start < FLAT:
-                bufs = finish_tail(err_flat, start, bufs)
+                bufs = finish_tail(errors, start, bufs)
             return bufs
 
         return run
 
     new_errors, approx = lax.cond(sec == 0, finish_for(0), finish_for(1))
-    shard_len = master.shape[1]
     own_part = lax.dynamic_slice_in_dim(approx.reshape(-1), replica_id * shard_len, shard_len)
     rate = learning_rate()
     new_moment = moment_decay * momentum[0] + scale * own_part
     new_master = master[0] - rate * new_moment
-    vec_own = lax.dynamic_index_in_dim(vec_sum, sec, 0, keepdims=False)
+    vec_own = lax.dynamic_index_in_dim(vec_sum, sec, 0, keepdims=False).reshape(-1)[:VLEN]
     new_vm = moment_decay * vec_moment[0] + scale * vec_own
     new_vectors = vectors[0] - rate * new_vm
-    right_e, right_d = right_sum[:, : COLS_R[0]], right_sum[:, COLS_R[0] :]
-    cols_total = factors.shape[2]
-    right_d = jnp.pad(right_d, ((0, 0), (0, cols_total - COLS_R[1])))
-    right_e = jnp.pad(right_e, ((0, 0), (0, cols_total - COLS_R[0])))
-    new_factors = jnp.where(sec == 0, right_e, right_d)
+    new_factors = lax.dynamic_index_in_dim(right_both, sec, 0, keepdims=False)
     return (
         new_master[None],
         new_master.astype(bf16)[None],

time: 1430 us -> 780 us (0.55)
  waiting for transfers between devices: 353 us -> 0 us
  other arithmetic: 402 us -> 90.4 us
  Pallas kernels: 345 us -> 490 us
  blocking collectives: 90.3 us -> 0 us
  local copies, waits for them, and re-layouts: 96.7 us -> 66.9 us
  between operations: 27 us -> 5.08 us
  matrix products: 99 us -> 117 us
    unnamed x6 -> x8, other arithmetic: 306 us -> 1.01 us
    psum x2 -> x0, waiting for transfers between devices: 182 us -> none  [the longest x1 127 us: local(): right_sum = lax.psum(right_part, ('section', 'dp')) / replicas]
    all_gather x2 -> x0, waiting for transfers between devices: 171 us -> none  [the longest x1 171 us: local(): low_own = lax.all_gather(master[0].astype(bf16), 'dp', axis=0, tiled=True)]
    pallas_call x16 -> x15, Pallas kernels: 78.9 us -> 249 us  [the longest x1 103 us: gather(): pl.pallas_call(functools.partial(gather_body, replicas=replicas, size=siz...]
    psum x2 -> x0, blocking collectives: 78.9 us -> none  [the longest x1 45.9 us: local(): lax.psum((left_part, jnp.stack([vec_e, vec_d]), loss_part), ('section', '...]
    slice x33 -> x5, local copies, waits for them, and re-layouts: 34 us -> 5.4 us  [the longest x3 2.67 us: run(): factors[0][:, col_at:col_at + cols_n]]
    reduce_sum x35 -> x2, other arithmetic: 22.3 us -> 2.23 us  [the longest x1 1.59 us: local(): count = jnp.sum(counts[:, 0, 0])]
    pallas_call x17 -> x11, Pallas kernels: 68.6 us -> 49.8 us  [unflat(): pl.pallas_call(functools.partial(unflat_body, blocks=blocks, rows=rows, s...]
  transfers between devices with their start and end apart: 4 -> 0, of which waited for: 3 -> 0; matrix products, arithmetic and copies ran while one was open for 24% -> 0% of each run, Pallas kernels for 5% -> 0%
where the time goes in v2:
time: 780 us; the launch traced here: 770 us
  Pallas kernels  490 us (63%)
  matrix products  117 us (15%)
  other arithmetic  90.4 us (12%)
  local copies, waits for them, and re-layouts  66.9 us (9%)
    pallas_call x1, Pallas kernels, gather(): pl.pallas_call(functools.partial(gather_body, replicas=replicas, size=siz...  103 us
    dot_general x12, matrix products, nn(): lax.dot_general(left, right, (((1,), (0,)), ((), ())), preferred_element_...  78.7 us
    pallas_call x2, Pallas kernels, attend_back(): pl.pallas_call(functools.partial(attend_back_body, size=size, rows_q=rows...  60.5 us
    pallas_call x2, Pallas kernels, all_sum(): pl.pallas_call(functools.partial(sum_body, replicas=replicas), in_specs=[...  60.3 us
    pallas_call x6, Pallas kernels, finish(): pl.pallas_call(functools.partial(finish_body, rows=rows, blocks=blocks, g...  59.3 us
    pallas_call x11, Pallas kernels, unflat(): pl.pallas_call(functools.partial(unflat_body, blocks=blocks, rows=rows, s...  49.8 us
    pallas_call x2, Pallas kernels, attend(): pl.pallas_call(functools.partial(attend_body, size=size, rows_q=rows_q),...  42.6 us
    dot_general x10, matrix products, nt(): lax.dot_general(left, right, (((1,), (1,)), ((), ())), preferred_element_...  38.2 us

profile of v2, /device:TPU:1, one launch (start us, length us, event | category | flops | bytes accessed | tf_op | source)
XLA Modules:
  0.0 770.1 jit_solution(11448480651424905951)
XLA Ops:
  4.0 19.6 %convert_reduce_fusion.6 = bf16[451584]{0:T(1024)(128)(2,1)} fusion(f32[1,451584]{1,0:T(1,128)S(1)} %copy-done.44), kind=kLoop, calls=%fused_computation.80 | loop fusion | flops 451584 | bytes 2709504 | tf_op jit(solution)/shard_map/convert_element_type | solution.py:987
  26.2 103.2 %gather.1 = (bf16[32,3528,128]{2,1,0:T(8,128)(2,1)}, f32[16,8,128]{2,1,0:T(8,128)}, f32[2,96,128]{2,1,0:T(8,128)}, f32[2,8,7680]{2,1,0:T(8,128)}) custom-call(bf16[3528,128]{1,0:T(8,128)(2,1)} %bitcast.145, f32[8,128]{1,0:T(8,128)} %broadcast_in_dim.40.cnt_ref, f32[96,128]{1,0:T(8,128)} %pad_bitcast_fusion.vec_ref, f32[8,7680]{1,0:T(8,128)S(1)} %bitcast.146), custom_call_target="tpu_custom_call" | custom-call | tf_op jit(solution)/shard_map/gather/pallas_call | solution.py:815
  130.3 1.8 unflat.11
  132.0 3.9 fusion.82
  136.8 5.9 unflat.12
  142.7 4.1 fusion.7.q_ref.k_ref.v_ref
  146.8 6.0 attend.2
  154.0 3.4 unflat.13
  157.5 1.8 fusion.83
  160.2 7.2 unflat.14
  168.1 11.1 %multiply_convert_fusion.1 = (bf16[256,3072]{1,0:T(8,128)(2,1)S(1)}, f32[256,3072]{1,0:T(8,128)}, f32[256,3072]{1,0:T(8,128)}) fusion(f32[3072]{0:T(1024)S(1)} %slice_bitcast_fusion, bf16[256,768]{1,0:T(8,128)(2,1)S(1)} %add_convert_fusion.8.refs_14_.refs_3_.refs_4_, bf16[768,3072]{1,0:T(8,128)(2,1)} %unflat.14), kind=kOutput, calls=%fused_computation.43 | convolution fusion | flops 1259864064 | bytes 12988416 | tf_op jit(solution)/shard_map/dot_general | solution.py:34
  179.2 9.4 %unflat.15 = bf16[3072,768]{1,0:T(8,128)(2,1)} custom-call(bf16[112896,128]{1,0:T(8,128)(2,1)} %bitcast.128), custom_call_target="tpu_custom_call" | custom-call | tf_op jit(solution)/shard_map/unflat/pallas_call | solution.py:106
  188.6 3.8 fusion.84
  194.4 3.0 unflat.16
  199.1 8.4 %fusion.16 = f32[1024]{0:T(1024)S(1)} fusion(f32[768,512]{1,0:T(8,128)S(1)} %broadcast_in_dim.42, f32[256,512]{1,0:T(8,128)S(1)} %convolution_add_fusion.5, f32[512]{0:T(512)S(1)} %get-tuple-element.434, f32[512]{0:T(512)S(1)} %get-tuple-element.433, f32[1024]{0:T(1024)S(1)} %get-tuple-element.377), kind=kLoop, calls=%fused_computation.77 | loop fusion | flops 2620416 | bytes 2109440 | tf_op jit(solution)/shard_map/reduce_sum | solution.py:57
  207.5 8.7 %multiply_reduce_fusion.5 = f32[1024]{0:T(1024)S(1)} fusion(f32[768,512]{1,0:T(8,128)S(1)} %broadcast_in_dim.42, f32[256,512]{1,0:T(8,128)S(1)} %convolution_add_fusion.5, f32[1024]{0:T(1024)S(1)} %broadcast_multiply_fusion.4, f32[512]{0:T(512)S(1)} %get-tuple-element.434, f32[512]{0:T(512)S(1)} %get-tuple-element.433, f32[1024]{0:T(1024)S(1)} %get-tuple-element.377), kind=kLoop, calls=%fused_computation.74 | loop fusion | flops 3668992 | bytes 2113536 | tf_op jit(solution)/shard_map/reduce_sum | solution.py:58
  216.3 3.8 unflat.17
  220.1 12.3 %add_convert_fusion.1.q_ref.k_ref.v_ref = bf16[1024,1536]{1,0:T(8,128)(2,1)} fusion(bf16[512,1536]{1,0:T(8,128)(2,1)} %unflat.17, f32[1536]{0:T(1024)S(1)} %pad_maximum_fusion.2, f32[768,512]{1,0:T(8,128)S(1)} %broadcast_in_dim.42, f32[256,512]{1,0:T(8,128)S(1)} %convolution_add_fusion.5, f32[512]{0:T(512)S(1)} %get-tuple-element.400, ...), kind=kOutput, calls=%fused_computation.31 | convolution fusion | flops 1618477056 | bytes 6842368 | tf_op jit(solution)/shard_map/dot_general | solution.py:34
  232.4 36.6 %attend.3 = (f32[1024,512]{1,0:T(8,128)}, f32[4,4,1024]{2,1,0:T(4,128)}) custom-call(bf16[1024,1536]{1,0:T(8,128)(2,1)} %add_convert_fusion.1.q_ref.k_ref.v_ref, bf16[1024,1536]{1,0:T(8,128)(2,1)} %add_convert_fusion.1.q_ref.k_ref.v_ref, bf16[1024,1536]{1,0:T(8,128)(2,1)} %add_convert_fusion.1.q_ref.k_ref.v_ref), custom_call_target="tpu_custom_call" | custom-call | tf_op jit(solution)/shard_map/attend/pallas_call | solution.py:160
  270.7 2.6 unflat.18
  273.4 8.6 %fusion.85 = (f32[1024]{0:T(1024)S(1)}, f32[1024,512]{1,0:T(8,128)S(1)}) fusion(f32[512]{0:T(512)S(1)} %get-tuple-element.397, bf16[1024,512]{1,0:T(8,128)(2,1)S(1)} %convert_element_type.208.refs_18_.refs_7_.refs_12_, bf16[512,512]{1,0:T(8,128)(2,1)} %unflat.18, f32[512]{0:T(512)S(1)} %get-tuple-element.434, f32[512]{0:T(512)S(1)} %get-tuple-element.433, ...), kind=kOutput, calls=%fused_computation.293 | convolution fusion | flops 540539904 | bytes 5781504 | tf_op jit(solution)/shard_map/dot_general | solution.py:34
  283.8 5.0 unflat.19
  289.4 23.3 %multiply_convert_fusion = (bf16[1024,2048]{1,0:T(8,128)(2,1)}, f32[1024,2048]{1,0:T(8,128)}, f32[1024,2048]{1,0:T(8,128)}) fusion(f32[2048]{0:T(1024)S(1)} %slice_bitcast_fusion.1, bf16[1024,512]{1,0:T(8,128)(2,1)S(1)} %add_convert_fusion.3.refs_19_.refs_8_.refs_14_, bf16[512,2048]{1,0:T(8,128)(2,1)} %unflat.19), kind=kOutput, calls=%fused_computation.17 | convolution fusion | flops 2285895680 | bytes 24125440 | tf_op jit(solution)/shard_map/dot_general | solution.py:34
  312.8 5.9 unflat.20
  318.6 5.3 fusion.86
  325.7 1.9 unflat.21
  329.3 3.0 multiply_reduce_fusion.9
  338.3 8.5 %convert_reduce_fusion = (f32[2048]{0:T(1024)}, bf16[1024,2048]{1,0:T(8,128)(2,1)S(1)}) fusion(f32[1024,2048]{1,0:T(8,128)S(1)} %bitcast.161, bf16[1024,512]{1,0:T(8,128)(2,1)S(1)} %get-tuple-element.360.refs_9_.refs_20_.refs_17_, bf16[2048,512]{1,0:T(8,128)(2,1)S(1)} %copy-done.53, f32[1024,2048]{1,0:T(8,128)} %get-tuple-element.424, ...), kind=kOutput, calls=%fused_computation.15 | convolution fusion | flops 2183133184 | bytes 24133632 | tf_op jit(solution)/shard_map/dot_general | solution.py:38
  346.7 3.3 multiply_reduce_fusion
  354.6 53.0 %attend_back.2 = (bf16[1024,512]{1,0:T(8,128)(2,1)}, bf16[1024,512]{1,0:T(8,128)(2,1)}, bf16[1024,512]{1,0:T(8,128)(2,1)}) custom-call(bf16[1024,1536]{1,0:T(8,128)(2,1)} %add_convert_fusion.1.q_ref.k_ref.v_ref, bf16[1024,1536]{1,0:T(8,128)(2,1)} %add_convert_fusion.1.q_ref.k_ref.v_ref, bf16[1024,1536]{1,0:T(8,128)(2,1)} %add_convert_fusion.1.q_ref.k_ref.v_ref, ...), custom_call_target="tpu_custom_call" | custom-call | tf_op jit(solution)/shard_map/attend_back/pallas_call | solution.py:224
  410.5 9.3 %fusion.66 = (f32[512]{0:T(512)}, f32[1024]{0:T(1024)S(1)}, f32[1024,512]{1,0:T(8,128)S(1)}) fusion(f32[512]{0:T(512)S(1)} %get-tuple-element.401, f32[1024]{0:T(1024)S(1)} %broadcast_multiply_fusion.4, f32[512]{0:T(512)S(1)} %get-tuple-element.434, f32[512]{0:T(512)S(1)} %get-tuple-element.433, f32[1024]{0:T(1024)S(1)} %get-tuple-element.377, ...), kind=kOutput, calls=%fused_computation.279 | convolution fusion | flops 1615329792 | bytes 8933376 | tf_op jit(solution)/shard_map/dot_general | solution.py:38
  419.9 10.3 %multiply_reduce_fusion.1 = (f32[512]{0:T(512)}, f32[1024]{0:T(1024)S(1)}) fusion(f32[1024,512]{1,0:T(8,128)S(1)} %get-tuple-element.427, f32[768,512]{1,0:T(8,128)S(1)} %broadcast_in_dim.42, f32[256,512]{1,0:T(8,128)S(1)} %copy-done.33, f32[1024]{0:T(1024)S(1)} %fusion.46, f32[1024]{0:T(1024)S(1)} %broadcast_multiply_fusion.4, ...), kind=kLoop, calls=%fused_computation.66 | loop fusion | flops 7338496 | bytes 4222976 | tf_op jit(solution)/shard_map/transpose(jvp())/reduce_sum | solution.py:59
  430.3 9.8 %add_add_fusion.3 = (f32[1024,512]{1,0:T(8,128)S(1)}, bf16[1024,512]{1,0:T(8,128)(2,1)}) fusion(f32[1024]{0:T(1024)S(1)} %negate_multiply_fusion.2, f32[1024,512]{1,0:T(8,128)S(1)} %copy-done.25, f32[1024]{0:T(1024)S(1)} %negate_multiply_fusion.3, f32[768,512]{1,0:T(8,128)S(1)} %copy-done.19, f32[1024]{0:T(1024)S(1)} %multiply_multiply_fusion.10, ...), kind=kLoop, calls=%fused_computation.67 | loop fusion | flops 9437184 | bytes 11042816 | tf_op jit(solution)/shard_map/add | solution.py:279
  444.0 2.8 convert_reduce_fusion.1
  446.9 2.2 multiply_reduce_fusion.11
  452.2 7.5 attend_back.3
  462.9 5.1 multiply_reduce_fusion.12
  498.4 16.7 %skinny.2.part_ref = f32[2,512,128]{2,1,0:T(8,128)} custom-call(f32[2,8,7680]{2,1,0:T(8,128)} %get-tuple-element.283.refs_0_, bf16[256,2304]{1,0:T(8,128)(2,1)} %copy-done.22, bf16[256,768]{1,0:T(8,128)(2,1)} %copy-done.30, bf16[256,3072]{1,0:T(8,128)(2,1)} %copy-done.21, bf16[256,768]{1,0:T(8,128)(2,1)} %copy-done.40, ...), custom_call_target="tpu_custom_call" | custom-call | tf_op jit(solution)/shard_map/skinny/pallas_call | solution.py:331
  515.1 34.0 %conditional.3 = (bf16[56448,128]{1,0:T(8,128)(2,1)}, f32[512,128]{1,0:T(8,128)}) conditional(s32[]{:T(128)} %convert_element_type.239, (f32[1,8,7680]{2,1,0:T(8,128)}, bf16[1,1,7225344]{2,1,0:T(2,128)(2,1)}) %tuple.34, (f32[1,8,7680]{2,1,0:T(8,128)}, bf16[1,1,7225344]{2,1,0:T(2,128)(2,1)}) %tuple.34), branch_computations={%region_53.54_spmd, %region_54.55_spmd} | conditional | bytes 2015304 | solution.py:1026
  516.5 4.3 err_prep.11
  521.4 2.2 err_prep.12
  526.2 4.9 err_prep.13
  532.4 6.7 err_prep.14
  540.6 1.9 err_prep.15
  543.8 3.4 err_prep.16
  549.1 34.2 %all_sum.2.sum_ref = f32[2,512,128]{2,1,0:T(8,128)} custom-call(f32[2,512,128]{2,1,0:T(8,128)} %skinny.2.part_ref, f32[512,128]{1,0:T(8,128)} %get-tuple-element.297.extra_ref), custom_call_target="tpu_custom_call" | custom-call | tf_op jit(solution)/shard_map/all_sum/pallas_call | solution.py:896
  583.3 2.9 orthonormal.1.refs_0_.ortho_ref
  586.2 7.8 %conditional.4 = (f32[512,128]{1,0:T(8,128)}) conditional(s32[]{:T(128)} %convert_element_type.239, (f32[2,8,5632]{2,1,0:T(8,128)S(1)}, bf16[56448,128]{1,0:T(8,128)(2,1)}) %tuple.35, (f32[2,8,5632]{2,1,0:T(8,128)S(1)}, bf16[56448,128]{1,0:T(8,128)(2,1)}) %tuple.35), branch_computations={%region_55.56_spmd, %region_56.57_spmd} | conditional | bytes 8 | solution.py:1079
  586.2 7.6 err_right.2
  594.0 16.4 %skinny.3.part_ref = f32[2,512,128]{2,1,0:T(8,128)} custom-call(f32[2,8,5632]{2,1,0:T(8,128)S(1)} %orthonormal.1.refs_0_.ortho_ref, bf16[256,768]{1,0:T(8,128)(2,1)} %copy-done.42, bf16[256,768]{1,0:T(8,128)(2,1)S(1)} %copy-done.27, bf16[256,768]{1,0:T(8,128)(2,1)} %copy-done.39, bf16[256,3072]{1,0:T(8,128)(2,1)} %copy-done.20, ...), custom_call_target="tpu_custom_call" | custom-call | tf_op jit(solution)/shard_map/skinny/pallas_call | solution.py:331
  610.5 26.1 %all_sum.3.sum_ref = f32[2,512,128]{2,1,0:T(8,128)} custom-call(f32[2,512,128]{2,1,0:T(8,128)} %skinny.3.part_ref, f32[512,128]{1,0:T(8,128)} %get-tuple-element.445.extra_ref), custom_call_target="tpu_custom_call" | custom-call | tf_op jit(solution)/shard_map/all_sum/pallas_call | solution.py:896
  638.2 2.7 final_right.1
  643.1 28.5 %swap.1 = (bf16[256,768]{1,0:T(8,128)(2,1)}, bf16[256,2304]{1,0:T(8,128)(2,1)}, bf16[256,768]{1,0:T(8,128)(2,1)}, bf16[256,768]{1,0:T(8,128)(2,1)}, bf16[256,768...) custom-call(bf16[256,768]{1,0:T(8,128)(2,1)} %copy-done.42, ...), custom_call_target="tpu_custom_call" | custom-call | tf_op jit(solution)/shard_map/swap/pallas_call | solution.py:955
  671.6 77.8 %conditional.5 = (f32[1,1,7225344]{2,1,0:T(1,128)}, f32[7225344]{0:T(1024)}) conditional(s32[]{:T(128)} %convert_element_type.239, (bf16[1024,512]{1,0:T(8,128)(2,1)}, bf16[1024,512]{1,0:T(8,128)(2,1)}, bf16[1024,1536]{1,0:T(8,128)(2,1)}, bf16[1024,1536]{1,0:T(8,128)(2,1)}, bf16[56448,128]{1,0:T(8,128)(2,1)}, ...), branch_computations={%region_57.58_spmd, %region_58.59_spmd} | conditional | bytes 9961572 | solution.py:1109
  673.8 12.2 %finish.11 = (f32[56448,128]{1,0:T(8,128)}, f32[56448,128]{1,0:T(8,128)}) custom-call(bf16[1024,512]{1,0:T(8,128)(2,1)} %get-tuple-element.181.a0, bf16[1024,512]{1,0:T(8,128)(2,1)} %get-tuple-element.182.a1, bf16[1024,1536]{1,0:T(8,128)(2,1)} %get-tuple-element.183.b0, bf16[1024,1536]{1,0:T(8,128)(2,1)} %get-tuple-element.184.b1, ...), custom_call_target="tpu_custom_call" | custom-call | tf_op jit(solution)/shard_map/cond/branch_0_fun/finish/pallas_call | solution.py:558
  686.0 5.7 finish.12
  691.7 19.1 %finish.13 = (f32[56448,128]{1,0:T(8,128)}, f32[56448,128]{1,0:T(8,128)}) custom-call(bf16[1024,512]{1,0:T(8,128)(2,1)} %copy-done.13, bf16[1024,512]{1,0:T(8,128)(2,1)} %get-tuple-element.174.a1, bf16[1024,2048]{1,0:T(8,128)(2,1)} %get-tuple-element.175.b0, bf16[1024,2048]{1,0:T(8,128)(2,1)} %get-tuple-element.176.b1, ...), custom_call_target="tpu_custom_call", output_to_operand_aliasing={{0}: (7, {}), {1}: (8, {})} | custom-call | tf_op jit(solution)/shard_map/cond/branch_0_fun/finish/pallas_call | solution.py:558
  710.9 14.4 %finish.14 = (f32[56448,128]{1,0:T(8,128)}, f32[56448,128]{1,0:T(8,128)}) custom-call(bf16[1024,2048]{1,0:T(8,128)(2,1)} %get-tuple-element.169.a0, bf16[1024,2048]{1,0:T(8,128)(2,1)} %get-tuple-element.170.a1, bf16[1024,512]{1,0:T(8,128)(2,1)} %get-tuple-element.171.b0, ...), custom_call_target="tpu_custom_call", output_to_operand_aliasing={{0}: (7, {}), {1}: (8, {})} | custom-call | tf_op jit(solution)/shard_map/cond/branch_0_fun/finish/pallas_call | solution.py:558
  725.2 3.3 finish.15
  728.6 4.6 finish.16
  733.1 16.1 %finish_tail.1 = (f32[56448,128]{1,0:T(8,128)}, f32[56448,128]{1,0:T(8,128)}) custom-call(bf16[1,1,7225344]{2,1,0:T(2,128)(2,1)} %get-tuple-element.157.e_ref, f32[56448,128]{1,0:T(8,128)} %get-tuple-element.195.buf0, f32[56448,128]{1,0:T(8,128)} %get-tuple-element.196.buf1), custom_call_target="tpu_custom_call", output_to_operand_aliasing={{0}: (1, {}), {1}: (2, {})} | custom-call | tf_op jit(solution)/shard_map/cond/branch_0_fun/finish_tail/pallas_call | solution.py:582
  749.5 3.6 broadcast_multiply_fusion
  753.1 3.7 fusion.67
  756.9 11.0 %broadcast_in_dim.116 = bf16[1,451584]{1,0:T(2,128)(2,1)} reshape(bf16[451584]{0:T(1024)(128)(2,1)S(1)} %get-tuple-element.346) | data formatting | bytes 1806336 | tf_op jit(solution)/shard_map/broadcast_in_dim | solution.py:1120
  (357 shorter events, 90.5 us)
Async XLA Ops:
  0.7 22.9 %copy-start.61 = (f32[1,11520]{1,0:T(1,128)S(1)}, f32[1,11520]{1,0:T(1,128)}, u32[]{:S(2)}) copy-start(f32[1,11520]{1,0:T(1,128)} %param.22) | copy-start | bytes 138244
  2.3 22.1 %copy-start.83 = (s32[2,768]{1,0:T(2,128)S(1)}, s32[2,768]{1,0:T(2,128)}, u32[]{:S(2)}) copy-start(s32[2,768]{1,0:T(2,128)} %param.19) | copy-start | bytes 18436
  2.3 24.0 %copy-start.54 = (f32[1,8,7680]{2,1,0:T(8,128)S(1)}, f32[1,8,7680]{2,1,0:T(8,128)}, u32[]{:S(2)}) copy-start(f32[1,8,7680]{2,1,0:T(8,128)} %param.24) | copy-start | bytes 737284
  130.2 5.9 copy-start.65
  130.3 29.3 %copy-start.67 = (f32[768]{0:T(1024)}, f32[768]{0:T(1024)S(1)}, u32[]{:S(2)}) copy-start(f32[768]{0:T(1024)S(1)} %get-tuple-element.408) | copy-start | bytes 9220
  130.3 62.4 %copy-start.69 = (f32[768]{0:T(1024)}, f32[768]{0:T(1024)S(1)}, u32[]{:S(2)}) copy-start(f32[768]{0:T(1024)S(1)} %get-tuple-element.404) | copy-start | bytes 9220
  135.9 21.6 %copy-start.34 = (f32[256,768]{1,0:T(8,128)}, f32[256,768]{1,0:T(8,128)S(1)}, u32[]{:S(2)}) copy-start(f32[256,768]{1,0:T(8,128)S(1)} %get-tuple-element.416) | copy-start | bytes 2359300
  135.9 6.8 copy-start.75
  136.4 6.3 copy-start.42
  159.3 29.3 %copy-start.36 = (f32[256,768]{1,0:T(8,128)}, f32[256,768]{1,0:T(8,128)S(1)}, u32[]{:S(2)}) copy-start(f32[256,768]{1,0:T(8,128)S(1)} %get-tuple-element.418) | copy-start | bytes 2359300
  159.3 8.0 %copy-start.77 = (f32[256]{0:T(256)}, f32[256]{0:T(256)S(1)}, u32[]{:S(2)}) copy-start(f32[256]{0:T(256)S(1)} %broadcast_multiply_fusion.6) | copy-start | bytes 3076
  160.2 7.9 %copy-start.39 = (bf16[256,768]{1,0:T(8,128)(2,1)}, bf16[256,768]{1,0:T(8,128)(2,1)S(1)}, u32[]{:S(2)}) copy-start(bf16[256,768]{1,0:T(8,128)(2,1)S(1)} %add_convert_fusion.8.refs_14_.refs_3_.refs_4_) | copy-start | bytes 1179652
  179.2 9.5 %copy-start.20 = (bf16[256,3072]{1,0:T(8,128)(2,1)}, bf16[256,3072]{1,0:T(8,128)(2,1)S(1)}, u32[]{:S(2)}) copy-start(bf16[256,3072]{1,0:T(8,128)(2,1)S(1)} %get-tuple-element.379.refs_15_.refs_4_.refs_6_) | copy-start | bytes 4718596
  192.4 4.9 copy-start.79
  192.7 4.7 copy-start.95
  192.7 4.7 copy-start.89
  193.5 3.9 copy-start.28
  198.9 21.2 %copy-start.31 = (f32[256,512]{1,0:T(8,128)}, f32[256,512]{1,0:T(8,128)S(1)}, u32[]{:S(2)}) copy-start(f32[256,512]{1,0:T(8,128)S(1)} %convolution_add_fusion.5) | copy-start | bytes 1572868
  216.2 3.8 copy-start.71
  283.7 5.7 copy-start.11
  318.6 5.3 copy-start.6
  325.7 172.7 %copy-start.23 = (bf16[768,512]{1,0:T(8,128)(2,1)}, bf16[768,512]{1,0:T(8,128)(2,1)S(1)}, u32[]{:S(2)}) copy-start(bf16[768,512]{1,0:T(8,128)(2,1)S(1)} %add_convert_fusion.5.refs_10_.refs_21_.refs_19_) | copy-start | bytes 2359300
  327.7 5.3 copy-start.17
  327.7 5.3 copy-start.60
  329.3 6.6 slice-start.4
  335.1 15.8 %copy-start.18 = (f32[768,512]{1,0:T(8,128)}, f32[768,512]{1,0:T(8,128)S(1)}, u32[]{:S(2)}) copy-start(f32[768,512]{1,0:T(8,128)S(1)} %broadcast_add_fusion) | copy-start | bytes 4718596
  335.9 10.8 %copy-start.14 = (bf16[1024,512]{1,0:T(8,128)(2,1)}, bf16[1024,512]{1,0:T(8,128)(2,1)S(1)}, u32[]{:S(2)}) copy-start(bf16[1024,512]{1,0:T(8,128)(2,1)S(1)} %get-tuple-element.360.refs_9_.refs_20_.refs_17_) | copy-start | bytes 3145732
  338.2 8.5 %copy-start.7 = (f32[1024,512]{1,0:T(8,128)S(1)}, f32[1024,512]{1,0:T(8,128)}, u32[]{:S(2)}) copy-start(f32[1024,512]{1,0:T(8,128)} %copy-done.5) | copy-start | bytes 6291460
  338.2 8.5 %copy-start.52 = (bf16[512,2048]{1,0:T(8,128)(2,1)S(1)}, bf16[512,2048]{1,0:T(8,128)(2,1)}, u32[]{:S(2)}) copy-start(bf16[512,2048]{1,0:T(8,128)(2,1)} %unflat.19) | copy-start | bytes 6291460
  410.5 9.4 %copy-start.4 = (bf16[1024,1536]{1,0:T(8,128)(2,1)}, bf16[1024,1536]{1,0:T(8,128)(2,1)S(1)}, u32[]{:S(2)}) copy-start(bf16[1024,1536]{1,0:T(8,128)(2,1)S(1)} %constant_dynamic-update-slice_fusion.11.refs_6_.refs_17_.refs_11_) | copy-start | bytes 9437188
  410.5 9.4 %copy-start.72 = (f32[1024]{0:T(1024)S(1)}, f32[1024]{0:T(1024)}, u32[]{:S(2)}) copy-start(f32[1024]{0:T(1024)} %copy-done.71) | copy-start | bytes 12292
  419.9 10.3 %copy-start.19 = (f32[768,512]{1,0:T(8,128)S(1)}, f32[768,512]{1,0:T(8,128)}, u32[]{:S(2)}) copy-start(f32[768,512]{1,0:T(8,128)} %copy-done.18) | copy-start | bytes 4718596
  419.9 10.3 %copy-start.25 = (f32[1024,512]{1,0:T(8,128)S(1)}, f32[1024,512]{1,0:T(8,128)}, u32[]{:S(2)}) copy-start(f32[1024,512]{1,0:T(8,128)} %copy-done.24) | copy-start | bytes 6291460
  430.2 12.2 %slice-start.2 = ((s8[4718592]{0:T(1024)(128)(4,1)}), s8[4194304]{0:T(1024)(128)(4,1)S(1)}, s32[]{:S(2)}) async-start(s8[4718592]{0:T(1024)(128)(4,1)} %bitcast.143), calls=%async_computation.2 | async-start | bytes 8388608
  430.2 10.5 %copy-start.47 = (f32[256,768]{1,0:T(8,128)S(1)}, f32[256,768]{1,0:T(8,128)}, u32[]{:S(2)}) copy-start(f32[256,768]{1,0:T(8,128)} %copy-done.46) | copy-start | bytes 2359300
  430.2 10.5 %copy-start.51 = (bf16[768,512]{1,0:T(8,128)(2,1)S(1)}, bf16[768,512]{1,0:T(8,128)(2,1)}, u32[]{:S(2)}) copy-start(bf16[768,512]{1,0:T(8,128)(2,1)} %unflat.16) | copy-start | bytes 2359300
  430.2 10.5 %copy-start.70 = (f32[768]{0:T(1024)S(1)}, f32[768]{0:T(1024)}, u32[]{:S(2)}) copy-start(f32[768]{0:T(1024)} %copy-done.69) | copy-start | bytes 9220
  430.2 10.5 %copy-start.80 = (f32[256]{0:T(256)S(1)}, f32[256]{0:T(256)}, u32[]{:S(2)}) copy-start(f32[256]{0:T(256)} %copy-done.79) | copy-start | bytes 3076
  430.3 10.5 %copy-start.90 = (f32[256]{0:T(256)S(1)}, f32[256]{0:T(256)}, u32[]{:S(2)}) copy-start(f32[256]{0:T(256)} %copy-done.89) | copy-start | bytes 3076
  430.3 12.1 %slice-start.3 = ((s8[4718592]{0:T(1024)(128)(4,1)}), s8[524288]{0:T(1024)(128)(4,1)S(1)}, s32[]{:S(2)}) async-start(s8[4718592]{0:T(1024)(128)(4,1)} %bitcast.143), calls=%async_computation.3 | async-start | bytes 1048576
  440.8 6.0 slice-start
  442.2 7.2 copy-start.82
  442.4 4.4 copy-start.40
  449.4 10.3 %copy-start.91 = (f32[256]{0:T(256)}, f32[256]{0:T(256)S(1)}, u32[]{:S(2)}) copy-start(f32[256]{0:T(256)S(1)} %negate_multiply_fusion.6) | copy-start | bytes 3076
  452.2 10.6 %copy-start.35 = (f32[256,768]{1,0:T(8,128)S(1)}, f32[256,768]{1,0:T(8,128)}, u32[]{:S(2)}) copy-start(f32[256,768]{1,0:T(8,128)} %copy-done.34) | copy-start | bytes 2359300
  452.2 10.6 %copy-start.66 = (f32[768]{0:T(1024)S(1)}, f32[768]{0:T(1024)}, u32[]{:S(2)}) copy-start(f32[768]{0:T(1024)} %copy-done.65) | copy-start | bytes 9220
  452.2 10.6 %copy-start.76 = (f32[256]{0:T(256)S(1)}, f32[256]{0:T(256)}, u32[]{:S(2)}) copy-start(f32[256]{0:T(256)} %copy-done.75) | copy-start | bytes 3076
  462.9 5.1 copy-start.22
  462.9 15.3 %copy-start.57 = (bf16[256,768]{1,0:T(8,128)(2,1)S(1)}, bf16[256,768]{1,0:T(8,128)(2,1)}, u32[]{:S(2)}) copy-start(bf16[256,768]{1,0:T(8,128)(2,1)} %get-tuple-element.296) | copy-start | bytes 1179652
  468.0 18.0 %copy-start.85 = (f32[3072]{0:T(1024)S(1)}, f32[3072]{0:T(1024)}, u32[]{:S(2)}) copy-start(f32[3072]{0:T(1024)} %get-tuple-element.349) | copy-start | bytes 36868
  482.2 3.8 copy-start.63
  482.8 10.1 %copy-start.97 = (f32[512]{0:T(512)S(1)}, f32[512]{0:T(512)}, u32[]{:S(2)}) copy-start(f32[512]{0:T(512)} %get-tuple-element.361) | copy-start | bytes 6148
  482.8 10.1 %copy-start.100 = (f32[512]{0:T(512)S(1)}, f32[512]{0:T(512)}, u32[]{:S(2)}) copy-start(f32[512]{0:T(512)} %get-tuple-element.359) | copy-start | bytes 6148
  484.3 10.2 %copy-start.99 = (f32[2048]{0:T(1024)S(1)}, f32[2048]{0:T(1024)}, u32[]{:S(2)}) copy-start(f32[2048]{0:T(1024)} %get-tuple-element.431) | copy-start | bytes 24580
  484.3 10.3 %copy-start.98 = (f32[512]{0:T(512)S(1)}, f32[512]{0:T(512)}, u32[]{:S(2)}) copy-start(f32[512]{0:T(512)} %get-tuple-element.357) | copy-start | bytes 6148
  484.3 10.4 %copy-start.101 = (f32[768]{0:T(1024)S(1)}, f32[768]{0:T(1024)}, u32[]{:S(2)}) copy-start(f32[768]{0:T(1024)} %get-tuple-element.390) | copy-start | bytes 9220
  516.5 4.3 copy-start.55
  586.2 7.8 %copy-start.27 = (bf16[256,768]{1,0:T(8,128)(2,1)S(1)}, bf16[256,768]{1,0:T(8,128)(2,1)}, u32[]{:S(2)}) copy-start(bf16[256,768]{1,0:T(8,128)(2,1)} %copy-done.26) | copy-start | bytes 1179652
  594.0 48.3 %copy-start.62 = (f32[1,11520]{1,0:T(1,128)S(1)}, f32[1,11520]{1,0:T(1,128)}, u32[]{:S(2)}) copy-start(f32[1,11520]{1,0:T(1,128)} %param.22) | copy-start | bytes 138244
  594.0 48.3 %copy-start.64 = (f32[1,11520]{1,0:T(1,128)S(1)}, f32[1,11520]{1,0:T(1,128)}, u32[]{:S(2)}) copy-start(f32[1,11520]{1,0:T(1,128)} %param.23) | copy-start | bytes 138244
  610.5 32.6 %copy-start.9 = (bf16[1024,512]{1,0:T(8,128)(2,1)S(1)}, bf16[1024,512]{1,0:T(8,128)(2,1)}, u32[]{:S(2)}) copy-start(bf16[1024,512]{1,0:T(8,128)(2,1)} %copy-done.8) | copy-start | bytes 3145732
  610.5 32.6 %copy-start.12 = (bf16[1024,512]{1,0:T(8,128)(2,1)S(1)}, bf16[1024,512]{1,0:T(8,128)(2,1)}, u32[]{:S(2)}) copy-start(bf16[1024,512]{1,0:T(8,128)(2,1)} %copy-done.11) | copy-start | bytes 3145732
  753.1 14.8 %copy-start.3 = (f32[2,8,7680]{2,1,0:T(8,128)S(1)}, f32[2,8,7680]{2,1,0:T(8,128)}, u32[]{:S(2)}) copy-start(f32[2,8,7680]{2,1,0:T(8,128)} %get-tuple-element.302) | copy-start | bytes 1474564
  753.1 16.7 %copy-start.1 = (bf16[2,1024,192]{1,2,0:T(8,128)(2,1)S(1)}, bf16[2,1024,192]{1,2,0:T(8,128)(2,1)}, u32[]{:S(2)}) copy-start(bf16[2,1024,192]{1,2,0:T(8,128)(2,1)} %param.16) | copy-start | bytes 2359300
  (43 other events, 93.8 us)

commit v3 on v2

--- a/solution.py
+++ b/solution.py
@@ -3,6 +3,7 @@
 
 import jax
 import jax.numpy as jnp
+import numpy as np
 from jax import lax
 from jax.experimental import pallas as pl
 from jax.experimental.pallas import tpu as pltpu
@@ -27,6 +28,10 @@
 moment_decay = 0.9
 rate_base = 0.5
 LANES = 128
+STEP = 32
+BLOCK = 256
+CHUNK = 256
+SPARE = 6144
 BIG = 66000000
 
 
@@ -53,16 +58,44 @@
     return value[:RANK] + value[RANK : 2 * RANK] + value[2 * RANK :]
 
 
-def layer_norm(tokens, gain, shift):
+def norm_parts(tokens):
     centred = tokens - jnp.mean(tokens, axis=-1, keepdims=True)
-    spread = jnp.mean(centred * centred, axis=-1, keepdims=True)
-    return centred * lax.rsqrt(spread + 1e-06) * gain + shift
-
-
-def positions_at(places, width):
-    column = jnp.arange(width)
-    freqs = jnp.exp(-(column // 2 * 2).astype(f32) / width * math.log(10000.0))
-    return jnp.sin(places.astype(f32)[:, None] * freqs + (column % 2).astype(f32) * (math.pi / 2))
+    spread = lax.rsqrt(jnp.mean(centred * centred, axis=-1, keepdims=True) + 1e-06)
+    return centred * spread, spread
+
+
+def norm_back(grad, hat, spread, gain):
+    inner = grad * gain
+    return spread * (
+        inner - jnp.mean(inner, axis=-1, keepdims=True) - hat * jnp.mean(inner * hat, axis=-1, keepdims=True)
+    )
+
+
+def column_sum(value):
+    return jnp.sum(value.astype(f32), axis=0, keepdims=True)
+
+
+def angle_tables(width):
+    column = np.arange(width)
+    freqs = np.exp(-(column // 2 * 2) / width * math.log(10000.0))
+    coarse = (np.arange(0, SEQ, STEP)[:, None] * freqs).astype(np.float64)
+    fine = np.arange(STEP)[:, None] * freqs + (column % 2) * (math.pi / 2)
+    return jnp.asarray(np.stack([np.sin(coarse), np.cos(coarse), np.cos(fine), np.sin(fine)]), f32)
+
+
+def positions_of(place, tables):
+    column = lax.broadcasted_iota(jnp.int32, (1, STEP), 1)
+    coarse = (place // STEP == column).astype(bf16)
+    fine = (place % STEP == column).astype(bf16)
+
+    def take(pick, table):
+        high = table.astype(bf16)
+        rest = table - high.astype(f32)
+        middle = rest.astype(bf16)
+        low = (rest - middle.astype(f32)).astype(bf16)
+        return nn(pick, high) + nn(pick, middle) + nn(pick, low)
+
+    return take(coarse, tables[0]) * take(fine, tables[2]) + take(coarse, tables[1]) * take(fine, tables[3])
 
 
 def section_shapes(section):
@@ -239,46 +272,330 @@
     )(joined, joined, joined, grad_out, out, lse)
 
 
-def block_forward(tokens, mats, rows, bias_up, heads):
-    normed = layer_norm(tokens, rows[0], rows[1]).astype(bf16)
-    qkv_bias = jnp.concatenate([rows[6], jnp.zeros_like(rows[6]), rows[7]])
-    joined = (nn(normed, mats[0]) + qkv_bias).astype(bf16)
+GRID = pltpu.CompilerParams(vmem_limit_bytes=BIG, dimension_semantics=("arbitrary",))
+
+
+def tokens_spec(width, rows=BLOCK):
+    return pl.BlockSpec((rows, width), lambda i: (i, 0))
+
+
+def fixed(array):
+    rank = len(array.shape)
+    return pl.BlockSpec(array.shape, lambda i: (0,) * rank, pipeline_mode=pl.Buffered(1))
+
+
+def kept_spec(shape):
+    return pl.BlockSpec(shape, lambda i: (0,) * len(shape))
+
+
+def shape_of(rows, cols, dtype=f32):
+    return jax.ShapeDtypeStruct((rows, cols), dtype)
+
+
+def embed_body(pix_ref, e_ref, vec_ref, place_ref, table_ref, out_ref):
+    out_ref[...] = nn(pix_ref[...], e_ref[...]) + vec_ref[10:11] + positions_of(place_ref[...], table_ref)
+
+
+def embed(pix, weight, vecs, place, tables):
+    args = [pix, weight, vecs, place, tables]
+    return pl.pallas_call(
+        embed_body,
+        grid=(1,),
+        in_specs=[fixed(x) for x in args],
+        out_specs=tokens_spec(weight.shape[1]),
+        out_shape=shape_of(pix.shape[0], weight.shape[1]),
+        compiler_params=GRID,
+        name="embed",
+    )(*args)
+
+
+def relay_body(coded_ref, vec_e_ref, w_ref, extra_ref, vec_d_ref, place_ref, table_ref, sent_ref, out_ref):
+    step = pl.program_id(0)
+    place = positions_of(place_ref[...], table_ref)
+
+    @pl.when(step == 0)
+    def _():
+        hat, unused = norm_parts(coded_ref[...])
+        sent = (hat * vec_e_ref[4:5] + vec_e_ref[5:6]).astype(bf16)
+        sent_ref[...] = sent
+        out_ref[...] = nn(sent, w_ref[...]) + extra_ref[...] + place
+
+    @pl.when(step > 0)
+    def _():
+        out_ref[...] = vec_d_ref[10:11] + place
+
+
+def relay(coded, vec_e, weight, extra, vec_d, place, tables):
+    args = [coded, vec_e, weight, extra, vec_d]
+    return pl.pallas_call(
+        relay_body,
+        grid=(SEQ // VIS,),
+        in_specs=[fixed(x) for x in args] + [pl.BlockSpec((VIS, 1), lambda i: (i, 0)), fixed(tables)],
+        out_specs=[kept_spec((VIS, DE)), tokens_spec(DD, VIS)],
+        out_shape=[shape_of(VIS, DE, bf16), shape_of(SEQ, DD)],
+        compiler_params=GRID,
+        name="relay",
+    )(*args, place, tables)
+
+
+def relay_back_body(b_ref, w_ref, coded_ref, vec_ref, out_ref, sums_ref):
+    grad = nt(b_ref[...], w_ref[...]).astype(bf16).astype(f32)
+    hat, spread = norm_parts(coded_ref[...])
+    out_ref[...] = norm_back(grad, hat, spread, vec_ref[4:5])
+    sums_ref[...] = jnp.zeros_like(sums_ref)
+    sums_ref[0:1] = column_sum(grad * hat)
+    sums_ref[1:2] = column_sum(grad)
+
+
+def relay_back(b_proj, weight, coded, vecs):
+    args = [b_proj, weight, coded, vecs]
+    return pl.pallas_call(
+        relay_back_body,
+        grid=(1,),
+        in_specs=[fixed(x) for x in args],
+        out_specs=[tokens_spec(DE), kept_spec((8, DE))],
+        out_shape=[shape_of(VIS, DE), shape_of(8, DE)],
+        compiler_params=GRID,
+        name="relay_back",
+    )(*args)
+
+
+def open_body(tok_ref, vec_ref, w_ref, normed_ref, joined_ref):
+    width = tok_ref.shape[1]
+    hat, unused = norm_parts(tok_ref[...])
+    normed = (hat * vec_ref[0:1] + vec_ref[1:2]).astype(bf16)
+    normed_ref[...] = normed
+    for part, bias in ((0, vec_ref[6:7]), (1, None), (2, vec_ref[7:8])):
+        cols = slice(part * width, (part + 1) * width)
+        value = nn(normed, w_ref[:, cols])
+        joined_ref[:, cols] = (value if bias is None else value + bias).astype(bf16)
+
+
+def open_block(tokens, vecs, weight):
+    seq, width = tokens.shape
+    return pl.pallas_call(
+        open_body,
+        grid=(seq // BLOCK,),
+        in_specs=[tokens_spec(width), fixed(vecs), fixed(weight)],
+        out_specs=[tokens_spec(width), tokens_spec(3 * width)],
+        out_shape=[shape_of(seq, width, bf16), shape_of(seq, 3 * width, bf16)],
+        compiler_params=GRID,
+        name="open_block",
+    )(tokens, vecs, weight)
+
+
+def erf(value):
+    return lax.erf(value)
+
+
+def close_body(tok_ref, o_ref, vec_ref, bias_ref, wo_ref, w1_ref, w2_ref, att_ref, mid_ref, sec_ref, act_ref, slope_ref, out_ref):
+    attended = o_ref[...].astype(bf16)
+    att_ref[...] = attended
+    middle = tok_ref[...] + nn(attended, wo_ref[...]) + vec_ref[8:9]
+    mid_ref[...] = middle
+    hat, unused = norm_parts(middle)
+    sec_ref[...] = (hat * vec_ref[2:3] + vec_ref[3:4]).astype(bf16)
+    out_ref[...] = middle + vec_ref[9:10]
+
+    def one(step, carry):
+        cols = pl.ds(pl.multiple_of(step * CHUNK, CHUNK), CHUNK)
+        hidden = nn(sec_ref[...], w1_ref[:, cols]) + bias_ref[:, cols]
+        share = 0.5 * (1.0 + erf(hidden * math.sqrt(0.5)))
+        active = (hidden * share).astype(bf16)
+        act_ref[:, cols] = active
+        slope_ref[:, cols] = share + hidden * (jnp.exp(-0.5 * hidden * hidden) * (1.0 / math.sqrt(2.0 * math.pi)))
+        out_ref[...] += nn(active, w2_ref[cols, :])
+        return carry
+
+    lax.fori_loop(0, w1_ref.shape[1] // CHUNK, one, 0)
+
+
+def close_block(tokens, out, vecs, bias_up, wo, w1, w2):
+    seq, width = tokens.shape
+    hidden = w1.shape[1]
+    return pl.pallas_call(
+        close_body,
+        grid=(seq // BLOCK,),
+        in_specs=[tokens_spec(width), tokens_spec(width)] + [fixed(x) for x in (vecs, bias_up, wo, w1, w2)],
+        out_specs=[tokens_spec(width)] * 3 + [tokens_spec(hidden)] * 2 + [tokens_spec(width)],
+        out_shape=[
+            shape_of(seq, width, bf16), shape_of(seq, width), shape_of(seq, width, bf16),
+            shape_of(seq, hidden, bf16), shape_of(seq, hidden), shape_of(seq, width),
+        ],
+        compiler_params=GRID,
+        name="close_block",
+    )(tokens, out, vecs, bias_up, wo, w1, w2)
+
+
+def head_body(res_ref, vec_ref, w_ref, target_ref, mask_ref, count_ref, fin_ref, pred_ref, grad_ref, sums_ref, loss_ref):
+    step = pl.program_id(0)
+
+    @pl.when(step == 0)
+    def _():
+        grad_ref[...] = jnp.zeros_like(grad_ref)
+        sums_ref[...] = jnp.zeros_like(sums_ref)
+        loss_ref[...] = jnp.zeros_like(loss_ref)
+
+    @pl.when(step > 0)
+    def _():
+        count = count_ref[0, 0]
+        hat, spread = norm_parts(res_ref[...])
+        final = (hat * vec_ref[4:5] + vec_ref[5:6]).astype(bf16)
+        fin_ref[...] = final
+        residual = nt(final, w_ref[...]) - target_ref[...].astype(f32)
+        weight = mask_ref[...]
+        rows = weight * jnp.mean(residual * residual, axis=1, keepdims=True)
+        loss_ref[...] += jnp.broadcast_to(jnp.sum(rows, axis=0, keepdims=True) / count, loss_ref.shape)
+        grad_pred = (weight * (2.0 * residual / PATCH) / count).astype(bf16)
+        pred_ref[...] = grad_pred
+        grad = nn(grad_pred, w_ref[...])
+        grad_ref[...] = norm_back(grad, hat, spread, vec_ref[4:5])
+        sums_ref[0:1] += column_sum(grad * hat)
+        sums_ref[1:2] += column_sum(grad)
+
+
+def head(result, vecs, weight, target, mask, count):
+    late = lambda i: (jnp.maximum(i - 1, 0), 0)
+    return pl.pallas_call(
+        head_body,
+        grid=(SEQ // VIS,),
+        in_specs=[
+            tokens_spec(DD, VIS), fixed(vecs), fixed(weight), pl.BlockSpec((VIS, PATCH), late),
+            pl.BlockSpec((VIS, 1), late), fixed(count),
+        ],
+        out_specs=[
+            pl.BlockSpec((VIS, DD), late), pl.BlockSpec((VIS, PATCH), late), tokens_spec(DD, VIS),
+            kept_spec((8, DD)), kept_spec((8, LANES)),
+        ],
+        out_shape=[
+            shape_of(SEQ - VIS, DD, bf16), shape_of(SEQ - VIS, PATCH, bf16), shape_of(SEQ, DD),
+            shape_of(8, DD), shape_of(8, LANES),
+        ],
+        compiler_params=GRID,
+        name="head",
+    )(result, vecs, weight, target, mask, count)
+
+
+def back_up_body(
+    grad_ref, slope_ref, mid_ref, vec_ref, wo_ref, w1_ref, w2_ref,
+    down_ref, up_ref, proj_ref, att_ref, out_ref, sums_ref, bias_ref, total,
+):
+    @pl.when(pl.program_id(0) == 0)
+    def _():
+        sums_ref[...] = jnp.zeros_like(sums_ref)
+        bias_ref[...] = jnp.zeros_like(bias_ref)
+
+    down = grad_ref[...].astype(bf16)
+    down_ref[...] = down
+    total[...] = jnp.zeros_like(total)
+
+    def one(step, carry):
+        cols = pl.ds(pl.multiple_of(step * CHUNK, CHUNK), CHUNK)
+        part = (nt(down_ref[...], w2_ref[cols, :]) * slope_ref[:, cols]).astype(bf16)
+        up_ref[:, cols] = part
+        bias_ref[:, cols] += column_sum(part)
+        total[...] += nt(part, w1_ref[:, cols])
+        return carry
+
+    lax.fori_loop(0, w1_ref.shape[1] // CHUNK, one, 0)
+    grad = total[...]
+    hat, spread = norm_parts(mid_ref[...])
+    middle = grad_ref[...] + norm_back(grad, hat, spread, vec_ref[2:3])
+    out_ref[...] = middle
+    proj = middle.astype(bf16)
+    proj_ref[...] = proj
+    att_ref[...] = nt(proj, wo_ref[...]).astype(bf16)
+    sums_ref[0:1] += column_sum(grad * hat)
+    sums_ref[1:2] += column_sum(grad)
+    sums_ref[2:3] += column_sum(proj)
+    sums_ref[3:4] += column_sum(down)
+
+
+def back_up(grad_result, slope, middle, vecs, wo, w1, w2):
+    seq, width = middle.shape
+    hidden = w1.shape[1]
+    return pl.pallas_call(
+        back_up_body,
+        grid=(seq // BLOCK,),
+        in_specs=[tokens_spec(width), tokens_spec(hidden), tokens_spec(width)] + [fixed(x) for x in (vecs, wo, w1, w2)],
+        out_specs=[
+            tokens_spec(width), tokens_spec(hidden), tokens_spec(width), tokens_spec(width), tokens_spec(width),
+            kept_spec((8, width)), kept_spec((1, hidden)),
+        ],
+        out_shape=[
+            shape_of(seq, width, bf16), shape_of(seq, hidden, bf16), shape_of(seq, width, bf16),
+            shape_of(seq, width, bf16), shape_of(seq, width), shape_of(8, width), shape_of(1, hidden),
+        ],
+        scratch_shapes=[pltpu.VMEM((BLOCK, width), f32)],
+        compiler_params=GRID,
+        name="back_up",
+    )(grad_result, slope, middle, vecs, wo, w1, w2)
+
+
+def back_in_body(dq_ref, dk_ref, dv_ref, mid_ref, tok_ref, vec_ref, w_ref, join_ref, first_ref, sums_ref):
+    step = pl.program_id(0)
+    width = tok_ref.shape[1]
+
+    @pl.when(step == 0)
+    def _():
+        sums_ref[...] = jnp.zeros_like(sums_ref)
+
+    grad = jnp.zeros(tok_ref.shape, f32)
+    for part, ref in enumerate((dq_ref, dk_ref, dv_ref)):
+        cols = slice(part * width, (part + 1) * width)
+        value = ref[...]
+        join_ref[:, cols] = value
+        grad = grad + nt(value, w_ref[:, cols])
+        if part != 1:
+            sums_ref[2 + part // 2 : 3 + part // 2] += column_sum(value)
+    hat, spread = norm_parts(tok_ref[...])
+    tokens = mid_ref[...] + norm_back(grad, hat, spread, vec_ref[0:1])
+    sums_ref[0:1] += column_sum(grad * hat)
+    sums_ref[1:2] += column_sum(grad)
+
+    @pl.when(step == 0)
+    def _():
+        first = tokens.astype(bf16)
+        first_ref[...] = first
+        sums_ref[4:5] = column_sum(first)
+
+    @pl.when(step > 0)
+    def _():
+        sums_ref[5:6] += column_sum(tokens)
+
+
+def back_in(dq, dk, dv, middle, tokens, vecs, weight):
+    seq, width = tokens.shape
+    return pl.pallas_call(
+        back_in_body,
+        grid=(seq // BLOCK,),
+        in_specs=[tokens_spec(width)] * 5 + [fixed(vecs), fixed(weight)],
+        out_specs=[tokens_spec(3 * width), kept_spec((BLOCK, width)), kept_spec((8, width))],
+        out_shape=[shape_of(seq, 3 * width, bf16), shape_of(BLOCK, width, bf16), shape_of(8, width)],
+        compiler_params=GRID,
+        name="back_in",
+    )(dq, dk, dv, middle, tokens, vecs, weight)
+
+
+def block_forward(tokens, mats, vecs, bias_up, heads):
+    normed, joined = open_block(tokens, vecs, mats[0])
     out, lse = attend(joined, heads)
-    attended = out.astype(bf16)
-    middle = tokens + nn(attended, mats[1]) + rows[8]
-    second = layer_norm(middle, rows[2], rows[3]).astype(bf16)
-    hidden = nn(second, mats[2]) + bias_up
-    active = jax.nn.gelu(hidden, approximate=False).astype(bf16)
-    result = middle + nn(active, mats[3]) + rows[9]
-    return result, (tokens, normed, joined, out, lse, attended, middle, second, hidden, active)
-
-
-def block_backward(kept, grad_result, mats, rows, heads):
-    tokens, normed, joined, out, lse, attended, middle, second, hidden, active = kept
-    width = tokens.shape[1]
-    b_down = grad_result.astype(bf16)
-    v_down = jnp.sum(b_down.astype(f32), axis=0)
-    grad_active = nt(b_down, mats[3])
-    unused, pull = jax.vjp(lambda v: jax.nn.gelu(v, approximate=False), hidden)
-    b_up = pull(grad_active)[0].astype(bf16)
-    v_up = jnp.sum(b_up.astype(f32), axis=0)
-    grad_second = nt(b_up, mats[2])
-    unused, pull = jax.vjp(layer_norm, middle, rows[2], rows[3])
-    grad_norm, v_gain2, v_shift2 = pull(grad_second)
-    grad_middle = grad_result + grad_norm
-    b_proj = grad_middle.astype(bf16)
-    v_proj = jnp.sum(b_proj.astype(f32), axis=0)
-    grad_att = nt(b_proj, mats[1]).astype(bf16)
+    attended, middle, second, active, slope, result = close_block(
+        tokens, out, vecs, bias_up, mats[1], mats[2], mats[3]
+    )
+    return result, (tokens, normed, joined, out, lse, attended, middle, second, active, slope)
+
+
+def block_backward(kept, grad_result, mats, vecs, heads):
+    tokens, normed, joined, out, lse, attended, middle, second, active, slope = kept
+    b_down, b_up, b_proj, grad_att, grad_middle, sums_up, bias_up = back_up(
+        grad_result, slope, middle, vecs, mats[1], mats[2], mats[3]
+    )
     dq, dk, dv = attend_back(joined, grad_att, out, lse, heads)
-    b_qkv = jnp.concatenate([dq, dk, dv], axis=1)
-    v_q = jnp.sum(dq.astype(f32), axis=0)
-    v_v = jnp.sum(dv.astype(f32), axis=0)
-    grad_normed = nt(b_qkv, mats[0])
-    unused, pull = jax.vjp(layer_norm, tokens, rows[0], rows[1])
-    grad_norm, v_gain1, v_shift1 = pull(grad_normed)
-    grad_tokens = grad_middle + grad_norm
+    b_qkv, first, sums_in = back_in(dq, dk, dv, grad_middle, tokens, vecs, mats[0])
     pairs = [(normed, b_qkv), (attended, b_proj), (second, b_up), (active, b_down)]
-    return grad_tokens, pairs, [v_gain1, v_shift1, v_gain2, v_shift2, None, None, v_q, v_v, v_proj, v_down, None], v_up
+    rows = [sums_in[0], sums_in[1], sums_up[0], sums_up[1], None, None, sums_in[2], sums_in[3], sums_up[2], sums_up[3], None]
+    return first, pairs, rows, bias_up[0], sums_in
 
 
 def tiles_of(width):
@@ -371,7 +688,7 @@
 def chunk_rows(rows_n, cols_n):
     if rows_n == PATCH:
         return PATCH
-    return 128 if cols_n > 8 * LANES else 256
+    return 256
 
 
 def err_prep_body(e_ref, x_ref, *rest, blocks, rows):
@@ -507,7 +824,7 @@
     )(sums, ortho, vecs)
 
 
-def finish_body(a0, a1, b0, b1, e_ref, o_ref, r_ref, *rest, rows, blocks, gain):
+def finish_body(me_ref, a0, a1, b0, b1, e_ref, o_ref, r_ref, *rest, rows, blocks, gain, start, shard):
     err_out, app_out = rest[-2:]
     o_part = o_ref[0]
     o_high = o_part.astype(bf16)
@@ -515,19 +832,33 @@
     left_t = jnp.concatenate([o_high, o_low, o_high], axis=0).T[:rows]
     lhs0 = a0[...].T
     lhs1 = a1[...].T
-    for block in range(blocks):
-        cols = slice(block * LANES, (block + 1) * LANES)
+    err_rows = err_out.at[0].reshape(rows * blocks, LANES)
+    keep = overlaps(pl.program_id(0), me_ref[0], start, rows * blocks, shard)
+    for pair in range(blocks // 2):
+        cols = slice(pair * 2 * LANES, (pair + 1) * 2 * LANES)
         r_part = r_ref[0, :, cols]
         r_high = r_part.astype(bf16)
         r_low = (r_part - r_high.astype(f32)).astype(bf16)
         approx = nn(left_t, jnp.concatenate([r_high, r_high, r_low], axis=0))
         grad = nn(lhs0, b0[:, cols]) + nn(lhs1, b1[:, cols])
-        at = pl.ds(block, rows, stride=blocks)
-        app_out[at, :] = approx
-        err_out[at, :] = (gain * grad + e_ref[block * rows : (block + 1) * rows].astype(f32)) - approx
-
-
-def finish(pair0, pair1, err, ortho, right, section, row_at, col_at, start, gain, bufs):
+        for side in range(2):
+            block = pair * 2 + side
+            half = slice(side * LANES, (side + 1) * LANES)
+            err_rows[pl.ds(block, rows, stride=blocks), :] = (
+                gain * grad[:, half] + e_ref[block * rows : (block + 1) * rows].astype(f32)
+            ) - approx[:, half]
+
+            @pl.when(keep)
+            def _():
+                app_out[pl.ds(block, rows, stride=blocks), :] = approx[:, half]
+
+
+def overlaps(i, me, start, step, shard):
+    first = start + i * step * LANES
+    return (first < (me + 1) * shard) & (first + step * LANES > me * shard)
+
+
+def finish(me, pair0, pair1, err, ortho, right, section, row_at, col_at, start, gain, shard, bufs):
     a0, b0 = pair0
     a1, b1 = pair1
     rows_n, cols_n = a0.shape[1], b0.shape[1]
@@ -536,17 +867,23 @@
     rows = chunk_rows(rows_n, cols_n)
     step = rows * blocks
     flat_rows = FLAT // LANES
-    whole = lambda i: (0, 0)
-    flat_spec = pl.BlockSpec((pl.Element(step), pl.Element(LANES)), lambda i: (pl.multiple_of(start // LANES + i * step, 16), 0))
+    whole = lambda i, me: (0, 0)
+    flat_at = lambda i: pl.multiple_of(start // LANES + i * step, 16)
     wide_rows = tiles_of(rows) * LANES
+
+    def shard_at(i, me):
+        return pl.multiple_of(jnp.where(overlaps(i, me[0], start, step, shard), start // LANES + i * step, flat_rows), 8), 0
+
     in_specs = [
-        pl.BlockSpec((seq, rows), lambda i: (0, i)),
-        pl.BlockSpec((seq, rows), lambda i: (0, i)),
+        pl.BlockSpec((seq, rows), lambda i, me: (0, i)),
+        pl.BlockSpec((seq, rows), lambda i, me: (0, i)),
         pl.BlockSpec((seq, cols_n), whole, pipeline_mode=pl.Buffered(1)),
         pl.BlockSpec((seq, cols_n), whole, pipeline_mode=pl.Buffered(1)),
-        flat_spec,
-        pl.BlockSpec((1, RANK, wide_rows), lambda i: (section, 0, row_at // wide_rows + i)),
-        pl.BlockSpec((pl.Element(1), pl.Element(RANK), pl.Element(cols_n)), lambda i: (section, 0, col_at), pipeline_mode=pl.Buffered(1)),
+        pl.BlockSpec((pl.Element(step), pl.Element(LANES)), lambda i, me: (flat_at(i), 0)),
+        pl.BlockSpec((1, RANK, wide_rows), lambda i, me: (section, 0, row_at // wide_rows + i)),
+        pl.BlockSpec(
+            (pl.Element(1), pl.Element(RANK), pl.Element(cols_n)), lambda i, me: (section, 0, col_at), pipeline_mode=pl.Buffered(1)
+        ),
     ]
     assert row_at % wide_rows == 0
     args = [a0, a1, b0, b1, err, ortho, right]
@@ -554,42 +891,51 @@
     if bufs is not None:
         in_specs += [pl.BlockSpec(memory_space=pl.ANY)] * 2
         args += list(bufs)
-        aliases = {7: 0, 8: 1}
-    return pl.pallas_call(
-        functools.partial(finish_body, rows=rows, blocks=blocks, gain=gain),
-        grid=(rows_n // rows,),
-        in_specs=in_specs,
-        out_specs=[flat_spec, flat_spec],
-        out_shape=[jax.ShapeDtypeStruct((flat_rows, LANES), f32)] * 2,
+        aliases = {8: 0, 9: 1}
+    return pl.pallas_call(
+        functools.partial(finish_body, rows=rows, blocks=blocks, gain=gain, start=start, shard=shard),
+        grid_spec=pltpu.PrefetchScalarGridSpec(
+            num_scalar_prefetch=1,
+            grid=(rows_n // rows,),
+            in_specs=in_specs,
+            out_specs=[
+                pl.BlockSpec(
+                    (pl.Element(1), pl.Element(1), pl.Element(step * LANES)),
+                    lambda i, me: (0, 0, pl.multiple_of(start + i * step * LANES, 1024)),
+                ),
+                pl.BlockSpec((pl.Element(step), pl.Element(LANES)), shard_at),
+            ],
+        ),
+        out_shape=[
+            jax.ShapeDtypeStruct((1, 1, FLAT), f32),
+            jax.ShapeDtypeStruct((flat_rows + SPARE, LANES), f32),
+        ],
         input_output_aliases=aliases,
         compiler_params=pltpu.CompilerParams(vmem_limit_bytes=BIG),
         name="finish",
-    )(*args)
-
-
-def tail_body(e_ref, buf0, buf1, err_out, app_out):
-    err_out[...] = e_ref[0].reshape(err_out.shape).astype(f32)
-    app_out[...] = jnp.zeros_like(app_out)
-
-
-def finish_tail(errors, start, bufs):
-    flat_rows = FLAT // LANES
-    count = flat_rows - start // LANES
-    steps = 12
+    )(me, *args)
+
+
+def tail_body(e_ref, buf0, err_out):
+    err_out[...] = e_ref[...].astype(f32)
+
+
+def finish_tail(errors, start, buf):
+    count = FLAT - start
+    steps = 6
     step = count // steps
-    assert step * steps == count and step % 16 == 0
-    spec = pl.BlockSpec((pl.Element(step), pl.Element(LANES)), lambda i: (pl.multiple_of(start // LANES + i * step, 16), 0))
+    assert step * steps == count and step % 1024 == 0
+    spec = pl.BlockSpec((pl.Element(1), pl.Element(1), pl.Element(step)), lambda i: (0, 0, pl.multiple_of(start + i * step, 1024)))
     return pl.pallas_call(
         tail_body,
         grid=(steps,),
-        in_specs=[pl.BlockSpec((pl.Element(1), pl.Element(1), pl.Element(step * LANES)), lambda i: (0, 0, pl.multiple_of(start + i * step * LANES, 1024)))]
-        + [pl.BlockSpec(memory_space=pl.ANY)] * 2,
-        out_specs=[spec, spec],
-        out_shape=[jax.ShapeDtypeStruct((flat_rows, LANES), f32)] * 2,
-        input_output_aliases={1: 0, 2: 1},
+        in_specs=[spec, pl.BlockSpec(memory_space=pl.ANY)],
+        out_specs=spec,
+        out_shape=jax.ShapeDtypeStruct((1, 1, FLAT), f32),
+        input_output_aliases={1: 0},
         compiler_params=pltpu.CompilerParams(vmem_limit_bytes=BIG),
         name="finish_tail",
-    )(errors, *bufs)
+    )(errors, buf)
 
 
 MESH = pl.DeviceIdType.MESH
@@ -807,6 +1153,17 @@
     side(fac_ref, fac2_ref, 1).wait()
 
 
+def cast_body(src_ref, out_ref):
+    out_ref[...] = src_ref[...].reshape(out_ref.shape).astype(bf16)
+
+
+def cast_shard(master, size):
+    full = pl.BlockSpec(memory_space=pltpu.VMEM)
+    return pl.pallas_call(
+        cast_body, in_specs=[full], out_specs=full, out_shape=jax.ShapeDtypeStruct((size, LANES), bf16), name="cast"
+    )(master)
+
+
 def gather(low, cnt, vec, fac, replicas):
     size = low.shape[0]
     vmem = pl.BlockSpec(memory_space=pltpu.VMEM)
@@ -831,9 +1188,14 @@
     )(low, cnt, vec, fac)
 
 
-def sum_body(
-    part_ref, extra_ref, total_ref, mine, came, slots, seg, swap_send, swap_recv, send_a, recv_a, send_b, recv_b,
-    *, replicas,
+def sum_body(*refs, replicas, n_enc, n_dec):
+    n = n_enc + n_dec
+    sum_run(*refs[:2], refs[2 : 2 + n], refs[2 + n], refs[3 + n : 3 + 2 * n], *refs[3 + 2 * n :], replicas=replicas, n_enc=n_enc)
+
+
+def sum_run(
+    part_ref, extra_ref, given, total_ref, taken, mine, came, slots, seg, swap_send, swap_recv, send_a, recv_a, send_b, recv_b,
+    give_sem, take_sem, *, replicas, n_enc,
 ):
     section, me = lax.axis_index("section"), lax.axis_index("dp")
     other = 1 - section
@@ -851,6 +1213,20 @@
     swap.start()
     mine[...] = part_ref[section] + extra_ref[...]
     swap.wait()
+
+    def give(i):
+        return pltpu.make_async_remote_copy(
+            src_ref=given[i], dst_ref=taken[i], send_sem=give_sem.at[i], recv_sem=take_sem.at[i],
+            device_id={"section": other}, device_id_type=MESH,
+        )
+
+    n = len(given)
+    for i in range(n):
+
+        @pl.when(section == (1 if i < n_enc else 0))
+        def _():
+            give(i).start()
+
     mine[...] = mine[...] + came[...]
 
     def scatter(step):
@@ -886,82 +1262,40 @@
     )
     back.start()
     back.wait()
-
-
-def all_sum(part, extra, replicas, collective_id):
+    for i in range(n):
+
+        @pl.when(section == (1 if i < n_enc else 0))
+        def _():
+            give(i).wait_send()
+
+        @pl.when(section == (0 if i < n_enc else 1))
+        def _():
+            give(i).wait_recv()
+
+
+def all_sum(part, extra, replicas, collective_id, enc=(), dec=()):
     rows = part.shape[1]
     vmem = pl.BlockSpec(memory_space=pltpu.VMEM)
     dma = pltpu.SemaphoreType.DMA
     size = rows // replicas
-    return pl.pallas_call(
-        functools.partial(sum_body, replicas=replicas),
-        in_specs=[vmem, vmem],
-        out_specs=vmem,
-        out_shape=jax.ShapeDtypeStruct(part.shape, f32),
+    given = list(enc) + list(dec)
+    n = len(given)
+    anywhere = pl.BlockSpec(memory_space=pl.ANY)
+    outs = pl.pallas_call(
+        functools.partial(sum_body, replicas=replicas, n_enc=len(enc), n_dec=len(dec)),
+        in_specs=[vmem, vmem] + [anywhere] * n,
+        out_specs=[vmem] + [anywhere] * n,
+        out_shape=[jax.ShapeDtypeStruct(part.shape, f32)] + [jax.ShapeDtypeStruct(x.shape, x.dtype) for x in given],
         scratch_shapes=[
             pltpu.VMEM((rows, LANES), f32), pltpu.VMEM((rows, LANES), f32),
             pltpu.VMEM((replicas, size, LANES), f32), pltpu.VMEM((size, LANES), f32),
             dma((2,)), dma((2,)), dma((replicas,)), dma((replicas,)), dma((replicas,)), dma((replicas,)),
+            dma((max(n, 1),)), dma((max(n, 1),)),
         ],
         compiler_params=pltpu.CompilerParams(collective_id=collective_id, has_side_effects=True),
         name="all_sum",
-    )(part, extra)
-
-
-def swap_body(*refs, n_enc, n_dec):
-    n = n_enc + n_dec
-    src, dst = refs[:n], refs[n : 2 * n]
-    send, recv = refs[2 * n :]
-    me = lax.axis_index("section")
-    other = 1 - me
-    barrier = pltpu.get_barrier_semaphore()
-    pl.semaphore_signal(barrier, inc=1, device_id={"section": other}, device_id_type=pl.DeviceIdType.MESH)
-    pl.semaphore_wait(barrier, 1)
-
-    def copy(i):
-        return pltpu.make_async_remote_copy(
-            src_ref=src[i],
-            dst_ref=dst[i],
-            send_sem=send.at[i],
-            recv_sem=recv.at[i],
-            device_id={"section": other},
-            device_id_type=pl.DeviceIdType.MESH,
-        )
-
-    enc, dec = range(n_enc), range(n_enc, n)
-
-    @pl.when(me == 0)
-    def _():
-        for i in dec:
-            copy(i).start()
-        for i in dec:
-            copy(i).wait_send()
-        for i in enc:
-            copy(i).wait_recv()
-
-    @pl.when(me == 1)
-    def _():
-        for i in enc:
-            copy(i).start()
-        for i in enc:
-            copy(i).wait_send()
-        for i in dec:
-            copy(i).wait_recv()
-
-
-def swap(enc, dec):
-    arrays = list(enc) + list(dec)
-    n = len(arrays)
-    outs = pl.pallas_call(
-        functools.partial(swap_body, n_enc=len(enc), n_dec=len(dec)),
-        in_specs=[pl.BlockSpec(memory_space=pl.ANY)] * n,
-        out_specs=[pl.BlockSpec(memory_space=pl.ANY)] * n,
-        out_shape=[jax.ShapeDtypeStruct(a.shape, a.dtype) for a in arrays],
-        scratch_shapes=[pltpu.SemaphoreType.DMA((n,)), pltpu.SemaphoreType.DMA((n,))],
-        compiler_params=pltpu.CompilerParams(collective_id=1, has_side_effects=True),
-        name="swap",
-    )(*arrays)
-    return outs[: len(enc)], outs[len(enc) :]
+    )(part, extra, *given)
+    return outs[0], outs[1 : 1 + len(enc)], outs[1 + len(enc) :]
 
 
 def pack_rows(rows, pieces, width, length):
@@ -984,7 +1318,7 @@
     count_tile = jnp.full((RANK, LANES), jnp.sum(loss_mask).astype(f32))
     vec_tile = jnp.pad(vectors[0], (0, VEC_TILES * RANK * LANES - VLEN)).reshape(-1, LANES)
     flat_both, counts, vec_both, fac_both = gather(
-        master[0].astype(bf16).reshape(size, LANES), count_tile, vec_tile, factors[0], replicas
+        cast_shard(master, size), count_tile, vec_tile, factors[0], replicas
     )
     low_both = flat_both.reshape(-1, LANES)
     vec_both = vec_both.reshape(2, -1)
@@ -998,9 +1332,9 @@
     pick = (order[:, None] == jnp.arange(SEQ, dtype=jnp.int32)[None, :]).astype(bf16)
     pix_order = nn(pick, pix).astype(bf16)
     pix_vis = pix_order[:VIS]
-    target = pix_order[VIS:].astype(f32)
-    table_dec = positions_at(order, DD)
-    table_enc = positions_at(vis, DE)
+    target = pix_order[VIS:]
+    place = order[:, None]
+    mask_col = mask_row[:, None]
     tail_row = ROW_PAD // LANES * RANK
     tail_rows = (VEC_TILES + 1) * RANK
     left_rows = sum_rows(replicas, ROW_PAD // LANES + VEC_TILES + 1)
@@ -1030,31 +1364,22 @@
     rows_e, bias_e, unused = unpack_vecs(vec_both[0], DE, FFE)
     rows_d, bias_d, extra_d = unpack_vecs(vec_both[1], DD, FFD)
 
-    embedded = nn(pix_vis, enc[4]) + rows_e[10] + table_enc
-    coded, kept_e = block_forward(embedded, enc, rows_e, bias_e, HEADS_ENC)
-    sent_full, sent_pull = jax.vjp(layer_norm, coded, rows_e[4], rows_e[5])
-    sent = sent_full.astype(bf16)
-    projected = nn(sent, dec[5]) + extra_d
-    filled = jnp.concatenate([projected, jnp.broadcast_to(rows_d[10], (SEQ - VIS, DD))]) + table_dec
-    result, kept_d = block_forward(filled, dec, rows_d, bias_d, HEADS_DEC)
-    final_full, final_pull = jax.vjp(layer_norm, result[VIS:], rows_d[4], rows_d[5])
-    final = final_full.astype(bf16)
-    residual = nt(final, dec[4]) - target
-    loss_part = jnp.sum(mask_row * jnp.mean(residual * residual, axis=1)) / count
-    grad_pred = (mask_row[:, None] * (2.0 * residual / PATCH) / count).astype(bf16)
-    grad_picked, v_gain3, v_shift3 = final_pull(nn(grad_pred, dec[4]))
-    grad_result = jnp.concatenate([jnp.zeros((VIS, DD), f32), grad_picked])
-    grad_filled, pairs_d, vrows_d, v_up_d = block_backward(kept_d, grad_result, dec, rows_d, HEADS_DEC)
-    b_proj = grad_filled[:VIS].astype(bf16)
-    pairs_d = pairs_d + [(grad_pred, final), (sent, b_proj)]
-    vrows_d[4], vrows_d[5], vrows_d[10] = v_gain3, v_shift3, jnp.sum(grad_filled[VIS:], axis=0)
-    vec_d = pack_rows(vrows_d, [v_up_d, jnp.sum(b_proj.astype(f32), axis=0)], DD, VLEN)
-    grad_sent = nt(b_proj, dec[5]).astype(bf16)
-    grad_coded, v_gain3, v_shift3 = sent_pull(grad_sent.astype(f32))
-    grad_start, pairs_e, vrows_e, v_up_e = block_backward(kept_e, grad_coded, enc, rows_e, HEADS_ENC)
-    b_start = grad_start.astype(bf16)
+    tokens_e = embed(pix_vis, enc[4], rows_e, place[:VIS], angle_tables(DE))
+    coded, kept_e = block_forward(tokens_e, enc, rows_e, bias_e[None], HEADS_ENC)
+    sent, filled = relay(coded, rows_e, dec[5], extra_d[None], rows_d, place, angle_tables(DD))
+    result, kept_d = block_forward(filled, dec, rows_d, bias_d[None], HEADS_DEC)
+    final, grad_pred, grad_result, sums_h, loss_row = head(
+        result, rows_d, dec[4], target, mask_col, count.reshape(1, 1)
+    )
+    loss_part = loss_row[0, 0]
+    b_first, pairs_d, vrows_d, v_up_d, sums_d = block_backward(kept_d, grad_result, dec, rows_d, HEADS_DEC)
+    pairs_d = pairs_d + [(grad_pred, final), (sent, b_first)]
+    vrows_d[4], vrows_d[5], vrows_d[10] = sums_h[0], sums_h[1], sums_d[5]
+    vec_d = pack_rows(vrows_d, [v_up_d, sums_d[4]], DD, VLEN)
+    grad_coded, sums_r = relay_back(b_first, dec[5], coded, rows_e)
+    b_start, pairs_e, vrows_e, v_up_e, sums_e = block_backward(kept_e, grad_coded, enc, rows_e, HEADS_ENC)
     pairs_e = pairs_e + [(pix_vis, b_start)]
-    vrows_e[4], vrows_e[5], vrows_e[10] = v_gain3, v_shift3, jnp.sum(b_start.astype(f32), axis=0)
+    vrows_e[4], vrows_e[5], vrows_e[10] = sums_r[0], sums_r[1], sums_e[4]
     vec_e = pack_rows(vrows_e, [v_up_e], DE, VLEN)
 
     pairs = pairs_e + pairs_d
@@ -1067,8 +1392,7 @@
     left_part = skinny(
         fac_both, [b for a, b in pairs], [a for a, b in pairs], COL_SPANS, ROW_SPANS, tail, tail_row, gain, left_rows
     )
-    other_e, other_d = swap(flat_e, flat_d)
-    left_sum = all_sum(left_part, err_lefts, replicas, 3)
+    left_sum, other_e, other_d = all_sum(left_part, err_lefts, replicas, 3, flat_e, flat_d)
     vec_sum = left_sum[:, tail_row : tail_row + VEC_TILES * RANK]
     loss_sum = left_sum[0, tail_row + VEC_TILES * RANK, 0]
 
@@ -1081,7 +1405,7 @@
         lambda: err_right(ortho, err_stack, 0, right_rows),
         lambda: err_right(ortho, err_stack, 1, right_rows),
     )
-    sums = all_sum(right_part, err_rights, replicas, 4)
+    sums, unused, unused = all_sum(right_part, err_rights, replicas, 4)
     right_both, norm_row = final_right(sums, ortho, vec_sum, factors.shape[2], 1.0 / replicas)
     norm = norm_row[0, 0]
     scale = jnp.minimum(1.0, clip_limit / (norm + 1e-06))
@@ -1096,18 +1420,22 @@
             base = 0 if section == 0 else n_enc
             for i, (rows_n, cols_n) in enumerate(section_shapes(section)):
                 bufs = finish(
-                    mine[i], theirs[i], err_stack, ortho, right_both, section,
-                    ROW_SPANS[base + i][1], COL_SPANS[base + i][1], start, gain, bufs,
+                    me_row, mine[i], theirs[i], err_stack, ortho, right_both, section,
+                    ROW_SPANS[base + i][1], COL_SPANS[base + i][1], start, gain, shard_len, bufs,
                 )
                 start += rows_n * cols_n
             if start < FLAT:
-                bufs = finish_tail(errors, start, bufs)
-            return bufs
+                bufs = [finish_tail(errors, start, bufs[0]), bufs[1]]
+            return bufs[0], bufs[1]
 
         return run
 
+    me_row = replica_id.astype(jnp.int32).reshape(1)
     new_errors, approx = lax.cond(sec == 0, finish_for(0), finish_for(1))
     own_part = lax.dynamic_slice_in_dim(approx.reshape(-1), replica_id * shard_len, shard_len)
+    used = jnp.where(sec == 0, *[sum(rows_n * cols_n for rows_n, cols_n in section_shapes(s)) for s in range(2)])
+    inside = replica_id * shard_len + lax.iota(jnp.int32, shard_len) < used
+    own_part = jnp.where(inside, own_part, 0.0)
     rate = learning_rate()
     new_moment = moment_decay * momentum[0] + scale * own_part
     new_master = master[0] - rate * new_moment
@@ -1122,7 +1450,7 @@
         new_vectors[None],
         new_vm[None],
         new_factors[None],
-        new_errors.reshape(1, 1, -1),
+        new_errors,
         loss_sum.reshape(1),
         norm.reshape(1),
     )

time: 780 us -> 664 us (0.85)
  matrix products: 117 us -> 0.88 us
  Pallas kernels: 490 us -> 598 us
  other arithmetic: 90.4 us -> 12.9 us
  local copies, waits for them, and re-layouts: 66.9 us -> 41 us
    pallas_call x4 -> x16, Pallas kernels: 105 us -> 211 us  [the longest x2 72.4 us: all_sum(): pl.pallas_call(functools.partial(sum_body, replicas=replicas, n_enc=len(e...]
    dot_general x12 -> x1, matrix products: 78.7 us -> 0.88 us  [nn(): lax.dot_general(left, right, (((1,), (0,)), ((), ())), preferred_element_...]
    reduce_sum x26 -> x0, other arithmetic: 43.7 us -> none  [the longest x7 12.3 us: layer_norm(): centred = tokens - jnp.mean(tokens, axis=-1, keepdims=True)]
    dot_general x10 -> x0, matrix products: 38.2 us -> none  [nt(): lax.dot_general(left, right, (((1,), (1,)), ((), ())), preferred_element_...]
    unnamed x233 -> x71, local copies, waits for them, and re-layouts: 31.6 us -> 0.26 us
    convert_element_type x10 -> x0, other arithmetic: 23.8 us -> none  [the longest x1 19.6 us: local(): master[0].astype(bf16).reshape(size, LANES)]
    add x1 -> x0, other arithmetic: 9.84 us -> none  [block_backward(): grad_tokens = grad_middle + grad_norm]
    slice x0 -> x15, local copies, waits for them, and re-layouts: none -> 7.96 us  [the longest x2 1.8 us: local(): vrows_e[4], vrows_e[5], vrows_e[10] = (sums_r[0], sums_r[1], sums_e[4])]
where the time goes in v3:
time: 664 us; the launch traced here: 656 us
  Pallas kernels  598 us (90%)
  local copies, waits for them, and re-layouts  41 us (6%)
  other arithmetic  12.9 us (2%)
    pallas_call x1, Pallas kernels, gather(): pl.pallas_call(functools.partial(gather_body, replicas=replicas, size=siz...  103 us
    pallas_call x2, Pallas kernels, all_sum(): pl.pallas_call(functools.partial(sum_body, replicas=replicas, n_enc=len(e...  72.4 us
    pallas_call x6, Pallas kernels, finish(): pl.pallas_call(functools.partial(finish_body, rows=rows, blocks=blocks, g...  66 us
    pallas_call x2, Pallas kernels, attend_back(): pl.pallas_call(functools.partial(attend_back_body, size=size, rows_q=rows...  59.8 us
    pallas_call x11, Pallas kernels, unflat(): pl.pallas_call(functools.partial(unflat_body, blocks=blocks, rows=rows, s...  48.1 us
    pallas_call x2, Pallas kernels, attend(): pl.pallas_call(functools.partial(attend_body, size=size, rows_q=rows_q),...  42.7 us
    pallas_call x2, Pallas kernels, back_up(): pl.pallas_call(back_up_body, grid=(seq // BLOCK,), in_specs=[tokens_spec(...  40.2 us
    pallas_call x2, Pallas kernels, close_block(): pl.pallas_call(close_body, grid=(seq // BLOCK,), in_specs=[tokens_spec(wi...  40 us

profile of v3, /device:TPU:1, one launch (start us, length us, event | category | flops | bytes accessed | tf_op | source)
XLA Modules:
  0.0 655.9 jit_solution(17709331424805853672)
XLA Ops:
  4.7 2.5 cast.1.low_ref
  9.8 103.2 %gather.1 = (bf16[32,3528,128]{2,1,0:T(8,128)(2,1)}, f32[16,8,128]{2,1,0:T(8,128)}, f32[2,96,128]{2,1,0:T(8,128)}, f32[2,8,7680]{2,1,0:T(8,128)}) custom-call(bf16[3528,128]{1,0:T(8,128)(2,1)} %cast.1.low_ref, f32[8,128]{1,0:T(8,128)} %broadcast_in_dim.37.cnt_ref, f32[96,128]{1,0:T(8,128)} %pad_bitcast_fusion.vec_ref, f32[8,7680]{1,0:T(8,128)S(1)} %bitcast.68), custom_call_target="tpu_custom_call" | custom-call | tf_op jit(solution)/shard_map/gather/pallas_call | solution.py:1172
  113.0 1.8 unflat.11.e_ref
  115.5 3.6 embed.1.tok_ref
  119.1 5.9 unflat.12.w_ref
  124.9 4.6 open_block.2
  129.5 6.1 attend.2
  135.6 7.0 %unflat.14.w1_ref = bf16[768,3072]{1,0:T(8,128)(2,1)} custom-call(bf16[112896,128]{1,0:T(8,128)(2,1)} %bitcast.56), custom_call_target="tpu_custom_call" | custom-call | tf_op jit(solution)/shard_map/unflat/pallas_call | solution.py:139
  142.6 9.1 %unflat.15.w2_ref = bf16[3072,768]{1,0:T(8,128)(2,1)} custom-call(bf16[112896,128]{1,0:T(8,128)(2,1)} %bitcast.57), custom_call_target="tpu_custom_call" | custom-call | tf_op jit(solution)/shard_map/unflat/pallas_call | solution.py:139
  151.7 3.3 unflat.13.wo_ref
  155.6 15.7 %close_block.2 = (bf16[256,768]{1,0:T(8,128)(2,1)}, f32[256,768]{1,0:T(8,128)}, bf16[256,768]{1,0:T(8,128)(2,1)}, bf16[256,3072]{1,0:T(8,128)(2,1)}, f32[256,3072]{1,0:T(8,128)}, /*index=5*/f32[256,768]{1,0:T(8,128)}) custom-call(f32[256,768]{1,0:T(8,128)} %embed.1.tok_ref, f32[256,768]{1,0:T(8,128)} %get-tuple-element.329.o_ref, ...), custom_call_target="tpu_custom_call" | custom-call | tf_op jit(solution)/shard_map/close_block/pallas_call | solution.py:416
  172.3 3.0 unflat.16.w_ref
  176.5 7.6 %relay.1 = (bf16[256,768]{1,0:T(8,128)(2,1)}, f32[1024,512]{1,0:T(8,128)}) custom-call(f32[256,768]{1,0:T(8,128)} %get-tuple-element.330.coded_ref, f32[11,768]{1,0:T(8,128)} %reshape.99.vec_ref.vec_e_ref, bf16[768,512]{1,0:T(8,128)(2,1)} %unflat.16.w_ref, f32[1,512]{1,0:T(1,128)} %bitcast.95, f32[11,512]{1,0:T(8,128)} %reshape.100.vec_d_ref.vec_ref, ...), custom_call_target="tpu_custom_call" | custom-call | tf_op jit(solution)/shard_map/relay/pallas_call | solution.py:330
  184.1 3.7 unflat.17.w_ref
  187.8 6.3 open_block.3
  194.1 36.6 %attend.3 = (f32[1024,512]{1,0:T(8,128)}, f32[4,4,1024]{2,1,0:T(4,128)}) custom-call(bf16[1024,1536]{1,0:T(8,128)(2,1)} %get-tuple-element.332.q_ref.k_ref.v_ref, bf16[1024,1536]{1,0:T(8,128)(2,1)} %get-tuple-element.332.q_ref.k_ref.v_ref, bf16[1024,1536]{1,0:T(8,128)(2,1)} %get-tuple-element.332.q_ref.k_ref.v_ref), custom_call_target="tpu_custom_call" | custom-call | tf_op jit(solution)/shard_map/attend/pallas_call | solution.py:193
  230.7 5.0 unflat.19.w1_ref
  235.7 5.9 unflat.20.w2_ref
  241.6 1.9 unflat.18.wo_ref
  244.0 24.3 %close_block.3 = (bf16[1024,512]{1,0:T(8,128)(2,1)}, f32[1024,512]{1,0:T(8,128)}, bf16[1024,512]{1,0:T(8,128)(2,1)}, bf16[1024,2048]{1,0:T(8,128)(2,1)}, f32[1024,2048]{1,0:T(8,128)}, /*index=5*/f32[1024,512]{1,0:T(8,128)}) custom-call(f32[1024,512]{1,0:T(8,128)} %get-tuple-element.331.tok_ref, f32[1024,512]{1,0:T(8,128)} %get-tuple-element.333.o_ref, ...), custom_call_target="tpu_custom_call" | custom-call | tf_op jit(solution)/shard_map/close_block/pallas_call | solution.py:416
  270.1 1.7 unflat.21.w_ref
  271.7 1.5 slice_reduce_fusion
  273.2 5.9 head.1
  279.1 24.7 %back_up.2 = (bf16[1024,512]{1,0:T(8,128)(2,1)}, bf16[1024,2048]{1,0:T(8,128)(2,1)}, bf16[1024,512]{1,0:T(8,128)(2,1)}, bf16[1024,512]{1,0:T(8,128)(2,1)}, f32[1...) custom-call(f32[1024,512]{1,0:T(8,128)} %get-tuple-element.336.grad_ref, ...), custom_call_target="tpu_custom_call" | custom-call | tf_op jit(solution)/shard_map/back_up/pallas_call | solution.py:517
  303.8 52.8 %attend_back.2 = (bf16[1024,512]{1,0:T(8,128)(2,1)}, bf16[1024,512]{1,0:T(8,128)(2,1)}, bf16[1024,512]{1,0:T(8,128)(2,1)}) custom-call(bf16[1024,1536]{1,0:T(8,128)(2,1)} %get-tuple-element.332.q_ref.k_ref.v_ref, bf16[1024,1536]{1,0:T(8,128)(2,1)} %get-tuple-element.332.q_ref.k_ref.v_ref, bf16[1024,1536]{1,0:T(8,128)(2,1)} %get-tuple-element.332.q_ref.k_ref.v_ref, ...), custom_call_target="tpu_custom_call" | custom-call | tf_op jit(solution)/shard_map/attend_back/pallas_call | solution.py:257
  356.6 7.7 %back_in.2 = (bf16[1024,1536]{1,0:T(8,128)(2,1)}, bf16[256,512]{1,0:T(8,128)(2,1)}, f32[8,512]{1,0:T(8,128)}) custom-call(bf16[1024,512]{1,0:T(8,128)(2,1)} %get-tuple-element.341.dq_ref, bf16[1024,512]{1,0:T(8,128)(2,1)} %get-tuple-element.342.dk_ref, bf16[1024,512]{1,0:T(8,128)(2,1)} %get-tuple-element.343.dv_ref, f32[1024,512]{1,0:T(8,128)} %get-tuple-element.344.mid_ref, ...), custom_call_target="tpu_custom_call" | custom-call | tf_op jit(solution)/shard_map/back_in/pallas_call | solution.py:569
  364.3 3.0 relay_back.1
  367.3 15.5 %back_up.3 = (bf16[256,768]{1,0:T(8,128)(2,1)}, bf16[256,3072]{1,0:T(8,128)(2,1)}, bf16[256,768]{1,0:T(8,128)(2,1)}, bf16[256,768]{1,0:T(8,128)(2,1)}, f32[256,7...) custom-call(f32[256,768]{1,0:T(8,128)} %get-tuple-element.346.grad_ref, f32[256,3072]{1,0:T(8,128)} %get-tuple-element.347.slope_ref, ...), custom_call_target="tpu_custom_call" | custom-call | tf_op jit(solution)/shard_map/back_up/pallas_call | solution.py:517
  382.8 7.0 %attend_back.3 = (bf16[256,768]{1,0:T(8,128)(2,1)}, bf16[256,768]{1,0:T(8,128)(2,1)}, bf16[256,768]{1,0:T(8,128)(2,1)}) custom-call(bf16[256,2304]{1,0:T(8,128)(2,1)} %get-tuple-element.328.q_ref.k_ref.v_ref, bf16[256,2304]{1,0:T(8,128)(2,1)} %get-tuple-element.328.q_ref.k_ref.v_ref, bf16[256,2304]{1,0:T(8,128)(2,1)} %get-tuple-element.328.q_ref.k_ref.v_ref, ...), custom_call_target="tpu_custom_call" | custom-call | tf_op jit(solution)/shard_map/attend_back/pallas_call | solution.py:257
  389.9 5.1 back_in.3
  400.8 16.6 %skinny.2.refs_0_ = f32[2,512,128]{2,1,0:T(8,128)} custom-call(f32[2,8,7680]{2,1,0:T(8,128)} %get-tuple-element.325.refs_0_, bf16[256,2304]{1,0:T(8,128)(2,1)} %get-tuple-element.355.refs_1_.refs_3_.refs_12_, bf16[256,768]{1,0:T(8,128)(2,1)} %get-tuple-element.356.refs_2_.refs_5_.refs_13_, bf16[256,3072]{1,0:T(8,128)(2,1)} %get-tuple-element.357.refs_3_.refs_7_.refs_14_, ...), custom_call_target="tpu_custom_call" | custom-call | tf_op jit(solution)/shard_map/skinny/pallas_call | solution.py:648
  417.5 34.4 %conditional.3 = (bf16[56448,128]{1,0:T(8,128)(2,1)}, f32[512,128]{1,0:T(8,128)}) conditional(s32[]{:T(128)} %convert_element_type.36, (f32[1,8,7680]{2,1,0:T(8,128)}, bf16[1,1,7225344]{2,1,0:T(2,128)(2,1)}) %tuple.29, (f32[1,8,7680]{2,1,0:T(8,128)}, bf16[1,1,7225344]{2,1,0:T(2,128)(2,1)}) %tuple.29), branch_computations={%region_2.3_spmd, %region_3.4_spmd} | conditional | bytes 933904 | solution.py:1360
  417.5 1.6 slice.202.x_ref
  419.0 3.1 err_prep.11
  422.2 1.4 fusion.9
  423.5 2.2 err_prep.12
  426.4 1.3 constant_dynamic-update-slice_fusion.4
  427.7 1.5 slice.200.x_ref
  429.2 4.3 err_prep.13
  433.4 1.3 constant_dynamic-update-slice_fusion.3
  434.8 6.7 %err_prep.14 = (bf16[56448,128]{1,0:T(8,128)(2,1)}, f32[128,128]{1,0:T(8,128)}) custom-call(bf16[1,1,7225344]{2,1,0:T(2,128)(2,1)} %get-tuple-element.97.e_ref, f32[8,512]{1,0:T(8,128)} %get-tuple-element.430.x_ref, bf16[56448,128]{1,0:T(8,128)(2,1)} %get-tuple-element.129.rest_0_), custom_call_target="tpu_custom_call", output_to_operand_aliasing={{0}: (2, {})} | custom-call | tf_op jit(solution)/shard_map/cond/branch_0_fun/err_prep/pallas_call | solution.py:726
  441.4 1.5 constant_dynamic-update-slice_fusion.2
  442.9 1.9 err_prep.15
  446.1 3.4 err_prep.16
  449.4 1.3 constant_dynamic-update-slice_fusion
  451.9 49.5 %all_sum.2 = (f32[2,512,128]{2,1,0:T(8,128)}, bf16[256,768]{1,0:T(8,128)(2,1)}, bf16[256,2304]{1,0:T(8,128)(2,1)}, bf16[256,768]{1,0:T(8,128)(2,1)}, bf16[256,76...) custom-call(f32[2,512,128]{2,1,0:T(8,128)} %skinny.2.refs_0_, ...), custom_call_target="tpu_custom_call" | custom-call | tf_op jit(solution)/shard_map/all_sum/pallas_call | solution.py:1284
  501.4 2.9 orthonormal.1.refs_0_.ortho_ref
  504.3 6.9 %conditional.4 = (f32[512,128]{1,0:T(8,128)}) conditional(s32[]{:T(128)} %convert_element_type.36, (f32[2,8,5632]{2,1,0:T(8,128)S(1)}, bf16[56448,128]{1,0:T(8,128)(2,1)}) %tuple.30, (f32[2,8,5632]{2,1,0:T(8,128)S(1)}, bf16[56448,128]{1,0:T(8,128)(2,1)}) %tuple.30), branch_computations={%region_4.5_spmd, %region_5.6_spmd} | conditional | bytes 8 | solution.py:1403
  504.3 6.9 %err_right.2 = f32[512,128]{1,0:T(8,128)} custom-call(f32[2,8,5632]{2,1,0:T(8,128)S(1)} %get-tuple-element.151.x_ref, bf16[56448,128]{1,0:T(8,128)(2,1)} %get-tuple-element.152.e_ref), custom_call_target="tpu_custom_call" | custom-call | tf_op jit(solution)/shard_map/cond/branch_0_fun/err_right/pallas_call | solution.py:786
  511.3 16.4 %skinny.3.refs_0_ = f32[2,512,128]{2,1,0:T(8,128)} custom-call(f32[2,8,5632]{2,1,0:T(8,128)S(1)} %orthonormal.1.refs_0_.ortho_ref, bf16[256,768]{1,0:T(8,128)(2,1)} %get-tuple-element.365.refs_12_.refs_2_.refs_1_, bf16[256,768]{1,0:T(8,128)(2,1)} %get-tuple-element.366.refs_13_.refs_4_.refs_2_, bf16[256,768]{1,0:T(8,128)(2,1)} %get-tuple-element.367.refs_14_.refs_6_.refs_3_, ...), custom_call_target="tpu_custom_call" | custom-call | tf_op jit(solution)/shard_map/skinny/pallas_call | solution.py:648
  527.7 22.9 %all_sum.3.sum_ref = f32[2,512,128]{2,1,0:T(8,128)} custom-call(f32[2,512,128]{2,1,0:T(8,128)} %skinny.3.refs_0_, f32[512,128]{1,0:T(8,128)} %get-tuple-element.458.refs_1_), custom_call_target="tpu_custom_call" | custom-call | tf_op jit(solution)/shard_map/all_sum/pallas_call | solution.py:1284
  550.6 1.5 slice.193.vec_ref
  552.1 2.6 final_right.1
  557.0 78.1 %conditional.5 = ((f32[1,1,7225344]{2,1,0:T(1,128)}, f32[62592,128]{1,0:T(8,128)})) conditional(s32[]{:T(128)} %convert_element_type.36, (s32[1]{0:T(128)}, bf16[1024,512]{1,0:T(8,128)(2,1)}, bf16[1024,512]{1,0:T(8,128)(2,1)}, bf16[1024,1536]{1,0:T(8,128)(2,1)}, bf16[1024,1536]{1,0:T(8,128)(2,1)}, /*index=5*/bf16[56448,128]{1,0:T(8,128)(2,1)}, ...), branch_computations={%region_6.7_spmd, %region_7.8_spmd} | conditional | bytes 3932280 | solution.py:1434
  557.0 14.8 %finish.11 = (f32[1,1,7225344]{2,1,0:T(1,128)}, f32[62592,128]{1,0:T(8,128)}) custom-call(s32[1]{0:T(128)} %get-tuple-element.156.me_ref, bf16[1024,512]{1,0:T(8,128)(2,1)} %get-tuple-element.180.a0, bf16[1024,512]{1,0:T(8,128)(2,1)} %get-tuple-element.181.a1, bf16[1024,1536]{1,0:T(8,128)(2,1)} %get-tuple-element.182.b0, ...), custom_call_target="tpu_custom_call" | custom-call | tf_op jit(solution)/shard_map/cond/branch_0_fun/finish/pallas_call | solution.py:895
  571.8 6.4 finish.12
  578.2 19.8 %finish.13 = (f32[1,1,7225344]{2,1,0:T(1,128)}, f32[62592,128]{1,0:T(8,128)}) custom-call(s32[1]{0:T(128)} %get-tuple-element.156.me_ref, bf16[1024,512]{1,0:T(8,128)(2,1)} %get-tuple-element.172.a0, bf16[1024,512]{1,0:T(8,128)(2,1)} %get-tuple-element.173.a1, ...), custom_call_target="tpu_custom_call", output_to_operand_aliasing={{0}: (8, {}), {1}: (9, {})} | custom-call | tf_op jit(solution)/shard_map/cond/branch_0_fun/finish/pallas_call | solution.py:895
  598.0 16.4 %finish.14 = (f32[1,1,7225344]{2,1,0:T(1,128)}, f32[62592,128]{1,0:T(8,128)}) custom-call(s32[1]{0:T(128)} %get-tuple-element.156.me_ref, bf16[1024,2048]{1,0:T(8,128)(2,1)} %get-tuple-element.168.a0, bf16[1024,2048]{1,0:T(8,128)(2,1)} %get-tuple-element.169.a1, ...), custom_call_target="tpu_custom_call", output_to_operand_aliasing={{0}: (8, {}), {1}: (9, {})} | custom-call | tf_op jit(solution)/shard_map/cond/branch_0_fun/finish/pallas_call | solution.py:895
  614.4 3.6 finish.15
  617.9 5.1 finish.16
  623.0 12.0 %finish_tail.1 = f32[1,1,7225344]{2,1,0:T(1,128)} custom-call(bf16[1,1,7225344]{2,1,0:T(2,128)(2,1)} %get-tuple-element.155.e_ref, f32[1,1,7225344]{2,1,0:T(1,128)} %get-tuple-element.194.buf0), custom_call_target="tpu_custom_call", output_to_operand_aliasing={{}: (1, {})} | custom-call | tf_op jit(solution)/shard_map/cond/branch_0_fun/finish_tail/pallas_call | solution.py:929
  635.2 3.6 broadcast_multiply_fusion
  638.9 3.9 fusion.8
  642.8 11.0 %broadcast_in_dim.45 = bf16[1,451584]{1,0:T(2,128)(2,1)} reshape(bf16[451584]{0:T(1024)(128)(2,1)S(1)} %get-tuple-element.426) | data formatting | bytes 1806336 | tf_op jit(solution)/shard_map/broadcast_in_dim | solution.py:1448
  (118 shorter events, 23.4 us)
Async XLA Ops:
  0.6 1.6 copy-start
  0.7 7.3 %copy-start.22 = (s32[2,768]{1,0:T(2,128)S(1)}, s32[2,768]{1,0:T(2,128)}, u32[]{:S(2)}) copy-start(s32[2,768]{1,0:T(2,128)} %param.21) | copy-start | bytes 18436
  0.7 6.5 copy-start.17
  0.7 9.1 %copy-start.14 = (f32[1,8,7680]{2,1,0:T(8,128)S(1)}, f32[1,8,7680]{2,1,0:T(8,128)}, u32[]{:S(2)}) copy-start(f32[1,8,7680]{2,1,0:T(8,128)} %param.26) | copy-start | bytes 737284
  3.1 111.7 %copy-start.15 = (bf16[1024,192]{1,0:T(8,128)(2,1)}, bf16[1024,192]{1,0:T(8,128)(2,1)S(1)}, u32[]{:S(2)}) copy-start(bf16[1024,192]{1,0:T(8,128)(2,1)S(1)} %fusion.2) | copy-start | bytes 1179652
  3.1 397.7 %copy-start.10 = (bf16[256,192]{1,0:T(8,128)(2,1)}, bf16[256,192]{1,0:T(8,128)(2,1)S(1)}, u32[]{:S(2)}) copy-start(bf16[256,192]{1,0:T(8,128)(2,1)S(1)} %slice.208.pix_ref.refs_16_.refs_10_.refs_5_) | copy-start | bytes 294916
  113.0 1.8 copy-start.19
  244.0 24.3 %copy-start.16 = (bf16[1024,192]{1,0:T(8,128)(2,1)S(1)}, bf16[1024,192]{1,0:T(8,128)(2,1)}, u32[]{:S(2)}) copy-start(bf16[1024,192]{1,0:T(8,128)(2,1)} %copy-done.15) | copy-start | bytes 1179652
  279.1 172.7 %copy-start.5 = (bf16[768,512]{1,0:T(8,128)(2,1)}, bf16[768,512]{1,0:T(8,128)(2,1)S(1)}, u32[]{:S(2)}) copy-start(bf16[768,512]{1,0:T(8,128)(2,1)S(1)} %get-tuple-element.364.refs_10_.refs_21_) | copy-start | bytes 2359300
  389.8 6.1 copy-start.26
  389.8 7.1 %copy-start.23 = (f32[1,3072]{1,0:T(1,128)S(1)}, f32[1,3072]{1,0:T(1,128)}, u32[]{:S(2)}) copy-start(f32[1,3072]{1,0:T(1,128)} %get-tuple-element.378) | copy-start | bytes 36868
  389.8 7.2 %copy-start.24 = (f32[8,512]{1,0:T(8,128)S(1)}, f32[8,512]{1,0:T(8,128)}, u32[]{:S(2)}) copy-start(f32[8,512]{1,0:T(8,128)} %get-tuple-element.379) | copy-start | bytes 49156
  389.8 7.3 %copy-start.27 = (f32[8,512]{1,0:T(8,128)S(1)}, f32[8,512]{1,0:T(8,128)}, u32[]{:S(2)}) copy-start(f32[8,512]{1,0:T(8,128)} %get-tuple-element.380) | copy-start | bytes 49156
  389.9 8.2 %copy-start.25 = (f32[1,2048]{1,0:T(1,128)S(1)}, f32[1,2048]{1,0:T(1,128)}, u32[]{:S(2)}) copy-start(f32[1,2048]{1,0:T(1,128)} %get-tuple-element.382) | copy-start | bytes 24580
  417.4 34.4 %copy-start.3 = (bf16[256,3072]{1,0:T(8,128)(2,1)S(1)}, bf16[256,3072]{1,0:T(8,128)(2,1)}, u32[]{:S(2)}) copy-start(bf16[256,3072]{1,0:T(8,128)(2,1)} %get-tuple-element.368.refs_15_.refs_8_.refs_4_) | copy-start | bytes 4718596
  417.4 34.4 %copy-start.4 = (bf16[256,2304]{1,0:T(8,128)(2,1)S(1)}, bf16[256,2304]{1,0:T(8,128)(2,1)}, u32[]{:S(2)}) copy-start(bf16[256,2304]{1,0:T(8,128)(2,1)} %get-tuple-element.355.refs_1_.refs_3_.refs_12_) | copy-start | bytes 3538948
  423.5 2.3 copy-start.21
  504.3 7.0 %copy-start.7 = (bf16[256,512]{1,0:T(8,128)(2,1)S(1)}, bf16[256,512]{1,0:T(8,128)(2,1)}, u32[]{:S(2)}) copy-start(bf16[256,512]{1,0:T(8,128)(2,1)} %get-tuple-element.345.b_ref.refs_11_.refs_23_.refs_22_) | copy-start | bytes 786436
  504.3 7.0 %copy-start.11 = (bf16[256,192]{1,0:T(8,128)(2,1)S(1)}, bf16[256,192]{1,0:T(8,128)(2,1)}, u32[]{:S(2)}) copy-start(bf16[256,192]{1,0:T(8,128)(2,1)} %copy-done.10) | copy-start | bytes 294916
  511.3 45.0 %copy-start.18 = (f32[1,11520]{1,0:T(1,128)S(1)}, f32[1,11520]{1,0:T(1,128)}, u32[]{:S(2)}) copy-start(f32[1,11520]{1,0:T(1,128)} %param.24) | copy-start | bytes 138244
  511.3 45.0 %copy-start.20 = (f32[1,11520]{1,0:T(1,128)S(1)}, f32[1,11520]{1,0:T(1,128)}, u32[]{:S(2)}) copy-start(f32[1,11520]{1,0:T(1,128)} %param.25) | copy-start | bytes 138244
  635.2 3.7 copy-start.6
  638.8 16.9 %copy-start.1 = (bf16[2,1024,192]{1,2,0:T(8,128)(2,1)S(1)}, bf16[2,1024,192]{1,2,0:T(8,128)(2,1)}, u32[]{:S(2)}) copy-start(bf16[2,1024,192]{1,2,0:T(8,128)(2,1)} %param.18) | copy-start | bytes 2359300
  638.9 15.0 %copy-start.2 = (f32[2,8,7680]{2,1,0:T(8,128)S(1)}, f32[2,8,7680]{2,1,0:T(8,128)}, u32[]{:S(2)}) copy-start(f32[2,8,7680]{2,1,0:T(8,128)} %get-tuple-element.390) | copy-start | bytes 1474564

commit v4 on v3

v4 whole, which is shorter than its diff:
```python
import functools
import math

import jax
import jax.numpy as jnp
import numpy as np
from jax import lax
from jax.experimental import pallas as pl
from jax.experimental.pallas import tpu as pltpu
from jax.sharding import PartitionSpec as P

DE = 768
FFE = 3072
HEADS_ENC = 12
DD = 512
FFD = 2048
HEADS_DEC = 16
PATCH = 192
RANK = 8
SEQ = 1024
VIS = 256
FLAT = 7225344
VLEN = 11520

(K_TOKENS, K_NORMED, K_JOINED, K_OUT, K_LSE, K_ATTENDED, K_MIDDLE, K_SECOND, K_ACTIVE, K_SLOPE, K_CODED, K_B_QKV, K_B_PROJ, K_B_UP, K_B_DOWN, K_B_PRED, K_FINAL, K_SENT, K_FIRST, K_GRAD, K_ATT, K_DK, K_DV, K_SUMS, K_BIAS, K_START) = range(26)

f32 = jnp.float32
bf16 = jnp.bfloat16
clip_limit = 0.0001
moment_decay = 0.9
rate_base = 0.5
LANES = 128
SEC, DP = "section", "dp"
STEP = 32
DEC_ROWS = 512
CHUNK = 256
SPARE = 6144
BIG = 66000000


def nn(left, right):
    return lax.dot_general(left, right, (((1,), (0,)), ((), ())), preferred_element_type=f32)


def nt(left, right):
    return lax.dot_general(left, right, (((1,), (1,)), ((), ())), preferred_element_type=f32)


def tn(left, right):
    return lax.dot_general(left, right, (((0,), (0,)), ((), ())), preferred_element_type=f32)


def split3(value):
    high = value.astype(bf16)
    rest = value - high.astype(f32)
    middle = rest.astype(bf16)
    return jnp.concatenate([high, middle, (rest - middle.astype(f32)).astype(bf16)], axis=0)


def join3(value):
    return value[:RANK] + value[RANK : 2 * RANK] + value[2 * RANK :]


def norm_parts(tokens):
    centred = tokens - jnp.mean(tokens, axis=-1, keepdims=True)
    spread = lax.rsqrt(jnp.mean(centred * centred, axis=-1, keepdims=True) + 1e-06)
    return centred * spread, spread


def norm_back(grad, hat, spread, gain):
    inner = grad * gain
    return spread * (
        inner - jnp.mean(inner, axis=-1, keepdims=True) - hat * jnp.mean(inner * hat, axis=-1, keepdims=True)
    )


def column_sum(value):
    return jnp.sum(value.astype(f32), axis=0, keepdims=True)


def angle_tables(width):
    column = np.arange(width)
    freqs = np.exp(-(column // 2 * 2) / width * math.log(10000.0))
    coarse = (np.arange(0, SEQ, STEP)[:, None] * freqs).astype(np.float64)
    fine = np.arange(STEP)[:, None] * freqs + (column % 2) * (math.pi / 2)
    return jnp.asarray(np.stack([np.sin(coarse), np.cos(coarse), np.cos(fine), np.sin(fine)]), f32)


def positions_of(place, tables):
    column = lax.broadcasted_iota(jnp.int32, (1, STEP), 1)
    coarse = (place // STEP == column).astype(bf16)
    fine = (place % STEP == column).astype(bf16)

    def take(pick, table):
        high = table.astype(bf16)
        rest = table - high.astype(f32)
        middle = rest.astype(bf16)
        low = (rest - middle.astype(f32)).astype(bf16)
        return nn(pick, high) + nn(pick, middle) + nn(pick, low)

    return take(coarse, tables[0]) * take(fine, tables[2]) + take(coarse, tables[1]) * take(fine, tables[3])


def section_shapes(section):
    if section == 0:
        return [(DE, 3 * DE), (DE, DE), (DE, FFE), (FFE, DE), (PATCH, DE)]
    return [(DD, 3 * DD), (DD, DD), (DD, FFD), (FFD, DD), (PATCH, DD), (DE, DD)]


def learning_rate():
    return rate_base * math.sqrt(2.0 * (FLAT + VLEN) / DD) / clip_limit


def head_mask(head, size):
    lane = lax.broadcasted_iota(jnp.int32, (1, LANES), 1)
    return (lane // size == head).astype(bf16)


def attend_body(q_ref, k_ref, v_ref, o_ref, lse_ref, *, size, rows_q):
    seq = k_ref.shape[0]
    scale = size ** (-0.5)
    fold = scale * math.log2(math.e)

    def one(step, carry):
        at = pl.ds(pl.multiple_of(step * rows_q, rows_q), rows_q)
        queries = q_ref[at, :]
        total = jnp.zeros((rows_q, LANES), f32)
        for head in range(LANES // size):
            mask = head_mask(head, size)
            scores = nt(k_ref[...], queries * mask)
            peak = jnp.max(scores, axis=0, keepdims=True) * fold
            power = jnp.exp2(scores * fold - peak)
            mass = jnp.sum(power, axis=0, keepdims=True)
            share = jnp.transpose(jnp.broadcast_to(1.0 / mass, (8, rows_q)))[:, :1]
            total = total + tn(power.astype(bf16), v_ref[...] * mask) * share
            lse_ref[0, head : head + 1, at] = peak + jnp.log2(mass)
        o_ref[at, :] = total
        return carry

    lax.fori_loop(0, seq // rows_q, one, 0)


def attend_back_body(q_ref, k_ref, v_ref, do_ref, o_ref, lse_ref, dq_ref, dk_ref, dv_ref, dk_sum, dv_sum, *, size, rows_q):
    seq = k_ref.shape[0]
    scale = size ** (-0.5)
    fold = scale * math.log2(math.e)
    dk_sum[...] = jnp.zeros_like(dk_sum)
    dv_sum[...] = jnp.zeros_like(dv_sum)

    def one(step, carry):
        at = pl.ds(pl.multiple_of(step * rows_q, rows_q), rows_q)
        queries = q_ref[at, :]
        grads = do_ref[at, :]
        prod = grads.astype(f32) * o_ref[at, :]
        total = jnp.zeros((rows_q, LANES), f32)
        high = prod.astype(bf16)
        rest = prod - high.astype(f32)
        middle = rest.astype(bf16)
        for head in range(LANES // size):
            mask = head_mask(head, size)
            wide = jnp.broadcast_to(mask, (16, LANES))
            delta = (nt(wide, high) + nt(wide, middle))[0:1]
            q_one = queries * mask
            g_one = grads * mask
            scores = nt(k_ref[...], q_one)
            probs = jnp.exp2(scores * fold - lse_ref[0, head : head + 1, at])
            slope = nt(v_ref[...], g_one)
            grad_s = (probs * (slope - delta)).astype(bf16)
            dv_sum[...] += nn(probs.astype(bf16), g_one)
            dk_sum[...] += nn(grad_s, q_one)
            total = total + tn(grad_s, k_ref[...] * mask)
        dq_ref[at, :] = (total * scale).astype(bf16)
        return carry

    lax.fori_loop(0, seq // rows_q, one, 0)
    dk_ref[...] = (dk_sum[...] * scale).astype(bf16)
    dv_ref[...] = dv_sum[...].astype(bf16)


def rows_at(step, count):
    return pl.ds(pl.multiple_of(step * count, count), count)


def cols_at(step, count=LANES):
    return pl.ds(pl.multiple_of(step * count, count), count)


def shape_of(rows, cols, dtype=f32):
    return jax.ShapeDtypeStruct((rows, cols), dtype)


def loop(count, body):
    def one(step, carry):
        body(step)
        return carry

    lax.fori_loop(0, count, one, 0)


def over_blocks(seq, rows, body, *refs):
    loop(seq // rows, lambda step: body(*[ref.at[rows_at(step, rows)] for ref in refs]))


def open_stage(tok_ref, normed_ref, joined_ref, vec_ref, w_ref):
    width = tok_ref.shape[1]
    hat, unused = norm_parts(tok_ref[...])
    normed = (hat * vec_ref[0:1] + vec_ref[1:2]).astype(bf16)
    normed_ref[...] = normed
    for part, bias in ((0, vec_ref[6:7]), (1, None), (2, vec_ref[7:8])):
        cols = slice(part * width, (part + 1) * width)
        value = nn(normed, w_ref[:, cols])
        joined_ref[:, cols] = (value if bias is None else value + bias).astype(bf16)


def attend_stage(joined, out, lse, size):
    seq, width = out.shape
    groups = width // LANES

    def one(group):
        attend_body(
            joined.at[:, cols_at(group)], joined.at[:, cols_at(groups + group)],
            joined.at[:, cols_at(2 * groups + group)], out.at[:, cols_at(group)], lse.at[pl.ds(group, 1)],
            size=size, rows_q=min(512, seq),
        )

    loop(groups, one)


def attend_back_stage(joined, grad_att, out, lse, b_qkv, dk_sum, dv_sum, size):
    seq, width = out.shape
    groups = width // LANES

    def one(group):
        here = [cols_at(part * groups + group) for part in range(3)]
        attend_back_body(
            *[joined.at[:, cols] for cols in here], grad_att.at[:, here[0]], out.at[:, here[0]],
            lse.at[pl.ds(group, 1)], *[b_qkv.at[:, cols] for cols in here], dk_sum, dv_sum,
            size=size, rows_q=min(512, seq),
        )

    loop(groups, one)


def close_stage(
    tok_ref, o_ref, att_ref, mid_ref, sec_ref, act_ref, slope_ref, out_ref, vec_ref, bias_ref, wo_ref, w1_ref, w2_ref
):
    attended = o_ref[...].astype(bf16)
    att_ref[...] = attended
    middle = tok_ref[...] + nn(attended, wo_ref[...]) + vec_ref[8:9]
    mid_ref[...] = middle
    hat, unused = norm_parts(middle)
    sec_ref[...] = (hat * vec_ref[2:3] + vec_ref[3:4]).astype(bf16)
    out_ref[...] = middle + vec_ref[9:10]

    def one(step):
        cols = cols_at(step, CHUNK)
        hidden = nn(sec_ref[...], w1_ref[:, cols]) + bias_ref[:, cols]
        share = 0.5 * (1.0 + lax.erf(hidden * math.sqrt(0.5)))
        active = (hidden * share).astype(bf16)
        act_ref[:, cols] = active
        slope_ref[:, cols] = share + hidden * (jnp.exp(-0.5 * hidden * hidden) * (1.0 / math.sqrt(2.0 * math.pi)))
        out_ref[...] += nn(active, w2_ref[cols, :])

    loop(w1_ref.shape[1] // CHUNK, one)


def back_up_stage(
    grad_ref, slope_ref, mid_ref, down_ref, up_ref, proj_ref, att_ref, total, vec_ref, wo_ref, w1_ref, w2_ref, sums_ref, bias_ref
):
    down = grad_ref[...].astype(bf16)
    down_ref[...] = down
    total[...] = jnp.zeros_like(total)

    def one(step):
        cols = cols_at(step, CHUNK)
        part = (nt(down_ref[...], w2_ref[cols, :]) * slope_ref[:, cols]).astype(bf16)
        up_ref[:, cols] = part
        bias_ref[:, cols] += column_sum(part)
        total[...] += nt(part, w1_ref[:, cols])

    loop(w1_ref.shape[1] // CHUNK, one)
    grad = total[...]
    hat, spread = norm_parts(mid_ref[...])
    middle = grad_ref[...] + norm_back(grad, hat, spread, vec_ref[2:3])
    grad_ref[...] = middle
    proj = middle.astype(bf16)
    proj_ref[...] = proj
    att_ref[...] = nt(proj, wo_ref[...]).astype(bf16)
    sums_ref[2:3] += column_sum(grad * hat)
    sums_ref[3:4] += column_sum(grad)
    sums_ref[8:9] += column_sum(proj)
    sums_ref[9:10] += column_sum(down)


def back_in_stage(join_ref, grad_ref, tok_ref, vec_ref, w_ref, sums_ref):
    width = tok_ref.shape[1]
    grad = nt(join_ref[...], w_ref[...])
    sums_ref[6:7] += column_sum(join_ref[:, :width])
    sums_ref[7:8] += column_sum(join_ref[:, 2 * width :])
    hat, spread = norm_parts(tok_ref[...])
    grad_ref[...] += norm_back(grad, hat, spread, vec_ref[0:1])
    sums_ref[0:1] += column_sum(grad * hat)
    sums_ref[1:2] += column_sum(grad)


def widen(flat_ref, wide, w_ref):
    rows_n, cols_n = w_ref.shape
    blocks = cols_n // LANES
    count = 64 * blocks

    def one(step):
        wide[:count] = flat_ref[rows_at(step, count), :].astype(f32)
        for block in range(blocks):
            w_ref[rows_at(step, 64), block * LANES : (block + 1) * LANES] = wide[
                pl.ds(block, 64, stride=blocks), :
            ].astype(bf16)

    loop(rows_n // 64, one)


class Weights:
    def __init__(self, flat, section, order, slots, wide, mats, sems):
        self.flat, self.slots, self.wide, self.mats, self.sems = flat, slots, wide, mats, sems
        self.order, self.shapes, self.next = order, section_shapes(section), 0
        self.base = section * (FLAT // LANES)
        for position in range(2):
            self.fetch(position).start()

    def fetch(self, position):
        index = self.order[position]
        start = self.base + sum(rows * cols for rows, cols in self.shapes[:index]) // LANES
        count = self.shapes[index][0] * self.shapes[index][1] // LANES
        return pltpu.make_async_copy(
            self.flat.at[pl.ds(start, count)], self.slots.at[position % 2, pl.ds(0, count)], self.sems.at[position]
        )

    def take(self):
        position = self.next
        self.fetch(position).wait()
        mat = self.mats[self.order[position]]
        widen(self.slots.at[position % 2], self.wide, mat)
        if position + 2 < len(self.order):
            self.fetch(position + 2).start()
        self.next += 1
        return mat


def take_rows(vec_ref, section, width, rows_ref, bias_ref, extra_ref=None):
    places = [(rows_ref, line, line * width, width) for line in range(11)]
    places.append((bias_ref, 0, 11 * width, bias_ref.shape[1]))
    if extra_ref is not None:
        places.append((extra_ref, 0, 11 * width + bias_ref.shape[1], width))
    for ref, line, offset, count in places:
        for tile in range(count // LANES):
            row = offset // LANES + tile
            ref[line : line + 1, tile * LANES : (tile + 1) * LANES] = vec_ref[section, row : row + 1]


class Copies:
    def __init__(self, sems):
        self.sems, self.made = sems, []

    def start(self, src, dst):
        copy = pltpu.make_async_copy(src, dst, self.sems.at[len(self.made)])
        copy.start()
        self.made.append(copy)
        return copy


def flat_count(section):
    return max(rows * cols for rows, cols in section_shapes(section)) // LANES


ANYWHERE = pl.BlockSpec(memory_space=pl.ANY)
WHOLE = pl.BlockSpec(memory_space=pltpu.VMEM)
ENC_KEPT = [
    (K_TOKENS, (VIS, DE), f32), (K_NORMED, (VIS, DE), bf16), (K_JOINED, (VIS, 3 * DE), bf16), (K_OUT, (VIS, DE), f32),
    (K_LSE, (DE // LANES, 2, VIS), f32), (K_ATTENDED, (VIS, DE), bf16), (K_MIDDLE, (VIS, DE), f32),
    (K_SECOND, (VIS, DE), bf16), (K_ACTIVE, (VIS, FFE), bf16), (K_SLOPE, (VIS, FFE), f32), (K_CODED, (VIS, DE), f32),
]


def encode_body(flat, pix, place, table, vec_ref, *rest):
    kept_n, mats_n = len(ENC_KEPT), len(section_shapes(0))
    kept_out, mats_out = rest[:kept_n], rest[kept_n : kept_n + mats_n]
    rest = rest[kept_n + mats_n :]
    kept = dict(zip([name for name, shape, kind in ENC_KEPT], rest[:kept_n]))
    mats = rest[kept_n : kept_n + mats_n]
    slots, wide, vecs, bias, in_sems, out_sems = rest[kept_n + mats_n :]
    take_rows(vec_ref, 0, DE, vecs, bias)
    weights = Weights(flat, 0, [4, 0, 1, 2, 3], slots, wide, mats, in_sems)
    copies = Copies(out_sems)

    def give(*names):
        for name in names:
            which = [entry[0] for entry in ENC_KEPT].index(name)
            copies.start(kept[name], kept_out[which])

    def take(index):
        mat = weights.take()
        copies.start(mat, mats_out[index])
        return mat

    kept[K_TOKENS][...] = positions_of(place[...], table) + vecs[10:11] + nn(pix[...], take(4)[...])
    open_stage(kept[K_TOKENS], kept[K_NORMED], kept[K_JOINED], vecs, take(0))
    give(K_TOKENS, K_NORMED, K_JOINED)
    attend_stage(kept[K_JOINED], kept[K_OUT], kept[K_LSE], DE // HEADS_ENC)
    give(K_OUT, K_LSE)
    wo, w1, w2 = take(1), take(2), take(3)
    keys = [K_TOKENS, K_OUT, K_ATTENDED, K_MIDDLE, K_SECOND, K_ACTIVE, K_SLOPE, K_CODED]
    close_stage(*[kept[name] for name in keys], vecs, bias, wo, w1, w2)
    give(K_ATTENDED, K_MIDDLE, K_SECOND, K_ACTIVE, K_SLOPE, K_CODED)
    for copy in copies.made:
        copy.wait()


def encode(flat, pix, place, table, vecs):
    mats = section_shapes(0)
    dma = pltpu.SemaphoreType.DMA
    outs = pl.pallas_call(
        encode_body,
        in_specs=[ANYWHERE] + [WHOLE] * 4,
        out_specs=[ANYWHERE] * (len(ENC_KEPT) + len(mats)),
        out_shape=[jax.ShapeDtypeStruct(shape, kind) for name, shape, kind in ENC_KEPT] + [shape_of(*shape, bf16) for shape in mats],
        scratch_shapes=[pltpu.VMEM(shape, kind) for name, shape, kind in ENC_KEPT]
        + [pltpu.VMEM(shape, bf16) for shape in mats]
        + [
            pltpu.VMEM((2, flat_count(0), LANES), bf16), pltpu.VMEM((64 * FFE // LANES, LANES), f32),
            pltpu.VMEM((16, DE), f32), pltpu.VMEM((1, FFE), f32), dma((len(mats),)), dma((len(ENC_KEPT) + len(mats),)),
        ],
        compiler_params=pltpu.CompilerParams(vmem_limit_bytes=BIG),
        name="encode",
    )(flat, pix, place, table, vecs)
    return dict(zip([name for name, shape, kind in ENC_KEPT], outs)), outs[len(ENC_KEPT) :]


def put_vec(part_ref, tail_row, offset, value):
    for tile in range(value.shape[1] // LANES):
        row = tail_row + offset // LANES + tile
        part_ref[row : row + 1] = value[:, tile * LANES : (tile + 1) * LANES]


def put_left(part_ref, section, index, factor_ref, u_ref, v_ref, gain):
    base = len(section_shapes(0)) * section + index
    unused, start, width = COL_SPANS[base]
    part = join3(nt(split3(factor_ref[section, :, start : start + width]), u_ref[...]))
    value = gain * join3(nn(split3(part), v_ref[...]))
    unused, start, width = ROW_SPANS[base]
    for tile in range(tiles_of(width)):
        here = min(LANES, width - tile * LANES)
        row = (start // LANES + tile) * RANK
        part_ref[row : row + RANK, :here] = value[:, tile * LANES : tile * LANES + here]


DEC_GIVEN = [
    (K_NORMED, (SEQ, DD), bf16), (K_B_QKV, (SEQ, 3 * DD), bf16), (K_ATTENDED, (SEQ, DD), bf16), (K_B_PROJ, (SEQ, DD), bf16),
    (K_SECOND, (SEQ, DD), bf16), (K_B_UP, (SEQ, FFD), bf16), (K_ACTIVE, (SEQ, FFD), bf16), (K_B_DOWN, (SEQ, DD), bf16),
    (K_B_PRED, (SEQ - VIS, PATCH), bf16), (K_FINAL, (SEQ - VIS, DD), bf16), (K_SENT, (VIS, DE), bf16), (K_FIRST, (VIS, DD), bf16),
]
DEC_HELD = [
    (K_TOKENS, (SEQ, DD), f32), (K_JOINED, (SEQ, 3 * DD), bf16), (K_OUT, (SEQ, DD), f32), (K_LSE, (DD // LANES, 4, SEQ), f32),
    (K_MIDDLE, (SEQ, DD), f32), (K_SLOPE, (SEQ, FFD), f32), (K_GRAD, (SEQ, DD), f32), (K_ATT, (SEQ, DD), bf16),
    (K_DK, (SEQ, LANES), f32), (K_DV, (SEQ, LANES), f32), (K_SUMS, (16, DD), f32), (K_BIAS, (1, FFD), f32),
]


def decode_body(
    flat, coded, place, table, vec_ref, target, mask, count_ref, factor, *rest, tail_row, gain
):
    given_n, held_n, mats_n = len(DEC_GIVEN), len(DEC_HELD), len(section_shapes(1))
    given_out, grad_coded, sums_e, part_ref = rest[:given_n], rest[given_n], rest[given_n + 1], rest[given_n + 2]
    rest = rest[given_n + 3 :]
    have = dict(zip([name for name, shape, kind in DEC_GIVEN + DEC_HELD], rest[: given_n + held_n]))
    mats = rest[given_n + held_n : given_n + held_n + mats_n]
    slots, wide, total, vec_e, bias_e, vec_d, bias, extra, in_sems, out_sems = rest[given_n + held_n + mats_n :]
    take_rows(vec_ref, 0, DE, vec_e, bias_e)
    take_rows(vec_ref, 1, DD, vec_d, bias, extra)
    weights = Weights(flat, 1, [5, 0, 1, 2, 3, 4], slots, wide, mats, in_sems)
    copies = Copies(out_sems)
    blk = total.shape[0]
    sums, bias_sum = have[K_SUMS], have[K_BIAS]

    def give(*names):
        for name in names:
            which = [entry[0] for entry in DEC_GIVEN].index(name)
            copies.start(have[name], given_out[which])

    part_ref[...] = jnp.zeros_like(part_ref)
    sums[...] = jnp.zeros_like(sums)
    bias_sum[...] = jnp.zeros_like(bias_sum)

    w_emb = weights.take()
    hat_e, spread_e = norm_parts(coded[...])
    have[K_SENT][...] = (hat_e * vec_e[4:5] + vec_e[5:6]).astype(bf16)
    give(K_SENT)
    have[K_TOKENS][:VIS] = nn(have[K_SENT][...], w_emb[...]) + extra[...] + positions_of(place[:VIS], table)

    def fill(step):
        rows = pl.ds(pl.multiple_of(VIS + step * VIS, VIS), VIS)
        have[K_TOKENS][rows] = vec_d[10:11] + positions_of(place[rows], table)

    loop(SEQ // VIS - 1, fill)
    w_qkv = weights.take()
    over_blocks(
        SEQ, blk, lambda *refs: open_stage(*refs, vec_d, w_qkv), *[have[name] for name in (K_TOKENS, K_NORMED, K_JOINED)]
    )
    give(K_NORMED)
    attend_stage(have[K_JOINED], have[K_OUT], have[K_LSE], DD // HEADS_DEC)
    wo, w1, w2 = weights.take(), weights.take(), weights.take()
    keys = [K_TOKENS, K_OUT, K_ATTENDED, K_MIDDLE, K_SECOND, K_ACTIVE, K_SLOPE, K_GRAD]
    over_blocks(SEQ, blk, lambda *refs: close_stage(*refs, vec_d, bias, wo, w1, w2), *[have[name] for name in keys])
    give(K_ATTENDED, K_SECOND, K_ACTIVE)

    w_head = weights.take()
    count = count_ref[...]

    def head(step):
        rows = pl.ds(pl.multiple_of(VIS + step * VIS, VIS), VIS)
        late = rows_at(step, VIS)
        hat, spread = norm_parts(have[K_GRAD][rows])
        final = (hat * vec_d[4:5] + vec_d[5:6]).astype(bf16)
        have[K_FINAL][late] = final
        residual = nt(final, w_head[...]) - target[late].astype(f32)
        weight = mask[late]
        loss = jnp.sum(weight * jnp.mean(residual * residual, axis=1, keepdims=True), axis=0, keepdims=True) / count
        row = tail_row + VEC_TILES * RANK
        part_ref[row : row + RANK] += jnp.broadcast_to(loss, (RANK, LANES))
        b_pred = (weight * (2.0 * residual / PATCH) / count).astype(bf16)
        have[K_B_PRED][late] = b_pred
        grad = nn(b_pred, w_head[...])
        have[K_GRAD][rows] = norm_back(grad, hat, spread, vec_d[4:5])
        sums[4:5] += column_sum(grad * hat)
        sums[5:6] += column_sum(grad)

    loop(SEQ // VIS - 1, head)
    have[K_GRAD][:VIS] = jnp.zeros((VIS, DD), f32)
    give(K_FINAL, K_B_PRED)

    keys = [K_GRAD, K_SLOPE, K_MIDDLE, K_B_DOWN, K_B_UP, K_B_PROJ, K_ATT]
    over_blocks(
        SEQ, blk, lambda *refs: back_up_stage(*refs, total, vec_d, wo, w1, w2, sums, bias_sum), *[have[name] for name in keys]
    )
    give(K_B_DOWN, K_B_UP, K_B_PROJ)
    attend_back_stage(
        have[K_JOINED], have[K_ATT], have[K_OUT], have[K_LSE], have[K_B_QKV], have[K_DK], have[K_DV], DD // HEADS_DEC
    )
    give(K_B_QKV)
    over_blocks(
        SEQ, blk, lambda *refs: back_in_stage(*refs, vec_d, w_qkv, sums), *[have[name] for name in (K_B_QKV, K_GRAD, K_TOKENS)]
    )
    first = have[K_GRAD][:VIS].astype(bf16)
    have[K_FIRST][...] = first
    give(K_FIRST)
    sums[10:11] = column_sum(have[K_GRAD][VIS:])
    back = nt(first, w_emb[...]).astype(bf16).astype(f32)
    grad_coded[...] = norm_back(back, hat_e, spread_e, vec_e[4:5])
    sums_e[...] = jnp.zeros_like(sums_e)
    sums_e[0:1] = column_sum(back * hat_e)
    sums_e[1:2] = column_sum(back)
    for line in range(11):
        put_vec(part_ref, tail_row, line * DD, sums[line : line + 1])
    put_vec(part_ref, tail_row, 11 * DD, bias_sum[...])
    put_vec(part_ref, tail_row, 11 * DD + FFD, column_sum(first))
    pairs = [(K_NORMED, K_B_QKV), (K_ATTENDED, K_B_PROJ), (K_SECOND, K_B_UP), (K_ACTIVE, K_B_DOWN), (K_B_PRED, K_FINAL), (K_SENT, K_FIRST)]
    for index, (a, b) in enumerate(pairs):
        put_left(part_ref, 1, index, factor, have[b], have[a], gain)
    for copy in copies.made:
        copy.wait()


def decode(flat, coded, place, table, vecs, target, mask, count, factor, tail_row, gain, rows):
    mats = section_shapes(1)
    dma = pltpu.SemaphoreType.DMA
    outs = pl.pallas_call(
        functools.partial(decode_body, tail_row=tail_row, gain=gain),
        in_specs=[ANYWHERE] + [WHOLE] * 8,
        out_specs=[ANYWHERE] * len(DEC_GIVEN) + [WHOLE] * 3,
        out_shape=[jax.ShapeDtypeStruct(shape, kind) for name, shape, kind in DEC_GIVEN]
        + [shape_of(VIS, DE), shape_of(8, DE), shape_of(rows, LANES)],
        scratch_shapes=[pltpu.VMEM(shape, kind) for name, shape, kind in DEC_GIVEN + DEC_HELD]
        + [pltpu.VMEM(shape, bf16) for shape in mats]
        + [
            pltpu.VMEM((2, flat_count(1), LANES), bf16), pltpu.VMEM((64 * FFD // LANES, LANES), f32),
            pltpu.VMEM((DEC_ROWS, DD), f32), pltpu.VMEM((16, DE), f32), pltpu.VMEM((1, FFE), f32), pltpu.VMEM((16, DD), f32),
            pltpu.VMEM((1, FFD), f32), pltpu.VMEM((1, DD), f32), dma((len(mats),)), dma((len(DEC_GIVEN),)),
        ],
        compiler_params=pltpu.CompilerParams(vmem_limit_bytes=BIG),
        name="decode",
    )(flat, coded, place, table, vecs, target, mask, count, factor)
    given = dict(zip([name for name, shape, kind in DEC_GIVEN], outs))
    return given, outs[-3], outs[-2], outs[-1]


ENC_GIVEN = [
    (K_B_QKV, (VIS, 3 * DE), bf16), (K_B_PROJ, (VIS, DE), bf16), (K_B_UP, (VIS, FFE), bf16), (K_B_DOWN, (VIS, DE), bf16),
    (K_START, (VIS, DE), bf16),
]
ENC_HELD = [
    (K_ATT, (VIS, DE), bf16), (K_DK, (VIS, LANES), f32), (K_DV, (VIS, LANES), f32), (K_SUMS, (16, DE), f32), (K_BIAS, (1, FFE), f32),
]
ENC_USED = [K_SLOPE, K_MIDDLE, K_JOINED, K_OUT, K_LSE, K_TOKENS, K_SECOND, K_ACTIVE, K_ATTENDED, K_NORMED]


def encode_back_body(*refs, tail_row, gain):
    used_n, given_n, held_n = len(ENC_USED), len(ENC_GIVEN), len(ENC_HELD)
    kept_in, mats_in, refs = refs[:used_n], refs[used_n : used_n + 4], refs[used_n + 4 :]
    grad_in, sums_e, vec_ref, pix, factor = refs[:5]
    given_out, part_ref, refs = refs[5 : 5 + given_n], refs[5 + given_n], refs[6 + given_n :]
    have = dict(zip(ENC_USED, refs[:used_n]))
    refs = refs[used_n:]
    have.update(zip([name for name, shape, kind in ENC_GIVEN + ENC_HELD], refs[: given_n + held_n]))
    mats = refs[given_n + held_n : given_n + held_n + 4]
    grad, total, vecs, bias_e, in_sems, out_sems = refs[given_n + held_n + 4 :]
    reads, copies = Copies(in_sems), Copies(out_sems)
    w2 = reads.start(mats_in[3], mats[3])
    take_rows(vec_ref, 0, DE, vecs, bias_e)
    waits = {name: reads.start(src, have[name]) for name, src in list(zip(ENC_USED, kept_in))[:2]}
    w1 = reads.start(mats_in[2], mats[2])
    wo = reads.start(mats_in[1], mats[1])
    waits.update({name: reads.start(src, have[name]) for name, src in list(zip(ENC_USED, kept_in))[2:]})
    w_qkv = reads.start(mats_in[0], mats[0])
    sums, bias_sum = have[K_SUMS], have[K_BIAS]

    def give(*names):
        for name in names:
            which = [entry[0] for entry in ENC_GIVEN].index(name)
            copies.start(have[name], given_out[which])

    part_ref[...] = jnp.zeros_like(part_ref)
    sums[...] = jnp.zeros_like(sums)
    bias_sum[...] = jnp.zeros_like(bias_sum)
    sums[4:5] = sums_e[0:1]
    sums[5:6] = sums_e[1:2]
    grad[...] = grad_in[...]
    for wait in (w2, waits[K_SLOPE], waits[K_MIDDLE], w1, wo):
        wait.wait()
    back_up_stage(
        grad, have[K_SLOPE], have[K_MIDDLE], have[K_B_DOWN], have[K_B_UP], have[K_B_PROJ], have[K_ATT], total,
        vecs, mats[1], mats[2], mats[3], sums, bias_sum,
    )
    give(K_B_DOWN, K_B_UP, K_B_PROJ)
    for name in (K_JOINED, K_OUT, K_LSE, K_TOKENS):
        waits[name].wait()
    attend_back_stage(
        have[K_JOINED], have[K_ATT], have[K_OUT], have[K_LSE], have[K_B_QKV], have[K_DK], have[K_DV], DE // HEADS_ENC
    )
    give(K_B_QKV)
    w_qkv.wait()
    back_in_stage(have[K_B_QKV], grad, have[K_TOKENS], vecs, mats[0], sums)
    start = grad[...].astype(bf16)
    have[K_START][...] = start
    give(K_START)
    sums[10:11] = column_sum(start)
    for line in range(11):
        put_vec(part_ref, tail_row, line * DE, sums[line : line + 1])
    put_vec(part_ref, tail_row, 11 * DE, bias_sum[...])
    for name in (K_SECOND, K_ACTIVE, K_ATTENDED, K_NORMED):
        waits[name].wait()
    pairs = [(K_NORMED, K_B_QKV), (K_ATTENDED, K_B_PROJ), (K_SECOND, K_B_UP), (K_ACTIVE, K_B_DOWN)]
    for index, (a, b) in enumerate(pairs):
        put_left(part_ref, 0, index, factor, have[b], have[a], gain)
    put_left(part_ref, 0, 4, factor, have[K_START], pix, gain)
    for copy in copies.made:
        copy.wait()


def encode_back(kept, mats, grad_coded, sums_e, vecs, pix, factor, tail_row, gain, rows):
    shapes = {name: (shape, kind) for name, shape, kind in ENC_KEPT}
    dma = pltpu.SemaphoreType.DMA
    outs = pl.pallas_call(
        functools.partial(encode_back_body, tail_row=tail_row, gain=gain),
        in_specs=[ANYWHERE] * (len(ENC_USED) + 4) + [WHOLE] * 5,
        out_specs=[ANYWHERE] * len(ENC_GIVEN) + [WHOLE],
        out_shape=[jax.ShapeDtypeStruct(shape, kind) for name, shape, kind in ENC_GIVEN] + [shape_of(rows, LANES)],
        scratch_shapes=[pltpu.VMEM(*shapes[name]) for name in ENC_USED]
        + [pltpu.VMEM(shape, kind) for name, shape, kind in ENC_GIVEN + ENC_HELD]
        + [pltpu.VMEM(shape, bf16) for shape in section_shapes(0)[:4]]
        + [
            pltpu.VMEM((VIS, DE), f32), pltpu.VMEM((VIS, DE), f32), pltpu.VMEM((16, DE), f32), pltpu.VMEM((1, FFE), f32),
            dma((len(ENC_USED) + 4,)), dma((len(ENC_GIVEN),)),
        ],
        compiler_params=pltpu.CompilerParams(vmem_limit_bytes=BIG),
        name="encode_back",
    )(*[kept[name] for name in ENC_USED], *mats[:4], grad_coded, sums_e, vecs, pix, factor)
    return dict(zip([name for name, shape, kind in ENC_GIVEN], outs)), outs[-1]


def tiles_of(width):
    return -(-width // LANES)


def spans(which):
    at, found = [], []
    for section in range(2):
        start = 0
        for shape in section_shapes(section):
            found.append((section, start, shape[which]))
            start += tiles_of(shape[which]) * LANES
        at.append(start)
    return found, at


ROW_SPANS, ROW_WIDTHS = spans(0)
COL_SPANS, COL_WIDTHS = spans(1)
ROW_PAD = max(ROW_WIDTHS)
VEC_TILES = -(-VLEN // (RANK * LANES))


def sum_rows(replicas, tiles):
    return -(-tiles // replicas) * replicas * RANK


def put_tiles(out_ref, section, start, value):
    width = value.shape[1]
    for tile in range(tiles_of(width)):
        here = min(LANES, width - tile * LANES)
        row = (start // LANES + tile) * RANK
        out_ref[section, row : row + RANK, :here] = value[:, tile * LANES : tile * LANES + here]


def chunk_rows(rows_n, cols_n):
    if rows_n == PATCH:
        return PATCH
    return 256


def err_prep_body(e_ref, x_ref, *rest, blocks, rows):
    out_ref, left_ref, wide = rest[-3:]
    wide[...] = e_ref[0].reshape(rows * blocks, LANES).astype(f32)
    pieces = split3(x_ref[...])
    total = jnp.zeros((rows, 3 * RANK), f32)
    for block in range(blocks):
        part = wide[pl.ds(block, rows, stride=blocks), :].astype(bf16)
        out_ref[block * rows : (block + 1) * rows, :] = part
        total = total + nt(part, pieces[:, block * LANES : (block + 1) * LANES])
    value = join3(total.T)
    left_ref[...] = jnp.zeros_like(left_ref)
    for tile in range(tiles_of(rows)):
        here = min(LANES, rows - tile * LANES)
        left_ref[tile * RANK : (tile + 1) * RANK, :here] = value[:, tile * LANES : tile * LANES + here]


def err_prep(errors, factor, start, rows_n, cols_n, buf):
    blocks = cols_n // LANES
    rows = chunk_rows(rows_n, cols_n)
    step = rows * blocks
    steps = rows_n // rows
    tiles = tiles_of(rows)
    in_specs = [
        pl.BlockSpec((pl.Element(1), pl.Element(1), pl.Element(step * LANES)), lambda i: (0, 0, pl.multiple_of(start + i * step * LANES, 1024))),
        pl.BlockSpec((RANK, cols_n), lambda i: (0, 0)),
    ]
    args = [errors, factor]
    aliases = {}
    if buf is not None:
        in_specs.append(pl.BlockSpec(memory_space=pl.ANY))
        args.append(buf)
        aliases = {2: 0}
    return pl.pallas_call(
        functools.partial(err_prep_body, blocks=blocks, rows=rows),
        grid=(steps,),
        in_specs=in_specs,
        out_specs=[
            pl.BlockSpec((pl.Element(step), pl.Element(LANES)), lambda i: (pl.multiple_of(start // LANES + i * step, 16), 0)),
            pl.BlockSpec((tiles * RANK, LANES), lambda i: (i, 0)),
        ],
        out_shape=[
            jax.ShapeDtypeStruct((FLAT // LANES, LANES), bf16),
            jax.ShapeDtypeStruct((steps * tiles * RANK, LANES), f32),
        ],
        input_output_aliases=aliases,
        scratch_shapes=[pltpu.VMEM((step, LANES), f32)],
        name="err_prep",
    )(*args)


def ortho_stage(sum_ref, out_ref, wide, scale):
    rank_id = lax.broadcasted_iota(jnp.int32, (RANK, 1), 0)
    for section, start, width in ROW_SPANS:
        padded = tiles_of(width) * LANES
        for tile in range(padded // LANES):
            row = (start // LANES + tile) * RANK
            wide[:, tile * LANES : (tile + 1) * LANES] = sum_ref[section, row : row + RANK] * scale
        basis = wide[:, :padded]
        for column in range(RANK):
            current = basis[column : column + 1]
            current = current * lax.rsqrt(jnp.sum(current * current, axis=1, keepdims=True) + 1e-12)
            dots = jnp.sum(basis * current, axis=1, keepdims=True)
            basis = jnp.where(
                rank_id > column, basis - dots * current, jnp.where(rank_id == column, current, basis)
            )
        out_ref[section, :, start : start + padded] = basis


def err_plan(section):
    plan = []
    start = 0
    spans = [(row, col) for row, col in zip(ROW_SPANS, COL_SPANS) if row[0] == section]
    for (rows_n, cols_n), (row_span, col_span) in zip(section_shapes(section), spans):
        rows = chunk_rows(rows_n, cols_n)
        blocks = cols_n // LANES
        for chunk in range(rows_n // rows):
            plan.append((start // LANES + chunk * rows * blocks, rows, blocks, row_span[1] + chunk * rows, col_span[1], chunk))
        start += rows_n * cols_n
    return plan


def put_tiles(out_ref, row, value):
    for tile in range(value.shape[1] // LANES):
        out_ref[row + tile * RANK : row + (tile + 1) * RANK] = value[:, tile * LANES : (tile + 1) * LANES]


def rights_body(*refs, n, scale, gain):
    sum_ref, err_ref, u_in, v_in = refs[0], refs[1], refs[2 : 2 + n], refs[2 + n : 2 + 2 * n]
    ortho_ref, part_ref, extra_ref = refs[2 + 2 * n : 5 + 2 * n]
    refs = refs[5 + 2 * n :]
    u_refs, v_refs = refs[:n], refs[n : 2 * n]
    wide, ring, ring_sems, in_sems = refs[2 * n :]
    section = lax.axis_index(SEC)
    depth = ring.shape[0]
    plans = [err_plan(which) for which in range(2)]

    def fetch(plan, index):
        at, rows, blocks = plan[index][:3]
        slot = index % depth
        return pltpu.make_async_copy(
            err_ref.at[pl.ds(at, rows * blocks)], ring.at[slot, pl.ds(0, rows * blocks)], ring_sems.at[slot]
        )

    for which, plan in enumerate(plans):

        @pl.when(section == which)
        def _():
            for index in range(depth - 1):
                fetch(plan, index).start()

    reads = Copies(in_sems)
    waits = [(reads.start(u_in[i], u_refs[i]), reads.start(v_in[i], v_refs[i])) for i in range(n)]
    ortho_stage(sum_ref, ortho_ref, wide, scale)
    extra_ref[...] = jnp.zeros_like(extra_ref)
    part_ref[...] = jnp.zeros_like(part_ref)
    for which, plan in enumerate(plans):

        @pl.when(section == which)
        def _():
            for index, (at, rows, blocks, row_at, col_at, chunk) in enumerate(plan):
                if index + depth - 1 < len(plan):
                    fetch(plan, index + depth - 1).start()
                fetch(plan, index).wait()
                pieces = split3(ortho_ref[which, :, row_at : row_at + rows])
                for block in range(0, blocks, 2):
                    pair = [ring[index % depth, (block + side) * rows : (block + side + 1) * rows] for side in range(2)]
                    part = join3(nn(pieces, jnp.concatenate(pair, axis=1)))
                    row = (col_at // LANES + block) * RANK
                    if chunk == 0:
                        put_tiles(extra_ref, row, part)
                    else:
                        for side in range(2):
                            extra_ref[row + side * RANK : row + (side + 1) * RANK] += part[:, side * LANES : (side + 1) * LANES]

    for (wait_u, wait_v), u_ref, v_ref, (which, row_at, rows), (unused, col_at, cols) in zip(waits, u_refs, v_refs, ROW_SPANS, COL_SPANS):
        wait_u.wait()
        wait_v.wait()
        part = join3(nt(split3(ortho_ref[which, :, row_at : row_at + rows]), u_ref[...]))
        put_tiles(part_ref.at[which], col_at // LANES * RANK, gain * join3(nn(split3(part), v_ref[...])))


def rights(sums, err, us, vs, scale, gain, rows):
    n = len(us)
    most = max(chunk_rows(*shape) * shape[1] // LANES for which in range(2) for shape in section_shapes(which))
    dma = pltpu.SemaphoreType.DMA
    return pl.pallas_call(
        functools.partial(rights_body, n=n, scale=scale, gain=gain),
        in_specs=[WHOLE] + [ANYWHERE] * (2 * n + 1),
        out_specs=[WHOLE] * 3,
        out_shape=[
            jax.ShapeDtypeStruct((2, RANK, ROW_PAD), f32), jax.ShapeDtypeStruct((2, rows, LANES), f32), shape_of(rows, LANES)
        ],
        scratch_shapes=[pltpu.VMEM(x.shape, bf16) for x in [*us, *vs]]
        + [pltpu.VMEM((RANK, FFE), f32), pltpu.VMEM((4, most, LANES), bf16), dma((4,)), dma((2 * n,))],
        compiler_params=pltpu.CompilerParams(vmem_limit_bytes=BIG),
        name="rights",
    )(sums, err, *us, *vs)


def final_right_body(sum_ref, ortho_ref, vec_ref, right_ref, norm_ref, *, scale):
    squares = jnp.sum(vec_ref[...] * vec_ref[...], keepdims=True)[0]
    for (section, start, width), (unused, row_at, row_width) in zip(COL_SPANS, ROW_SPANS):
        for tile in range(width // LANES):
            row = (start // LANES + tile) * RANK
            right_ref[section, :, start + tile * LANES : start + (tile + 1) * LANES] = sum_ref[section, row : row + RANK] * scale
        o_part = ortho_ref[section, :, row_at : row_at + tiles_of(row_width) * LANES]
        r_part = right_ref[section, :, start : start + width]
        for line in range(RANK):
            gram_o = jnp.sum(o_part * o_part[line : line + 1], axis=1, keepdims=True)
            gram_r = jnp.sum(r_part * r_part[line : line + 1], axis=1, keepdims=True)
            squares = squares + jnp.sum(gram_o * gram_r, keepdims=True)
    for section in range(2):
        used = COL_WIDTHS[section]
        if used < right_ref.shape[2]:
            right_ref[section, :, used:] = jnp.zeros((RANK, right_ref.shape[2] - used), f32)
    norm_ref[...] = jnp.broadcast_to(jnp.sqrt(squares), norm_ref.shape)


def final_right(sums, ortho, vecs, cols, scale):
    full = pl.BlockSpec(memory_space=pltpu.VMEM)
    return pl.pallas_call(
        functools.partial(final_right_body, scale=scale),
        in_specs=[full] * 3,
        out_specs=[full] * 2,
        out_shape=[jax.ShapeDtypeStruct((2, RANK, cols), f32), jax.ShapeDtypeStruct((1, LANES), f32)],
        name="final_right",
    )(sums, ortho, vecs)


def finish_body(me_ref, a0, a1, b0, b1, e_ref, o_ref, r_ref, *rest, rows, blocks, gain, start, shard):
    err_out, app_out = rest[-2:]
    o_part = o_ref[0]
    o_high = o_part.astype(bf16)
    o_low = (o_part - o_high.astype(f32)).astype(bf16)
    left_t = jnp.concatenate([o_high, o_low, o_high], axis=0).T[:rows]
    lhs0 = a0[...].T
    lhs1 = a1[...].T
    err_rows = err_out.at[0].reshape(rows * blocks, LANES)
    keep = overlaps(pl.program_id(0), me_ref[0], start, rows * blocks, shard)
    for pair in range(blocks // 2):
        cols = slice(pair * 2 * LANES, (pair + 1) * 2 * LANES)
        r_part = r_ref[0, :, cols]
        r_high = r_part.astype(bf16)
        r_low = (r_part - r_high.astype(f32)).astype(bf16)
        approx = nn(left_t, jnp.concatenate([r_high, r_high, r_low], axis=0))
        grad = nn(lhs0, b0[:, cols]) + nn(lhs1, b1[:, cols])
        for side in range(2):
            block = pair * 2 + side
            half = slice(side * LANES, (side + 1) * LANES)
            err_rows[pl.ds(block, rows, stride=blocks), :] = (
                gain * grad[:, half] + e_ref[block * rows : (block + 1) * rows].astype(f32)
            ) - approx[:, half]

            @pl.when(keep)
            def _():
                app_out[pl.ds(block, rows, stride=blocks), :] = approx[:, half]


def overlaps(i, me, start, step, shard):
    first = start + i * step * LANES
    return (first < (me + 1) * shard) & (first + step * LANES > me * shard)


def finish(me, pair0, pair1, err, ortho, right, section, row_at, col_at, start, gain, shard, bufs):
    a0, b0 = pair0
    a1, b1 = pair1
    rows_n, cols_n = a0.shape[1], b0.shape[1]
    seq = a0.shape[0]
    blocks = cols_n // LANES
    rows = chunk_rows(rows_n, cols_n)
    step = rows * blocks
    flat_rows = FLAT // LANES
    whole = lambda i, me: (0, 0)
    flat_at = lambda i: pl.multiple_of(start // LANES + i * step, 16)
    wide_rows = tiles_of(rows) * LANES

    def shard_at(i, me):
        return pl.multiple_of(jnp.where(overlaps(i, me[0], start, step, shard), start // LANES + i * step, flat_rows), 8), 0

    in_specs = [
        pl.BlockSpec((seq, rows), lambda i, me: (0, i)),
        pl.BlockSpec((seq, rows), lambda i, me: (0, i)),
        pl.BlockSpec((seq, cols_n), whole, pipeline_mode=pl.Buffered(1)),
        pl.BlockSpec((seq, cols_n), whole, pipeline_mode=pl.Buffered(1)),
        pl.BlockSpec((pl.Element(step), pl.Element(LANES)), lambda i, me: (flat_at(i), 0)),
        pl.BlockSpec((1, RANK, wide_rows), lambda i, me: (section, 0, row_at // wide_rows + i)),
        pl.BlockSpec(
            (pl.Element(1), pl.Element(RANK), pl.Element(cols_n)), lambda i, me: (section, 0, col_at), pipeline_mode=pl.Buffered(1)
        ),
    ]
    assert row_at % wide_rows == 0
    args = [a0, a1, b0, b1, err, ortho, right]
    aliases = {}
    if bufs is not None:
        in_specs += [pl.BlockSpec(memory_space=pl.ANY)] * 2
        args += list(bufs)
        aliases = {8: 0, 9: 1}
    return pl.pallas_call(
        functools.partial(finish_body, rows=rows, blocks=blocks, gain=gain, start=start, shard=shard),
        grid_spec=pltpu.PrefetchScalarGridSpec(
            num_scalar_prefetch=1,
            grid=(rows_n // rows,),
            in_specs=in_specs,
            out_specs=[
                pl.BlockSpec(
                    (pl.Element(1), pl.Element(1), pl.Element(step * LANES)),
                    lambda i, me: (0, 0, pl.multiple_of(start + i * step * LANES, 1024)),
                ),
                pl.BlockSpec((pl.Element(step), pl.Element(LANES)), shard_at),
            ],
        ),
        out_shape=[
            jax.ShapeDtypeStruct((1, 1, FLAT), f32),
            jax.ShapeDtypeStruct((flat_rows + SPARE, LANES), f32),
        ],
        input_output_aliases=aliases,
        compiler_params=pltpu.CompilerParams(vmem_limit_bytes=BIG),
        name="finish",
    )(me, *args)


def tail_body(e_ref, buf0, err_out):
    err_out[...] = e_ref[...].astype(f32)


def finish_tail(errors, start, buf):
    count = FLAT - start
    steps = 6
    step = count // steps
    assert step * steps == count and step % 1024 == 0
    spec = pl.BlockSpec((pl.Element(1), pl.Element(1), pl.Element(step)), lambda i: (0, 0, pl.multiple_of(start + i * step, 1024)))
    return pl.pallas_call(
        tail_body,
        grid=(steps,),
        in_specs=[spec, pl.BlockSpec(memory_space=pl.ANY)],
        out_specs=spec,
        out_shape=jax.ShapeDtypeStruct((1, 1, FLAT), f32),
        input_output_aliases={1: 0},
        compiler_params=pltpu.CompilerParams(vmem_limit_bytes=BIG),
        name="finish_tail",
    )(errors, buf)


MESH = pl.DeviceIdType.MESH


def grid_of(replicas):
    side = 2 if replicas < 64 else 4
    return replicas // (side * side), side, side


def used_rows(section):
    counts = [sum(rows * cols for rows, cols in section_shapes(s)) // LANES for s in range(2)]
    return jnp.where(section == 0, counts[0], counts[1])


def meet(replicas):
    section, me = lax.axis_index(SEC), lax.axis_index(DP)
    barrier = pltpu.get_barrier_semaphore()
    pl.semaphore_signal(barrier, inc=1, device_id={SEC: 1 - section}, device_id_type=MESH)
    for step in range(1, replicas):
        pl.semaphore_signal(
            barrier, inc=1, device_id={DP: lax.rem(me + step, replicas)}, device_id_type=MESH
        )
    pl.semaphore_wait(barrier, replicas)


def gather_body(
    low_ref, cnt_ref, vec_ref, fac_ref, flat_ref, cnts_ref, vec2_ref, fac2_ref,
    send_sem, recv_sem, swap_sem, cnt_send, cnt_recv, side_send, side_recv, own_sem, *, replicas, size,
):
    section, me = lax.axis_index(SEC), lax.axis_index(DP)
    other = 1 - section
    nz, ny, nx = grid_of(replicas)
    x, y, z = lax.rem(me, nx), lax.rem(me // nx, ny), me // (nx * ny)
    cut = size // 2 // 8 * 8 if size % 8 == 0 else size
    halves = [(0, cut), (cut, size - cut)] if cut < size else [(0, cut)]
    used = used_rows(section)
    used_other = used_rows(other)

    def block_id(at_z, at_y, at_x):
        return (at_z * ny + at_y) * nx + at_x

    meet(replicas)

    def side(src, dst, slot):
        return pltpu.make_async_remote_copy(
            src_ref=src, dst_ref=dst.at[section], send_sem=side_send.at[slot], recv_sem=side_recv.at[slot],
            device_id={SEC: other}, device_id_type=MESH,
        )

    def count_copy(step):
        return pltpu.make_async_remote_copy(
            src_ref=cnt_ref, dst_ref=cnts_ref.at[me], send_sem=cnt_send.at[step],
            recv_sem=cnt_recv.at[step], device_id={DP: lax.rem(me + step, replicas)}, device_id_type=MESH,
        )

    for step in range(1, replicas):
        count_copy(step).start()
    side(vec_ref, vec2_ref, 0).start()
    side(fac_ref, fac2_ref, 1).start()
    own = pltpu.make_async_copy(low_ref, flat_ref.at[section * replicas + me], own_sem)
    own.start()

    def copy(block, half, target, way, mine=False, swap=False):
        start, rows = halves[half]
        at = flat_ref.at[section * replicas + block, pl.ds(start, rows)]
        src = low_ref.at[pl.ds(start, rows)] if mine else at
        return pltpu.make_async_remote_copy(
            src_ref=src, dst_ref=at, send_sem=send_sem.at[block, half, way],
            recv_sem=(swap_sem if swap else recv_sem).at[block, half], device_id=target, device_id_type=MESH,
        )

    def needed(block, half, limit):
        return block * size + halves[half][0] < limit

    def at_z(value):
        return {DP: block_id(value, y, x)}

    def along_x(block, half, mine=False):
        for step in range(1, nx):
            copy(block, half, {DP: block_id(z, y, lax.rem(x + step, nx))}, 1 + step, mine).start()

    def along_y(block, half, mine=False):
        for step in range(1, ny):
            copy(block, half, {DP: block_id(z, lax.rem(y + step, ny), x)}, nx + step, mine).start()

    def across(block, half, mine=False):
        copy(block, half, {SEC: other}, nx + ny, mine, True).start()

    def arrived(block, half):
        copy(block, half, {SEC: other}, 0).wait_recv()

    def layers(k):
        return [z] if k == 0 else [z - k, z + k]

    def valid(at):
        return (at >= 0) & (at < nz)

    def first(k):
        for which, layer in enumerate(layers(k)):
            block = block_id(layer, y, x)
            for half in range(len(halves)):

                @pl.when(valid(layer) & needed(block, half, used))
                def _():
                    if k > 0:
                        arrived(block, half)
                    mine = k == 0
                    if k == 0 or which == 0:

                        @pl.when(z + 1 < nz)
                        def _():
                            copy(block, half, at_z(z + 1), 0, mine).start()

                    if k == 0 or which == 1:

                        @pl.when(z > 0)
                        def _():
                            copy(block, half, at_z(z - 1), 1, mine).start()

                    if half == 0:
                        along_x(block, half, mine)
                        along_y(block, half, mine)
                    else:
                        along_y(block, half, mine)
                        along_x(block, half, mine)
                    across(block, half, mine)

    def second(k):
        for layer in layers(k):
            for half in range(len(halves)):
                for step in range(1, nx if half == 0 else ny):
                    if half == 0:
                        block = block_id(layer, y, lax.rem(x + step, nx))
                    else:
                        block = block_id(layer, lax.rem(y + step, ny), x)

                    @pl.when(valid(layer) & needed(block, half, used))
                    def _():
                        arrived(block, half)
                        if half == 0:
                            along_y(block, half)
                        else:
                            along_x(block, half)
                        across(block, half)

    def third(k):
        for layer in layers(k):
            for half in range(len(halves)):
                for far in range(1, ny if half == 0 else nx):
                    for near in range(nx if half == 0 else ny):
                        if half == 0:
                            block = block_id(layer, lax.rem(y + far, ny), lax.rem(x + near, nx))
                        else:
                            block = block_id(layer, lax.rem(y + near, ny), lax.rem(x + far, nx))

                        @pl.when(valid(layer) & needed(block, half, used))
                        def _():
                            arrived(block, half)
                            across(block, half)

    for k in range(nz + 2):
        if k < nz:
            first(k)
        if 0 <= k - 1 < nz:
            second(k - 1)
        if 0 <= k - 2 < nz:
            third(k - 2)

    def drain(block, carry):
        at_x_, at_y_, at_z_ = lax.rem(block, nx), lax.rem(block // nx, ny), block // (nx * ny)
        for half in range(len(halves)):
            column = (at_x_ == x) & (at_y_ == y)

            @pl.when(needed(block, half, used))
            def _():
                @pl.when(column & (at_z_ <= z) & (z + 1 < nz))
                def _():
                    copy(block, half, {SEC: other}, 0).wait_send()

                @pl.when(column & (at_z_ >= z) & (z > 0))
                def _():
                    copy(block, half, {SEC: other}, 1).wait_send()

                single = len(halves) == 1
                sent_x = (column if half == 0 else at_x_ == x)
                sent_y = (at_y_ == y) if half == 0 else column

                @pl.when(sent_x)
                def _():
                    for step in range(1, nx):
                        copy(block, half, {SEC: other}, 1 + step).wait_send()

                @pl.when(sent_y)
                def _():
                    for step in range(1, ny):
                        copy(block, half, {SEC: other}, nx + step).wait_send()

                copy(block, half, {SEC: other}, nx + ny).wait_send()

            @pl.when(needed(block, half, used_other))
            def _():
                copy(block, half, {SEC: other}, 0, False, True).wait_recv()

        return carry

    lax.fori_loop(0, replicas, drain, 0)
    own.wait()
    for step in range(1, replicas):
        count_copy(step).wait()
    cnts_ref[me] = cnt_ref[...]
    vec2_ref[section] = vec_ref[...]
    fac2_ref[section] = fac_ref[...]
    side(vec_ref, vec2_ref, 0).wait()
    side(fac_ref, fac2_ref, 1).wait()


def update_body(master_ref, moment_ref, approx_ref, scale_ref, master_out, low_out, moment_out):
    moment = moment_decay * moment_ref[...] + scale_ref[...] * approx_ref[...].reshape(moment_ref.shape)
    moment_out[...] = moment
    master = master_ref[...] - learning_rate() * moment
    master_out[...] = master
    low_out[...] = master.astype(bf16)


def update(master, moment, approx, scale):
    full = pl.BlockSpec(memory_space=pltpu.VMEM)
    return pl.pallas_call(
        update_body,
        in_specs=[full] * 4,
        out_specs=[full] * 3,
        out_shape=[
            jax.ShapeDtypeStruct(master.shape, f32), jax.ShapeDtypeStruct(master.shape, bf16),
            jax.ShapeDtypeStruct(master.shape, f32),
        ],
        name="update",
    )(master, moment, approx, scale)


def cast_body(src_ref, out_ref):
    out_ref[...] = src_ref[...].reshape(out_ref.shape).astype(bf16)


def cast_shard(master, size):
    full = pl.BlockSpec(memory_space=pltpu.VMEM)
    return pl.pallas_call(
        cast_body, in_specs=[full], out_specs=full, out_shape=jax.ShapeDtypeStruct((size, LANES), bf16), name="cast"
    )(master)


def gather(low, cnt, vec, fac, replicas):
    size = low.shape[0]
    vmem = pl.BlockSpec(memory_space=pltpu.VMEM)
    nz, ny, nx = grid_of(replicas)
    dma = pltpu.SemaphoreType.DMA
    return pl.pallas_call(
        functools.partial(gather_body, replicas=replicas, size=size),
        in_specs=[vmem] * 4,
        out_specs=[pl.BlockSpec(memory_space=pl.ANY), vmem, vmem, vmem],
        out_shape=[
            jax.ShapeDtypeStruct((2 * replicas, size, LANES), bf16),
            jax.ShapeDtypeStruct((replicas,) + cnt.shape, f32),
            jax.ShapeDtypeStruct((2,) + vec.shape, f32),
            jax.ShapeDtypeStruct((2,) + fac.shape, f32),
        ],
        scratch_shapes=[
            dma((replicas, 2, nx + ny + 1)), dma((replicas, 2)), dma((replicas, 2)),
            dma((replicas,)), dma((replicas,)), dma((2,)), dma((2,)), dma(()),
        ],
        compiler_params=pltpu.CompilerParams(collective_id=2, has_side_effects=True),
        name="gather",
    )(low, cnt, vec, fac)


def sum_body(*refs, replicas, n_enc, n_dec):
    n = n_enc + n_dec
    sum_run(*refs[:2], refs[2 : 2 + n], refs[2 + n], refs[3 + n : 3 + 2 * n], *refs[3 + 2 * n :], replicas=replicas, n_enc=n_enc)


def sum_run(
    part_ref, extra_ref, given, total_ref, taken, mine, came, slots, seg, swap_send, swap_recv, send_a, recv_a, send_b, recv_b,
    give_sem, take_sem, *, replicas, n_enc,
):
    section, me = lax.axis_index(SEC), lax.axis_index(DP)
    other = 1 - section
    rows = part_ref.shape[1]
    size = rows // replicas
    meet(replicas)

    def rows_of(index):
        return pl.ds(pl.multiple_of(index * size, 8), size)

    swap = pltpu.make_async_remote_copy(
        src_ref=part_ref.at[other], dst_ref=came, send_sem=swap_send.at[0], recv_sem=swap_recv.at[0],
        device_id={SEC: other}, device_id_type=MESH,
    )
    swap.start()
    mine[...] = part_ref[section] + extra_ref[...]
    swap.wait()

    def give(i):
        return pltpu.make_async_remote_copy(
            src_ref=given[i], dst_ref=taken[i], send_sem=give_sem.at[i], recv_sem=take_sem.at[i],
            device_id={SEC: other}, device_id_type=MESH,
        )

    n = len(given)
    for i in range(n):

        @pl.when(section == (1 if i < n_enc else 0))
        def _():
            give(i).start()

    mine[...] = mine[...] + came[...]

    def scatter(step):
        peer = lax.rem(me + step, replicas)
        return pltpu.make_async_remote_copy(
            src_ref=mine.at[rows_of(peer)], dst_ref=slots.at[step], send_sem=send_a.at[step],
            recv_sem=recv_a.at[step], device_id={DP: peer}, device_id_type=MESH,
        )

    def spread(step):
        peer = lax.rem(me + step, replicas)
        return pltpu.make_async_remote_copy(
            src_ref=seg, dst_ref=total_ref.at[section, rows_of(me)], send_sem=send_b.at[step],
            recv_sem=recv_b.at[step], device_id={DP: peer}, device_id_type=MESH,
        )

    for step in range(1, replicas):
        scatter(step).start()
    total = mine[rows_of(me), :]
    for step in range(1, replicas):
        scatter(step).wait_recv()
        total = total + slots[step]
    seg[...] = total
    for step in range(1, replicas):
        spread(step).start()
    total_ref[section, rows_of(me)] = total
    for step in range(1, replicas):
        scatter(step).wait_send()
        spread(step).wait()
    back = pltpu.make_async_remote_copy(
        src_ref=total_ref.at[section], dst_ref=total_ref.at[section], send_sem=swap_send.at[1],
        recv_sem=swap_recv.at[1], device_id={SEC: other}, device_id_type=MESH,
    )
    back.start()
    back.wait()
    for i in range(n):

        @pl.when(section == (1 if i < n_enc else 0))
        def _():
            give(i).wait_send()

        @pl.when(section == (0 if i < n_enc else 1))
        def _():
            give(i).wait_recv()


def all_sum(part, extra, replicas, collective_id, enc=(), dec=()):
    rows = part.shape[1]
    vmem = pl.BlockSpec(memory_space=pltpu.VMEM)
    dma = pltpu.SemaphoreType.DMA
    size = rows // replicas
    given = list(enc) + list(dec)
    n = len(given)
    anywhere = pl.BlockSpec(memory_space=pl.ANY)
    outs = pl.pallas_call(
        functools.partial(sum_body, replicas=replicas, n_enc=len(enc), n_dec=len(dec)),
        in_specs=[vmem, vmem] + [anywhere] * n,
        out_specs=[vmem] + [anywhere] * n,
        out_shape=[jax.ShapeDtypeStruct(part.shape, f32)] + [jax.ShapeDtypeStruct(x.shape, x.dtype) for x in given],
        scratch_shapes=[
            pltpu.VMEM((rows, LANES), f32), pltpu.VMEM((rows, LANES), f32),
            pltpu.VMEM((replicas, size, LANES), f32), pltpu.VMEM((size, LANES), f32),
            dma((2,)), dma((2,)), dma((replicas,)), dma((replicas,)), dma((replicas,)), dma((replicas,)),
            dma((max(n, 1),)), dma((max(n, 1),)),
        ],
        compiler_params=pltpu.CompilerParams(collective_id=collective_id, has_side_effects=True),
        name="all_sum",
    )(part, extra, *given)
    return outs[0], outs[1 : 1 + len(enc)], outs[1 + len(enc) :]


def local(pixels, visible, masked, loss_mask, master, momentum, vectors, vec_moment, factors, errors):
    sec = lax.axis_index(SEC)
    replicas = lax.axis_size(DP)
    replica_id = lax.axis_index(DP)

    replicas_n = replicas
    shard_len = master.shape[1]
    size = shard_len // LANES
    gain = float(replicas)

    count_tile = jnp.full((RANK, LANES), jnp.sum(loss_mask).astype(f32))
    vec_tile = jnp.pad(vectors[0], (0, VEC_TILES * RANK * LANES - VLEN)).reshape(-1, LANES)
    flat_both, counts, vec_both, fac_both = gather(
        cast_shard(master, size), count_tile, vec_tile, factors[0], replicas
    )
    low_both = flat_both.reshape(-1, LANES)
    count = jnp.sum(counts[:, 0, 0])

    vis = lax.dynamic_index_in_dim(visible, sec, 0, keepdims=False)
    mas = lax.dynamic_index_in_dim(masked, sec, 0, keepdims=False)
    mask_row = lax.dynamic_index_in_dim(loss_mask, sec, 0, keepdims=False).astype(f32)
    order = jnp.concatenate([vis, mas])
    pix = lax.dynamic_index_in_dim(pixels, sec, 0, keepdims=False)
    pick = (order[:, None] == jnp.arange(SEQ, dtype=jnp.int32)[None, :]).astype(bf16)
    pix_order = nn(pick, pix).astype(bf16)
    pix_vis = pix_order[:VIS]
    target = pix_order[VIS:]
    place = order[:, None]
    mask_col = mask_row[:, None]
    tail_row = ROW_PAD // LANES * RANK
    tail_rows = (VEC_TILES + 1) * RANK
    left_rows = sum_rows(replicas, ROW_PAD // LANES + VEC_TILES + 1)
    right_rows = sum_rows(replicas, max(COL_WIDTHS) // LANES)

    def errs_for(section):
        def run():
            buf = None
            lefts = []
            start = 0
            col_at = 0
            for rows_n, cols_n in section_shapes(section):
                buf, left = err_prep(errors, factors[0][:, col_at : col_at + cols_n], start, rows_n, cols_n, buf)
                lefts.append(left)
                start += rows_n * cols_n
                col_at += cols_n
            done = sum(left.shape[0] for left in lefts)
            lefts.append(jnp.zeros((left_rows - done, LANES), f32))
            return buf, jnp.concatenate(lefts)

        return run

    err_stack, err_lefts = lax.cond(sec == 0, errs_for(0), errs_for(1))

    kept, enc = encode(low_both, pix_vis, place[:VIS], angle_tables(DE), vec_both)
    given, grad_coded, sums_e, part_d = decode(
        low_both, kept[K_CODED], place, angle_tables(DD), vec_both, target, mask_col, count.reshape(1, 1), fac_both, tail_row, gain, left_rows,
    )
    back, part_e = encode_back(kept, enc, grad_coded, sums_e, vec_both, pix_vis, fac_both, tail_row, gain, left_rows)
    pairs_e = [
        (kept[K_NORMED], back[K_B_QKV]), (kept[K_ATTENDED], back[K_B_PROJ]), (kept[K_SECOND], back[K_B_UP]),
        (kept[K_ACTIVE], back[K_B_DOWN]), (pix_vis, back[K_START]),
    ]
    pairs_d = [
        (given[K_NORMED], given[K_B_QKV]), (given[K_ATTENDED], given[K_B_PROJ]), (given[K_SECOND], given[K_B_UP]),
        (given[K_ACTIVE], given[K_B_DOWN]), (given[K_B_PRED], given[K_FINAL]), (given[K_SENT], given[K_FIRST]),
    ]
    pairs = pairs_e + pairs_d
    n_enc = len(pairs_e)
    flat_e = [x for pair in pairs_e for x in pair]
    flat_d = [x for pair in pairs_d for x in pair]
    left_part = jnp.stack([part_e, part_d])
    early_e = [5, 6]
    late_e = [i for i in range(len(flat_e)) if i not in early_e]
    early_d = [5, 6]
    late_d = [i for i in range(len(flat_d)) if i not in early_d]
    left_sum, first_e, first_d = all_sum(
        left_part, err_lefts, replicas, 3, [flat_e[i] for i in early_e], [flat_d[i] for i in early_d]
    )
    vec_sum = left_sum[:, tail_row : tail_row + VEC_TILES * RANK]
    loss_sum = left_sum[1, tail_row + VEC_TILES * RANK, 0]

    ortho, right_part, err_rights = rights(
        left_sum, err_stack, [a for a, b in pairs], [b for a, b in pairs], 1.0 / replicas, gain, right_rows
    )
    sums, second_e, second_d = all_sum(
        right_part, err_rights, replicas, 4, [flat_e[i] for i in late_e], [flat_d[i] for i in late_d]
    )
    other_e = [x for i, x in sorted([*zip(early_e, first_e), *zip(late_e, second_e)], key=lambda entry: entry[0])]
    other_d = [x for i, x in sorted([*zip(early_d, first_d), *zip(late_d, second_d)], key=lambda entry: entry[0])]
    right_both, norm_row = final_right(sums, ortho, vec_sum, factors.shape[2], 1.0 / replicas)
    norm = norm_row[0, 0]
    scale = jnp.minimum(1.0, clip_limit / (norm + 1e-06))

    def finish_for(section):
        def run():
            mine = pairs_e if section == 0 else pairs_d
            flat = other_e if section == 0 else other_d
            theirs = [(flat[2 * i], flat[2 * i + 1]) for i in range(len(mine))]
            bufs = None
            start = 0
            base = 0 if section == 0 else n_enc
            for i, (rows_n, cols_n) in enumerate(section_shapes(section)):
                bufs = finish(
                    me_row, mine[i], theirs[i], err_stack, ortho, right_both, section,
                    ROW_SPANS[base + i][1], COL_SPANS[base + i][1], start, gain, shard_len, bufs,
                )
                start += rows_n * cols_n
            if start < FLAT:
                bufs = [finish_tail(errors, start, bufs[0]), bufs[1]]
            return bufs[0], bufs[1]

        return run

    me_row = replica_id.astype(jnp.int32).reshape(1)
    new_errors, approx = lax.cond(sec == 0, finish_for(0), finish_for(1))
    own_part = lax.dynamic_slice_in_dim(approx, replica_id * size, size)
    used = jnp.where(sec == 0, *[sum(rows_n * cols_n for rows_n, cols_n in section_shapes(s)) // LANES for s in range(2)])
    inside = replica_id * size + lax.broadcasted_iota(jnp.int32, (size, 1), 0) < used
    own_part = jnp.where(inside, own_part, 0.0)
    rate = learning_rate()
    new_master, new_low, new_moment = update(master, momentum, own_part, scale.reshape(1, 1))
    vec_own = lax.dynamic_index_in_dim(vec_sum, sec, 0, keepdims=False).reshape(-1)[:VLEN]
    new_vm = moment_decay * vec_moment[0] + scale * vec_own
    new_vectors = vectors[0] - rate * new_vm
    new_factors = lax.dynamic_index_in_dim(right_both, sec, 0, keepdims=False)
    return (
        new_master,
        new_low,
        new_moment,
        new_vectors[None],
        new_vm[None],
        new_factors[None],
        new_errors,
        loss_sum.reshape(1),
        norm.reshape(1),
    )


def solution(mesh):
    return jax.shard_map(
        local,
        mesh=mesh,
        in_specs=(
            P(DP, None, None),
            P(DP, None),
            P(DP, None),
            P(DP, None),
            P(SEC, DP),
            P(SEC, DP),
            P(SEC, None),
            P(SEC, None),
            P(SEC, None, None),
            P(SEC, DP, None),
        ),
        out_specs=(
            P(SEC, DP),
            P(SEC, DP),
            P(SEC, DP),
            P(SEC, None),
            P(SEC, None),
            P(SEC, None, None),
            P(SEC, DP, None),
            P(),
            P(),
        ),
        check_vma=False,
    )
```

time: 664 us -> 545 us (0.82)
  Pallas kernels: 598 us -> 496 us
  local copies, waits for them, and re-layouts: 41 us -> 20 us
    pallas_call x31 -> x5, Pallas kernels: 317 us -> 224 us  [the longest x1 138 us: decode(): pl.pallas_call(functools.partial(decode_body, tail_row=tail_row, gain=gai...]
    pallas_call x2, Pallas kernels: 72.4 us -> 59.9 us  [all_sum(): pl.pallas_call(functools.partial(sum_body, replicas=replicas, n_enc=len(e...]
    broadcast_in_dim x1 -> x0, local copies, waits for them, and re-layouts: 11 us -> none  [local(): new_master.astype(bf16)[None]]
where the time goes in v4:
time: 545 us; the launch traced here: 538 us
  Pallas kernels  496 us (91%)
  local copies, waits for them, and re-layouts  20 us (4%)
  other arithmetic  13 us (2%)
    pallas_call x1, Pallas kernels, decode(): pl.pallas_call(functools.partial(decode_body, tail_row=tail_row, gain=gai...  138 us
    pallas_call x1, Pallas kernels, gather(): pl.pallas_call(functools.partial(gather_body, replicas=replicas, size=siz...  108 us
    pallas_call x6, Pallas kernels, finish(): pl.pallas_call(functools.partial(finish_body, rows=rows, blocks=blocks, g...  65.9 us
    pallas_call x2, Pallas kernels, all_sum(): pl.pallas_call(functools.partial(sum_body, replicas=replicas, n_enc=len(e...  59.9 us
    pallas_call x1, Pallas kernels, encode(): pl.pallas_call(encode_body, in_specs=[ANYWHERE] + [WHOLE] * 4, out_specs=...  27.6 us
    pallas_call x1, Pallas kernels, encode_back(): pl.pallas_call(functools.partial(encode_back_body, tail_row=tail_row, gai...  26.1 us
    pallas_call x1, Pallas kernels, rights(): pl.pallas_call(functools.partial(rights_body, n=n, scale=scale, gain=gain...  23.6 us
    pallas_call x6, Pallas kernels, err_prep(): pl.pallas_call(functools.partial(err_prep_body, blocks=blocks, rows=rows)...  21.7 us

profile of v4, /device:TPU:1, one launch (start us, length us, event | category | flops | bytes accessed | tf_op | source)
XLA Modules:
  0.0 537.6 jit_solution(2723932511669187574)
XLA Ops:
  0.6 0.0 copy-start
  0.7 1.4 reduce_sum.18
  2.7 0.7 fusion.9
  3.4 0.7 constant_dynamic-slice_fusion.1
  4.1 0.6 add_compare_fusion
  4.7 0.6 broadcast_in_dim.25.cnt_ref
  5.3 0.7 convert_bitcast_fusion
  6.0 0.9 reduce.1
  7.0 0.6 pad_bitcast_fusion.vec_ref
  7.6 0.8 copy.51.place
  8.4 1.0 copy.53.mask
  9.3 0.0 copy-done
  9.3 0.9 fusion.2
  10.2 0.8 slice.79.target
  11.0 1.0 copy.52.place
  12.1 2.5 cast.1.low_ref
  14.6 31.0 %conditional.2 = (bf16[56448,128]{1,0:T(8,128)(2,1)}, f32[512,128]{1,0:T(8,128)}) conditional(s32[]{:T(128)} %convert_element_type.26, (f32[1,8,7680]{2,1,0:T(8,128)}, bf16[1,1,7225344]{2,1,0:T(2,128)(2,1)}) %tuple.23, (f32[1,8,7680]{2,1,0:T(8,128)}, bf16[1,1,7225344]{2,1,0:T(2,128)(2,1)}) %tuple.23), branch_computations={%region_2.3_spmd, %region_3.4_spmd} | conditional | bytes 1622144 | solution.py:1463
  14.6 1.4 slice.72.x_ref
  16.0 1.5 slice.70.x_ref
  17.5 1.4 fusion.7
  18.9 3.1 err_prep.11
  22.0 2.3 err_prep.12
  24.3 4.3 err_prep.13
  28.5 6.7 %err_prep.14 = (bf16[56448,128]{1,0:T(8,128)(2,1)}, f32[128,128]{1,0:T(8,128)}) custom-call(bf16[1,1,7225344]{2,1,0:T(2,128)(2,1)} %get-tuple-element.114.e_ref, f32[8,512]{1,0:T(8,128)} %get-tuple-element.377.x_ref, bf16[56448,128]{1,0:T(8,128)(2,1)} %get-tuple-element.118.rest_0_), custom_call_target="tpu_custom_call", output_to_operand_aliasing={{0}: (2, {})} | custom-call | tf_op jit(solution)/shard_map/cond/branch_0_fun/err_prep/pallas_call | solution.py:759
  35.3 1.9 err_prep.15
  37.1 0.0 copy-start.17
  37.2 3.4 err_prep.16
  40.6 0.0 copy-done.14
  40.6 0.6 constant_dynamic-update-slice_fusion.5
  41.2 0.6 constant_dynamic-update-slice_fusion.4
  41.8 0.6 constant_dynamic-update-slice_fusion.3
  42.4 0.6 constant_dynamic-update-slice_fusion.2
  43.0 0.0 copy-done.17
  43.0 0.6 constant_dynamic-update-slice_fusion.1
  43.6 1.3 constant_dynamic-update-slice_fusion
  45.0 0.6 broadcast_dynamic-update-slice_fusion
  45.6 107.7 %gather.1 = (bf16[32,3528,128]{2,1,0:T(8,128)(2,1)}, f32[16,8,128]{2,1,0:T(8,128)}, f32[2,96,128]{2,1,0:T(8,128)}, f32[2,8,7680]{2,1,0:T(8,128)}) custom-call(bf16[3528,128]{1,0:T(8,128)(2,1)} %cast.1.low_ref, f32[8,128]{1,0:T(8,128)} %broadcast_in_dim.25.cnt_ref, f32[96,128]{1,0:T(8,128)} %pad_bitcast_fusion.vec_ref, f32[8,7680]{1,0:T(8,128)} %bitcast.30), custom_call_target="tpu_custom_call" | custom-call | tf_op jit(solution)/shard_map/gather/pallas_call | solution.py:1283
  153.4 1.5 slice_reduce_fusion
  154.8 27.6 %encode.1 = (f32[256,768]{1,0:T(8,128)}, bf16[256,768]{1,0:T(8,128)(2,1)}, bf16[256,2304]{1,0:T(8,128)(2,1)}, f32[256,768]{1,0:T(8,128)}, f32[6,2,256]{2,1,0:T(2...) custom-call(bf16[112896,128]{1,0:T(8,128)(2,1)} %bitcast.28, ...), custom_call_target="tpu_custom_call" | custom-call | tf_op jit(solution)/shard_map/encode/pallas_call | solution.py:420
  182.4 137.9 %decode.1 = (bf16[1024,512]{1,0:T(8,128)(2,1)}, bf16[1024,1536]{1,0:T(8,128)(2,1)}, bf16[1024,512]{1,0:T(8,128)(2,1)}, bf16[1024,512]{1,0:T(8,128)(2,1)}, bf16[1...) custom-call(bf16[112896,128]{1,0:T(8,128)(2,1)} %bitcast.29, ...), custom_call_target="tpu_custom_call" | custom-call | tf_op jit(solution)/shard_map/decode/pallas_call | solution.py:574
  320.3 26.1 %encode_back.1 = (bf16[256,2304]{1,0:T(8,128)(2,1)}, bf16[256,768]{1,0:T(8,128)(2,1)}, bf16[256,3072]{1,0:T(8,128)(2,1)}, bf16[256,768]{1,0:T(8,128)(2,1)}, bf16...) custom-call(f32[256,3072]{1,0:T(8,128)} %get-tuple-element.304.refs_0_, f32[256,768]{1,0:T(8,128)} %get-tuple-element.305.refs_1_, ...), custom_call_target="tpu_custom_call" | custom-call | tf_op jit(solution)/shard_map/encode_back/pallas_call | solution.py:670
  346.4 0.0 copy-done.5
  346.4 1.8 pad_maximum_fusion.refs_0_
  348.2 32.0 %all_sum.2 = (f32[2,512,128]{2,1,0:T(8,128)}, bf16[256,3072]{1,0:T(8,128)(2,1)}, bf16[256,3072]{1,0:T(8,128)(2,1)}, bf16[1024,2048]{1,0:T(8,128)(2,1)}, bf16[1024,2048]{1,0:T(8,128)(2,1)}) custom-call(f32[2,512,128]{2,1,0:T(8,128)} %pad_maximum_fusion.refs_0_, f32[512,128]{1,0:T(8,128)} %get-tuple-element.322.refs_1_, ...), custom_call_target="tpu_custom_call" | custom-call | tf_op jit(solution)/shard_map/all_sum/pallas_call | solution.py:1395
  380.2 1.2 slice.66
  381.4 1.5 slice.63.vec_ref
  382.9 23.6 %rights.1 = (f32[2,8,5632]{2,1,0:T(8,128)S(1)}, f32[2,512,128]{2,1,0:T(8,128)}, f32[512,128]{1,0:T(8,128)}) custom-call(f32[2,512,128]{2,1,0:T(8,128)} %get-tuple-element.326.refs_0_, bf16[56448,128]{1,0:T(8,128)(2,1)} %get-tuple-element.327.refs_1_, bf16[256,768]{1,0:T(8,128)(2,1)} %get-tuple-element.313.refs_9_.refs_2_, ...), custom_call_target="tpu_custom_call" | custom-call | tf_op jit(solution)/shard_map/rights/pallas_call | solution.py:872
  406.5 0.0 copy-start.4
  406.6 27.9 %all_sum.3 = (f32[2,512,128]{2,1,0:T(8,128)}, bf16[256,768]{1,0:T(8,128)(2,1)}, bf16[256,2304]{1,0:T(8,128)(2,1)}, bf16[256,768]{1,0:T(8,128)(2,1)}, bf16[256,76...) custom-call(f32[2,512,128]{2,1,0:T(8,128)} %get-tuple-element.341.re, ...), custom_call_target="tpu_custom_call" | custom-call | tf_op jit(solution)/shard_map/all_sum/pallas_call | solution.py:1395
  434.5 2.6 final_right.1
  437.8 0.6 fusion.5
  438.5 83.0 %conditional.3 = ((f32[1,1,7225344]{2,1,0:T(1,128)}, f32[62592,128]{1,0:T(8,128)})) conditional(s32[]{:T(128)} %convert_element_type.26, (s32[1]{0:T(128)}, bf16[1024,512]{1,0:T(8,128)(2,1)}, bf16[1024,512]{1,0:T(8,128)(2,1)}, bf16[1024,1536]{1,0:T(8,128)(2,1)}, bf16[1024,1536]{1,0:T(8,128)(2,1)}, /*index=5*/bf16[56448,128]{1,0:T(8,128)(2,1)}, ...), branch_computations={%region_4.5_spmd, %region_5.6_spmd} | conditional | bytes 1572900 | solution.py:1526
  438.9 14.8 %finish.11 = (f32[1,1,7225344]{2,1,0:T(1,128)}, f32[62592,128]{1,0:T(8,128)}) custom-call(s32[1]{0:T(128)} %get-tuple-element.141.me_ref, bf16[1024,512]{1,0:T(8,128)(2,1)} %get-tuple-element.165.a0, bf16[1024,512]{1,0:T(8,128)(2,1)} %get-tuple-element.166.a1, bf16[1024,1536]{1,0:T(8,128)(2,1)} %get-tuple-element.167.b0, ...), custom_call_target="tpu_custom_call" | custom-call | tf_op jit(solution)/shard_map/cond/branch_0_fun/finish/pallas_call | solution.py:984
  453.7 6.4 %finish.12 = (f32[1,1,7225344]{2,1,0:T(1,128)}, f32[62592,128]{1,0:T(8,128)}) custom-call(s32[1]{0:T(128)} %get-tuple-element.141.me_ref, bf16[1024,512]{1,0:T(8,128)(2,1)} %get-tuple-element.161.a0, bf16[1024,512]{1,0:T(8,128)(2,1)} %get-tuple-element.162.a1, ...), custom_call_target="tpu_custom_call", output_to_operand_aliasing={{0}: (8, {}), {1}: (9, {})} | custom-call | tf_op jit(solution)/shard_map/cond/branch_0_fun/finish/pallas_call | solution.py:984
  460.0 19.8 %finish.13 = (f32[1,1,7225344]{2,1,0:T(1,128)}, f32[62592,128]{1,0:T(8,128)}) custom-call(s32[1]{0:T(128)} %get-tuple-element.141.me_ref, bf16[1024,512]{1,0:T(8,128)(2,1)} %get-tuple-element.157.a0, bf16[1024,512]{1,0:T(8,128)(2,1)} %get-tuple-element.158.a1, ...), custom_call_target="tpu_custom_call", output_to_operand_aliasing={{0}: (8, {}), {1}: (9, {})} | custom-call | tf_op jit(solution)/shard_map/cond/branch_0_fun/finish/pallas_call | solution.py:984
  479.8 16.4 %finish.14 = (f32[1,1,7225344]{2,1,0:T(1,128)}, f32[62592,128]{1,0:T(8,128)}) custom-call(s32[1]{0:T(128)} %get-tuple-element.141.me_ref, bf16[1024,2048]{1,0:T(8,128)(2,1)} %get-tuple-element.153.a0, bf16[1024,2048]{1,0:T(8,128)(2,1)} %get-tuple-element.154.a1, ...), custom_call_target="tpu_custom_call", output_to_operand_aliasing={{0}: (8, {}), {1}: (9, {})} | custom-call | tf_op jit(solution)/shard_map/cond/branch_0_fun/finish/pallas_call | solution.py:984
  496.2 3.5 finish.15
  499.7 5.1 finish.16
  504.8 12.0 %finish_tail.1 = f32[1,1,7225344]{2,1,0:T(1,128)} custom-call(bf16[1,1,7225344]{2,1,0:T(2,128)(2,1)} %get-tuple-element.140.e_ref, f32[1,1,7225344]{2,1,0:T(1,128)} %get-tuple-element.179.buf0), custom_call_target="tpu_custom_call", output_to_operand_aliasing={{}: (1, {})} | custom-call | tf_op jit(solution)/shard_map/cond/branch_0_fun/finish_tail/pallas_call | solution.py:1018
  521.5 0.0 copy-start.1
  521.5 3.9 dynamic-slice_select_fusion.approx_ref
  525.5 1.6 multiply_subtract_fusion
  527.0 1.7 constant_dynamic-slice_fusion
  528.7 8.7 %update.1 = (f32[1,451584]{1,0:T(1,128)}, bf16[1,451584]{1,0:T(2,128)(2,1)}, f32[1,451584]{1,0:T(1,128)}) custom-call(f32[1,451584]{1,0:T(1,128)} %master_ref.1, f32[1,451584]{1,0:T(1,128)} %moment_ref.1, f32[3528,128]{1,0:T(8,128)} %dynamic-slice_select_fusion.approx_ref, f32[1,1]{1,0:T(1,128)} %min_shard_map.6.scale_ref), custom_call_target="tpu_custom_call" | custom-call | tf_op jit(solution)/shard_map/update/pallas_call | solution.py:1255
  (20 shorter events, 0.1 us)
Async XLA Ops:
  0.6 8.7 %copy-start = (bf16[2,1024,192]{1,2,0:T(8,128)(2,1)S(1)}, bf16[2,1024,192]{1,2,0:T(8,128)(2,1)}, u32[]{:S(2)}) copy-start(bf16[2,1024,192]{1,2,0:T(8,128)(2,1)} %param.16) | copy-start | bytes 2359300
  37.1 3.5 copy-start.14
  37.1 4.1 copy-start.15
  37.1 4.7 copy-start.16
  37.1 5.3 copy-start.9
  37.1 5.9 %copy-start.17 = (f32[16,128]{1,0:T(8,128)S(1)}, f32[16,128]{1,0:T(8,128)}, u32[]{:S(2)}) copy-start(f32[16,128]{1,0:T(8,128)} %get-tuple-element.126) | copy-start | bytes 24580 | tf_op jit(solution)/shard_map/cond
  320.3 26.1 %copy-start.5 = (f32[512,128]{1,0:T(8,128)S(1)}, f32[512,128]{1,0:T(8,128)}, u32[]{:S(2)}) copy-start(f32[512,128]{1,0:T(8,128)} %get-tuple-element.321) | copy-start | bytes 786436
  406.5 31.3 %copy-start.4 = (f32[2,96,128]{2,1,0:T(8,128)S(1)}, f32[2,96,128]{2,1,0:T(8,128)}, u32[]{:S(2)}) copy-start(f32[2,96,128]{2,1,0:T(8,128)} %slice.63.vec_ref) | copy-start | bytes 294916
  438.5 83.0 %copy-start.13 = (pred[3528]{0:T(1024)(128)(4,1)S(1)}, pred[3528]{0:T(1024)(128)(4,1)}, u32[]{:S(2)}) copy-start(pred[3528]{0:T(1024)(128)(4,1)} %add_compare_fusion) | copy-start | bytes 10588
  438.5 87.0 %copy-start.6 = (f32[1,1,90,128]{3,2,1,0:T(8,128)S(1)}, f32[1,1,90,128]{3,2,1,0:T(8,128)}, u32[]{:S(2)}) copy-start(f32[1,1,90,128]{3,2,1,0:T(8,128)} %fusion.5) | copy-start | bytes 138244
  438.5 87.0 %copy-start.7 = (f32[1,11520]{1,0:T(1,128)S(1)}, f32[1,11520]{1,0:T(1,128)}, u32[]{:S(2)}) copy-start(f32[1,11520]{1,0:T(1,128)} %param.22) | copy-start | bytes 138244
  479.8 16.4 %copy-start.2 = (bf16[768,192]{1,0:T(8,128)(2,1)S(1)}, bf16[768,192]{1,0:T(8,128)(2,1)}, u32[]{:S(2)}) copy-start(bf16[768,192]{1,0:T(8,128)(2,1)} %get-tuple-element.149.a0) | copy-start | bytes 884740 | tf_op jit(solution)/shard_map/cond
  521.5 15.8 %copy-start.1 = (bf16[2,1024,192]{1,2,0:T(8,128)(2,1)S(1)}, bf16[2,1024,192]{1,2,0:T(8,128)(2,1)}, u32[]{:S(2)}) copy-start(bf16[2,1024,192]{1,2,0:T(8,128)(2,1)} %param.16) | copy-start | bytes 2359300

commit v5 on v4

--- a/solution.py
+++ b/solution.py
@@ -16,6 +16,7 @@
 FFD = 2048
 HEADS_DEC = 16
 PATCH = 192
+PATCH_PAD = 256
 RANK = 8
 SEQ = 1024
 VIS = 256
@@ -34,7 +35,6 @@
 STEP = 32
 DEC_ROWS = 512
 CHUNK = 256
-SPARE = 6144
 BIG = 66000000
 
 
@@ -401,7 +401,7 @@
         copies.start(mat, mats_out[index])
         return mat
 
-    kept[K_TOKENS][...] = positions_of(place[...], table) + vecs[10:11] + nn(pix[...], take(4)[...])
+    kept[K_TOKENS][...] = positions_of(place[...], table) + vecs[10:11] + nn(pix[:, :PATCH], take(4)[...])
     open_stage(kept[K_TOKENS], kept[K_NORMED], kept[K_JOINED], vecs, take(0))
     give(K_TOKENS, K_NORMED, K_JOINED)
     attend_stage(kept[K_JOINED], kept[K_OUT], kept[K_LSE], DE // HEADS_ENC)
@@ -455,7 +455,7 @@
 DEC_GIVEN = [
     (K_NORMED, (SEQ, DD), bf16), (K_B_QKV, (SEQ, 3 * DD), bf16), (K_ATTENDED, (SEQ, DD), bf16), (K_B_PROJ, (SEQ, DD), bf16),
     (K_SECOND, (SEQ, DD), bf16), (K_B_UP, (SEQ, FFD), bf16), (K_ACTIVE, (SEQ, FFD), bf16), (K_B_DOWN, (SEQ, DD), bf16),
-    (K_B_PRED, (SEQ - VIS, PATCH), bf16), (K_FINAL, (SEQ - VIS, DD), bf16), (K_SENT, (VIS, DE), bf16), (K_FIRST, (VIS, DD), bf16),
+    (K_B_PRED, (SEQ - VIS, PATCH_PAD), bf16), (K_FINAL, (SEQ - VIS, DD), bf16), (K_SENT, (VIS, DE), bf16), (K_FIRST, (VIS, DD), bf16),
 ]
 DEC_HELD = [
     (K_TOKENS, (SEQ, DD), f32), (K_JOINED, (SEQ, 3 * DD), bf16), (K_OUT, (SEQ, DD), f32), (K_LSE, (DD // LANES, 4, SEQ), f32),
@@ -526,7 +526,8 @@
         row = tail_row + VEC_TILES * RANK
         part_ref[row : row + RANK] += jnp.broadcast_to(loss, (RANK, LANES))
         b_pred = (weight * (2.0 * residual / PATCH) / count).astype(bf16)
-        have[K_B_PRED][late] = b_pred
+        have[K_B_PRED][late, :PATCH] = b_pred
+        have[K_B_PRED][late, PATCH:] = jnp.zeros((VIS, PATCH_PAD - PATCH), bf16)
         grad = nn(b_pred, w_head[...])
         have[K_GRAD][rows] = norm_back(grad, hat, spread, vec_d[4:5])
         sums[4:5] += column_sum(grad * hat)
@@ -724,54 +725,113 @@
     return 256
 
 
-def err_prep_body(e_ref, x_ref, *rest, blocks, rows):
-    out_ref, left_ref, wide = rest[-3:]
-    wide[...] = e_ref[0].reshape(rows * blocks, LANES).astype(f32)
-    pieces = split3(x_ref[...])
-    total = jnp.zeros((rows, 3 * RANK), f32)
-    for block in range(blocks):
-        part = wide[pl.ds(block, rows, stride=blocks), :].astype(bf16)
-        out_ref[block * rows : (block + 1) * rows, :] = part
-        total = total + nt(part, pieces[:, block * LANES : (block + 1) * LANES])
-    value = join3(total.T)
-    left_ref[...] = jnp.zeros_like(left_ref)
-    for tile in range(tiles_of(rows)):
-        here = min(LANES, rows - tile * LANES)
-        left_ref[tile * RANK : (tile + 1) * RANK, :here] = value[:, tile * LANES : tile * LANES + here]
-
-
-def err_prep(errors, factor, start, rows_n, cols_n, buf):
-    blocks = cols_n // LANES
-    rows = chunk_rows(rows_n, cols_n)
-    step = rows * blocks
-    steps = rows_n // rows
-    tiles = tiles_of(rows)
-    in_specs = [
-        pl.BlockSpec((pl.Element(1), pl.Element(1), pl.Element(step * LANES)), lambda i: (0, 0, pl.multiple_of(start + i * step * LANES, 1024))),
-        pl.BlockSpec((RANK, cols_n), lambda i: (0, 0)),
+TAIL_STEPS = 12
+MOST = max(chunk_rows(*shape) * shape[1] for which in range(2) for shape in section_shapes(which)) // LANES
+
+
+def used_length(section):
+    return sum(rows_n * cols_n for rows_n, cols_n in section_shapes(section))
+
+
+class Prep:
+    def __init__(self, errors, factor, stack, left, whole, raw, wide, made, pieces, total, tail, raw_sem, out_sem):
+        self.errors, self.factor, self.stack, self.left, self.whole = errors, factor, stack, left, whole
+        self.raw, self.wide, self.made, self.pieces, self.total, self.tail = raw, wide, made, pieces, total, tail
+        self.raw_sem, self.out_sem = raw_sem, out_sem
+
+    def fetch(self, start, step, chunk):
+        slot = lax.rem(chunk, 2)
+        at = pl.multiple_of(start + chunk * step * LANES, 1024)
+        return pltpu.make_async_copy(
+            self.errors.at[:, :, pl.ds(at, step * LANES)], self.raw.at[slot, :, :, pl.ds(0, step * LANES)], self.raw_sem.at[slot]
+        )
+
+    def run(self, count, start, step, store, work):
+        self.fetch(start, step, jnp.int32(0)).start()
+
+        def one(chunk):
+            slot = lax.rem(chunk, 2)
+
+            @pl.when(chunk + 1 < count)
+            def _():
+                self.fetch(start, step, chunk + 1).start()
+
+            self.fetch(start, step, chunk).wait()
+
+            @pl.when(chunk >= 2)
+            def _():
+                store(chunk - 2, slot).wait()
+
+            work(chunk, slot)
+            store(chunk, slot).start()
+
+        loop(count, one)
+        for chunk in range(max(count - 2, 0), count):
+            store(jnp.int32(chunk), chunk % 2).wait()
+
+    def matrix(self, section, index):
+        shapes = section_shapes(section)
+        start = sum(rows_n * cols_n for rows_n, cols_n in shapes[:index])
+        rows_n, cols_n = shapes[index]
+        base = len(section_shapes(0)) * section + index
+        blocks, rows = cols_n // LANES, chunk_rows(rows_n, cols_n)
+        step, tiles = rows * blocks, tiles_of(rows)
+        col_at, row_tile = COL_SPANS[base][1], ROW_SPANS[base][1] // LANES
+        self.pieces[:, :cols_n] = split3(self.factor[:, col_at : col_at + cols_n])
+
+        def store(chunk, slot):
+            at = pl.multiple_of(start // LANES + chunk * step, 16)
+            return pltpu.make_async_copy(
+                self.made.at[slot, pl.ds(0, step)], self.stack.at[pl.ds(at, step)], self.out_sem.at[slot]
+            )
+
+        def work(chunk, slot):
+            def widen_one(part):
+                here = pl.ds(pl.multiple_of(part * LANES * LANES, 1024), LANES * LANES)
+                self.wide[rows_at(part, LANES)] = self.raw[slot, 0, :, here].reshape(LANES, LANES).astype(f32)
+
+            loop(step // LANES, widen_one)
+            self.total[...] = jnp.zeros_like(self.total)
+
+            def block_one(block):
+                part = self.wide[pl.ds(block, rows, stride=blocks), :].astype(bf16)
+                self.made[slot, rows_at(block, rows)] = part
+                self.total[:rows] += nt(part, self.pieces[:, cols_at(block)])
+
+            loop(blocks, block_one)
+            value = join3(self.total[:rows].T)
+            for tile in range(tiles):
+                here = min(LANES, rows - tile * LANES)
+                at = pl.multiple_of((row_tile + chunk * tiles + tile) * RANK, RANK)
+                self.left[pl.ds(at, RANK), :here] = value[:, tile * LANES : tile * LANES + here]
+
+        self.run(rows_n // rows, start, step, store, work)
+
+    def rest(self, section):
+        start = used_length(section)
+        step = (FLAT - start) // TAIL_STEPS // LANES
+
+        def store(chunk, slot):
+            at = pl.multiple_of(start + chunk * step * LANES, 1024)
+            return pltpu.make_async_copy(self.tail.at[slot], self.whole.at[:, :, pl.ds(at, step * LANES)], self.out_sem.at[slot])
+
+        def work(chunk, slot):
+            def one(part):
+                here = pl.ds(pl.multiple_of(part * 4096, 1024), 4096)
+                self.tail[slot, 0, :, here] = self.raw[slot, 0, :, here].astype(f32)
+
+            loop(step * LANES // 4096, one)
+
+        self.run(TAIL_STEPS, start, step, store, work)
+
+
+def prep_scratch():
+    tail = (FLAT - used_length(1)) // TAIL_STEPS
+    dma = pltpu.SemaphoreType.DMA
+    return [
+        pltpu.VMEM((2, 1, 1, MOST * LANES), bf16), pltpu.VMEM((MOST, LANES), f32), pltpu.VMEM((2, MOST, LANES), bf16),
+        pltpu.VMEM((3 * RANK, FFE), bf16), pltpu.VMEM((256, 3 * RANK), f32), pltpu.VMEM((2, 1, 1, tail), f32), dma((2,)), dma((2,)),
     ]
-    args = [errors, factor]
-    aliases = {}
-    if buf is not None:
-        in_specs.append(pl.BlockSpec(memory_space=pl.ANY))
-        args.append(buf)
-        aliases = {2: 0}
-    return pl.pallas_call(
-        functools.partial(err_prep_body, blocks=blocks, rows=rows),
-        grid=(steps,),
-        in_specs=in_specs,
-        out_specs=[
-            pl.BlockSpec((pl.Element(step), pl.Element(LANES)), lambda i: (pl.multiple_of(start // LANES + i * step, 16), 0)),
-            pl.BlockSpec((tiles * RANK, LANES), lambda i: (i, 0)),
-        ],
-        out_shape=[
-            jax.ShapeDtypeStruct((FLAT // LANES, LANES), bf16),
-            jax.ShapeDtypeStruct((steps * tiles * RANK, LANES), f32),
-        ],
-        input_output_aliases=aliases,
-        scratch_shapes=[pltpu.VMEM((step, LANES), f32)],
-        name="err_prep",
-    )(*args)
 
 
 def ortho_stage(sum_ref, out_ref, wide, scale):
@@ -861,7 +921,8 @@
     for (wait_u, wait_v), u_ref, v_ref, (which, row_at, rows), (unused, col_at, cols) in zip(waits, u_refs, v_refs, ROW_SPANS, COL_SPANS):
         wait_u.wait()
         wait_v.wait()
-        part = join3(nt(split3(ortho_ref[which, :, row_at : row_at + rows]), u_ref[...]))
+        padded = tiles_of(rows) * LANES
+        part = join3(nt(split3(ortho_ref[which, :, row_at : row_at + padded]), u_ref[...]))
         put_tiles(part_ref.at[which], col_at // LANES * RANK, gain * join3(nn(split3(part), v_ref[...])))
 
 
@@ -913,118 +974,179 @@
     )(sums, ortho, vecs)
 
 
-def finish_body(me_ref, a0, a1, b0, b1, e_ref, o_ref, r_ref, *rest, rows, blocks, gain, start, shard):
-    err_out, app_out = rest[-2:]
-    o_part = o_ref[0]
-    o_high = o_part.astype(bf16)
-    o_low = (o_part - o_high.astype(f32)).astype(bf16)
-    left_t = jnp.concatenate([o_high, o_low, o_high], axis=0).T[:rows]
-    lhs0 = a0[...].T
-    lhs1 = a1[...].T
-    err_rows = err_out.at[0].reshape(rows * blocks, LANES)
-    keep = overlaps(pl.program_id(0), me_ref[0], start, rows * blocks, shard)
-    for pair in range(blocks // 2):
-        cols = slice(pair * 2 * LANES, (pair + 1) * 2 * LANES)
-        r_part = r_ref[0, :, cols]
-        r_high = r_part.astype(bf16)
-        r_low = (r_part - r_high.astype(f32)).astype(bf16)
-        approx = nn(left_t, jnp.concatenate([r_high, r_high, r_low], axis=0))
-        grad = nn(lhs0, b0[:, cols]) + nn(lhs1, b1[:, cols])
-        for side in range(2):
-            block = pair * 2 + side
-            half = slice(side * LANES, (side + 1) * LANES)
-            err_rows[pl.ds(block, rows, stride=blocks), :] = (
-                gain * grad[:, half] + e_ref[block * rows : (block + 1) * rows].astype(f32)
-            ) - approx[:, half]
+def overlaps(first, count, me, shard):
+    return (first < (me + 1) * shard) & (first + count > me * shard)
+
+
+def finish_plan(section, heights):
+    plan, start = [], 0
+    for index, ((rows_n, cols_n), height) in enumerate(zip(section_shapes(section), heights)):
+        base = len(section_shapes(0)) * section + index
+        rows = chunk_rows(rows_n, cols_n)
+        plan.append((start, rows_n // rows, rows, cols_n // LANES, rows_n, height, ROW_SPANS[base][1], COL_SPANS[base][1]))
+        start += rows_n * cols_n
+    return plan
+
+
+def finish_section(
+    section, heights, pairs, err, ortho, right, err_out, app_out, a_slots, b_slots, lhs, left, ring, made, kept,
+    pair_sems, ring_sem, made_sem, kept_sem, *, gain, shard,
+):
+    plan = finish_plan(section, heights)
+    offsets = [sum(entry[1] for entry in plan[:index]) for index in range(len(plan) + 1)]
+    flat_plan = [(index, chunk) for index, entry in enumerate(plan) for chunk in range(entry[1])]
+    me = lax.axis_index(DP)
+
+    def load(index):
+        height, rows_n, cols_n = plan[index][5], tiles_of(plan[index][4]) * LANES, plan[index][3] * LANES
+        slot, copies = index % 2, []
+        for sample in range(2):
+            for side, (slots, width) in enumerate(((a_slots, rows_n), (b_slots, cols_n))):
+                copies.append(pltpu.make_async_copy(
+                    pairs[sample][2 * index + side],
+                    slots.at[slot, pl.ds(sample * height, height), pl.ds(0, width)], pair_sems.at[slot, 2 * sample + side],
+                ))
+        return copies
+
+    def fetch(index, chunk):
+        start, unused, rows, blocks = plan[index][:4]
+        slot = lax.rem(offsets[index] + chunk, 2)
+        at = pl.multiple_of(start // LANES + chunk * rows * blocks, 16)
+        return pltpu.make_async_copy(
+            err.at[pl.ds(at, rows * blocks)], ring.at[slot, pl.ds(0, rows * blocks)], ring_sem.at[slot]
+        )
+
+    def store(index, chunk):
+        start, unused, rows, blocks = plan[index][:4]
+        slot, count = lax.rem(offsets[index] + chunk, 2), rows * blocks * LANES
+        at = pl.multiple_of(start + chunk * count, 1024)
+        return pltpu.make_async_copy(
+            made.at[slot, :, :, pl.ds(0, count)], err_out.at[:, :, pl.ds(at, count)], made_sem.at[slot]
+        )
+
+    for copy in load(0):
+        copy.start()
+    fetch(0, jnp.int32(0)).start()
+    for index, (start, count, rows, blocks, rows_n, height, row_at, col_at) in enumerate(plan):
+        for copy in load(index):
+            copy.wait()
+        if index + 1 < len(plan):
+            for copy in load(index + 1):
+                copy.start()
+        pair_slot, step, wide_rows = index % 2, rows * blocks, tiles_of(rows) * LANES
+
+        def one(chunk):
+            slot = lax.rem(offsets[index] + chunk, 2)
+
+            @pl.when(chunk + 1 < count)
+            def _():
+                fetch(index, chunk + 1).start()
+
+            if index + 1 < len(plan):
+
+                @pl.when(chunk + 1 == count)
+                def _():
+                    fetch(index + 1, jnp.int32(0)).start()
+
+            o_part = ortho[section, :, pl.ds(pl.multiple_of(row_at + chunk * wide_rows, LANES), wide_rows)]
+            o_high = o_part.astype(bf16)
+            o_low = (o_part - o_high.astype(f32)).astype(bf16)
+            left[:wide_rows] = jnp.concatenate([o_high, o_low, o_high], axis=0).T
+
+            def turn(part):
+                lhs[:, cols_at(part, 256)] = a_slots[pair_slot, rows_at(part, 256), cols_at(chunk, 256)].T
+
+            loop(2 * height // 256, turn)
+            fetch(index, chunk).wait()
+            for back in range(2):
+                before = offsets[index] + back - 2
+                if before >= 0 and back < count:
+                    old_index, old_chunk = flat_plan[before]
+
+                    @pl.when(chunk == back)
+                    def _():
+                        store(old_index, jnp.int32(old_chunk)).wait()
+
+            @pl.when(chunk >= 2)
+            def _():
+                store(index, chunk - 2).wait()
+
+            first = start + chunk * step * LANES
+            keep = overlaps(first, step * LANES, me, shard)
+            lines = made.at[slot, 0, :, pl.ds(0, step * LANES)].reshape(step, LANES)
+
+            def pair_one(pair):
+                cols = cols_at(pair, 2 * LANES)
+                r_part = right[section, :, pl.ds(pl.multiple_of(col_at + pair * 2 * LANES, LANES), 2 * LANES)]
+                r_high = r_part.astype(bf16)
+                r_low = (r_part - r_high.astype(f32)).astype(bf16)
+                approx = nn(left[:rows], jnp.concatenate([r_high, r_high, r_low], axis=0))
+                grad = nn(lhs[:rows, : 2 * height], b_slots[pair_slot, : 2 * height, cols])
+                for side in range(2):
+                    half = slice(side * LANES, (side + 1) * LANES)
+                    block = 2 * pair + side
+                    given = ring[slot, pl.ds(pl.multiple_of(block * rows, 16), rows)].astype(f32)
+                    lines[pl.ds(block, rows, stride=blocks), :] = (gain * grad[:, half] + given) - approx[:, half]
+
+                    @pl.when(keep)
+                    def _():
+                        kept[pl.ds(block, rows, stride=blocks), :] = approx[:, half]
+
+            loop(blocks // 2, pair_one)
+            store(index, chunk).start()
 
             @pl.when(keep)
             def _():
-                app_out[pl.ds(block, rows, stride=blocks), :] = approx[:, half]
-
-
-def overlaps(i, me, start, step, shard):
-    first = start + i * step * LANES
-    return (first < (me + 1) * shard) & (first + step * LANES > me * shard)
-
-
-def finish(me, pair0, pair1, err, ortho, right, section, row_at, col_at, start, gain, shard, bufs):
-    a0, b0 = pair0
-    a1, b1 = pair1
-    rows_n, cols_n = a0.shape[1], b0.shape[1]
-    seq = a0.shape[0]
-    blocks = cols_n // LANES
-    rows = chunk_rows(rows_n, cols_n)
-    step = rows * blocks
-    flat_rows = FLAT // LANES
-    whole = lambda i, me: (0, 0)
-    flat_at = lambda i: pl.multiple_of(start // LANES + i * step, 16)
-    wide_rows = tiles_of(rows) * LANES
-
-    def shard_at(i, me):
-        return pl.multiple_of(jnp.where(overlaps(i, me[0], start, step, shard), start // LANES + i * step, flat_rows), 8), 0
-
-    in_specs = [
-        pl.BlockSpec((seq, rows), lambda i, me: (0, i)),
-        pl.BlockSpec((seq, rows), lambda i, me: (0, i)),
-        pl.BlockSpec((seq, cols_n), whole, pipeline_mode=pl.Buffered(1)),
-        pl.BlockSpec((seq, cols_n), whole, pipeline_mode=pl.Buffered(1)),
-        pl.BlockSpec((pl.Element(step), pl.Element(LANES)), lambda i, me: (flat_at(i), 0)),
-        pl.BlockSpec((1, RANK, wide_rows), lambda i, me: (section, 0, row_at // wide_rows + i)),
-        pl.BlockSpec(
-            (pl.Element(1), pl.Element(RANK), pl.Element(cols_n)), lambda i, me: (section, 0, col_at), pipeline_mode=pl.Buffered(1)
-        ),
-    ]
-    assert row_at % wide_rows == 0
-    args = [a0, a1, b0, b1, err, ortho, right]
-    aliases = {}
-    if bufs is not None:
-        in_specs += [pl.BlockSpec(memory_space=pl.ANY)] * 2
-        args += list(bufs)
-        aliases = {8: 0, 9: 1}
+                at = pl.multiple_of(start // LANES + chunk * step, 16)
+                copy = pltpu.make_async_copy(kept.at[pl.ds(0, step)], app_out.at[pl.ds(at, step)], kept_sem)
+                copy.start()
+                copy.wait()
+
+        loop(count, one)
+    for old_index, old_chunk in flat_plan[-2:]:
+        store(old_index, jnp.int32(old_chunk)).wait()
+
+
+def finish_body(*refs, n_enc, n_dec, gain, shard, heights):
+    mine, refs = refs[: n_enc + n_dec], refs[n_enc + n_dec :]
+    theirs, refs = refs[: n_enc + n_dec], refs[n_enc + n_dec :]
+    err, ortho, right, unused, err_out, app_out = refs[:6]
+    a_enc, b_enc, a_dec, b_dec = refs[6:10]
+    section = lax.axis_index(SEC)
+    for which, (a_slots, b_slots, lo, hi) in enumerate(((a_enc, b_enc, 0, n_enc), (a_dec, b_dec, n_enc, n_enc + n_dec))):
+
+        @pl.when(section == which)
+        def _():
+            finish_section(
+                which, heights[which], (mine[lo:hi], theirs[lo:hi]), err, ortho, right, err_out, app_out, a_slots, b_slots,
+                *refs[10:], gain=gain, shard=shard,
+            )
+
+
+def finish(mine_e, mine_d, theirs_e, theirs_d, err, ortho, right, whole, gain, shard):
+    n_enc, n_dec = len(mine_e), len(mine_d)
+    heights = [[x.shape[0] for x in mine[::2]] for mine in (mine_e, mine_d)]
+    dma = pltpu.SemaphoreType.DMA
+    slots = []
+    for which in range(2):
+        for side in range(2):
+            slots.append(pltpu.VMEM((2, 2 * max(heights[which]), max(shape[side] for shape in section_shapes(which))), bf16))
+    total = 2 * (n_enc + n_dec)
     return pl.pallas_call(
-        functools.partial(finish_body, rows=rows, blocks=blocks, gain=gain, start=start, shard=shard),
-        grid_spec=pltpu.PrefetchScalarGridSpec(
-            num_scalar_prefetch=1,
-            grid=(rows_n // rows,),
-            in_specs=in_specs,
-            out_specs=[
-                pl.BlockSpec(
-                    (pl.Element(1), pl.Element(1), pl.Element(step * LANES)),
-                    lambda i, me: (0, 0, pl.multiple_of(start + i * step * LANES, 1024)),
-                ),
-                pl.BlockSpec((pl.Element(step), pl.Element(LANES)), shard_at),
-            ],
-        ),
-        out_shape=[
-            jax.ShapeDtypeStruct((1, 1, FLAT), f32),
-            jax.ShapeDtypeStruct((flat_rows + SPARE, LANES), f32),
+        functools.partial(finish_body, n_enc=n_enc, n_dec=n_dec, gain=gain, shard=shard, heights=heights),
+        in_specs=[ANYWHERE] * (total + 1) + [WHOLE] * 2 + [ANYWHERE],
+        out_specs=[ANYWHERE] * 2,
+        out_shape=[jax.ShapeDtypeStruct((1, 1, FLAT), f32), jax.ShapeDtypeStruct((FLAT // LANES, LANES), f32)],
+        input_output_aliases={total + 3: 0},
+        scratch_shapes=slots
+        + [
+            pltpu.VMEM((256, 2 * SEQ), bf16), pltpu.VMEM((256, 3 * RANK), bf16), pltpu.VMEM((2, MOST, LANES), bf16),
+            pltpu.VMEM((2, 1, 1, MOST * LANES), f32), pltpu.VMEM((MOST, LANES), f32),
+            dma((2, 4)), dma((2,)), dma((2,)), dma(()),
         ],
-        input_output_aliases=aliases,
         compiler_params=pltpu.CompilerParams(vmem_limit_bytes=BIG),
         name="finish",
-    )(me, *args)
-
-
-def tail_body(e_ref, buf0, err_out):
-    err_out[...] = e_ref[...].astype(f32)
-
-
-def finish_tail(errors, start, buf):
-    count = FLAT - start
-    steps = 6
-    step = count // steps
-    assert step * steps == count and step % 1024 == 0
-    spec = pl.BlockSpec((pl.Element(1), pl.Element(1), pl.Element(step)), lambda i: (0, 0, pl.multiple_of(start + i * step, 1024)))
-    return pl.pallas_call(
-        tail_body,
-        grid=(steps,),
-        in_specs=[spec, pl.BlockSpec(memory_space=pl.ANY)],
-        out_specs=spec,
-        out_shape=jax.ShapeDtypeStruct((1, 1, FLAT), f32),
-        input_output_aliases={1: 0},
-        compiler_params=pltpu.CompilerParams(vmem_limit_bytes=BIG),
-        name="finish_tail",
-    )(errors, buf)
+    )(*mine_e, *mine_d, *theirs_e, *theirs_d, err, ortho, right, whole)
 
 
 MESH = pl.DeviceIdType.MESH
@@ -1052,8 +1174,8 @@
 
 
 def gather_body(
-    low_ref, cnt_ref, vec_ref, fac_ref, flat_ref, cnts_ref, vec2_ref, fac2_ref,
-    send_sem, recv_sem, swap_sem, cnt_send, cnt_recv, side_send, side_recv, own_sem, *, replicas, size,
+    low_ref, cnt_ref, vec_ref, fac_ref, err_ref, flat_ref, cnts_ref, vec2_ref, fac2_ref, stack_ref, left_ref, whole_ref,
+    send_sem, recv_sem, swap_sem, cnt_send, cnt_recv, side_send, side_recv, own_sem, *scratch, replicas, size,
 ):
     section, me = lax.axis_index(SEC), lax.axis_index(DP)
     other = 1 - section
@@ -1186,6 +1308,9 @@
                             arrived(block, half)
                             across(block, half)
 
+    prep = Prep(err_ref, fac_ref, stack_ref, left_ref, whole_ref, *scratch)
+    left_ref[...] = jnp.zeros_like(left_ref)
+    shares = [[[0], [2], [3], [1], [4]], [[0, 1], [2], [3], [4, 5], [None]]]
     for k in range(nz + 2):
         if k < nz:
             first(k)
@@ -1193,6 +1318,16 @@
             second(k - 1)
         if 0 <= k - 2 < nz:
             third(k - 2)
+        for which in range(2):
+            if k < len(shares[which]):
+
+                @pl.when(section == which)
+                def _():
+                    for index in shares[which][k]:
+                        if index is None:
+                            prep.rest(which)
+                        else:
+                            prep.matrix(which, index)
 
     def drain(block, carry):
         at_x_, at_y_, at_z_ = lax.rem(block, nx), lax.rem(block // nx, ny), block // (nx * ny)
@@ -1251,11 +1386,14 @@
 
 
 def update(master, moment, approx, scale):
-    full = pl.BlockSpec(memory_space=pltpu.VMEM)
+    size = approx.shape[0]
+    steps = 7 if size % 56 == 0 else 1
+    line = pl.BlockSpec((1, master.shape[1] // steps), lambda i: (0, i))
     return pl.pallas_call(
         update_body,
-        in_specs=[full] * 4,
-        out_specs=[full] * 3,
+        grid=(steps,),
+        in_specs=[line, line, pl.BlockSpec((size // steps, LANES), lambda i: (i, 0)), pl.BlockSpec((1, 1), lambda i: (0, 0))],
+        out_specs=[line] * 3,
         out_shape=[
             jax.ShapeDtypeStruct(master.shape, f32), jax.ShapeDtypeStruct(master.shape, bf16),
             jax.ShapeDtypeStruct(master.shape, f32),
@@ -1275,28 +1413,32 @@
     )(master)
 
 
-def gather(low, cnt, vec, fac, replicas):
+def gather(low, cnt, vec, fac, errors, replicas, left_rows):
     size = low.shape[0]
     vmem = pl.BlockSpec(memory_space=pltpu.VMEM)
     nz, ny, nx = grid_of(replicas)
     dma = pltpu.SemaphoreType.DMA
     return pl.pallas_call(
         functools.partial(gather_body, replicas=replicas, size=size),
-        in_specs=[vmem] * 4,
-        out_specs=[pl.BlockSpec(memory_space=pl.ANY), vmem, vmem, vmem],
+        in_specs=[vmem] * 4 + [ANYWHERE],
+        out_specs=[ANYWHERE, vmem, vmem, vmem, ANYWHERE, vmem, ANYWHERE],
         out_shape=[
             jax.ShapeDtypeStruct((2 * replicas, size, LANES), bf16),
             jax.ShapeDtypeStruct((replicas,) + cnt.shape, f32),
             jax.ShapeDtypeStruct((2,) + vec.shape, f32),
             jax.ShapeDtypeStruct((2,) + fac.shape, f32),
+            jax.ShapeDtypeStruct((FLAT // LANES, LANES), bf16),
+            jax.ShapeDtypeStruct((left_rows, LANES), f32),
+            jax.ShapeDtypeStruct((1, 1, FLAT), f32),
         ],
         scratch_shapes=[
             dma((replicas, 2, nx + ny + 1)), dma((replicas, 2)), dma((replicas, 2)),
             dma((replicas,)), dma((replicas,)), dma((2,)), dma((2,)), dma(()),
-        ],
-        compiler_params=pltpu.CompilerParams(collective_id=2, has_side_effects=True),
+        ]
+        + prep_scratch(),
+        compiler_params=pltpu.CompilerParams(collective_id=2, has_side_effects=True, vmem_limit_bytes=BIG),
         name="gather",
-    )(low, cnt, vec, fac)
+    )(low, cnt, vec, fac, errors)
 
 
 def sum_body(*refs, replicas, n_enc, n_dec):
@@ -1421,8 +1563,9 @@
 
     count_tile = jnp.full((RANK, LANES), jnp.sum(loss_mask).astype(f32))
     vec_tile = jnp.pad(vectors[0], (0, VEC_TILES * RANK * LANES - VLEN)).reshape(-1, LANES)
-    flat_both, counts, vec_both, fac_both = gather(
-        cast_shard(master, size), count_tile, vec_tile, factors[0], replicas
+    left_rows = sum_rows(replicas, ROW_PAD // LANES + VEC_TILES + 1)
+    flat_both, counts, vec_both, fac_both, err_stack, err_lefts, whole = gather(
+        cast_shard(master, size), count_tile, vec_tile, factors[0], errors, replicas, left_rows
     )
     low_both = flat_both.reshape(-1, LANES)
     count = jnp.sum(counts[:, 0, 0])
@@ -1434,33 +1577,12 @@
     pix = lax.dynamic_index_in_dim(pixels, sec, 0, keepdims=False)
     pick = (order[:, None] == jnp.arange(SEQ, dtype=jnp.int32)[None, :]).astype(bf16)
     pix_order = nn(pick, pix).astype(bf16)
-    pix_vis = pix_order[:VIS]
+    pix_vis = jnp.pad(pix_order[:VIS], ((0, 0), (0, PATCH_PAD - PATCH)))
     target = pix_order[VIS:]
     place = order[:, None]
     mask_col = mask_row[:, None]
     tail_row = ROW_PAD // LANES * RANK
-    tail_rows = (VEC_TILES + 1) * RANK
-    left_rows = sum_rows(replicas, ROW_PAD // LANES + VEC_TILES + 1)
     right_rows = sum_rows(replicas, max(COL_WIDTHS) // LANES)
-
-    def errs_for(section):
-        def run():
-            buf = None
-            lefts = []
-            start = 0
-            col_at = 0
-            for rows_n, cols_n in section_shapes(section):
-                buf, left = err_prep(errors, factors[0][:, col_at : col_at + cols_n], start, rows_n, cols_n, buf)
-                lefts.append(left)
-                start += rows_n * cols_n
-                col_at += cols_n
-            done = sum(left.shape[0] for left in lefts)
-            lefts.append(jnp.zeros((left_rows - done, LANES), f32))
-            return buf, jnp.concatenate(lefts)
-
-        return run
-
-    err_stack, err_lefts = lax.cond(sec == 0, errs_for(0), errs_for(1))
 
     kept, enc = encode(low_both, pix_vis, place[:VIS], angle_tables(DE), vec_both)
     given, grad_coded, sums_e, part_d = decode(
@@ -1502,28 +1624,9 @@
     norm = norm_row[0, 0]
     scale = jnp.minimum(1.0, clip_limit / (norm + 1e-06))
 
-    def finish_for(section):
-        def run():
-            mine = pairs_e if section == 0 else pairs_d
-            flat = other_e if section == 0 else other_d
-            theirs = [(flat[2 * i], flat[2 * i + 1]) for i in range(len(mine))]
-            bufs = None
-            start = 0
-            base = 0 if section == 0 else n_enc
-            for i, (rows_n, cols_n) in enumerate(section_shapes(section)):
-                bufs = finish(
-                    me_row, mine[i], theirs[i], err_stack, ortho, right_both, section,
-                    ROW_SPANS[base + i][1], COL_SPANS[base + i][1], start, gain, shard_len, bufs,
-                )
-                start += rows_n * cols_n
-            if start < FLAT:
-                bufs = [finish_tail(errors, start, bufs[0]), bufs[1]]
-            return bufs[0], bufs[1]
-
-        return run
-
-    me_row = replica_id.astype(jnp.int32).reshape(1)
-    new_errors, approx = lax.cond(sec == 0, finish_for(0), finish_for(1))
+    new_errors, approx = finish(
+        flat_e, flat_d, other_e, other_d, err_stack, ortho, right_both, whole, gain, shard_len
+    )
     own_part = lax.dynamic_slice_in_dim(approx, replica_id * size, size)
     used = jnp.where(sec == 0, *[sum(rows_n * cols_n for rows_n, cols_n in section_shapes(s)) // LANES for s in range(2)])
     inside = replica_id * size + lax.broadcasted_iota(jnp.int32, (size, 1), 0) < used

time: 545 us -> 494 us (0.906)
  Pallas kernels: 496 us -> 443 us
  local copies, waits for them, and re-layouts: 20 us -> 30.2 us
    pallas_call x14 -> x2, Pallas kernels: 108 us -> 60 us  [the longest x1 51.2 us: finish(): pl.pallas_call(functools.partial(finish_body, n_enc=n_enc, n_dec=n_dec, g...]
    unnamed x14 -> x17, local copies, waits for them, and re-layouts: 0.04 us -> 19.9 us
where the time goes in v5:
time: 494 us; the launch traced here: 487 us
  Pallas kernels  443 us (90%)
  local copies, waits for them, and re-layouts  30.2 us (6%)
  other arithmetic  11 us (2%)
    pallas_call x1, Pallas kernels, decode(): pl.pallas_call(functools.partial(decode_body, tail_row=tail_row, gain=gai...  138 us
    pallas_call x1, Pallas kernels, gather(): pl.pallas_call(functools.partial(gather_body, replicas=replicas, size=siz...  103 us
    pallas_call x2, Pallas kernels, all_sum(): pl.pallas_call(functools.partial(sum_body, replicas=replicas, n_enc=len(e...  58.7 us
    pallas_call x1, Pallas kernels, finish(): pl.pallas_call(functools.partial(finish_body, n_enc=n_enc, n_dec=n_dec, g...  51.2 us
    pallas_call x1, Pallas kernels, encode(): pl.pallas_call(encode_body, in_specs=[ANYWHERE] + [WHOLE] * 4, out_specs=...  26.9 us
    pallas_call x1, Pallas kernels, encode_back(): pl.pallas_call(functools.partial(encode_back_body, tail_row=tail_row, gai...  26.2 us
    pallas_call x1, Pallas kernels, rights(): pl.pallas_call(functools.partial(rights_body, n=n, scale=scale, gain=gain...  24.4 us
    unnamed x17, local copies, waits for them, and re-layouts  19.9 us

profile of v5, /device:TPU:1, one launch (start us, length us, event | category | flops | bytes accessed | tf_op | source)
XLA Modules:
  0.0 486.5 jit_solution(14874977806236485806)
XLA Ops:
  0.6 0.0 copy-start
  0.7 1.4 reduce_sum.18
  2.7 0.7 fusion.7
  3.4 0.7 constant_dynamic-slice_fusion.1
  4.1 0.6 broadcast_in_dim.25.cnt_ref
  4.7 0.7 convert_bitcast_fusion
  5.5 0.9 reduce.1
  6.4 0.6 pad_bitcast_fusion.vec_ref
  7.0 0.8 copy.24.place
  7.8 0.9 copy.26.mask
  8.7 0.0 copy-done
  8.7 0.9 fusion.2
  9.6 0.8 slice.35.target
  10.4 0.7 pad.9.pix.refs_17_.refs_6_.refs_8_
  11.1 1.1 copy.25.place
  12.2 2.5 cast.1.low_ref
  14.7 103.4 %gather.1 = (bf16[32,3528,128]{2,1,0:T(8,128)(2,1)}, f32[16,8,128]{2,1,0:T(8,128)}, f32[2,96,128]{2,1,0:T(8,128)}, f32[2,8,7680]{2,1,0:T(8,128)}, bf16[56448,128...) custom-call(bf16[3528,128]{1,0:T(8,128)(2,1)} %cast.1.low_ref, f32[8,128]{1,0:T(8,128)} %broadcast_in_dim.25.cnt_ref, ...), custom_call_target="tpu_custom_call" | custom-call | tf_op jit(solution)/shard_map/gather/pallas_call | solution.py:1421
  118.0 1.5 slice_reduce_fusion
  119.5 26.9 %encode.1 = (f32[256,768]{1,0:T(8,128)}, bf16[256,768]{1,0:T(8,128)(2,1)}, bf16[256,2304]{1,0:T(8,128)(2,1)}, f32[256,768]{1,0:T(8,128)}, f32[6,2,256]{2,1,0:T(2...) custom-call(bf16[112896,128]{1,0:T(8,128)(2,1)} %bitcast.25, ...), custom_call_target="tpu_custom_call" | custom-call | tf_op jit(solution)/shard_map/encode/pallas_call | solution.py:420
  146.4 137.8 %decode.1 = (bf16[1024,512]{1,0:T(8,128)(2,1)}, bf16[1024,1536]{1,0:T(8,128)(2,1)}, bf16[1024,512]{1,0:T(8,128)(2,1)}, bf16[1024,512]{1,0:T(8,128)(2,1)}, bf16[1...) custom-call(bf16[112896,128]{1,0:T(8,128)(2,1)} %bitcast.26, ...), custom_call_target="tpu_custom_call" | custom-call | tf_op jit(solution)/shard_map/decode/pallas_call | solution.py:575
  284.3 0.0 copy-start.4
  284.3 26.2 %encode_back.1 = (bf16[256,2304]{1,0:T(8,128)(2,1)}, bf16[256,768]{1,0:T(8,128)(2,1)}, bf16[256,3072]{1,0:T(8,128)(2,1)}, bf16[256,768]{1,0:T(8,128)(2,1)}, bf16...) custom-call(f32[256,3072]{1,0:T(8,128)} %get-tuple-element.89.refs_0_, f32[256,768]{1,0:T(8,128)} %get-tuple-element.90.refs_1_, ...), custom_call_target="tpu_custom_call" | custom-call | tf_op jit(solution)/shard_map/encode_back/pallas_call | solution.py:671
  310.5 0.0 copy-done.4
  310.5 1.8 pad_maximum_fusion.refs_0_
  312.3 31.0 %all_sum.2 = (f32[2,512,128]{2,1,0:T(8,128)}, bf16[256,3072]{1,0:T(8,128)(2,1)}, bf16[256,3072]{1,0:T(8,128)(2,1)}, bf16[1024,2048]{1,0:T(8,128)(2,1)}, bf16[1024,2048]{1,0:T(8,128)(2,1)}) custom-call(f32[2,512,128]{2,1,0:T(8,128)} %pad_maximum_fusion.refs_0_, f32[512,128]{1,0:T(8,128)} %get-tuple-element.126.refs_1_, ...), custom_call_target="tpu_custom_call" | custom-call | tf_op jit(solution)/shard_map/all_sum/pallas_call | solution.py:1537
  343.2 1.2 slice.33
  344.4 1.5 slice.30.vec_ref
  345.9 24.4 %rights.1 = (f32[2,8,5632]{2,1,0:T(8,128)}, f32[2,512,128]{2,1,0:T(8,128)}, f32[512,128]{1,0:T(8,128)}) custom-call(f32[2,512,128]{2,1,0:T(8,128)} %get-tuple-element.127.refs_0_, bf16[56448,128]{1,0:T(8,128)(2,1)} %get-tuple-element.128.refs_1_.refs_44_, bf16[256,768]{1,0:T(8,128)(2,1)} %get-tuple-element.88.refs_9_.refs_2_.refs_0_, ...), custom_call_target="tpu_custom_call" | custom-call | tf_op jit(solution)/shard_map/rights/pallas_call | solution.py:933
  370.3 27.8 %all_sum.3 = (f32[2,512,128]{2,1,0:T(8,128)}, bf16[256,768]{1,0:T(8,128)(2,1)}, bf16[256,2304]{1,0:T(8,128)(2,1)}, bf16[256,768]{1,0:T(8,128)(2,1)}, bf16[256,76...) custom-call(f32[2,512,128]{2,1,0:T(8,128)} %get-tuple-element.129.re, ...), custom_call_target="tpu_custom_call" | custom-call | tf_op jit(solution)/shard_map/all_sum/pallas_call | solution.py:1537
  398.1 2.8 final_right.1
  400.9 0.0 copy-start.7
  400.9 0.0 copy-start.3
  400.9 0.0 copy-start.2
  400.9 51.2 %finish.1 = (f32[1,1,7225344]{2,1,0:T(1,128)}, f32[56448,128]{1,0:T(8,128)}) custom-call(bf16[256,768]{1,0:T(8,128)(2,1)} %get-tuple-element.88.refs_9_.refs_2_.refs_0_, bf16[256,2304]{1,0:T(8,128)(2,1)} %get-tuple-element.107.refs_13_.refs_3_.refs_1_, ...), custom_call_target="tpu_custom_call", output_to_operand_aliasing={{0}: (47, {})} | custom-call | tf_op jit(solution)/shard_map/finish/pallas_call | solution.py:1135
  452.1 0.0 copy-start.5
  452.1 0.0 copy-start.6
  452.2 0.0 copy-done.7
  452.2 0.0 copy-done.3
  452.3 0.0 copy-done.2
  452.3 0.7 constant_dynamic-slice_fusion
  453.0 3.9 dynamic-slice_select_fusion.approx_ref
  456.9 0.0 copy-done.5
  456.9 0.0 copy-done.6
  456.9 0.8 multiply_subtract_fusion
  457.7 8.8 %update.1 = (f32[1,451584]{1,0:T(1,128)}, bf16[1,451584]{1,0:T(2,128)(2,1)}, f32[1,451584]{1,0:T(1,128)}) custom-call(f32[1,451584]{1,0:T(1,128)} %master_ref.1, f32[1,451584]{1,0:T(1,128)} %moment_ref.1, f32[3528,128]{1,0:T(8,128)} %dynamic-slice_select_fusion.approx_ref, f32[1,1]{1,0:T(1,128)} %min_shard_map.6.scale_ref), custom_call_target="tpu_custom_call" | custom-call | tf_op jit(solution)/shard_map/update/pallas_call | solution.py:1392
  466.4 0.0 copy-start.1
  466.4 19.9 %copy.33 = f32[1,1,7225344]{2,1,0:T(1,128)} copy(f32[1,1,7225344]{2,1,0:T(1,128)} %get-tuple-element.182) | data formatting | bytes 57802752
  486.3 0.0 copy-done.1
  (4 shorter events, 0.0 us)
Async XLA Ops:
  0.6 8.1 %copy-start = (bf16[2,1024,192]{1,2,0:T(8,128)(2,1)S(1)}, bf16[2,1024,192]{1,2,0:T(8,128)(2,1)}, u32[]{:S(2)}) copy-start(bf16[2,1024,192]{1,2,0:T(8,128)(2,1)} %param.12) | copy-start | bytes 2359300
  284.3 26.2 %copy-start.4 = (f32[512,128]{1,0:T(8,128)S(1)}, f32[512,128]{1,0:T(8,128)}, u32[]{:S(2)}) copy-start(f32[512,128]{1,0:T(8,128)} %get-tuple-element.125) | copy-start | bytes 786436
  400.9 51.3 %copy-start.7 = (f32[1,128]{1,0:T(1,128)S(1)}, f32[1,128]{1,0:T(1,128)}, u32[]{:S(2)}) copy-start(f32[1,128]{1,0:T(1,128)} %get-tuple-element.158) | copy-start | bytes 1540
  400.9 51.4 %copy-start.3 = (f32[2,96,128]{2,1,0:T(8,128)S(1)}, f32[2,96,128]{2,1,0:T(8,128)}, u32[]{:S(2)}) copy-start(f32[2,96,128]{2,1,0:T(8,128)} %slice.30.vec_ref) | copy-start | bytes 294916
  400.9 51.4 %copy-start.2 = (f32[2,8,7680]{2,1,0:T(8,128)S(1)}, f32[2,8,7680]{2,1,0:T(8,128)}, u32[]{:S(2)}) copy-start(f32[2,8,7680]{2,1,0:T(8,128)} %get-tuple-element.155.refs_46_) | copy-start | bytes 1474564
  452.1 4.8 copy-start.5
  452.1 4.8 copy-start.6
  466.4 19.9 %copy-start.1 = (bf16[2,1024,192]{1,2,0:T(8,128)(2,1)S(1)}, bf16[2,1024,192]{1,2,0:T(8,128)(2,1)}, u32[]{:S(2)}) copy-start(bf16[2,1024,192]{1,2,0:T(8,128)(2,1)} %param.12) | copy-start | bytes 2359300

commit v6 on v5

--- a/solution.py
+++ b/solution.py
@@ -120,21 +120,20 @@
     seq = k_ref.shape[0]
     scale = size ** (-0.5)
     fold = scale * math.log2(math.e)
+    turned = v_ref[...].T
 
     def one(step, carry):
         at = pl.ds(pl.multiple_of(step * rows_q, rows_q), rows_q)
         queries = q_ref[at, :]
-        total = jnp.zeros((rows_q, LANES), f32)
+        parts = []
         for head in range(LANES // size):
-            mask = head_mask(head, size)
-            scores = nt(k_ref[...], queries * mask)
+            scores = nt(k_ref[...], queries * head_mask(head, size))
             peak = jnp.max(scores, axis=0, keepdims=True) * fold
             power = jnp.exp2(scores * fold - peak)
             mass = jnp.sum(power, axis=0, keepdims=True)
-            share = jnp.transpose(jnp.broadcast_to(1.0 / mass, (8, rows_q)))[:, :1]
-            total = total + tn(power.astype(bf16), v_ref[...] * mask) * share
+            parts.append(nn(turned[head * size : (head + 1) * size], power.astype(bf16)) * (1.0 / mass))
             lse_ref[0, head : head + 1, at] = peak + jnp.log2(mass)
-        o_ref[at, :] = total
+        o_ref[at, :] = jnp.concatenate(parts, axis=0).T
         return carry
 
     lax.fori_loop(0, seq // rows_q, one, 0)
@@ -144,6 +143,7 @@
     seq = k_ref.shape[0]
     scale = size ** (-0.5)
     fold = scale * math.log2(math.e)
+    turned = k_ref[...].T
     dk_sum[...] = jnp.zeros_like(dk_sum)
     dv_sum[...] = jnp.zeros_like(dv_sum)
 
@@ -152,7 +152,7 @@
         queries = q_ref[at, :]
         grads = do_ref[at, :]
         prod = grads.astype(f32) * o_ref[at, :]
-        total = jnp.zeros((rows_q, LANES), f32)
+        parts = []
         high = prod.astype(bf16)
         rest = prod - high.astype(f32)
         middle = rest.astype(bf16)
@@ -168,8 +168,8 @@
             grad_s = (probs * (slope - delta)).astype(bf16)
             dv_sum[...] += nn(probs.astype(bf16), g_one)
             dk_sum[...] += nn(grad_s, q_one)
-            total = total + tn(grad_s, k_ref[...] * mask)
-        dq_ref[at, :] = (total * scale).astype(bf16)
+            parts.append(nn(turned[head * size : (head + 1) * size], grad_s))
+        dq_ref[at, :] = (jnp.concatenate(parts, axis=0).T * scale).astype(bf16)
         return carry
 
     lax.fori_loop(0, seq // rows_q, one, 0)
@@ -725,7 +725,7 @@
     return 256
 
 
-TAIL_STEPS = 12
+TAIL_STEPS = 24
 MOST = max(chunk_rows(*shape) * shape[1] for which in range(2) for shape in section_shapes(which)) // LANES
 
 
@@ -733,10 +733,13 @@
     return sum(rows_n * cols_n for rows_n, cols_n in section_shapes(section))
 
 
+TAIL_LENGTH = (FLAT - used_length(1)) // TAIL_STEPS
+
+
 class Prep:
-    def __init__(self, errors, factor, stack, left, whole, raw, wide, made, pieces, total, tail, raw_sem, out_sem):
-        self.errors, self.factor, self.stack, self.left, self.whole = errors, factor, stack, left, whole
-        self.raw, self.wide, self.made, self.pieces, self.total, self.tail = raw, wide, made, pieces, total, tail
+    def __init__(self, errors, factor, stack, left, raw, wide, made, pieces, total, raw_sem, out_sem):
+        self.errors, self.factor, self.stack, self.left = errors, factor, stack, left
+        self.raw, self.wide, self.made, self.pieces, self.total = raw, wide, made, pieces, total
         self.raw_sem, self.out_sem = raw_sem, out_sem
 
     def fetch(self, start, step, chunk):
@@ -807,30 +810,11 @@
 
         self.run(rows_n // rows, start, step, store, work)
 
-    def rest(self, section):
-        start = used_length(section)
-        step = (FLAT - start) // TAIL_STEPS // LANES
-
-        def store(chunk, slot):
-            at = pl.multiple_of(start + chunk * step * LANES, 1024)
-            return pltpu.make_async_copy(self.tail.at[slot], self.whole.at[:, :, pl.ds(at, step * LANES)], self.out_sem.at[slot])
-
-        def work(chunk, slot):
-            def one(part):
-                here = pl.ds(pl.multiple_of(part * 4096, 1024), 4096)
-                self.tail[slot, 0, :, here] = self.raw[slot, 0, :, here].astype(f32)
-
-            loop(step * LANES // 4096, one)
-
-        self.run(TAIL_STEPS, start, step, store, work)
-
-
 def prep_scratch():
-    tail = (FLAT - used_length(1)) // TAIL_STEPS
     dma = pltpu.SemaphoreType.DMA
     return [
         pltpu.VMEM((2, 1, 1, MOST * LANES), bf16), pltpu.VMEM((MOST, LANES), f32), pltpu.VMEM((2, MOST, LANES), bf16),
-        pltpu.VMEM((3 * RANK, FFE), bf16), pltpu.VMEM((256, 3 * RANK), f32), pltpu.VMEM((2, 1, 1, tail), f32), dma((2,)), dma((2,)),
+        pltpu.VMEM((3 * RANK, FFE), bf16), pltpu.VMEM((256, 3 * RANK), f32), dma((2,)), dma((2,)),
     ]
 
 
@@ -872,8 +856,8 @@
 
 def rights_body(*refs, n, scale, gain):
     sum_ref, err_ref, u_in, v_in = refs[0], refs[1], refs[2 : 2 + n], refs[2 + n : 2 + 2 * n]
-    ortho_ref, part_ref, extra_ref = refs[2 + 2 * n : 5 + 2 * n]
-    refs = refs[5 + 2 * n :]
+    ortho_ref, *part_refs, extra_ref = refs[2 + 2 * n : 6 + 2 * n]
+    refs = refs[6 + 2 * n :]
     u_refs, v_refs = refs[:n], refs[n : 2 * n]
     wide, ring, ring_sems, in_sems = refs[2 * n :]
     section = lax.axis_index(SEC)
@@ -898,7 +882,8 @@
     waits = [(reads.start(u_in[i], u_refs[i]), reads.start(v_in[i], v_refs[i])) for i in range(n)]
     ortho_stage(sum_ref, ortho_ref, wide, scale)
     extra_ref[...] = jnp.zeros_like(extra_ref)
-    part_ref[...] = jnp.zeros_like(part_ref)
+    for part_ref in part_refs:
+        part_ref[...] = jnp.zeros_like(part_ref)
     for which, plan in enumerate(plans):
 
         @pl.when(section == which)
@@ -912,18 +897,15 @@
                     pair = [ring[index % depth, (block + side) * rows : (block + side + 1) * rows] for side in range(2)]
                     part = join3(nn(pieces, jnp.concatenate(pair, axis=1)))
                     row = (col_at // LANES + block) * RANK
-                    if chunk == 0:
-                        put_tiles(extra_ref, row, part)
-                    else:
-                        for side in range(2):
-                            extra_ref[row + side * RANK : row + (side + 1) * RANK] += part[:, side * LANES : (side + 1) * LANES]
+                    for side in range(2):
+                        extra_ref[row + side * RANK : row + (side + 1) * RANK] += part[:, side * LANES : (side + 1) * LANES]
 
     for (wait_u, wait_v), u_ref, v_ref, (which, row_at, rows), (unused, col_at, cols) in zip(waits, u_refs, v_refs, ROW_SPANS, COL_SPANS):
         wait_u.wait()
         wait_v.wait()
         padded = tiles_of(rows) * LANES
         part = join3(nt(split3(ortho_ref[which, :, row_at : row_at + padded]), u_ref[...]))
-        put_tiles(part_ref.at[which], col_at // LANES * RANK, gain * join3(nn(split3(part), v_ref[...])))
+        put_tiles(part_refs[which], col_at // LANES * RANK, gain * join3(nn(split3(part), v_ref[...])))
 
 
 def rights(sums, err, us, vs, scale, gain, rows):
@@ -933,10 +915,8 @@
     return pl.pallas_call(
         functools.partial(rights_body, n=n, scale=scale, gain=gain),
         in_specs=[WHOLE] + [ANYWHERE] * (2 * n + 1),
-        out_specs=[WHOLE] * 3,
-        out_shape=[
-            jax.ShapeDtypeStruct((2, RANK, ROW_PAD), f32), jax.ShapeDtypeStruct((2, rows, LANES), f32), shape_of(rows, LANES)
-        ],
+        out_specs=[WHOLE] * 4,
+        out_shape=[jax.ShapeDtypeStruct((2, RANK, ROW_PAD), f32)] + [shape_of(rows, LANES)] * 3,
         scratch_shapes=[pltpu.VMEM(x.shape, bf16) for x in [*us, *vs]]
         + [pltpu.VMEM((RANK, FFE), f32), pltpu.VMEM((4, most, LANES), bf16), dma((4,)), dma((2 * n,))],
         compiler_params=pltpu.CompilerParams(vmem_limit_bytes=BIG),
@@ -944,8 +924,9 @@
     )(sums, err, *us, *vs)
 
 
-def final_right_body(sum_ref, ortho_ref, vec_ref, right_ref, norm_ref, *, scale):
-    squares = jnp.sum(vec_ref[...] * vec_ref[...], keepdims=True)[0]
+def final_right_body(sum_ref, ortho_ref, left_ref, right_ref, norm_ref, *, scale, tail_row):
+    vecs = left_ref[:, tail_row : tail_row + VEC_TILES * RANK]
+    squares = jnp.sum(vecs * vecs, keepdims=True)[0]
     for (section, start, width), (unused, row_at, row_width) in zip(COL_SPANS, ROW_SPANS):
         for tile in range(width // LANES):
             row = (start // LANES + tile) * RANK
@@ -963,15 +944,15 @@
     norm_ref[...] = jnp.broadcast_to(jnp.sqrt(squares), norm_ref.shape)
 
 
-def final_right(sums, ortho, vecs, cols, scale):
+def final_right(sums, ortho, lefts, cols, scale, tail_row):
     full = pl.BlockSpec(memory_space=pltpu.VMEM)
     return pl.pallas_call(
-        functools.partial(final_right_body, scale=scale),
+        functools.partial(final_right_body, scale=scale, tail_row=tail_row),
         in_specs=[full] * 3,
         out_specs=[full] * 2,
         out_shape=[jax.ShapeDtypeStruct((2, RANK, cols), f32), jax.ShapeDtypeStruct((1, LANES), f32)],
         name="final_right",
-    )(sums, ortho, vecs)
+    )(sums, ortho, lefts)
 
 
 def overlaps(first, count, me, shard):
@@ -989,8 +970,8 @@
 
 
 def finish_section(
-    section, heights, pairs, err, ortho, right, err_out, app_out, a_slots, b_slots, lhs, left, ring, made, kept,
-    pair_sems, ring_sem, made_sem, kept_sem, *, gain, shard,
+    section, heights, pairs, err, ortho, right, raw, err_out, app_out, a_slots, b_slots, lhs, left, ring, made, kept,
+    raw_in, raw_out, pair_sems, ring_sem, made_sem, kept_sem, raw_sem, tail_sem, *, gain, shard,
 ):
     plan = finish_plan(section, heights)
     offsets = [sum(entry[1] for entry in plan[:index]) for index in range(len(plan) + 1)]
@@ -1024,9 +1005,47 @@
             made.at[slot, :, :, pl.ds(0, count)], err_out.at[:, :, pl.ds(at, count)], made_sem.at[slot]
         )
 
+    steps = (FLAT - used_length(section)) // TAIL_LENGTH
+
+    def tail_at(step):
+        return pl.ds(pl.multiple_of(used_length(section) + step * TAIL_LENGTH, 1024), TAIL_LENGTH)
+
+    def tail_in(step):
+        slot = lax.rem(step, 2)
+        return pltpu.make_async_copy(raw.at[:, :, tail_at(step)], raw_in.at[slot], raw_sem.at[slot])
+
+    def tail_out(step):
+        slot = lax.rem(step, 2)
+        return pltpu.make_async_copy(raw_out.at[slot], err_out.at[:, :, tail_at(step)], tail_sem.at[slot])
+
+    def tail_step(step):
+        @pl.when(step < steps)
+        def _():
+            slot = lax.rem(step, 2)
+
+            @pl.when(step + 1 < steps)
+            def _():
+                tail_in(step + 1).start()
+
+            tail_in(step).wait()
+
+            @pl.when(step >= 2)
+            def _():
+                tail_out(step - 2).wait()
+
+            def one(part):
+                here = pl.ds(pl.multiple_of(part * 2048, 1024), 2048)
+                raw_out[slot, 0, :, here] = raw_in[slot, 0, :, here].astype(f32)
+
+            loop(TAIL_LENGTH // 2048, one)
+            tail_out(step).start()
+
+    per_chunk = -(-steps // len(flat_plan))
     for copy in load(0):
         copy.start()
     fetch(0, jnp.int32(0)).start()
+    if steps:
+        tail_in(jnp.int32(0)).start()
     for index, (start, count, rows, blocks, rows_n, height, row_at, col_at) in enumerate(plan):
         for copy in load(index):
             copy.wait()
@@ -1094,6 +1113,8 @@
 
             loop(blocks // 2, pair_one)
             store(index, chunk).start()
+            for extra in range(per_chunk):
+                tail_step((offsets[index] + chunk) * per_chunk + extra)
 
             @pl.when(keep)
             def _():
@@ -1105,12 +1126,14 @@
         loop(count, one)
     for old_index, old_chunk in flat_plan[-2:]:
         store(old_index, jnp.int32(old_chunk)).wait()
+    for step in range(max(steps - 2, 0), steps):
+        tail_out(jnp.int32(step)).wait()
 
 
 def finish_body(*refs, n_enc, n_dec, gain, shard, heights):
     mine, refs = refs[: n_enc + n_dec], refs[n_enc + n_dec :]
     theirs, refs = refs[: n_enc + n_dec], refs[n_enc + n_dec :]
-    err, ortho, right, unused, err_out, app_out = refs[:6]
+    err, ortho, right, raw, err_out, app_out = refs[:6]
     a_enc, b_enc, a_dec, b_dec = refs[6:10]
     section = lax.axis_index(SEC)
     for which, (a_slots, b_slots, lo, hi) in enumerate(((a_enc, b_enc, 0, n_enc), (a_dec, b_dec, n_enc, n_enc + n_dec))):
@@ -1118,12 +1141,12 @@
         @pl.when(section == which)
         def _():
             finish_section(
-                which, heights[which], (mine[lo:hi], theirs[lo:hi]), err, ortho, right, err_out, app_out, a_slots, b_slots,
+                which, heights[which], (mine[lo:hi], theirs[lo:hi]), err, ortho, right, raw, err_out, app_out, a_slots, b_slots,
                 *refs[10:], gain=gain, shard=shard,
             )
 
 
-def finish(mine_e, mine_d, theirs_e, theirs_d, err, ortho, right, whole, gain, shard):
+def finish(mine_e, mine_d, theirs_e, theirs_d, err, ortho, right, errors, gain, shard):
     n_enc, n_dec = len(mine_e), len(mine_d)
     heights = [[x.shape[0] for x in mine[::2]] for mine in (mine_e, mine_d)]
     dma = pltpu.SemaphoreType.DMA
@@ -1137,16 +1160,16 @@
         in_specs=[ANYWHERE] * (total + 1) + [WHOLE] * 2 + [ANYWHERE],
         out_specs=[ANYWHERE] * 2,
         out_shape=[jax.ShapeDtypeStruct((1, 1, FLAT), f32), jax.ShapeDtypeStruct((FLAT // LANES, LANES), f32)],
-        input_output_aliases={total + 3: 0},
         scratch_shapes=slots
         + [
             pltpu.VMEM((256, 2 * SEQ), bf16), pltpu.VMEM((256, 3 * RANK), bf16), pltpu.VMEM((2, MOST, LANES), bf16),
             pltpu.VMEM((2, 1, 1, MOST * LANES), f32), pltpu.VMEM((MOST, LANES), f32),
-            dma((2, 4)), dma((2,)), dma((2,)), dma(()),
+            pltpu.VMEM((2, 1, 1, TAIL_LENGTH), bf16), pltpu.VMEM((2, 1, 1, TAIL_LENGTH), f32),
+            dma((2, 4)), dma((2,)), dma((2,)), dma(()), dma((2,)), dma((2,)),
         ],
         compiler_params=pltpu.CompilerParams(vmem_limit_bytes=BIG),
         name="finish",
-    )(*mine_e, *mine_d, *theirs_e, *theirs_d, err, ortho, right, whole)
+    )(*mine_e, *mine_d, *theirs_e, *theirs_d, err, ortho, right, errors)
 
 
 MESH = pl.DeviceIdType.MESH
@@ -1174,7 +1197,7 @@
 
 
 def gather_body(
-    low_ref, cnt_ref, vec_ref, fac_ref, err_ref, flat_ref, cnts_ref, vec2_ref, fac2_ref, stack_ref, left_ref, whole_ref,
+    low_ref, cnt_ref, vec_ref, fac_ref, err_ref, flat_ref, cnts_ref, vec2_ref, fac2_ref, stack_ref, left_ref,
     send_sem, recv_sem, swap_sem, cnt_send, cnt_recv, side_send, side_recv, own_sem, *scratch, replicas, size,
 ):
     section, me = lax.axis_index(SEC), lax.axis_index(DP)
@@ -1308,9 +1331,9 @@
                             arrived(block, half)
                             across(block, half)
 
-    prep = Prep(err_ref, fac_ref, stack_ref, left_ref, whole_ref, *scratch)
+    prep = Prep(err_ref, fac_ref, stack_ref, left_ref, *scratch)
     left_ref[...] = jnp.zeros_like(left_ref)
-    shares = [[[0], [2], [3], [1], [4]], [[0, 1], [2], [3], [4, 5], [None]]]
+    shares = [[[0], [2], [3], [1], [4]], [[0, 1], [2], [3], [4], [5]]]
     for k in range(nz + 2):
         if k < nz:
             first(k)
@@ -1324,10 +1347,7 @@
                 @pl.when(section == which)
                 def _():
                     for index in shares[which][k]:
-                        if index is None:
-                            prep.rest(which)
-                        else:
-                            prep.matrix(which, index)
+                        prep.matrix(which, index)
 
     def drain(block, carry):
         at_x_, at_y_, at_z_ = lax.rem(block, nx), lax.rem(block // nx, ny), block // (nx * ny)
@@ -1377,27 +1397,33 @@
     side(fac_ref, fac2_ref, 1).wait()
 
 
-def update_body(master_ref, moment_ref, approx_ref, scale_ref, master_out, low_out, moment_out):
-    moment = moment_decay * moment_ref[...] + scale_ref[...] * approx_ref[...].reshape(moment_ref.shape)
+def update_body(master_ref, moment_ref, approx_ref, scale_ref, master_out, low_out, moment_out, own, sem):
+    size = own.shape[0]
+    first = lax.axis_index(DP) * size
+    at = pl.multiple_of(first, RANK) if approx_ref.shape[0] > size else 0
+    copy = pltpu.make_async_copy(approx_ref.at[pl.ds(at, size)], own, sem)
+    copy.start()
+    copy.wait()
+    used = used_rows(lax.axis_index(SEC))
+    inside = first + lax.broadcasted_iota(jnp.int32, (size, LANES), 0) < used
+    approx = jnp.where(inside, own[...], 0.0)
+    moment = moment_decay * moment_ref[...] + scale_ref[...] * approx.reshape(moment_ref.shape)
     moment_out[...] = moment
     master = master_ref[...] - learning_rate() * moment
     master_out[...] = master
     low_out[...] = master.astype(bf16)
 
 
-def update(master, moment, approx, scale):
-    size = approx.shape[0]
-    steps = 7 if size % 56 == 0 else 1
-    line = pl.BlockSpec((1, master.shape[1] // steps), lambda i: (0, i))
+def update(master, moment, approx, scale, size):
     return pl.pallas_call(
         update_body,
-        grid=(steps,),
-        in_specs=[line, line, pl.BlockSpec((size // steps, LANES), lambda i: (i, 0)), pl.BlockSpec((1, 1), lambda i: (0, 0))],
-        out_specs=[line] * 3,
+        in_specs=[WHOLE] * 2 + [ANYWHERE, WHOLE],
+        out_specs=[WHOLE] * 3,
         out_shape=[
             jax.ShapeDtypeStruct(master.shape, f32), jax.ShapeDtypeStruct(master.shape, bf16),
             jax.ShapeDtypeStruct(master.shape, f32),
         ],
+        scratch_shapes=[pltpu.VMEM((size, LANES), f32), pltpu.SemaphoreType.DMA(())],
         name="update",
     )(master, moment, approx, scale)
 
@@ -1421,7 +1447,7 @@
     return pl.pallas_call(
         functools.partial(gather_body, replicas=replicas, size=size),
         in_specs=[vmem] * 4 + [ANYWHERE],
-        out_specs=[ANYWHERE, vmem, vmem, vmem, ANYWHERE, vmem, ANYWHERE],
+        out_specs=[ANYWHERE, vmem, vmem, vmem, ANYWHERE, vmem],
         out_shape=[
             jax.ShapeDtypeStruct((2 * replicas, size, LANES), bf16),
             jax.ShapeDtypeStruct((replicas,) + cnt.shape, f32),
@@ -1429,7 +1455,6 @@
             jax.ShapeDtypeStruct((2,) + fac.shape, f32),
             jax.ShapeDtypeStruct((FLAT // LANES, LANES), bf16),
             jax.ShapeDtypeStruct((left_rows, LANES), f32),
-            jax.ShapeDtypeStruct((1, 1, FLAT), f32),
         ],
         scratch_shapes=[
             dma((replicas, 2, nx + ny + 1)), dma((replicas, 2)), dma((replicas, 2)),
@@ -1443,29 +1468,34 @@
 
 def sum_body(*refs, replicas, n_enc, n_dec):
     n = n_enc + n_dec
-    sum_run(*refs[:2], refs[2 : 2 + n], refs[2 + n], refs[3 + n : 3 + 2 * n], *refs[3 + 2 * n :], replicas=replicas, n_enc=n_enc)
+    sum_run(refs[:2], refs[2], refs[3 : 3 + n], refs[3 + n], refs[4 + n : 4 + 2 * n], *refs[4 + 2 * n :], replicas=replicas, n_enc=n_enc)
 
 
 def sum_run(
-    part_ref, extra_ref, given, total_ref, taken, mine, came, slots, seg, swap_send, swap_recv, send_a, recv_a, send_b, recv_b,
+    parts, extra_ref, given, total_ref, taken, mine, came, slots, seg, swap_send, swap_recv, send_a, recv_a, send_b, recv_b,
     give_sem, take_sem, *, replicas, n_enc,
 ):
     section, me = lax.axis_index(SEC), lax.axis_index(DP)
     other = 1 - section
-    rows = part_ref.shape[1]
+    rows = extra_ref.shape[0]
     size = rows // replicas
     meet(replicas)
 
     def rows_of(index):
         return pl.ds(pl.multiple_of(index * size, 8), size)
 
-    swap = pltpu.make_async_remote_copy(
-        src_ref=part_ref.at[other], dst_ref=came, send_sem=swap_send.at[0], recv_sem=swap_recv.at[0],
-        device_id={SEC: other}, device_id_type=MESH,
-    )
-    swap.start()
-    mine[...] = part_ref[section] + extra_ref[...]
-    swap.wait()
+    for which in range(2):
+
+        @pl.when(section == which)
+        def _():
+            swap = pltpu.make_async_remote_copy(
+                src_ref=parts[1 - which], dst_ref=came, send_sem=swap_send.at[0], recv_sem=swap_recv.at[0],
+                device_id={SEC: other}, device_id_type=MESH,
+            )
+            swap.start()
+            mine[...] = parts[which][...] + extra_ref[...]
+            swap.wait()
+
 
     def give(i):
         return pltpu.make_async_remote_copy(
@@ -1526,8 +1556,8 @@
             give(i).wait_recv()
 
 
-def all_sum(part, extra, replicas, collective_id, enc=(), dec=()):
-    rows = part.shape[1]
+def all_sum(parts, extra, replicas, collective_id, enc=(), dec=()):
+    rows = extra.shape[0]
     vmem = pl.BlockSpec(memory_space=pltpu.VMEM)
     dma = pltpu.SemaphoreType.DMA
     size = rows // replicas
@@ -1536,9 +1566,9 @@
     anywhere = pl.BlockSpec(memory_space=pl.ANY)
     outs = pl.pallas_call(
         functools.partial(sum_body, replicas=replicas, n_enc=len(enc), n_dec=len(dec)),
-        in_specs=[vmem, vmem] + [anywhere] * n,
+        in_specs=[vmem] * 3 + [anywhere] * n,
         out_specs=[vmem] + [anywhere] * n,
-        out_shape=[jax.ShapeDtypeStruct(part.shape, f32)] + [jax.ShapeDtypeStruct(x.shape, x.dtype) for x in given],
+        out_shape=[jax.ShapeDtypeStruct((2, rows, LANES), f32)] + [jax.ShapeDtypeStruct(x.shape, x.dtype) for x in given],
         scratch_shapes=[
             pltpu.VMEM((rows, LANES), f32), pltpu.VMEM((rows, LANES), f32),
             pltpu.VMEM((replicas, size, LANES), f32), pltpu.VMEM((size, LANES), f32),
@@ -1547,7 +1577,7 @@
         ],
         compiler_params=pltpu.CompilerParams(collective_id=collective_id, has_side_effects=True),
         name="all_sum",
-    )(part, extra, *given)
+    )(*parts, extra, *given)
     return outs[0], outs[1 : 1 + len(enc)], outs[1 + len(enc) :]
 
 
@@ -1564,7 +1594,7 @@
     count_tile = jnp.full((RANK, LANES), jnp.sum(loss_mask).astype(f32))
     vec_tile = jnp.pad(vectors[0], (0, VEC_TILES * RANK * LANES - VLEN)).reshape(-1, LANES)
     left_rows = sum_rows(replicas, ROW_PAD // LANES + VEC_TILES + 1)
-    flat_both, counts, vec_both, fac_both, err_stack, err_lefts, whole = gather(
+    flat_both, counts, vec_both, fac_both, err_stack, err_lefts = gather(
         cast_shard(master, size), count_tile, vec_tile, factors[0], errors, replicas, left_rows
     )
     low_both = flat_both.reshape(-1, LANES)
@@ -1601,38 +1631,35 @@
     n_enc = len(pairs_e)
     flat_e = [x for pair in pairs_e for x in pair]
     flat_d = [x for pair in pairs_d for x in pair]
-    left_part = jnp.stack([part_e, part_d])
     early_e = [5, 6]
     late_e = [i for i in range(len(flat_e)) if i not in early_e]
     early_d = [5, 6]
     late_d = [i for i in range(len(flat_d)) if i not in early_d]
     left_sum, first_e, first_d = all_sum(
-        left_part, err_lefts, replicas, 3, [flat_e[i] for i in early_e], [flat_d[i] for i in early_d]
+        (part_e, part_d), err_lefts, replicas, 3, [flat_e[i] for i in early_e], [flat_d[i] for i in early_d]
     )
     vec_sum = left_sum[:, tail_row : tail_row + VEC_TILES * RANK]
     loss_sum = left_sum[1, tail_row + VEC_TILES * RANK, 0]
 
-    ortho, right_part, err_rights = rights(
+    ortho, *right_parts, err_rights = rights(
         left_sum, err_stack, [a for a, b in pairs], [b for a, b in pairs], 1.0 / replicas, gain, right_rows
     )
     sums, second_e, second_d = all_sum(
-        right_part, err_rights, replicas, 4, [flat_e[i] for i in late_e], [flat_d[i] for i in late_d]
+        right_parts, err_rights, replicas, 4, [flat_e[i] for i in late_e], [flat_d[i] for i in late_d]
     )
     other_e = [x for i, x in sorted([*zip(early_e, first_e), *zip(late_e, second_e)], key=lambda entry: entry[0])]
     other_d = [x for i, x in sorted([*zip(early_d, first_d), *zip(late_d, second_d)], key=lambda entry: entry[0])]
-    right_both, norm_row = final_right(sums, ortho, vec_sum, factors.shape[2], 1.0 / replicas)
+    right_both, norm_row = final_right(sums, ortho, left_sum, factors.shape[2], 1.0 / replicas, tail_row)
     norm = norm_row[0, 0]
     scale = jnp.minimum(1.0, clip_limit / (norm + 1e-06))
 
     new_errors, approx = finish(
-        flat_e, flat_d, other_e, other_d, err_stack, ortho, right_both, whole, gain, shard_len
+        flat_e, flat_d, other_e, other_d, err_stack, ortho, right_both, errors, gain, shard_len
     )
-    own_part = lax.dynamic_slice_in_dim(approx, replica_id * size, size)
-    used = jnp.where(sec == 0, *[sum(rows_n * cols_n for rows_n, cols_n in section_shapes(s)) // LANES for s in range(2)])
-    inside = replica_id * size + lax.broadcasted_iota(jnp.int32, (size, 1), 0) < used
-    own_part = jnp.where(inside, own_part, 0.0)
+    if size % RANK:
+        approx = lax.dynamic_slice_in_dim(approx, replica_id * size, size)
     rate = learning_rate()
-    new_master, new_low, new_moment = update(master, momentum, own_part, scale.reshape(1, 1))
+    new_master, new_low, new_moment = update(master, momentum, approx, scale.reshape(1, 1), size)
     vec_own = lax.dynamic_index_in_dim(vec_sum, sec, 0, keepdims=False).reshape(-1)[:VLEN]
     new_vm = moment_decay * vec_moment[0] + scale * vec_own
     new_vectors = vectors[0] - rate * new_vm

time: 494 us -> 481 us (0.974)
  local copies, waits for them, and re-layouts: 30.2 us -> 9.7 us
  Pallas kernels: 443 us -> 457 us
  other arithmetic: 11 us -> 5.29 us
    pallas_call x1, Pallas kernels: 51.2 us -> 73 us  [finish(): pl.pallas_call(functools.partial(finish_body, n_enc=n_enc, n_dec=n_dec, g...]
    unnamed x17 -> x10, local copies, waits for them, and re-layouts: 19.9 us -> 0.03 us
where the time goes in v6:
time: 481 us; the launch traced here: 475 us
  Pallas kernels  457 us (95%)
  local copies, waits for them, and re-layouts  9.7 us (2%)
  other arithmetic  5.29 us (1%)
    pallas_call x1, Pallas kernels, decode(): pl.pallas_call(functools.partial(decode_body, tail_row=tail_row, gain=gai...  134 us
    pallas_call x1, Pallas kernels, gather(): pl.pallas_call(functools.partial(gather_body, replicas=replicas, size=siz...  103 us
    pallas_call x1, Pallas kernels, finish(): pl.pallas_call(functools.partial(finish_body, n_enc=n_enc, n_dec=n_dec, g...  73 us
    pallas_call x2, Pallas kernels, all_sum(): pl.pallas_call(functools.partial(sum_body, replicas=replicas, n_enc=len(e...  56.1 us
    pallas_call x1, Pallas kernels, encode(): pl.pallas_call(encode_body, in_specs=[ANYWHERE] + [WHOLE] * 4, out_specs=...  26.4 us
    pallas_call x1, Pallas kernels, encode_back(): pl.pallas_call(functools.partial(encode_back_body, tail_row=tail_row, gai...  26.3 us
    pallas_call x1, Pallas kernels, rights(): pl.pallas_call(functools.partial(rights_body, n=n, scale=scale, gain=gain...  24 us

profile of v6, /device:TPU:1, one launch (start us, length us, event | category | flops | bytes accessed | tf_op | source)
XLA Modules:
  0.0 474.7 jit_solution(3408938348281333512)
XLA Ops:
  0.6 0.0 copy-start
  0.7 1.4 reduce_sum.18
  2.7 0.7 fusion.7
  3.4 0.7 constant_dynamic-slice_fusion.1
  4.1 0.6 broadcast_in_dim.4.cnt_ref
  4.7 0.7 convert_bitcast_fusion
  5.4 0.9 reduce.1
  6.4 0.6 pad_bitcast_fusion.vec_ref
  7.0 0.8 copy.23.place
  7.8 1.0 copy.25.mask
  8.7 0.0 copy-done
  8.7 0.9 fusion.2
  9.6 0.8 slice.35.target
  10.4 0.7 pad.9.pix.refs_17_.refs_6_.refs_9_.refs_8_
  11.1 1.0 copy.24.place
  12.1 2.5 cast.1.low_ref
  14.6 103.4 %gather.1 = (bf16[32,3528,128]{2,1,0:T(8,128)(2,1)}, f32[16,8,128]{2,1,0:T(8,128)}, f32[2,96,128]{2,1,0:T(8,128)}, f32[2,8,7680]{2,1,0:T(8,128)}, bf16[56448,128]{1,0:T(8,128)(2,1)}, /*index=5*/f32[512,128]{1,0:T(8,128)}) custom-call(bf16[3528,128]{1,0:T(8,128)(2,1)} %cast.1.low_ref, f32[8,128]{1,0:T(8,128)} %broadcast_in_dim.4.cnt_ref, ...), custom_call_target="tpu_custom_call" | custom-call | tf_op jit(solution)/shard_map/gather/pallas_call | solution.py:1447
  118.0 1.5 slice_reduce_fusion
  119.5 26.4 %encode.1 = (f32[256,768]{1,0:T(8,128)}, bf16[256,768]{1,0:T(8,128)(2,1)}, bf16[256,2304]{1,0:T(8,128)(2,1)}, f32[256,768]{1,0:T(8,128)}, f32[6,2,256]{2,1,0:T(2...) custom-call(bf16[112896,128]{1,0:T(8,128)(2,1)} %bitcast.23, ...), custom_call_target="tpu_custom_call" | custom-call | tf_op jit(solution)/shard_map/encode/pallas_call | solution.py:420
  145.9 133.9 %decode.1 = (bf16[1024,512]{1,0:T(8,128)(2,1)}, bf16[1024,1536]{1,0:T(8,128)(2,1)}, bf16[1024,512]{1,0:T(8,128)(2,1)}, bf16[1024,512]{1,0:T(8,128)(2,1)}, bf16[1...) custom-call(bf16[112896,128]{1,0:T(8,128)(2,1)} %bitcast.24, ...), custom_call_target="tpu_custom_call" | custom-call | tf_op jit(solution)/shard_map/decode/pallas_call | solution.py:575
  279.8 26.3 %encode_back.1 = (bf16[256,2304]{1,0:T(8,128)(2,1)}, bf16[256,768]{1,0:T(8,128)(2,1)}, bf16[256,3072]{1,0:T(8,128)(2,1)}, bf16[256,768]{1,0:T(8,128)(2,1)}, bf16...) custom-call(f32[256,3072]{1,0:T(8,128)} %get-tuple-element.89.refs_0_, f32[256,768]{1,0:T(8,128)} %get-tuple-element.90.refs_1_, ...), custom_call_target="tpu_custom_call" | custom-call | tf_op jit(solution)/shard_map/encode_back/pallas_call | solution.py:671
  306.1 28.7 %all_sum.2 = (f32[2,512,128]{2,1,0:T(8,128)}, bf16[256,3072]{1,0:T(8,128)(2,1)}, bf16[256,3072]{1,0:T(8,128)(2,1)}, bf16[1024,2048]{1,0:T(8,128)(2,1)}, bf16[1024,2048]{1,0:T(8,128)(2,1)}) custom-call(f32[512,128]{1,0:T(8,128)} %get-tuple-element.124.refs_0_, f32[512,128]{1,0:T(8,128)} %get-tuple-element.125.refs_1_, f32[512,128]{1,0:T(8,128)} %get-tuple-element.126.refs_2_, ...), custom_call_target="tpu_custom_call" | custom-call | tf_op jit(solution)/shard_map/all_sum/pallas_call | solution.py:1567
  334.9 1.2 slice.33
  336.1 0.9 slice.31
  337.0 24.0 %rights.1 = (f32[2,8,5632]{2,1,0:T(8,128)}, f32[512,128]{1,0:T(8,128)}, f32[512,128]{1,0:T(8,128)}, f32[512,128]{1,0:T(8,128)}) custom-call(f32[2,512,128]{2,1,0:T(8,128)} %get-tuple-element.127.refs_0_.left_ref, bf16[56448,128]{1,0:T(8,128)(2,1)} %get-tuple-element.128.refs_1_.refs_44_, bf16[256,768]{1,0:T(8,128)(2,1)} %get-tuple-element.88.refs_9_.refs_2_.refs_3_.refs_0_, ...), custom_call_target="tpu_custom_call" | custom-call | tf_op jit(solution)/shard_map/rights/pallas_call | solution.py:915
  360.9 27.4 %all_sum.3 = (f32[2,512,128]{2,1,0:T(8,128)}, bf16[256,768]{1,0:T(8,128)(2,1)}, bf16[256,2304]{1,0:T(8,128)(2,1)}, bf16[256,768]{1,0:T(8,128)(2,1)}, bf16[256,76...) custom-call(f32[512,128]{1,0:T(8,128)} %get-tuple-element.129.refs_0, ...), custom_call_target="tpu_custom_call" | custom-call | tf_op jit(solution)/shard_map/all_sum/pallas_call | solution.py:1567
  388.3 2.9 final_right.1
  392.0 0.0 copy-start.2
  392.0 73.0 %finish.1 = (f32[1,1,7225344]{2,1,0:T(1,128)}, f32[56448,128]{1,0:T(8,128)}) custom-call(bf16[256,768]{1,0:T(8,128)(2,1)} %get-tuple-element.88.refs_9_.refs_2_.refs_3_.refs_0_, bf16[256,2304]{1,0:T(8,128)(2,1)} %get-tuple-element.107.refs_13_.refs_4_.refs_1_, bf16[256,768]{1,0:T(8,128)(2,1)} %get-tuple-element.97.refs_8_.refs_3_.refs_5_.refs_2_, ...), custom_call_target="tpu_custom_call" | custom-call | tf_op jit(solution)/shard_map/finish/pallas_call | solution.py:1158
  465.0 0.0 copy-done.2
  465.0 0.7 constant_dynamic-slice_fusion
  465.7 0.0 copy-start.3
  465.7 0.0 copy-start.4
  465.7 0.0 copy-start.1
  465.7 8.0 %update.1 = (f32[1,451584]{1,0:T(1,128)}, bf16[1,451584]{1,0:T(2,128)(2,1)}, f32[1,451584]{1,0:T(1,128)}) custom-call(f32[1,451584]{1,0:T(1,128)} %master_ref.1, f32[1,451584]{1,0:T(1,128)} %moment_ref.1, f32[56448,128]{1,0:T(8,128)} %get-tuple-element.157.approx_ref, f32[1,1]{1,0:T(1,128)} %min_shard_map.6.scale_ref), custom_call_target="tpu_custom_call" | custom-call | tf_op jit(solution)/shard_map/update/pallas_call | solution.py:1418
  473.8 0.0 copy-done.3
  473.8 0.0 copy-done.4
  473.8 0.8 multiply_subtract_fusion
  474.5 0.0 copy-done.1
  (3 shorter events, 0.0 us)
Async XLA Ops:
  0.6 8.1 %copy-start = (bf16[2,1024,192]{1,2,0:T(8,128)(2,1)S(1)}, bf16[2,1024,192]{1,2,0:T(8,128)(2,1)}, u32[]{:S(2)}) copy-start(bf16[2,1024,192]{1,2,0:T(8,128)(2,1)} %param.12) | copy-start | bytes 2359300
  392.0 73.0 %copy-start.2 = (f32[2,8,7680]{2,1,0:T(8,128)S(1)}, f32[2,8,7680]{2,1,0:T(8,128)}, u32[]{:S(2)}) copy-start(f32[2,8,7680]{2,1,0:T(8,128)} %get-tuple-element.156.refs_46_) | copy-start | bytes 1474564
  465.7 8.0 %copy-start.3 = (f32[1,11520]{1,0:T(1,128)S(1)}, f32[1,11520]{1,0:T(1,128)}, u32[]{:S(2)}) copy-start(f32[1,11520]{1,0:T(1,128)} %param.18) | copy-start | bytes 138244
  465.7 8.0 %copy-start.4 = (f32[1,11520]{1,0:T(1,128)S(1)}, f32[1,11520]{1,0:T(1,128)}, u32[]{:S(2)}) copy-start(f32[1,11520]{1,0:T(1,128)} %param.19) | copy-start | bytes 138244
  465.7 8.8 %copy-start.1 = (bf16[2,1024,192]{1,2,0:T(8,128)(2,1)S(1)}, bf16[2,1024,192]{1,2,0:T(8,128)(2,1)}, u32[]{:S(2)}) copy-start(bf16[2,1024,192]{1,2,0:T(8,128)(2,1)} %param.12) | copy-start | bytes 2359300
